TPU v7x, 32 devices: a whole 2x2x4 slice. The times are simulated.
32 devices in a mesh: dp: 8 (over y, x, core), tensor: 4 (over z).
Axes of the slice: x: 2, y: 2, z: 4, core: 2. Of those that a mesh axis runs over, the one named last changes fastest.
Arguments:
- tokens: bfloat16 [8192, 1536], P(('dp', 'tensor')), may hold values from -6 to 6
- segments: int32 [8, 1024], P('dp'), may hold values from 0 to 3, never falling along the last dimension, each value on 1 to 512 neighbouring positions
- gain_one: bfloat16 [1536], P('dp'), may hold values from 0.25 to 1.75
- query_w: bfloat16 [1536, 1536], P('dp', 'tensor'), may hold values from -0.15625 to 0.15625
- query_b: bfloat16 [1536], P('tensor'), may hold values from -3 to 3
- key_w: bfloat16 [1536, 256], P('dp'), may hold values from -0.15625 to 0.15625
- key_b: bfloat16 [256], replicated, may hold values from -3 to 3
- value_w: bfloat16 [1536, 256], P('dp'), may hold values from -0.15625 to 0.15625
- value_b: bfloat16 [256], replicated, may hold values from -3 to 3
- out_w: bfloat16 [1536, 1536], P('dp', 'tensor'), may hold values from -0.4375 to 0.4375
- gain_two: bfloat16 [1536], P('dp'), may hold values from 0.25 to 1.75
- gate_w: bfloat16 [1536, 8960], P('dp', 'tensor'), may hold values from -0.15625 to 0.15625
- up_w: bfloat16 [1536, 8960], P('dp', 'tensor'), may hold values from -0.15625 to 0.15625
- down_w: bfloat16 [1536, 8960], P('dp', 'tensor'), may hold values from -0.0625 to 0.0625
- cotangent: bfloat16 [8192, 1536], P(('dp', 'tensor')), may hold values from -6 to 6
Outputs:
- mixed: bfloat16 [8192, 1536], P(('dp', 'tensor'))
- input_grad: bfloat16 [8192, 1536], P(('dp', 'tensor'))
- grad_gain_one: float32 [1536], P(('dp', 'tensor'))
- grad_query_w: float32 [1536, 1536], P('dp', 'tensor')
- grad_query_b: float32 [1536], P(('dp', 'tensor'))
- grad_key_w: float32 [1536, 256], P(('dp', 'tensor'))
- grad_key_b: float32 [256], replicated
- grad_value_w: float32 [1536, 256], P(('dp', 'tensor'))
- grad_value_b: float32 [256], replicated
- grad_out_w: float32 [1536, 1536], P('dp', 'tensor')
- grad_gain_two: float32 [1536], P(('dp', 'tensor'))
- grad_gate_w: float32 [1536, 8960], P('dp', 'tensor')
- grad_up_w: float32 [1536, 8960], P('dp', 'tensor')
- grad_down_w: float32 [1536, 8960], P('dp', 'tensor')
Inputs may be any that keep to these rules, and one draw needn't show every extreme that they name: `segments`: in each sequence of 1024 positions the document numbers never fall; each of the 4 documents covers 1 to 512 positions, and one covers exactly 512.
All inputs are finite; a program needn't handle non-finite values.
Results may differ from a plain program's by a relative error of at most 0.02.
Values may be sent and summed in bfloat16 or wider, within the bound.
A program may use at most 256 MiB of HBM per device.

v0:
```python
import jax
import jax.numpy as jnp
from jax import lax
from jax.sharding import PartitionSpec as P

KV_HEADS = 2
HEAD_DIM = 128


EPSILON = 1e-06
ROPE_BASE = 1000000.0
NEGATIVE = -1e30


def angle_tables(length, head_width):
    position = jnp.arange(length, dtype=jnp.float32)
    exponent = jnp.arange(head_width // 2, dtype=jnp.float32) * (2.0 / head_width)
    frequency = ROPE_BASE ** (-exponent)
    angle = position[:, None] * frequency[None, :]
    return (jnp.cos(angle), jnp.sin(angle))


def rotate(values, cosine, sine):
    half_width = values.shape[-1] // 2
    first_half = values[..., :half_width]
    second_half = values[..., half_width:]
    return jnp.concatenate(
        [first_half * cosine - second_half * sine, second_half * cosine + first_half * sine],
        axis=-1,
    )


def rotate_back(grads, cosine, sine):
    half_width = grads.shape[-1] // 2
    first_half = grads[..., :half_width]
    second_half = grads[..., half_width:]
    return jnp.concatenate(
        [first_half * cosine + second_half * sine, second_half * cosine - first_half * sine],
        axis=-1,
    )


def contract_rows(left, right):
    return lax.dot_general(
        left, right, (((0,), (0,)), ((), ())), preferred_element_type=jnp.float32
    )


def contract_cols(left, right):
    return lax.dot_general(
        left, right, (((1,), (1,)), ((), ())), preferred_element_type=jnp.float32
    )


def masked_scores(query_rot, key_rot, allowed, scale):
    scores = (
        jnp.einsum("thd,sd->hts", query_rot, key_rot, preferred_element_type=jnp.float32) * scale
    )
    return jnp.where(allowed[None, :, :], scores, NEGATIVE)


def norm_back(upstream, unit, inverse, gain):
    scaled = upstream * gain
    gain_term = jnp.sum(upstream * unit, axis=0)
    input_term = inverse * (scaled - unit * jnp.mean(scaled * unit, axis=-1, keepdims=True))
    return (gain_term, input_term)


def local(
    tokens,
    segments,
    gain_one,
    query_w,
    query_b,
    key_w,
    key_b,
    value_w,
    value_b,
    out_w,
    gain_two,
    gate_w,
    up_w,
    down_w,
    cotangent,
):
    model_width = tokens.shape[1]
    tensor_size = lax.axis_size("tensor")
    tensor_rank = lax.axis_index("tensor")
    head_width = HEAD_DIM
    local_heads = query_w.shape[1] // head_width
    query_width = local_heads * head_width
    kv_width = key_w.shape[1]
    own_start = tensor_rank * KV_HEADS // tensor_size * head_width
    scale = head_width ** (-0.5)
    (
        full_gain_one,
        full_query,
        full_key,
        full_value,
        full_out,
        full_gain_two,
        full_gate,
        full_up,
        full_down,
    ) = (
        lax.all_gather(gain_one, "dp", axis=0, tiled=True),
        lax.all_gather(query_w, "dp", axis=0, tiled=True),
        lax.all_gather(key_w, "dp", axis=0, tiled=True),
        lax.all_gather(value_w, "dp", axis=0, tiled=True),
        lax.all_gather(out_w, "dp", axis=0, tiled=True),
        lax.all_gather(gain_two, "dp", axis=0, tiled=True),
        lax.all_gather(gate_w, "dp", axis=0, tiled=True),
        lax.all_gather(up_w, "dp", axis=0, tiled=True),
        lax.all_gather(down_w, "dp", axis=0, tiled=True),
    )
    gain_one_wide = full_gain_one.astype(jnp.float32)
    gain_two_wide = full_gain_two.astype(jnp.float32)
    inputs = tokens.astype(jnp.float32)
    inverse_one = lax.rsqrt(jnp.mean(inputs * inputs, axis=-1, keepdims=True) + EPSILON)
    unit_one = inputs * inverse_one
    normed_one = (unit_one * gain_one_wide).astype(jnp.bfloat16)
    rows_one = lax.all_gather(normed_one, "tensor", axis=0, tiled=True)
    seq_length = rows_one.shape[0]
    key_own = lax.dynamic_slice_in_dim(full_key, own_start, head_width, 1)
    value_own = lax.dynamic_slice_in_dim(full_value, own_start, head_width, 1)
    key_bias_own = lax.dynamic_slice_in_dim(key_b, own_start, head_width, 0).astype(jnp.float32)
    value_bias_own = lax.dynamic_slice_in_dim(value_b, own_start, head_width, 0).astype(jnp.float32)
    joined = jnp.concatenate([full_query, key_own, value_own], axis=1)
    projected = jnp.dot(rows_one, joined, preferred_element_type=jnp.float32)
    query_lin = projected[:, :query_width] + query_b.astype(jnp.float32)
    key_lin = projected[:, query_width : query_width + head_width] + key_bias_own
    value_lin = projected[:, query_width + head_width :] + value_bias_own
    cosine, sine = angle_tables(seq_length, head_width)
    query_rot = rotate(
        query_lin.reshape(seq_length, local_heads, head_width), cosine[:, None, :], sine[:, None, :]
    ).astype(jnp.bfloat16)
    key_rot = rotate(key_lin, cosine, sine).astype(jnp.bfloat16)
    value_low = value_lin.astype(jnp.bfloat16)
    segment = segments[0]
    positions = jnp.arange(seq_length)
    allowed = (segment[:, None] == segment[None, :]) & (positions[None, :] <= positions[:, None])
    masked = masked_scores(query_rot, key_rot, allowed, scale)
    largest = jnp.max(masked, axis=-1, keepdims=True)
    log_total = largest + jnp.log(jnp.sum(jnp.exp(masked - largest), axis=-1, keepdims=True))
    probs_low = jnp.exp(masked - log_total).astype(jnp.bfloat16)
    context = jnp.einsum("hts,sd->thd", probs_low, value_low, preferred_element_type=jnp.float32)
    context = context.reshape(seq_length, query_width).astype(jnp.bfloat16)
    piece = context
    attended = lax.psum_scatter(
        contract_cols(piece, full_out), "tensor", scatter_dimension=0, tiled=True
    )
    middle = inputs + attended
    inverse_two = lax.rsqrt(jnp.mean(middle * middle, axis=-1, keepdims=True) + EPSILON)
    unit_two = middle * inverse_two
    normed_two = (unit_two * gain_two_wide).astype(jnp.bfloat16)
    rows_two = lax.all_gather(normed_two, "tensor", axis=0, tiled=True)
    ff_local = full_gate.shape[1]
    gate_up_w = jnp.concatenate([full_gate, full_up], axis=1)
    gate_up = jnp.dot(rows_two, gate_up_w, preferred_element_type=jnp.float32)
    gate = gate_up[:, :ff_local]
    upper = gate_up[:, ff_local:]
    sigmoid = jax.nn.sigmoid(gate)
    hidden_low = (gate * sigmoid * upper).astype(jnp.bfloat16)
    piece = hidden_low
    ffn_sum = lax.psum_scatter(
        contract_cols(piece, full_down).astype(jnp.bfloat16),
        "tensor",
        scatter_dimension=0,
        tiled=True,
    ).astype(jnp.float32)
    mixed = (middle + ffn_sum).astype(jnp.bfloat16)
    cot_rows = lax.all_gather(cotangent, "tensor", axis=0, tiled=True)
    d_hidden = jnp.dot(cot_rows, full_down, preferred_element_type=jnp.float32)
    d_upper = d_hidden * gate * sigmoid
    d_gate = d_hidden * upper * sigmoid * (1.0 + gate * (1.0 - sigmoid))
    d_gate_up = jnp.concatenate([d_gate, d_upper], axis=1).astype(jnp.bfloat16)
    grad_down = contract_rows(cot_rows, hidden_low)
    grad_gate_up = contract_rows(rows_two, d_gate_up)
    grad_gate = grad_gate_up[:, :ff_local]
    grad_up = grad_gate_up[:, ff_local:]
    piece = d_gate_up
    d_normed_two = lax.psum_scatter(
        contract_cols(piece, gate_up_w), "tensor", scatter_dimension=0, tiled=True
    )
    gain_two_term, d_from_two = norm_back(d_normed_two, unit_two, inverse_two, gain_two_wide)
    d_middle = cotangent.astype(jnp.float32) + d_from_two
    attn_rows_grad = lax.all_gather(d_middle.astype(jnp.bfloat16), "tensor", axis=0, tiled=True)
    d_context = jnp.dot(attn_rows_grad, full_out, preferred_element_type=jnp.float32).astype(
        jnp.bfloat16
    )
    grad_out = contract_rows(attn_rows_grad, context)
    d_context = d_context.reshape(seq_length, local_heads, head_width)
    masked_again = masked_scores(query_rot, key_rot, allowed, scale)
    probs = jnp.exp(masked_again - log_total)
    d_probs = jnp.einsum("thd,sd->hts", d_context, value_low, preferred_element_type=jnp.float32)
    row_delta = jnp.sum(probs * d_probs, axis=-1, keepdims=True)
    d_scores = (probs * (d_probs - row_delta)).astype(jnp.bfloat16)
    d_query_rot = (
        jnp.einsum("hts,sd->thd", d_scores, key_rot, preferred_element_type=jnp.float32) * scale
    )
    d_key_rot = (
        jnp.einsum("hts,thd->sd", d_scores, query_rot, preferred_element_type=jnp.float32) * scale
    )
    d_value = jnp.einsum("hts,thd->sd", probs_low, d_context, preferred_element_type=jnp.float32)
    d_query_lin = (
        rotate_back(d_query_rot, cosine[:, None, :], sine[:, None, :])
        .reshape(seq_length, query_width)
        .astype(jnp.bfloat16)
    )
    d_key_lin = rotate_back(d_key_rot, cosine, sine)
    grad_query = contract_rows(rows_one, d_query_lin)
    query_bias_full = lax.dynamic_update_slice(
        jnp.zeros((tensor_size * query_width,), jnp.float32),
        jnp.sum(d_query_lin.astype(jnp.float32), axis=0),
        (tensor_rank * query_width,),
    )
    kv_terms = jnp.zeros((seq_length, 2 * kv_width), jnp.float32)
    kv_terms = lax.dynamic_update_slice(kv_terms, d_key_lin, (0, own_start))
    kv_terms = lax.dynamic_update_slice(kv_terms, d_value, (0, kv_width + own_start))
    piece = d_query_lin
    from_query = contract_cols(piece, full_query)
    summed_back = lax.psum_scatter(
        jnp.concatenate([from_query, kv_terms], axis=1), "tensor", scatter_dimension=0, tiled=True
    )
    d_kv_low = summed_back[:, model_width:].astype(jnp.bfloat16)
    kv_weights = jnp.concatenate([full_key, full_value], axis=1)
    d_normed_one = summed_back[:, :model_width] + contract_cols(d_kv_low, kv_weights)
    grad_kv = contract_rows(normed_one, d_kv_low)
    kv_bias = jnp.sum(d_kv_low.astype(jnp.float32), axis=0)
    gain_one_term, d_from_one = norm_back(d_normed_one, unit_one, inverse_one, gain_one_wide)
    input_grad = (d_middle + d_from_one).astype(jnp.bfloat16)
    sum_query, sum_out, sum_gate, sum_up, sum_down = (
        lax.psum_scatter(
            grad_query.astype(jnp.bfloat16), "dp", scatter_dimension=0, tiled=True
        ).astype(jnp.float32),
        lax.psum_scatter(
            grad_out.astype(jnp.bfloat16), "dp", scatter_dimension=0, tiled=True
        ).astype(jnp.float32),
        lax.psum_scatter(
            grad_gate.astype(jnp.bfloat16), "dp", scatter_dimension=0, tiled=True
        ).astype(jnp.float32),
        lax.psum_scatter(
            grad_up.astype(jnp.bfloat16), "dp", scatter_dimension=0, tiled=True
        ).astype(jnp.float32),
        lax.psum_scatter(
            grad_down.astype(jnp.bfloat16), "dp", scatter_dimension=0, tiled=True
        ).astype(jnp.float32),
    )
    sum_key, sum_value, sum_gain_one, sum_gain_two, sum_query_bias = (
        lax.psum_scatter(grad_kv[:, :kv_width], ("dp", "tensor"), scatter_dimension=0, tiled=True),
        lax.psum_scatter(grad_kv[:, kv_width:], ("dp", "tensor"), scatter_dimension=0, tiled=True),
        lax.psum_scatter(gain_one_term, ("dp", "tensor"), scatter_dimension=0, tiled=True),
        lax.psum_scatter(gain_two_term, ("dp", "tensor"), scatter_dimension=0, tiled=True),
        lax.psum_scatter(query_bias_full, ("dp", "tensor"), scatter_dimension=0, tiled=True),
    )
    sum_key_bias, sum_value_bias = lax.psum(
        (kv_bias[:kv_width], kv_bias[kv_width:]), ("dp", "tensor")
    )
    return (
        mixed,
        input_grad,
        sum_gain_one,
        sum_query,
        sum_query_bias,
        sum_key,
        sum_key_bias,
        sum_value,
        sum_value_bias,
        sum_out,
        sum_gain_two,
        sum_gate,
        sum_up,
        sum_down,
    )


def solution(mesh):
    placed = (
        P(("dp", "tensor"), None),
        P("dp", None),
        P("dp"),
        P("dp", "tensor"),
        P("tensor"),
        P("dp", None),
        P(),
        P("dp", None),
        P(),
        P("dp", "tensor"),
        P("dp"),
        P("dp", "tensor"),
        P("dp", "tensor"),
        P("dp", "tensor"),
        P(("dp", "tensor"), None),
    )
    return jax.shard_map(
        local,
        mesh=mesh,
        in_specs=placed,
        out_specs=(
            P(("dp", "tensor"), None),
            P(("dp", "tensor"), None),
            P(("dp", "tensor")),
            P("dp", "tensor"),
            P(("dp", "tensor")),
            P(("dp", "tensor"), None),
            P(),
            P(("dp", "tensor"), None),
            P(),
            P("dp", "tensor"),
            P(("dp", "tensor")),
            P("dp", "tensor"),
            P("dp", "tensor"),
            P("dp", "tensor"),
        ),
        check_vma=False,
    )
```

profile of v0, /device:TPU:26, one launch (start us, length us, event | category | flops | bytes accessed | tf_op | source)
XLA Modules:
  0.0 1514.2 jit_solution(4256437010096748222)
XLA Ops:
  11.6 11.3 all-reduce.6
  27.5 12.1 all_gather.43
  39.6 9.5 all_gather.42
  50.9 47.7 %all-gather.10.cloned.1.call-done = bf16[1024,1536]{1,0:T(8,128)(2,1)} async-done(((bf16[256,1536]{1,0:T(8,128)(2,1)}), bf16[1024,1536]{1,0:T(8,128)(2,1)}) %all-gather.10.cloned.1.call-update) | async-done | bytes 3145744 | tf_op jit(solution)/shard_map/all_gather | solution.py:122
  98.7 4.5 fusion.13
  114.9 3.2 fusion.7
  118.1 4.4 exponential_reduce_fusion
  122.7 5.7 convolution_convert_fusion.6
  128.4 6.1 fusion.56
  135.8 110.3 %reduce-scatter.14.cloned.1.call-done = f32[256,1536]{1,0:T(8,128)} async-done(((f32[1024,1536]{1,0:T(8,128)}), f32[256,1536]{1,0:T(8,128)}) %reduce-scatter.14.cloned.1.call-update) | async-done | bytes 1572880 | tf_op jit(solution)/shard_map/reduce_scatter | solution.py:149
  250.4 47.1 %all-gather.20.cloned.1.call-done = bf16[1536,2240]{1,0:T(8,128)(2,1)} async-done(((bf16[192,2240]{1,0:T(8,128)(2,1)}), bf16[1536,2240]{1,0:T(8,128)(2,1)}) %all-gather.20.cloned.1.call-update) | async-done | bytes 6881296 | tf_op jit(solution)/shard_map/all_gather | solution.py:113
  297.6 50.5 %all-gather.18.cloned.1.call-done = bf16[1536,2240]{1,0:T(8,128)(2,1)} async-done(((bf16[192,2240]{1,0:T(8,128)(2,1)}), bf16[1536,2240]{1,0:T(8,128)(2,1)}) %all-gather.18.cloned.1.call-update) | async-done | bytes 6881296 | tf_op jit(solution)/shard_map/all_gather | solution.py:112
  348.1 62.7 %all-gather.16.cloned.1.call-done = bf16[1024,1536]{1,0:T(8,128)(2,1)} async-done(((bf16[256,1536]{1,0:T(8,128)(2,1)}), bf16[1024,1536]{1,0:T(8,128)(2,1)}) %all-gather.16.cloned.1.call-update) | async-done | bytes 3145744 | tf_op jit(solution)/shard_map/all_gather | solution.py:156
  410.7 23.3 %fusion.6 = f32[1024,4480]{1,0:T(8,128)} fusion(bf16[1024,1536]{1,0:T(8,128)(2,1)} %all-gather.16.cloned.1.call-done, bf16[1536,2240]{1,0:T(8,128)(2,1)} %all-gather.20.cloned.1.call-done, bf16[1536,2240]{1,0:T(8,128)(2,1)} %all-gather.18.cloned.1.call-done), kind=kOutput, calls=%fused_computation.19 | convolution fusion | flops 14120386560 | bytes 35258368 | tf_op jit(solution)/shard_map/dot_general | solution.py:159
  434.0 40.3 %all-gather.24.cloned.1.call-done = bf16[1024,1536]{1,0:T(8,128)(2,1)} async-done(((bf16[256,1536]{1,0:T(8,128)(2,1)}), bf16[1024,1536]{1,0:T(8,128)(2,1)}) %all-gather.24.cloned.1.call-update) | async-done | bytes 3145744 | tf_op jit(solution)/shard_map/all_gather | solution.py:172
  474.4 51.7 %all-gather.22.cloned.1.call-done = bf16[1536,2240]{1,0:T(8,128)(2,1)} async-done(((bf16[192,2240]{1,0:T(8,128)(2,1)}), bf16[1536,2240]{1,0:T(8,128)(2,1)}) %all-gather.22.cloned.1.call-update) | async-done | bytes 6881296 | tf_op jit(solution)/shard_map/all_gather | solution.py:114
  526.1 19.9 %multiply_convert_fusion.1 = (bf16[1024,2240]{1,0:T(8,128)(2,1)}, bf16[1024,2240]{1,0:T(8,128)(2,1)}, bf16[1024,2240]{1,0:T(8,128)(2,1)}) fusion(f32[1024,4480]{1,0:T(8,128)} %fusion.6, bf16[1024,1536]{1,0:T(8,128)(2,1)} %all-gather.24.cloned.1.call-done, bf16[1536,2240]{1,0:T(8,128)(2,1)} %all-gather.22.cloned.1.call-done), kind=kOutput, calls=%fused_computation.14 | convolution fusion | flops 7083130880 | bytes 42139648 | tf_op jit(solution)/shard_map/dot_general | solution.py:173
  546.0 26.6 %fusion.5 = f32[1024,1536]{1,0:T(8,128)} fusion(bf16[1536,2240]{1,0:T(8,128)(2,1)} %all-gather.20.cloned.1.call-done, bf16[1536,2240]{1,0:T(8,128)(2,1)} %all-gather.18.cloned.1.call-done, bf16[1024,2240]{1,0:T(8,128)(2,1)} %get-tuple-element.72, bf16[1024,2240]{1,0:T(8,128)(2,1)} %get-tuple-element.71), kind=kOutput, calls=%fused_computation.18 | convolution fusion | flops 14138736640 | bytes 29229056 | tf_op jit(solution)/shard_map/dot_general | solution.py:50
  572.7 110.4 %reduce-scatter.18.cloned.1.call-done = f32[256,1536]{1,0:T(8,128)} async-done(((f32[1024,1536]{1,0:T(8,128)}), f32[256,1536]{1,0:T(8,128)}) %reduce-scatter.18.cloned.1.call-update) | async-done | bytes 1572880 | tf_op jit(solution)/shard_map/reduce_scatter | solution.py:182
  686.6 62.1 %all-gather.26.cloned.1.call-done = bf16[1024,1536]{1,0:T(8,128)(2,1)} async-done(((bf16[256,1536]{1,0:T(8,128)(2,1)}), bf16[1024,1536]{1,0:T(8,128)(2,1)}) %all-gather.26.cloned.1.call-update) | async-done | bytes 3145744 | tf_op jit(solution)/shard_map/all_gather | solution.py:187
  748.7 3.6 convolution_convert_fusion.5
  752.4 11.7 fusion
  765.4 7.1 fusion.2
  774.9 3.8 multiply_bitcast_fusion
  782.8 2.7 multiply_add_fusion
  789.7 6.7 fusion.30
  799.6 5.8 pad_maximum_fusion.4
  805.4 12.3 fusion.3
  817.7 9.8 copy.99
  827.6 22.6 %convolution_convert_fusion = bf16[1536,4480]{1,0:T(8,128)(2,1)} fusion(bf16[1024,1536]{1,0:T(8,128)(2,1)} %all-gather.16.cloned.1.call-done, bf16[1024,2240]{1,0:T(8,128)(2,1)} %get-tuple-element.72, bf16[1024,2240]{1,0:T(8,128)(2,1)} %get-tuple-element.71), kind=kOutput, calls=%fused_computation | convolution fusion | flops 14118092800 | bytes 26083328 | tf_op jit(solution)/shard_map/dot_general | solution.py:44
  850.2 11.0 fusion.52
  861.8 4.8 convolution_convert_fusion.4
  866.7 4.8 convolution_convert_fusion.3
  871.6 12.6 convolution_convert_fusion.2
  884.3 66.5 %reduce-scatter.20.cloned.1.call-done = f32[256,2048]{1,0:T(8,128)} async-done(((f32[1024,2048]{1,0:T(8,128)}), f32[256,2048]{1,0:T(8,128)}) %reduce-scatter.20.cloned.1.call-update) | async-done | bytes 2097168 | tf_op jit(solution)/shard_map/reduce_scatter | solution.py:222
  954.9 65.9 %reduce-scatter.34.cloned.1.call-done = bf16[192,2240]{1,0:T(8,128)(2,1)} async-done(((bf16[1536,2240]{1,0:T(8,128)(2,1)}), bf16[192,2240]{1,0:T(8,128)(2,1)}) %reduce-scatter.34.cloned.1.call-update) | async-done | bytes 860176
  1024.3 65.5 %reduce-scatter.30.cloned.1.call-done = bf16[192,2240]{1,0:T(8,128)(2,1)} async-done(((bf16[1536,2240]{1,0:T(8,128)(2,1)}), bf16[192,2240]{1,0:T(8,128)(2,1)}) %reduce-scatter.30.cloned.1.call-update) | async-done | bytes 860176 | tf_op jit(solution)/shard_map/reduce_scatter | solution.py:239
  1089.8 2.5 convert_element_type.143
  1092.3 66.4 %reduce-scatter.32.cloned.1.call-done = bf16[192,2240]{1,0:T(8,128)(2,1)} async-done(((bf16[1536,2240]{1,0:T(8,128)(2,1)}), bf16[192,2240]{1,0:T(8,128)(2,1)}) %reduce-scatter.32.cloned.1.call-update) | async-done | bytes 860176 | tf_op jit(solution)/shard_map/reduce_scatter | solution.py:242
  1158.7 2.5 convert_element_type.144
  1161.3 37.2 %reduce-scatter.22.cloned.1.call-done = bf16[192,384]{1,0:T(8,128)(2,1)} async-done(((bf16[1536,384]{1,0:T(8,128)(2,1)}), bf16[192,384]{1,0:T(8,128)(2,1)}) %reduce-scatter.22.cloned.1.call-update) | async-done | bytes 147472 | tf_op jit(solution)/shard_map/reduce_scatter | solution.py:233
  1200.1 38.1 %reduce-scatter.28.cloned.1.call-done = bf16[192,384]{1,0:T(8,128)(2,1)} async-done(((bf16[1536,384]{1,0:T(8,128)(2,1)}), bf16[192,384]{1,0:T(8,128)(2,1)}) %reduce-scatter.28.cloned.1.call-update) | async-done | bytes 147472 | tf_op jit(solution)/shard_map/reduce_scatter | solution.py:236
  1241.0 4.2 fusion.25
  1245.3 43.4 %all-reduce.5 = (f32[1536]{0:T(1024)S(1)}, f32[1536]{0:T(1024)S(1)}, f32[256]{0:T(256)}, f32[256]{0:T(256)}, f32[1536]{0:T(1024)S(1)}) all-reduce(f32[1536]{0:T(1024)S(1)} %get-tuple-element.58, f32[1536]{0:T(1024)S(1)} %bitcast_dynamic-update-slice_fusion, ...), channel_id=6, replica_groups=mesh['dp'=8,'tensor'=4] {'dp','tensor'}, use_global_device_ids=true, to_apply=%region_12.13.clone | all-reduce | flops 5120 | bytes 40960
  1290.4 10.3 reduce-scatter.16.cloned.1.call-done
  1300.7 4.0 fusion.24
  1304.8 99.8 %reduce-scatter.24.cloned.1.call-done = f32[48,256]{1,0:T(8,128)} async-done(((f32[1536,256]{1,0:T(8,128)}), f32[48,256]{1,0:T(8,128)}) %reduce-scatter.24.cloned.1.call-update) | async-done | bytes 49168 | tf_op jit(solution)/shard_map/reduce_scatter | solution.py:250
  1404.5 102.6 %reduce-scatter.26.cloned.1.call-done = f32[48,256]{1,0:T(8,128)} async-done(((f32[1536,256]{1,0:T(8,128)}), f32[48,256]{1,0:T(8,128)}) %reduce-scatter.26.cloned.1.call-update) | async-done | bytes 49168 | tf_op jit(solution)/shard_map/reduce_scatter | solution.py:251
  (189 shorter events, 60.6 us)
Async XLA Ops:
  7.2 20.3 %copy-start.24 = (bf16[192,256]{1,0:T(8,128)(2,1)S(1)}, bf16[192,256]{1,0:T(8,128)(2,1)}, u32[]{:S(2)}) copy-start(bf16[192,256]{1,0:T(8,128)(2,1)} %param.22) | copy-start | bytes 294916
  7.2 32.4 %copy-start.25 = (bf16[192,256]{1,0:T(8,128)(2,1)S(1)}, bf16[192,256]{1,0:T(8,128)(2,1)}, u32[]{:S(2)}) copy-start(bf16[192,256]{1,0:T(8,128)(2,1)} %param.20) | copy-start | bytes 294916
  7.2 41.9 %copy-start.30 = (s32[1,1024]{1,0:T(1,128)S(1)}, s32[1,1024]{1,0:T(1,128)}, u32[]{:S(2)}) copy-start(s32[1,1024]{1,0:T(1,128)} %param.16) | copy-start | bytes 12292
  7.2 43.7 %all-gather.12.cloned.1.call-start = ((), (), s32[]{:S(2)}) async-start(), calls=%async_computation.12 | async-start | bytes 1327104 | tf_op jit(solution)/shard_map/all_gather | solution.py:107
  7.9 90.7 %all-gather.10.cloned.1.call-start = ((), (), s32[]{:S(2)}) async-start(), calls=%async_computation.11 | async-start | bytes 3932160 | tf_op jit(solution)/shard_map/all_gather | solution.py:122
  24.3 26.4 %copy-start.37 = (bf16[384]{0:T(512)(128)(2,1)S(1)}, bf16[384]{0:T(512)(128)(2,1)}, u32[]{:S(2)}) copy-start(bf16[384]{0:T(512)(128)(2,1)} %param.19) | copy-start | bytes 2308
  24.4 26.4 %copy-start.40 = (bf16[256]{0:T(256)(128)(2,1)S(1)}, bf16[256]{0:T(256)(128)(2,1)}, u32[]{:S(2)}) copy-start(bf16[256]{0:T(256)(128)(2,1)} %param.21) | copy-start | bytes 1540
  24.4 26.5 %copy-start.41 = (bf16[256]{0:T(256)(128)(2,1)S(1)}, bf16[256]{0:T(256)(128)(2,1)}, u32[]{:S(2)}) copy-start(bf16[256]{0:T(256)(128)(2,1)} %param.23) | copy-start | bytes 1540
  26.7 101.8 %all-gather.14.cloned.1.call-start = ((), (), s32[]{:S(2)}) async-start(), calls=%async_computation.13 | async-start | bytes 1327104 | tf_op jit(solution)/shard_map/all_gather | solution.py:110
  27.4 218.6 %reduce-scatter.14.cloned.1.call-start = ((), (), s32[]{:S(2)}) async-start(), calls=%async_computation.14 | async-start | bytes 7864320 | tf_op jit(solution)/shard_map/reduce_scatter | solution.py:149
  27.5 80.7 %copy-start.35 = (f32[64]{0:T(128)}, f32[64]{0:T(128)S(1)}, u32[]{:S(2)}) copy-start(f32[64]{0:T(128)S(1)} %negate_power_fusion) | copy-start | bytes 772
  39.6 63.5 %copy-start.15 = (bf16[1536,256]{1,0:T(8,128)(2,1)}, bf16[1536,256]{1,0:T(8,128)(2,1)S(1)}, u32[]{:S(2)}) copy-start(bf16[1536,256]{1,0:T(8,128)(2,1)S(1)} %all_gather.43) | copy-start | bytes 2359300
  49.1 54.0 %copy-start.16 = (bf16[1536,256]{1,0:T(8,128)(2,1)}, bf16[1536,256]{1,0:T(8,128)(2,1)S(1)}, u32[]{:S(2)}) copy-start(bf16[1536,256]{1,0:T(8,128)(2,1)S(1)} %all_gather.42) | copy-start | bytes 2359300
  50.9 71.6 %copy-start.38 = (f32[128]{0:T(128)}, f32[128]{0:T(128)S(1)}, u32[]{:S(2)}) copy-start(f32[128]{0:T(128)S(1)} %dynamic-slice_convert_fusion.1) | copy-start | bytes 1540
  122.7 641.4 %copy-start.22 = (f32[3,1024]{1,0:T(4,128)}, f32[3,1024]{1,0:T(4,128)S(1)}, u32[]{:S(2)}) copy-start(f32[3,1024]{1,0:T(4,128)S(1)} %log_add_fusion) | copy-start | bytes 36868
  134.5 111.5 %copy-start.5 = (bf16[256,1536]{1,0:T(8,128)(2,1)S(1)}, bf16[256,1536]{1,0:T(8,128)(2,1)}, u32[]{:S(2)}) copy-start(bf16[256,1536]{1,0:T(8,128)(2,1)} %param.15) | copy-start | bytes 2359300
  134.6 163.0 %all-gather.20.cloned.1.call-start = ((), (), s32[]{:S(2)}) async-start(), calls=%async_computation.17 | async-start | bytes 7962624 | tf_op jit(solution)/shard_map/all_gather | solution.py:113
  135.2 212.9 %all-gather.18.cloned.1.call-start = ((), (), s32[]{:S(2)}) async-start(), calls=%async_computation.16 | async-start | bytes 7962624 | tf_op jit(solution)/shard_map/all_gather | solution.py:112
  135.7 275.0 %all-gather.16.cloned.1.call-start = ((), (), s32[]{:S(2)}) async-start(), calls=%async_computation.15 | async-start | bytes 3932160 | tf_op jit(solution)/shard_map/all_gather | solution.py:156
  247.8 437.3 %copy-start.28 = (f32[256]{0:T(256)}, f32[256]{0:T(256)S(1)}, u32[]{:S(2)}) copy-start(f32[256]{0:T(256)S(1)} %add_rsqrt_fusion) | copy-start | bytes 3076
  248.9 225.5 %all-gather.24.cloned.1.call-start = ((), (), s32[]{:S(2)}) async-start(), calls=%async_computation.20 | async-start | bytes 3932160 | tf_op jit(solution)/shard_map/all_gather | solution.py:172
  249.6 276.4 %all-gather.22.cloned.1.call-start = ((), (), s32[]{:S(2)}) async-start(), calls=%async_computation.18 | async-start | bytes 7962624 | tf_op jit(solution)/shard_map/all_gather | solution.py:114
  250.4 432.7 %reduce-scatter.18.cloned.1.call-start = ((), (), s32[]{:S(2)}) async-start(), calls=%async_computation.21 | async-start | bytes 7864320 | tf_op jit(solution)/shard_map/reduce_scatter | solution.py:182
  572.6 112.4 %copy-start.8 = (bf16[256,1536]{1,0:T(8,128)(2,1)S(1)}, bf16[256,1536]{1,0:T(8,128)(2,1)}, u32[]{:S(2)}) copy-start(bf16[256,1536]{1,0:T(8,128)(2,1)} %param.29) | copy-start | bytes 2359300
  572.6 176.1 %all-gather.26.cloned.1.call-start = ((), (), s32[]{:S(2)}) async-start(), calls=%async_computation.22 | async-start | bytes 3932160 | tf_op jit(solution)/shard_map/all_gather | solution.py:187
  685.1 67.3 %copy-start.31 = (f32[256]{0:T(256)}, f32[256]{0:T(256)S(1)}, u32[]{:S(2)}) copy-start(f32[256]{0:T(256)S(1)} %broadcast_multiply_fusion.1) | copy-start | bytes 3076
  686.5 264.3 %reduce-scatter.20.cloned.1.call-start = ((), (), s32[]{:S(2)}) async-start(), calls=%async_computation.23 | async-start | bytes 10485760 | tf_op jit(solution)/shard_map/reduce_scatter | solution.py:222
  686.5 65.9 %copy-start.2 = (pred[1024,1024]{0,1:T(8,128)(4,1)S(1)}, pred[1024,1024]{0,1:T(8,128)(4,1)}, u32[]{:S(2)}) copy-start(pred[1024,1024]{0,1:T(8,128)(4,1)} %fusion.8) | copy-start | bytes 3145732
  686.6 65.9 %copy-start.39 = (f32[128]{0:T(128)S(1)}, f32[128]{0:T(128)}, u32[]{:S(2)}) copy-start(f32[128]{0:T(128)} %copy-done.38) | copy-start | bytes 1540
  752.4 11.7 copy-start.19
  752.4 11.7 slice-start
  752.4 11.7 slice-start.1
  752.4 13.0 slice-start.2
  789.7 8.0 copy-start.18
  805.4 215.5 %reduce-scatter.34.cloned.1.call-start = ((), (), s32[]{:S(2)}) async-start(), calls=%async_computation.30 | async-start | bytes 7962624
  827.5 262.3 %reduce-scatter.30.cloned.1.call-start = ((), (), s32[]{:S(2)}) async-start(), calls=%async_computation.28 | async-start | bytes 7962624 | tf_op jit(solution)/shard_map/reduce_scatter | solution.py:239
  861.2 297.5 %reduce-scatter.32.cloned.1.call-start = ((), (), s32[]{:S(2)}) async-start(), calls=%async_computation.29 | async-start | bytes 7962624 | tf_op jit(solution)/shard_map/reduce_scatter | solution.py:242
  861.8 336.7 %reduce-scatter.22.cloned.1.call-start = ((), (), s32[]{:S(2)}) async-start(), calls=%async_computation.24 | async-start | bytes 1327104 | tf_op jit(solution)/shard_map/reduce_scatter | solution.py:233
  866.7 371.5 %reduce-scatter.28.cloned.1.call-start = ((), (), s32[]{:S(2)}) async-start(), calls=%async_computation.27 | async-start | bytes 1327104 | tf_op jit(solution)/shard_map/reduce_scatter | solution.py:236
  871.5 429.2 %reduce-scatter.16.cloned.1.call-start = ((), (), s32[]{:S(2)}) async-start(), calls=%async_computation.19 | async-start | bytes 3932160 | tf_op jit(solution)/shard_map/reduce_scatter | solution.py:165
  884.2 66.6 %copy-start.7 = (bf16[256,1536]{1,0:T(8,128)(2,1)S(1)}, bf16[256,1536]{1,0:T(8,128)(2,1)}, u32[]{:S(2)}) copy-start(bf16[256,1536]{1,0:T(8,128)(2,1)} %fusion.19) | copy-start | bytes 2359300
  884.2 520.3 %reduce-scatter.24.cloned.1.call-start = ((), (), s32[]{:S(2)}) async-start(), calls=%async_computation.25 | async-start | bytes 1622016 | tf_op jit(solution)/shard_map/reduce_scatter | solution.py:250
  954.3 552.9 %reduce-scatter.26.cloned.1.call-start = ((), (), s32[]{:S(2)}) async-start(), calls=%async_computation.26 | async-start | bytes 1622016 | tf_op jit(solution)/shard_map/reduce_scatter | solution.py:251
  1024.3 216.7 %copy-start.27 = (f32[1536]{0:T(1024)S(1)}, f32[1536]{0:T(1024)}, u32[]{:S(2)}) copy-start(f32[1536]{0:T(1024)} %copy-done.26) | copy-start | bytes 18436
  1024.3 216.7 %copy-start.34 = (f32[256]{0:T(256)S(1)}, f32[256]{0:T(256)}, u32[]{:S(2)}) copy-start(f32[256]{0:T(256)} %copy-done.33) | copy-start | bytes 3076
  1241.0 59.7 %copy-start.4 = (f32[256,1536]{1,0:T(8,128)S(1)}, f32[256,1536]{1,0:T(8,128)}, u32[]{:S(2)}) copy-start(f32[256,1536]{1,0:T(8,128)} %reduce-scatter.18.cloned.1.call-done) | copy-start | bytes 4718596
  1241.0 59.7 %copy-start.29 = (f32[256]{0:T(256)S(1)}, f32[256]{0:T(256)}, u32[]{:S(2)}) copy-start(f32[256]{0:T(256)} %copy-done.28) | copy-start | bytes 3076
  1241.0 59.7 %copy-start.32 = (f32[256]{0:T(256)S(1)}, f32[256]{0:T(256)}, u32[]{:S(2)}) copy-start(f32[256]{0:T(256)} %copy-done.31) | copy-start | bytes 3076
  (17 other events, 60.0 us)
Sparse Core Ops, SparseCore 0:
  9.9 25.5 all-gather.11
  37.6 61.0 all-gather.9
  100.6 24.9 all-gather.13
  134.7 111.3 reduce-scatter.13
  247.8 49.7 all-gather.19
  299.3 48.7 all-gather.17
  349.6 61.0 all-gather.15
  412.3 62.0 all-gather.23
  476.3 49.7 all-gather.21
  572.7 110.2 reduce-scatter.17
  686.6 62.0 all-gather.25
  805.5 145.2 reduce-scatter.19
  954.3 66.5 reduce-scatter.33
  1024.2 65.4 reduce-scatter.29
  1093.1 65.4 reduce-scatter.31
  1161.8 36.6 reduce-scatter.21
  1201.5 36.6 reduce-scatter.27
  1240.4 60.2 reduce-scatter.15
  1306.5 97.9 reduce-scatter.23
  1410.2 96.9 reduce-scatter.25
where the time goes:
time: 1520 us; the launch traced here: 1510 us
  waiting for transfers between devices  1140 us (75%)
  matrix products  182 us (12%)
  blocking collectives  76.3 us (5%)
  other arithmetic  53.4 us (4%)
  local copies, waits for them, and re-layouts  45.3 us (3%)
  between operations  15.9 us (1%)
    reduce_scatter x1, waiting for transfers between devices, local(): lax.psum_scatter(contract_cols(piece, gate_up_w), 'tensor', scatter_dimen...  110 us
    reduce_scatter x1, waiting for transfers between devices, local(): lax.psum_scatter(contract_cols(piece, full_out), 'tensor', scatter_dimens...  110 us
    reduce_scatter x1, waiting for transfers between devices, local(): lax.psum_scatter(grad_kv[:, kv_width:], ('dp', 'tensor'), scatter_dimensi...  103 us
    reduce_scatter x1, waiting for transfers between devices, local(): lax.psum_scatter(grad_kv[:, :kv_width], ('dp', 'tensor'), scatter_dimensi...  99.8 us
    unnamed x21, waiting for transfers between devices  71 us
    reduce_scatter x1, waiting for transfers between devices, local(): lax.psum_scatter(jnp.concatenate([from_query, kv_terms], axis=1), 'tensor...  66.5 us
    reduce_scatter x1, waiting for transfers between devices, local(): lax.psum_scatter(grad_up.astype(jnp.bfloat16), 'dp', scatter_dimension=0,...  66.4 us
    reduce_scatter x1, waiting for transfers between devices, local(): lax.psum_scatter(grad_gate.astype(jnp.bfloat16), 'dp', scatter_dimension=...  65.5 us
  transfers between devices with their start and end apart: 20, of which 18 were waited for; matrix products, arithmetic and copies ran while one was open for 11% of the time, Pallas kernels for 0%

commit v1 on v0

v1 whole, which is shorter than its diff:
```python
import jax
import jax.numpy as jnp
from jax import lax
from jax.sharding import PartitionSpec as P

KV_HEADS = 2
HEAD_DIM = 128
DOC_MAX = 512
EPSILON = 1e-06
ROPE_BASE = 1000000.0
NEGATIVE = -1e30


def angle_tables(first, length, head_width):
    position = (first + jnp.arange(length)).astype(jnp.float32)
    exponent = jnp.arange(head_width // 2, dtype=jnp.float32) * (2.0 / head_width)
    frequency = ROPE_BASE ** (-exponent)
    angle = position[:, None] * frequency[None, :]
    return (jnp.cos(angle), jnp.sin(angle))


def rotate(values, cosine, sine):
    half_width = values.shape[-1] // 2
    first_half = values[..., :half_width]
    second_half = values[..., half_width:]
    return jnp.concatenate(
        [first_half * cosine - second_half * sine, second_half * cosine + first_half * sine],
        axis=-1,
    )


def rotate_back(grads, cosine, sine):
    return rotate(grads, cosine, -sine)


def dot_f32(left, right, dims):
    return lax.dot_general(left, right, (dims, ((), ())), preferred_element_type=jnp.float32)


def contract_rows(left, right):
    return dot_f32(left, right, ((0,), (0,)))


def contract_cols(left, right):
    return dot_f32(left, right, ((1,), (1,)))


def norm_back(upstream, unit, inverse, gain):
    scaled = upstream * gain
    gain_term = jnp.sum(upstream * unit, axis=0)
    input_term = inverse * (scaled - unit * jnp.mean(scaled * unit, axis=-1, keepdims=True))
    return (gain_term, input_term)


def local(
    tokens, segments, gain_one, query_w, query_b, key_w, key_b, value_w, value_b,
    out_w, gain_two, gate_w, up_w, down_w, cotangent,
):
    bf16, f32 = jnp.bfloat16, jnp.float32
    model_width = tokens.shape[1]
    rows = tokens.shape[0]
    tensor_size = lax.axis_size("tensor")
    rank = lax.axis_index("tensor")
    seq_length = rows * tensor_size
    kv_width = key_w.shape[1]
    query_width = query_w.shape[1] * tensor_size
    heads = query_width // HEAD_DIM
    group = heads // KV_HEADS
    scale = HEAD_DIM ** (-0.5)
    pair = lax.all_gather(jnp.stack([query_w, out_w]), "tensor", axis=2, tiled=True)
    joined = jnp.concatenate([pair[0], key_w, value_w, pair[1]], axis=1)
    joined = lax.all_gather(joined, "dp", axis=0, tiled=True)
    qkv_width = query_width + 2 * kv_width
    qkv_w = joined[:, :qkv_width]
    out_full = joined[:, qkv_width:]
    gains = lax.all_gather(jnp.stack([gain_one, gain_two]), "dp", axis=1, tiled=True).astype(f32)
    full_query_b = lax.all_gather(query_b, "tensor", axis=0, tiled=True)
    qkv_b = jnp.concatenate([full_query_b, key_b, value_b]).astype(f32)
    full_gate = lax.all_gather(gate_w, "dp", axis=0, tiled=True)
    full_up = lax.all_gather(up_w, "dp", axis=0, tiled=True)
    full_down = lax.all_gather(down_w, "dp", axis=0, tiled=True)
    cot_rows = lax.all_gather(cotangent, "tensor", axis=0, tiled=True)

    inputs = tokens.astype(f32)
    inverse_one = lax.rsqrt(jnp.mean(inputs * inputs, axis=-1, keepdims=True) + EPSILON)
    unit_one = inputs * inverse_one
    normed_one = (unit_one * gains[0]).astype(bf16)
    lin = jnp.dot(normed_one, qkv_w, preferred_element_type=f32) + qkv_b
    cosine, sine = angle_tables(rank * rows, rows, HEAD_DIM)
    cos_h, sin_h = cosine[:, None, :], sine[:, None, :]
    query_rot = rotate(lin[:, :query_width].reshape(rows, heads, HEAD_DIM), cos_h, sin_h).astype(bf16)
    key_rot = rotate(
        lin[:, query_width : query_width + kv_width].reshape(rows, KV_HEADS, HEAD_DIM), cos_h, sin_h
    ).astype(bf16)
    value_own = lin[:, query_width + kv_width :].astype(bf16)
    kv_own = jnp.concatenate([key_rot.reshape(rows, kv_width), value_own], axis=1)
    kv_all = lax.all_gather(kv_own, "tensor", axis=0, tiled=True)
    window = min(seq_length, rows + -(-DOC_MAX // rows) * rows)
    first = jnp.maximum((rank + 1) * rows - window, 0)
    kv_win = lax.dynamic_slice_in_dim(kv_all, first, window, 0)
    key_win = kv_win[:, :kv_width].reshape(window, KV_HEADS, HEAD_DIM)
    value_win = kv_win[:, kv_width:].reshape(window, KV_HEADS, HEAD_DIM)
    segment = segments[0]
    own_segment = lax.dynamic_slice_in_dim(segment, rank * rows, rows, 0)
    win_segment = lax.dynamic_slice_in_dim(segment, first, window, 0)
    own_pos = rank * rows + jnp.arange(rows)
    win_pos = first + jnp.arange(window)
    allowed = (own_segment[:, None] == win_segment[None, :]) & (win_pos[None, :] <= own_pos[:, None])
    grouped = query_rot.reshape(rows, KV_HEADS, group, HEAD_DIM)
    scores = jnp.einsum("tagd,sad->agts", grouped, key_win, preferred_element_type=f32) * scale
    masked = jnp.where(allowed, scores, NEGATIVE)
    largest = jnp.max(masked, axis=-1, keepdims=True)
    log_total = largest + jnp.log(jnp.sum(jnp.exp(masked - largest), axis=-1, keepdims=True))
    probs = jnp.exp(masked - log_total)
    probs_low = probs.astype(bf16)
    context = jnp.einsum("agts,sad->tagd", probs_low, value_win, preferred_element_type=f32)
    context = context.reshape(rows, query_width).astype(bf16)
    middle = inputs + contract_cols(context, out_full)
    inverse_two = lax.rsqrt(jnp.mean(middle * middle, axis=-1, keepdims=True) + EPSILON)
    unit_two = middle * inverse_two
    normed_two = (unit_two * gains[1]).astype(bf16)

    rows_two = lax.all_gather(normed_two, "tensor", axis=0, tiled=True)
    gate = jnp.dot(rows_two, full_gate, preferred_element_type=f32)
    upper = jnp.dot(rows_two, full_up, preferred_element_type=f32)
    sigmoid = jax.nn.sigmoid(gate)
    hidden_low = (gate * sigmoid * upper).astype(bf16)
    ffn_sum = lax.psum_scatter(
        contract_cols(hidden_low, full_down).astype(bf16), "tensor", scatter_dimension=0, tiled=True
    ).astype(f32)
    mixed = (middle + ffn_sum).astype(bf16)
    d_hidden = jnp.dot(cot_rows, full_down, preferred_element_type=f32)
    d_upper = (d_hidden * gate * sigmoid).astype(bf16)
    d_gate = (d_hidden * upper * sigmoid * (1.0 + gate * (1.0 - sigmoid))).astype(bf16)
    d_normed_two = lax.psum_scatter(
        (contract_cols(d_gate, full_gate) + contract_cols(d_upper, full_up)).astype(bf16),
        "tensor", scatter_dimension=0, tiled=True,
    ).astype(f32)
    grad_down = contract_rows(cot_rows, hidden_low).astype(bf16)
    grad_gate = contract_rows(rows_two, d_gate).astype(bf16)
    grad_up = contract_rows(rows_two, d_upper).astype(bf16)

    gain_two_term, d_from_two = norm_back(d_normed_two, unit_two, inverse_two, gains[1])
    d_middle = cotangent.astype(f32) + d_from_two
    d_attended = d_middle.astype(bf16)
    d_context = jnp.dot(d_attended, out_full, preferred_element_type=f32).astype(bf16)
    grad_out = contract_rows(d_attended, context).astype(bf16)
    d_context = d_context.reshape(rows, KV_HEADS, group, HEAD_DIM)
    d_probs = jnp.einsum("tagd,sad->agts", d_context, value_win, preferred_element_type=f32)
    row_delta = jnp.sum(probs * d_probs, axis=-1, keepdims=True)
    d_scores = (probs * (d_probs - row_delta)).astype(bf16)
    d_query_rot = jnp.einsum("agts,sad->tagd", d_scores, key_win, preferred_element_type=f32) * scale
    d_key_win = jnp.einsum("agts,tagd->sad", d_scores, grouped, preferred_element_type=f32) * scale
    d_value_win = jnp.einsum("agts,tagd->sad", probs_low, d_context, preferred_element_type=f32)
    d_query_lin = (
        rotate_back(d_query_rot.reshape(rows, heads, HEAD_DIM), cos_h, sin_h)
        .reshape(rows, query_width).astype(bf16)
    )
    d_kv_win = jnp.concatenate(
        [d_key_win.reshape(window, kv_width), d_value_win.reshape(window, kv_width)], axis=1
    ).astype(bf16)
    d_kv_all = lax.dynamic_update_slice(
        jnp.zeros((seq_length, 2 * kv_width), bf16), d_kv_win, (first, 0)
    )
    d_kv = lax.psum_scatter(d_kv_all, "tensor", scatter_dimension=0, tiled=True).astype(f32)
    d_key_lin = rotate_back(d_kv[:, :kv_width].reshape(rows, KV_HEADS, HEAD_DIM), cos_h, sin_h)
    d_lin = jnp.concatenate(
        [d_query_lin, d_key_lin.reshape(rows, kv_width).astype(bf16), d_kv[:, kv_width:].astype(bf16)],
        axis=1,
    )
    d_normed_one = contract_cols(d_lin, qkv_w)
    grad_qkv = contract_rows(normed_one, d_lin).astype(bf16)
    bias_term = jnp.sum(d_lin.astype(f32), axis=0)
    gain_one_term, d_from_one = norm_back(d_normed_one, unit_one, inverse_one, gains[0])
    input_grad = (d_middle + d_from_one).astype(bf16)

    def over_dp(grad):
        return lax.psum_scatter(grad, "dp", scatter_dimension=0, tiled=True)

    sum_gate, sum_up, sum_down = (over_dp(g).astype(f32) for g in (grad_gate, grad_up, grad_down))
    part = over_dp(jnp.concatenate([grad_qkv, grad_out], axis=1))
    pair = jnp.stack([part[:, :query_width], part[:, qkv_width:]])
    pair = lax.psum_scatter(pair, "tensor", scatter_dimension=2, tiled=True).astype(f32)
    kv_part = lax.psum_scatter(
        part[:, query_width:qkv_width], "tensor", scatter_dimension=0, tiled=True
    ).astype(f32)
    small = lax.psum(
        jnp.concatenate([bias_term, gain_one_term, gain_two_term]), ("dp", "tensor")
    )
    place = lax.axis_index("dp") * tensor_size + rank
    devices = lax.axis_size("dp") * tensor_size

    def own(start, size):
        share = size // devices
        return lax.dynamic_slice_in_dim(small, start + place * share, share, 0)

    return (
        mixed,
        input_grad,
        own(qkv_width, model_width),
        pair[0],
        own(0, query_width),
        kv_part[:, :kv_width],
        small[query_width : query_width + kv_width],
        kv_part[:, kv_width:],
        small[query_width + kv_width : qkv_width],
        pair[1],
        own(qkv_width + model_width, model_width),
        sum_gate,
        sum_up,
        sum_down,
    )


def solution(mesh):
    both = ("dp", "tensor")
    return jax.shard_map(
        local,
        mesh=mesh,
        in_specs=(
            P(both, None), P("dp", None), P("dp"), P("dp", "tensor"), P("tensor"), P("dp", None), P(),
            P("dp", None), P(), P("dp", "tensor"), P("dp"), P("dp", "tensor"), P("dp", "tensor"),
            P("dp", "tensor"), P(both, None),
        ),
        out_specs=(
            P(both, None), P(both, None), P(both), P("dp", "tensor"), P(both), P(both, None), P(),
            P(both, None), P(), P("dp", "tensor"), P(both), P("dp", "tensor"), P("dp", "tensor"),
            P("dp", "tensor"),
        ),
        check_vma=False,
    )
```

time: 1520 us -> 1040 us (0.68)
  waiting for transfers between devices: 1140 us -> 674 us
  blocking collectives: 76.3 us -> 59.7 us
    reduce_scatter x10 -> x7, waiting for transfers between devices: 707 us -> 310 us  [the longest x3 169 us: over_dp(): return lax.psum_scatter(grad, 'dp', scatter_dimension=0, tiled=True)]
    unnamed x2 -> x0, blocking collectives: 54.7 us -> none
    all_gather x7 -> x6, waiting for transfers between devices: 259 us -> 217 us  [the longest x1 51.7 us: local(): full_down = lax.all_gather(down_w, 'dp', axis=0, tiled=True)]
    psum x0 -> x1, blocking collectives: none -> 40 us  [local(): lax.psum(jnp.concatenate([bias_term, gain_one_term, gain_two_term]), ('dp...]
    unnamed x21 -> x19, waiting for transfers between devices: 71 us -> 34.8 us
    dot_general x20 -> x21, matrix products: 182 us -> 173 us  [the longest x10 88.5 us: dot_f32(): lax.dot_general(left, right, (dims, ((), ())), preferred_element_type=jnp...]
  transfers between devices with their start and end apart: 20 -> 17, of which waited for: 18 -> 17; matrix products, arithmetic and copies ran while one was open for 11% -> 15% of each run, Pallas kernels for 0% -> 0%
where the time goes in v1:
time: 1040 us; the launch traced here: 1030 us
  waiting for transfers between devices  674 us (65%)
  matrix products  173 us (17%)
  blocking collectives  59.7 us (6%)
  local copies, waits for them, and re-layouts  58.9 us (6%)
  other arithmetic  46.9 us (5%)
  between operations  14.9 us (1%)
    reduce_scatter x3, waiting for transfers between devices, over_dp(): return lax.psum_scatter(grad, 'dp', scatter_dimension=0, tiled=True)  169 us
    dot_general x10, matrix products, dot_f32(): lax.dot_general(left, right, (dims, ((), ())), preferred_element_type=jnp...  88.5 us
    all_gather x1, waiting for transfers between devices, local(): rows_two = lax.all_gather(normed_two, 'tensor', axis=0, tiled=True)  63.1 us
    reduce_scatter x1, waiting for transfers between devices, local(): lax.psum_scatter(contract_cols(hidden_low, full_down).astype(bf16), 'tens...  60.1 us
    all_gather x1, waiting for transfers between devices, local(): full_down = lax.all_gather(down_w, 'dp', axis=0, tiled=True)  51.7 us
    all_gather x1, waiting for transfers between devices, local(): cot_rows = lax.all_gather(cotangent, 'tensor', axis=0, tiled=True)  49.4 us
    reduce_scatter x1, waiting for transfers between devices, local(): lax.psum_scatter((contract_cols(d_gate, full_gate) + contract_cols(d_uppe...  46.8 us
    all_gather x1, waiting for transfers between devices, local(): joined = lax.all_gather(joined, 'dp', axis=0, tiled=True)  44.9 us
  transfers between devices with their start and end apart: 17, of which 17 were waited for; matrix products, arithmetic and copies ran while one was open for 15% of the time, Pallas kernels for 0%

profile of v1, /device:TPU:26, one launch (start us, length us, event | category | flops | bytes accessed | tf_op | source)
XLA Modules:
  0.0 1029.7 jit_solution(3349695426935198296)
XLA Ops:
  9.2 30.6 %all-gather.11.cloned.1.call-done = bf16[2,192,1536]{2,1,0:T(8,128)(2,1)} async-done(((bf16[2,192,384]{2,1,0:T(8,128)(2,1)}), bf16[2,192,1536]{2,1,0:T(8,128)(2,1)}) %all-gather.11.cloned.1.call-update) | async-done | bytes 1179664 | tf_op jit(solution)/shard_map/all_gather | solution.py:70
  43.4 8.9 all-gather
  52.4 10.8 %all-gather.1 = bf16[4,1,384]{2,1,0:T(2,128)(2,1)S(1)} all-gather(bf16[1,1,384]{2,1,0:T(2,128)(2,1)S(1)} %reshape.237), channel_id=1, replica_groups=mesh['dp'=8,'tensor'=4] {'tensor'}, dimensions={0}, use_global_device_ids=true | all-gather | bytes 3840 | tf_op jit(solution)/shard_map/all_gather | solution.py:77
  64.7 44.9 %all-gather.13.cloned.1.call-done = bf16[1536,3584]{1,0:T(8,128)(2,1)} async-done(((bf16[192,3584]{1,0:T(8,128)(2,1)}), bf16[1536,3584]{1,0:T(8,128)(2,1)}) %all-gather.13.cloned.1.call-update) | async-done | bytes 11010064 | tf_op jit(solution)/shard_map/all_gather | solution.py:72
  109.7 4.6 fusion.17
  118.8 2.7 slice.133
  124.4 19.8 %all-gather.15.cloned.1.call-done = bf16[1024,512]{1,0:T(8,128)(2,1)} async-done(((bf16[256,512]{1,0:T(8,128)(2,1)}), bf16[1024,512]{1,0:T(8,128)(2,1)}) %all-gather.15.cloned.1.call-update) | async-done | bytes 1048592 | tf_op jit(solution)/shard_map/all_gather | solution.py:97
  156.3 4.2 multiply_reduce_fusion
  164.1 31.5 %all-gather.19.cloned.1.call-done = bf16[1536,2240]{1,0:T(8,128)(2,1)} async-done(((bf16[192,2240]{1,0:T(8,128)(2,1)}), bf16[1536,2240]{1,0:T(8,128)(2,1)}) %all-gather.19.cloned.1.call-update) | async-done | bytes 6881296 | tf_op jit(solution)/shard_map/all_gather | solution.py:79
  195.6 63.1 %all-gather.17.cloned.1.call-done = bf16[1024,1536]{1,0:T(8,128)(2,1)} async-done(((bf16[256,1536]{1,0:T(8,128)(2,1)}), bf16[1024,1536]{1,0:T(8,128)(2,1)}) %all-gather.17.cloned.1.call-update) | async-done | bytes 3145744 | tf_op jit(solution)/shard_map/all_gather | solution.py:123
  258.7 13.2 %fusion.67 = f32[1024,2240]{0,1:T(8,128)} fusion(bf16[1024,1536]{1,0:T(8,128)(2,1)} %all-gather.17.cloned.1.call-done, bf16[1536,2240]{1,0:T(8,128)(2,1)} %all-gather.19.cloned.1.call-done), kind=kOutput, calls=%fused_computation.132 | convolution fusion | flops 7046430720 | bytes 19202048 | tf_op jit(solution)/shard_map/dot_general | solution.py:124
  271.9 38.3 %all-gather.21.cloned.1.call-done = bf16[1536,2240]{1,0:T(8,128)(2,1)} async-done(((bf16[192,2240]{1,0:T(8,128)(2,1)}), bf16[1536,2240]{1,0:T(8,128)(2,1)}) %all-gather.21.cloned.1.call-update) | async-done | bytes 6881296 | tf_op jit(solution)/shard_map/all_gather | solution.py:80
  310.2 13.3 %fusion.68 = f32[1024,2240]{0,1:T(8,128)} fusion(bf16[1024,1536]{1,0:T(8,128)(2,1)} %all-gather.17.cloned.1.call-done, bf16[1536,2240]{1,0:T(8,128)(2,1)} %all-gather.21.cloned.1.call-done), kind=kOutput, calls=%fused_computation.133 | convolution fusion | flops 7046430720 | bytes 19202048 | tf_op jit(solution)/shard_map/dot_general | solution.py:125
  323.5 49.4 %all-gather.25.cloned.1.call-done = bf16[1024,1536]{1,0:T(8,128)(2,1)} async-done(((bf16[256,1536]{1,0:T(8,128)(2,1)}), bf16[1024,1536]{1,0:T(8,128)(2,1)}) %all-gather.25.cloned.1.call-update) | async-done | bytes 3145744 | tf_op jit(solution)/shard_map/all_gather | solution.py:82
  372.9 51.7 %all-gather.23.cloned.1.call-done = bf16[1536,2240]{1,0:T(8,128)(2,1)} async-done(((bf16[192,2240]{1,0:T(8,128)(2,1)}), bf16[1536,2240]{1,0:T(8,128)(2,1)}) %all-gather.23.cloned.1.call-update) | async-done | bytes 6881296 | tf_op jit(solution)/shard_map/all_gather | solution.py:81
  424.5 20.7 %multiply_convert_fusion = (bf16[1024,2240]{0,1:T(8,128)(2,1)}, bf16[1024,2240]{0,1:T(8,128)(2,1)}, bf16[1024,2240]{0,1:T(8,128)(2,1)}) fusion(f32[1024,2240]{0,1:T(8,128)} %fusion.67, f32[1024,2240]{0,1:T(8,128)} %fusion.68, bf16[1024,1536]{1,0:T(8,128)(2,1)} %all-gather.25.cloned.1.call-done, bf16[1536,2240]{1,0:T(8,128)(2,1)} %all-gather.23.cloned.1.call-done), kind=kOutput, calls=%fused_computation.13 | convolution fusion | flops 7083130880 | bytes 42139648 | tf_op jit(solution)/shard_map/dot_general | solution.py:132
  445.2 11.4 %fusion.69 = f32[1024,1536]{1,0:T(8,128)S(1)} fusion(bf16[1024,2240]{0,1:T(8,128)(2,1)} %get-tuple-element.91, bf16[1536,2240]{1,0:T(8,128)(2,1)} %all-gather.19.cloned.1.call-done), kind=kOutput, calls=%fused_computation.134 | convolution fusion | flops 7046430720 | bytes 17760256 | tf_op jit(solution)/shard_map/dot_general | solution.py:37
  456.7 9.3 add_convert_fusion
  466.1 12.5 %convolution_convert_fusion.5 = bf16[1024,1536]{1,0:T(8,128)(2,1)} fusion(bf16[1024,2240]{0,1:T(8,128)(2,1)} %get-tuple-element.92, bf16[1536,2240]{1,0:T(8,128)(2,1)} %all-gather.23.cloned.1.call-done), kind=kOutput, calls=%fused_computation.30 | convolution fusion | flops 7048003584 | bytes 14614528 | tf_op jit(solution)/shard_map/dot_general | solution.py:37
  478.6 46.8 %reduce-scatter.16.cloned.1.call-done = bf16[256,1536]{1,0:T(8,128)(2,1)} async-done(((bf16[1024,1536]{1,0:T(8,128)(2,1)}), bf16[256,1536]{1,0:T(8,128)(2,1)}) %reduce-scatter.16.cloned.1.call-update) | async-done | bytes 786448 | tf_op jit(solution)/shard_map/reduce_scatter | solution.py:135
  527.8 60.1 %reduce-scatter.14.cloned.1.call-done = bf16[256,1536]{1,0:T(8,128)(2,1)} async-done(((bf16[1024,1536]{1,0:T(8,128)(2,1)}), bf16[256,1536]{1,0:T(8,128)(2,1)}) %reduce-scatter.14.cloned.1.call-update) | async-done | bytes 786448 | tf_op jit(solution)/shard_map/reduce_scatter | solution.py:128
  587.9 3.6 fusion.31
  591.6 4.7 fusion.20
  598.5 9.0 fusion.1
  607.6 6.2 fusion.43
  613.8 11.1 %fusion.3 = bf16[2,6,256,768]{2,3,1,0:T(8,128)(2,1)} fusion(f32[2,768,256,6]{2,1,3,0:T(8,128)} %get-tuple-element.130, f32[2,768,256,6]{2,1,3,0:T(8,128)} %copy-done.2, f32[2,6,256]{2,1,0:T(8,128)S(1)} %get-tuple-element.129, f32[2,6,256]{2,1,0:T(8,128)S(1)} %copy-done.17, pred[256,768]{0,1:T(8,128)(4,1)S(1)} %compare_and_fusion), kind=kLoop, calls=%fused_computation.9 | loop fusion | flops 14155776 | bytes 23814144 | tf_op jit(solution)/shard_map/convert_element_type | solution.py:151
  625.0 4.7 fusion.42
  631.7 7.4 dynamic_update_slice.3
  640.2 3.2 convolution_multiply_fusion
  644.6 3.6 convolution_convert_fusion.4
  648.2 17.4 %reduce-scatter.18.cloned.1.call-done = bf16[256,512]{0,1:T(8,128)(2,1)} async-done(((bf16[1024,512]{0,1:T(8,128)(2,1)}), bf16[256,512]{0,1:T(8,128)(2,1)}) %reduce-scatter.18.cloned.1.call-update) | async-done | bytes 262160 | tf_op jit(solution)/shard_map/reduce_scatter | solution.py:165
  668.7 3.2 convolution_convert_fusion.3
  671.9 5.2 pad_maximum_fusion
  677.2 12.5 %fusion = bf16[1536,2240]{0,1:T(8,128)(2,1)} fusion(bf16[1024,2240]{0,1:T(8,128)(2,1)} %get-tuple-element.92, bf16[1024,1536]{1,0:T(8,128)(2,1)} %all-gather.25.cloned.1.call-done), kind=kOutput, calls=%fused_computation.4 | convolution fusion | flops 7049871360 | bytes 14614528 | tf_op jit(solution)/shard_map/dot_general | solution.py:37
  689.6 10.8 %copy.161 = bf16[1536,2240]{1,0:T(8,128)(2,1)} copy(bf16[1536,2240]{0,1:T(8,128)(2,1)} %fusion) | data formatting | bytes 13762560
  701.0 12.3 %convolution_convert_fusion.2 = bf16[1536,2240]{1,0:T(8,128)(2,1)} fusion(bf16[1024,1536]{1,0:T(8,128)(2,1)} %all-gather.17.cloned.1.call-done, bf16[1024,2240]{0,1:T(8,128)(2,1)} %get-tuple-element.91), kind=kOutput, calls=%fused_computation.2 | convolution fusion | flops 7049871360 | bytes 14614528 | tf_op jit(solution)/shard_map/dot_general | solution.py:37
  713.4 12.3 %convolution_convert_fusion.1 = bf16[1536,2240]{1,0:T(8,128)(2,1)} fusion(bf16[1024,1536]{1,0:T(8,128)(2,1)} %all-gather.17.cloned.1.call-done, bf16[1024,2240]{0,1:T(8,128)(2,1)} %get-tuple-element.90), kind=kOutput, calls=%fused_computation.1 | convolution fusion | flops 7049871360 | bytes 14614528 | tf_op jit(solution)/shard_map/dot_general | solution.py:37
  725.8 36.8 %reduce-scatter.20.cloned.1.call-done = bf16[192,3584]{1,0:T(8,128)(2,1)} async-done(((bf16[1536,3584]{1,0:T(8,128)(2,1)}), bf16[192,3584]{1,0:T(8,128)(2,1)}) %reduce-scatter.20.cloned.1.call-update) | async-done | bytes 1376272 | tf_op jit(solution)/shard_map/reduce_scatter | solution.py:178
  766.9 4.8 copy.159
  771.7 4.6 reshape.246
  778.0 7.2 fusion.39
  785.2 40.0 %psum.7 = f32[5120]{0:T(1024)S(1)} all-reduce(f32[5120]{0:T(1024)S(1)} %pad_maximum_fusion.13), channel_id=1, replica_groups=mesh['dp'=8,'tensor'=4] {'dp','tensor'}, use_global_device_ids=true, to_apply=%region_13.14 | all-reduce | flops 5120 | bytes 40960 | tf_op jit(solution)/shard_map/psum | solution.py:187
  826.3 2.8 fusion.38
  829.1 3.3 reduce-scatter.30.cloned.1.call-done
  835.8 65.6 %reduce-scatter.24.cloned.1.call-done = bf16[192,2240]{1,0:T(8,128)(2,1)} async-done(((bf16[1536,2240]{1,0:T(8,128)(2,1)}), bf16[192,2240]{1,0:T(8,128)(2,1)}) %reduce-scatter.24.cloned.1.call-update) | async-done | bytes 860176 | tf_op jit(solution)/shard_map/reduce_scatter | solution.py:178
  903.9 66.4 %reduce-scatter.26.cloned.1.call-done = bf16[192,2240]{1,0:T(8,128)(2,1)} async-done(((bf16[1536,2240]{1,0:T(8,128)(2,1)}), bf16[192,2240]{1,0:T(8,128)(2,1)}) %reduce-scatter.26.cloned.1.call-update) | async-done | bytes 860176 | tf_op jit(solution)/shard_map/reduce_scatter | solution.py:178
  972.8 17.0 %reduce-scatter.22.cloned.1.call-done = bf16[48,512]{1,0:T(8,128)(2,1)} async-done(((bf16[192,512]{1,0:T(8,128)(2,1)}), bf16[48,512]{1,0:T(8,128)(2,1)}) %reduce-scatter.22.cloned.1.call-update) | async-done | bytes 49168 | tf_op jit(solution)/shard_map/reduce_scatter | solution.py:184
  991.2 28.8 %reduce-scatter.28.cloned.1.call-done = bf16[384,384]{1,0:T(8,128)(2,1)} async-done(((bf16[1536,384]{1,0:T(8,128)(2,1)}), bf16[384,384]{1,0:T(8,128)(2,1)}) %reduce-scatter.28.cloned.1.call-update) | async-done | bytes 294928
  (176 shorter events, 62.2 us)
Async XLA Ops:
  7.2 111.2 %copy-start = (s32[1,1024]{1,0:T(1,128)S(1)}, s32[1,1024]{1,0:T(1,128)}, u32[]{:S(2)}) copy-start(s32[1,1024]{1,0:T(1,128)} %param.16) | copy-start | bytes 12292
  7.2 36.1 %copy-start.27 = (bf16[192]{0:T(256)(128)(2,1)S(1)}, bf16[192]{0:T(256)(128)(2,1)}, u32[]{:S(2)}) copy-start(bf16[192]{0:T(256)(128)(2,1)} %param.17) | copy-start | bytes 1156
  7.2 36.1 %copy-start.28 = (bf16[192]{0:T(256)(128)(2,1)S(1)}, bf16[192]{0:T(256)(128)(2,1)}, u32[]{:S(2)}) copy-start(bf16[192]{0:T(256)(128)(2,1)} %param.25) | copy-start | bytes 1156
  7.2 45.1 %copy-start.23 = (bf16[384]{0:T(512)(128)(2,1)S(1)}, bf16[384]{0:T(512)(128)(2,1)}, u32[]{:S(2)}) copy-start(bf16[384]{0:T(512)(128)(2,1)} %param.19) | copy-start | bytes 2308
  7.2 57.1 %copy-start.25 = (bf16[256]{0:T(256)(128)(2,1)S(1)}, bf16[256]{0:T(256)(128)(2,1)}, u32[]{:S(2)}) copy-start(bf16[256]{0:T(256)(128)(2,1)} %param.21) | copy-start | bytes 1540
  7.2 57.1 %copy-start.24 = (bf16[256]{0:T(256)(128)(2,1)S(1)}, bf16[256]{0:T(256)(128)(2,1)}, u32[]{:S(2)}) copy-start(bf16[256]{0:T(256)(128)(2,1)} %param.23) | copy-start | bytes 1540
  7.2 57.2 %copy-start.4 = (bf16[256,1536]{1,0:T(8,128)(2,1)S(1)}, bf16[256,1536]{1,0:T(8,128)(2,1)}, u32[]{:S(2)}) copy-start(bf16[256,1536]{1,0:T(8,128)(2,1)} %param.15) | copy-start | bytes 2359300
  7.3 32.5 %all-gather.11.cloned.1.call-start = ((), (), s32[]{:S(2)}) async-start(), calls=%async_computation.9 | async-start | bytes 1474560 | tf_op jit(solution)/shard_map/all_gather | solution.py:70
  9.1 100.5 %all-gather.13.cloned.1.call-start = ((), (), s32[]{:S(2)}) async-start(), calls=%async_computation.10 | async-start | bytes 12386304 | tf_op jit(solution)/shard_map/all_gather | solution.py:72
  43.3 100.9 %all-gather.15.cloned.1.call-start = ((), (), s32[]{:S(2)}) async-start(), calls=%async_computation.11 | async-start | bytes 1310720 | tf_op jit(solution)/shard_map/all_gather | solution.py:97
  64.3 51.7 %copy-start.11 = (f32[256,64]{1,0:T(8,128)}, f32[256,64]{1,0:T(8,128)S(1)}, u32[]{:S(2)}) copy-start(f32[256,64]{1,0:T(8,128)S(1)} %copy.116) | copy-start | bytes 196612
  64.5 49.9 %copy-start.18 = (f32[1536]{0:T(1024)}, f32[1536]{0:T(1024)S(1)}, u32[]{:S(2)}) copy-start(f32[1536]{0:T(1024)S(1)} %get-tuple-element.89) | copy-start | bytes 18436
  64.7 49.6 %copy-start.21 = (f32[256]{0:T(256)}, f32[256]{0:T(256)S(1)}, u32[]{:S(2)}) copy-start(f32[256]{0:T(256)S(1)} %add_rsqrt_fusion.1) | copy-start | bytes 3076
  117.6 78.0 %all-gather.19.cloned.1.call-start = ((), (), s32[]{:S(2)}) async-start(), calls=%async_computation.13 | async-start | bytes 7962624 | tf_op jit(solution)/shard_map/all_gather | solution.py:79
  118.2 140.5 %all-gather.17.cloned.1.call-start = ((), (), s32[]{:S(2)}) async-start(), calls=%async_computation.12 | async-start | bytes 3932160 | tf_op jit(solution)/shard_map/all_gather | solution.py:123
  124.0 26.3 %copy-start.5 = (bf16[256,12,64]{2,0,1:T(8,128)(2,1)}, bf16[256,12,64]{2,0,1:T(8,128)(2,1)S(1)}, u32[]{:S(2)}) copy-start(bf16[256,12,64]{2,0,1:T(8,128)(2,1)S(1)} %copy.119) | copy-start | bytes 1179652
  124.4 25.9 %copy-start.6 = (bf16[256,12,64]{2,0,1:T(8,128)(2,1)}, bf16[256,12,64]{2,0,1:T(8,128)(2,1)S(1)}, u32[]{:S(2)}) copy-start(bf16[256,12,64]{2,0,1:T(8,128)(2,1)S(1)} %copy.120) | copy-start | bytes 1179652
  147.9 4.3 copy-start.9
  150.3 3.5 copy-start.2
  152.3 4.0 copy-start.16
  156.3 4.2 copy-start.13
  160.5 365.0 %copy-start.3 = (f32[256,1536]{1,0:T(8,128)}, f32[256,1536]{1,0:T(8,128)S(1)}, u32[]{:S(2)}) copy-start(f32[256,1536]{1,0:T(8,128)S(1)} %get-tuple-element.128) | copy-start | bytes 4718596
  161.7 148.5 %all-gather.21.cloned.1.call-start = ((), (), s32[]{:S(2)}) async-start(), calls=%async_computation.14 | async-start | bytes 7962624 | tf_op jit(solution)/shard_map/all_gather | solution.py:80
  162.3 210.5 %all-gather.25.cloned.1.call-start = ((), (), s32[]{:S(2)}) async-start(), calls=%async_computation.17 | async-start | bytes 3932160 | tf_op jit(solution)/shard_map/all_gather | solution.py:82
  163.1 261.5 %all-gather.23.cloned.1.call-start = ((), (), s32[]{:S(2)}) async-start(), calls=%async_computation.15 | async-start | bytes 7962624 | tf_op jit(solution)/shard_map/all_gather | solution.py:81
  163.8 361.6 %reduce-scatter.16.cloned.1.call-start = ((), (), s32[]{:S(2)}) async-start(), calls=%async_computation.18 | async-start | bytes 3932160 | tf_op jit(solution)/shard_map/reduce_scatter | solution.py:135
  445.2 11.4 %copy-start.26 = (bf16[1536,2240]{1,0:T(8,128)(2,1)S(1)}, bf16[1536,2240]{1,0:T(8,128)(2,1)}, u32[]{:S(2)}) copy-start(bf16[1536,2240]{1,0:T(8,128)(2,1)} %all-gather.21.cloned.1.call-done) | copy-start | bytes 20643844
  445.2 11.4 %copy-start.29 = (bf16[1024,2240]{0,1:T(8,128)(2,1)S(1)}, bf16[1024,2240]{0,1:T(8,128)(2,1)}, u32[]{:S(2)}) copy-start(bf16[1024,2240]{0,1:T(8,128)(2,1)} %get-tuple-element.90) | copy-start | bytes 13762564
  466.0 121.9 %reduce-scatter.14.cloned.1.call-start = ((), (), s32[]{:S(2)}) async-start(), calls=%async_computation.16 | async-start | bytes 3932160 | tf_op jit(solution)/shard_map/reduce_scatter | solution.py:128
  478.6 187.0 %reduce-scatter.18.cloned.1.call-start = ((), (), s32[]{:S(2)}) async-start(), calls=%async_computation.19 | async-start | bytes 1310720 | tf_op jit(solution)/shard_map/reduce_scatter | solution.py:165
  591.6 7.0 copy-start.10
  591.6 7.0 copy-start.17
  598.5 9.0 copy-start.7
  625.0 14.5 %copy-start.15 = (f32[256,64]{0,1:T(8,128)S(1)}, f32[256,64]{0,1:T(8,128)}, u32[]{:S(2)}) copy-start(f32[256,64]{0,1:T(8,128)} %get-tuple-element.122) | copy-start | bytes 196612
  639.1 123.5 %reduce-scatter.20.cloned.1.call-start = ((), (), s32[]{:S(2)}) async-start(), calls=%async_computation.20 | async-start | bytes 12386304 | tf_op jit(solution)/shard_map/reduce_scatter | solution.py:178
  640.2 4.4 copy-start.14
  644.6 22.3 %copy-start.12 = (f32[256,64]{1,0:T(8,128)S(1)}, f32[256,64]{1,0:T(8,128)}, u32[]{:S(2)}) copy-start(f32[256,64]{1,0:T(8,128)} %copy-done.11) | copy-start | bytes 196612
  644.6 24.0 %copy-start.19 = (f32[1536]{0:T(1024)S(1)}, f32[1536]{0:T(1024)}, u32[]{:S(2)}) copy-start(f32[1536]{0:T(1024)} %copy-done.18) | copy-start | bytes 18436
  644.6 24.0 %copy-start.22 = (f32[256]{0:T(256)S(1)}, f32[256]{0:T(256)}, u32[]{:S(2)}) copy-start(f32[256]{0:T(256)} %copy-done.21) | copy-start | bytes 3076
  668.5 3.4 slice-start
  668.6 3.3 slice-start.1
  677.1 155.3 %reduce-scatter.30.cloned.1.call-start = ((), (), s32[]{:S(2)}) async-start(), calls=%async_computation.25 | async-start | bytes 7962624
  700.5 200.9 %reduce-scatter.24.cloned.1.call-start = ((), (), s32[]{:S(2)}) async-start(), calls=%async_computation.22 | async-start | bytes 7962624 | tf_op jit(solution)/shard_map/reduce_scatter | solution.py:178
  713.3 257.0 %reduce-scatter.26.cloned.1.call-start = ((), (), s32[]{:S(2)}) async-start(), calls=%async_computation.23 | async-start | bytes 7962624 | tf_op jit(solution)/shard_map/reduce_scatter | solution.py:178
  725.7 264.1 %reduce-scatter.22.cloned.1.call-start = ((), (), s32[]{:S(2)}) async-start(), calls=%async_computation.21 | async-start | bytes 245760 | tf_op jit(solution)/shard_map/reduce_scatter | solution.py:184
  764.2 255.8 %reduce-scatter.28.cloned.1.call-start = ((), (), s32[]{:S(2)}) async-start(), calls=%async_computation.24 | async-start | bytes 1474560
  778.0 7.2 copy-start.20
  834.1 188.8 %copy-start.1 = (s32[1,1024]{1,0:T(1,128)S(1)}, s32[1,1024]{1,0:T(1,128)}, u32[]{:S(2)}) copy-start(s32[1,1024]{1,0:T(1,128)} %param.16) | copy-start | bytes 12292
  (1 other events, 1.4 us)
Sparse Core Ops, SparseCore 0:
  10.2 29.5 all-gather.10
  43.4 66.2 all-gather.12
  117.7 26.4 all-gather.14
  145.9 49.6 all-gather.18
  197.6 61.0 all-gather.16
  260.4 49.7 all-gather.20
  311.8 61.0 all-gather.24
  374.8 49.7 all-gather.22
  466.1 59.2 reduce-scatter.15
  527.6 60.3 reduce-scatter.13
  639.2 26.2 reduce-scatter.17
  677.2 85.3 reduce-scatter.19
  766.1 66.2 reduce-scatter.29
  835.7 65.6 reduce-scatter.23
  904.8 65.4 reduce-scatter.25
  973.0 16.7 reduce-scatter.21
  992.0 28.0 reduce-scatter.27

commit v2 on v1

--- a/solution.py
+++ b/solution.py
@@ -1,7 +1,13 @@
+import functools
+
 import jax
 import jax.numpy as jnp
 from jax import lax
+from jax.experimental import pallas as pl
+from jax.experimental.pallas import tpu as pltpu
 from jax.sharding import PartitionSpec as P
+
+MESH = pl.DeviceIdType.MESH
 
 KV_HEADS = 2
 HEAD_DIM = 128
@@ -50,6 +56,301 @@
     gain_term = jnp.sum(upstream * unit, axis=0)
     input_term = inverse * (scaled - unit * jnp.mean(scaled * unit, axis=-1, keepdims=True))
     return (gain_term, input_term)
+
+
+def line_order(z, s):
+    upper = z // 2
+    near = z * (1 - upper) + (3 - z) * upper
+    inner = (1 - s // 3) * ((s + 1) % 3) + (s // 3) * 3
+    at = (1 - near) * s + near * inner
+    return at * (1 - upper) + (3 - at) * upper
+
+
+def ffn_body(
+    two_ref, cot_ref, gate_ref, up_ref, down_ref,
+    rows_out, hid_out, dg_out, du_out, sum_out, dn_out,
+    rows_v, cot_v, gate_v, up_v, down_v, hid_v, dg_v, du_v, part, land, below, above, res_v,
+    tile_sem, load_sem, ag_send, ag_recv, rs_send, rs_recv, own_recv, out_sem,
+    *, axis, ft, nt,
+):
+    f32, bf16 = jnp.float32, jnp.bfloat16
+    size = 4
+    rows, width = two_ref.shape
+    units = gate_ref.shape[1]
+    n_f, n_n = units // ft, width // nt
+    z = lax.axis_index(axis)
+    has_low, has_high = z > 0, z < size - 1
+
+    def to(dz):
+        return {axis: z + dz}
+
+    barrier = pltpu.get_barrier_semaphore()
+
+    @pl.when(has_low)
+    def _():
+        pl.semaphore_signal(barrier, inc=1, device_id=to(-1), device_id_type=MESH)
+
+    @pl.when(has_high)
+    def _():
+        pl.semaphore_signal(barrier, inc=1, device_id=to(1), device_id_type=MESH)
+
+    own_load = pltpu.make_async_copy(two_ref, rows_v.at[z], load_sem.at[0])
+    own_load.start()
+
+    def tile_loads(f):
+        cols = pl.ds(pl.multiple_of(f * ft, 128), ft)
+        return [
+            pltpu.make_async_copy(src.at[:, cols], dst.at[:, cols], tile_sem.at[k, f])
+            for k, (src, dst) in enumerate(((gate_ref, gate_v), (up_ref, up_v), (down_ref, down_v)))
+        ]
+
+    cot_load = pltpu.make_async_copy(cot_ref, cot_v, load_sem.at[1])
+    for f in range(n_f):
+        for copy in tile_loads(f):
+            copy.start()
+        if f == 0:
+            cot_load.start()
+
+    pl.semaphore_wait(barrier, (z + size - 1) // size + (2 * size - 2 - z) // size)
+
+    own_load.wait()
+
+    def ag_copy(j, dz):
+        way = (dz + 1) // 2
+        return pltpu.make_async_remote_copy(
+            src_ref=rows_v.at[j], dst_ref=rows_v.at[j], send_sem=ag_send.at[way, j],
+            recv_sem=ag_recv.at[j], device_id=to(dz), device_id_type=MESH,
+        )
+
+    @pl.when(has_low)
+    def _():
+        ag_copy(z, -1).start()
+
+    @pl.when(has_high)
+    def _():
+        ag_copy(z, 1).start()
+
+    def rs_copy(j, n, dz, own):
+        way = (dz + 1) // 2
+        if own:
+            dst = below.at[n] if dz == 1 else above.at[n]
+            sem = own_recv.at[1 - way, n]
+        else:
+            dst, sem = land.at[j, n], rs_recv.at[j, n]
+        return pltpu.make_async_remote_copy(
+            src_ref=part.at[j, n], dst_ref=dst, send_sem=rs_send.at[j, n],
+            recv_sem=sem, device_id=to(dz), device_id_type=MESH,
+        )
+
+    def pass_on(j, n, what):
+        for dz in (1, -1):
+            for own in (True, False):
+                hop = j == z + dz
+                going = (j > z) if dz == 1 else (j < z)
+                near = hop if own else jnp.logical_not(hop)
+
+                @pl.when(jnp.logical_and(going, near))
+                def _(dz=dz, own=own):
+                    copy = rs_copy(j, n, dz, own)
+                    copy.start() if what == "start" else copy.wait_send()
+
+    def out_copies(j):
+        at = pl.ds(pl.multiple_of(j * rows, rows), rows)
+        return [
+            pltpu.make_async_copy(src.at[j], dst.at[at, :], out_sem.at[k, j])
+            for k, (src, dst) in enumerate(
+                ((rows_v, rows_out), (hid_v, hid_out), (dg_v, dg_out), (du_v, du_out))
+            )
+        ]
+
+    def step(s, carry):
+        for sign in (-1, 1):
+            j = z + sign * s
+            inside = jnp.logical_and(s > 0, (j >= 0) if sign == -1 else (j < size))
+
+            @pl.when(inside)
+            def _(j=j, sign=sign):
+                ag_copy(j, -sign).wait_recv()
+
+            onward = has_high if sign == -1 else has_low
+
+            @pl.when(jnp.logical_and(inside, onward))
+            def _(j=j, sign=sign):
+                ag_copy(j, -sign).start()
+
+        j = line_order(z, s)
+        at = pl.ds(pl.multiple_of(j * rows, rows), rows)
+
+        @pl.when(s == 0)
+        def _():
+            cot_load.wait()
+
+        def units_tile(f, carry):
+            @pl.when(s == 0)
+            def _():
+                for copy in tile_loads(f):
+                    copy.wait()
+
+            cols = pl.ds(pl.multiple_of(f * ft, 128), ft)
+            mine = rows_v[j]
+            gate = jnp.dot(mine, gate_v[:, cols], preferred_element_type=f32)
+            upper = jnp.dot(mine, up_v[:, cols], preferred_element_type=f32)
+            d_hidden = jnp.dot(cot_v[at, :], down_v[:, cols], preferred_element_type=f32)
+            sig = 1.0 / (1.0 + jnp.exp(-gate))
+            act = gate * sig
+            hid_v[j, :, cols] = (act * upper).astype(bf16)
+            du_v[j, :, cols] = (d_hidden * act).astype(bf16)
+            dg_v[j, :, cols] = (d_hidden * upper * (sig + act * (1.0 - sig))).astype(bf16)
+            return carry
+
+        lax.fori_loop(0, n_f, units_tile, 0)
+        for copy in out_copies(j):
+            copy.start()
+        ends = jnp.logical_and(s > 0, jnp.logical_not(jnp.logical_and(has_low, has_high)))
+
+        def width_tile(n, carry):
+            at_n = pl.ds(pl.multiple_of(n * nt, nt), nt)
+            dims = (((1,), (1,)), ((), ()))
+            total = lax.dot_general(dg_v[j], gate_v[at_n, :], dims, preferred_element_type=f32)
+            total += lax.dot_general(du_v[j], up_v[at_n, :], dims, preferred_element_type=f32)
+            part[j, n] = total.astype(bf16)
+
+            @pl.when(ends)
+            def _():
+                pass_on(j, n, "start")
+
+            return carry
+
+        lax.fori_loop(0, n_n, width_tile, 0)
+        return carry
+
+    lax.fori_loop(0, size, step, 0)
+
+    def down_tile(i, carry):
+        j, n = i // n_n, i % n_n
+        at_n = pl.ds(pl.multiple_of(n * nt, nt), nt)
+        total = lax.dot_general(
+            hid_v[j], down_v[at_n, :], (((1,), (1,)), ((), ())), preferred_element_type=f32
+        )
+        res_v[j, :, at_n] = total.astype(bf16)
+        return carry
+
+    def forward(j, n):
+        pltpu.make_async_copy(land.at[j, n], land.at[j, n], rs_recv.at[j, n]).wait()
+        part[j, n] = (part[j, n].astype(f32) + land[j, n].astype(f32)).astype(bf16)
+        pass_on(j, n, "start")
+
+    middle = jnp.logical_and(has_low, has_high)
+
+    @pl.when(middle)
+    def _():
+        def first(n, carry):
+            forward(3 - z, n)
+            return carry
+
+        lax.fori_loop(0, n_n, first, 0)
+
+    lax.fori_loop(0, (size * n_n) // 2, down_tile, 0)
+
+    @pl.when(middle)
+    def _():
+        def second(n, carry):
+            forward(3 - 3 * (z // 2), n)
+            forward(3 * (z // 2), n)
+            return carry
+
+        lax.fori_loop(0, n_n, second, 0)
+
+    lax.fori_loop((size * n_n) // 2, size * n_n, down_tile, 0)
+    sum_copies = [
+        pltpu.make_async_copy(
+            res_v.at[j], sum_out.at[pl.ds(j * rows, rows), :], load_sem.at[2 + j]
+        )
+        for j in range(size)
+    ]
+    for copy in sum_copies:
+        copy.start()
+
+    def last(n, carry):
+        @pl.when(has_low)
+        def _():
+            pltpu.make_async_copy(below.at[n], below.at[n], own_recv.at[0, n]).wait()
+            part[z, n] = (part[z, n].astype(f32) + below[n].astype(f32)).astype(bf16)
+
+        @pl.when(has_high)
+        def _():
+            pltpu.make_async_copy(above.at[n], above.at[n], own_recv.at[1, n]).wait()
+            part[z, n] = (part[z, n].astype(f32) + above[n].astype(f32)).astype(bf16)
+
+        dn_out[:, pl.ds(pl.multiple_of(n * nt, nt), nt)] = part[z, n]
+        return carry
+
+    lax.fori_loop(0, n_n, last, 0)
+
+    def drain(j, carry):
+        for copy in out_copies(j):
+            copy.wait()
+        for dz in (-1, 1):
+            came = jnp.logical_or(j == z, (j > z) if dz == -1 else (j < z))
+            there = has_low if dz == -1 else has_high
+
+            @pl.when(jnp.logical_and(came, there))
+            def _(dz=dz):
+                ag_copy(j, dz).wait_send()
+
+        def sent(n, carry):
+            @pl.when(j != z)
+            def _():
+                pltpu.make_async_copy(part.at[j, n], part.at[j, n], rs_send.at[j, n]).wait()
+
+            return carry
+
+        lax.fori_loop(0, n_n, sent, 0)
+        return carry
+
+    lax.fori_loop(0, size, drain, 0)
+    for copy in sum_copies:
+        copy.wait()
+
+
+def ffn(two, cot_rows, gate, up, down, axis="tensor", ft=768, nt=512, collective_id=1, limit=66_000_000):
+    rows, width = two.shape
+    units = gate.shape[1]
+    size = 4
+    length = rows * size
+    n_f, n_n = units // ft, width // nt
+    bf16 = jnp.bfloat16
+    hbm = pl.BlockSpec(memory_space=pl.ANY)
+    vm = pltpu.VMEM
+    dma = pltpu.SemaphoreType.DMA
+    shape = lambda *s: jax.ShapeDtypeStruct(s, bf16)
+    return pl.pallas_call(
+        functools.partial(ffn_body, axis=axis, ft=ft, nt=nt),
+        out_shape=(
+            shape(length, width), shape(length, units), shape(length, units), shape(length, units),
+            shape(length, width), shape(rows, width),
+        ),
+        in_specs=[hbm] * 5,
+        out_specs=(hbm,) * 5 + (pl.BlockSpec(memory_space=pltpu.VMEM),),
+        scratch_shapes=[
+            vm((size, rows, width), bf16), vm((length, width), bf16),
+            vm((width, units), bf16), vm((width, units), bf16), vm((width, units), bf16),
+            vm((size, rows, units), bf16), vm((size, rows, units), bf16), vm((size, rows, units), bf16),
+            vm((size, n_n, rows, nt), bf16), vm((size, n_n, rows, nt), bf16),
+            vm((n_n, rows, nt), bf16), vm((n_n, rows, nt), bf16),
+            vm((size, rows, width), bf16),
+            dma((3, n_f)), dma((2 + size,)), dma((2, size)), dma((size,)), dma((size, n_n)), dma((size, n_n)),
+            dma((2, n_n)), dma((4, size)),
+        ],
+        compiler_params=pltpu.CompilerParams(
+            collective_id=collective_id, has_side_effects=True, vmem_limit_bytes=limit
+        ),
+        cost_estimate=pl.CostEstimate(
+            flops=12 * length * width * units, bytes_accessed=8 * width * units + 8 * length * units,
+            transcendentals=length * units,
+        ),
+        name="ffn",
+    )(two, cot_rows, gate, up, down)
 
 
 def local(
@@ -76,9 +377,14 @@
     gains = lax.all_gather(jnp.stack([gain_one, gain_two]), "dp", axis=1, tiled=True).astype(f32)
     full_query_b = lax.all_gather(query_b, "tensor", axis=0, tiled=True)
     qkv_b = jnp.concatenate([full_query_b, key_b, value_b]).astype(f32)
-    full_gate = lax.all_gather(gate_w, "dp", axis=0, tiled=True)
-    full_up = lax.all_gather(up_w, "dp", axis=0, tiled=True)
-    full_down = lax.all_gather(down_w, "dp", axis=0, tiled=True)
+    units = gate_w.shape[1]
+    padded = -(-units // 768) * 768
+
+    def whole(shard):
+        shard = jnp.pad(shard, ((0, 0), (0, padded - units)))
+        return lax.all_gather(shard, "dp", axis=0, tiled=True)
+
+    full_gate, full_up, full_down = whole(gate_w), whole(up_w), whole(down_w)
     cot_rows = lax.all_gather(cotangent, "tensor", axis=0, tiled=True)
 
     inputs = tokens.astype(f32)
@@ -120,22 +426,12 @@
     unit_two = middle * inverse_two
     normed_two = (unit_two * gains[1]).astype(bf16)
 
-    rows_two = lax.all_gather(normed_two, "tensor", axis=0, tiled=True)
-    gate = jnp.dot(rows_two, full_gate, preferred_element_type=f32)
-    upper = jnp.dot(rows_two, full_up, preferred_element_type=f32)
-    sigmoid = jax.nn.sigmoid(gate)
-    hidden_low = (gate * sigmoid * upper).astype(bf16)
-    ffn_sum = lax.psum_scatter(
-        contract_cols(hidden_low, full_down).astype(bf16), "tensor", scatter_dimension=0, tiled=True
-    ).astype(f32)
+    rows_two, hidden_low, d_gate, d_upper, ffn_part, d_normed_two = ffn(
+        normed_two, cot_rows, full_gate, full_up, full_down
+    )
+    ffn_sum = lax.psum_scatter(ffn_part, "tensor", scatter_dimension=0, tiled=True).astype(f32)
     mixed = (middle + ffn_sum).astype(bf16)
-    d_hidden = jnp.dot(cot_rows, full_down, preferred_element_type=f32)
-    d_upper = (d_hidden * gate * sigmoid).astype(bf16)
-    d_gate = (d_hidden * upper * sigmoid * (1.0 + gate * (1.0 - sigmoid))).astype(bf16)
-    d_normed_two = lax.psum_scatter(
-        (contract_cols(d_gate, full_gate) + contract_cols(d_upper, full_up)).astype(bf16),
-        "tensor", scatter_dimension=0, tiled=True,
-    ).astype(f32)
+    d_normed_two = d_normed_two.astype(f32)
     grad_down = contract_rows(cot_rows, hidden_low).astype(bf16)
     grad_gate = contract_rows(rows_two, d_gate).astype(bf16)
     grad_up = contract_rows(rows_two, d_upper).astype(bf16)
@@ -177,7 +473,7 @@
     def over_dp(grad):
         return lax.psum_scatter(grad, "dp", scatter_dimension=0, tiled=True)
 
-    sum_gate, sum_up, sum_down = (over_dp(g).astype(f32) for g in (grad_gate, grad_up, grad_down))
+    sum_gate, sum_up, sum_down = (over_dp(g)[:, :units].astype(f32) for g in (grad_gate, grad_up, grad_down))
     part = over_dp(jnp.concatenate([grad_qkv, grad_out], axis=1))
     pair = jnp.stack([part[:, :query_width], part[:, qkv_width:]])
     pair = lax.psum_scatter(pair, "tensor", scatter_dimension=2, tiled=True).astype(f32)

time: 1040 us -> 983 us (0.945)
  Pallas kernels: 0 us -> 108 us
  waiting for transfers between devices: 674 us -> 581 us
  matrix products: 173 us -> 90 us
  local copies, waits for them, and re-layouts: 58.9 us -> 72.7 us
    pallas_call x0 -> x1, Pallas kernels: none -> 108 us  [ffn(): pl.pallas_call(functools.partial(ffn_body, axis=axis, ft=ft, nt=nt), out_...]
    reduce_scatter x2 -> x1, waiting for transfers between devices: 107 us -> 56.5 us  [local(): lax.psum_scatter(ffn_part, 'tensor', scatter_dimension=0, tiled=True)]
    dot_general x3 -> x0, matrix products: 47.2 us -> none  [the longest x1 20.7 us: local(): d_hidden = jnp.dot(cot_rows, full_down, preferred_element_type=f32)]
    unnamed x19 -> x17, waiting for transfers between devices: 34.8 us -> 71.6 us
    reduce_scatter x3, waiting for transfers between devices: 169 us -> 132 us  [over_dp(): return lax.psum_scatter(grad, 'dp', scatter_dimension=0, tiled=True)]
    dot_general x10 -> x7, matrix products: 88.5 us -> 53.5 us  [dot_f32(): lax.dot_general(left, right, (dims, ((), ())), preferred_element_type=jnp...]
    all_gather x4 -> x3, waiting for transfers between devices: 185 us -> 154 us  [whole(): return lax.all_gather(shard, 'dp', axis=0, tiled=True)]
    unnamed x76 -> x88, local copies, waits for them, and re-layouts: 29 us -> 33.7 us
  transfers between devices with their start and end apart: 17 -> 15, of which waited for: 17 -> 14; matrix products, arithmetic and copies ran while one was open for 15% -> 12% of each run, Pallas kernels for 0% -> 0%
where the time goes in v2:
time: 983 us; the launch traced here: 973 us
  waiting for transfers between devices  581 us (59%)
  Pallas kernels  108 us (11%)
  matrix products  90 us (9%)
  local copies, waits for them, and re-layouts  72.7 us (7%)
  blocking collectives  61.3 us (6%)
  other arithmetic  43.9 us (4%)
  between operations  15 us (2%)
    all_gather x3, waiting for transfers between devices, whole(): return lax.all_gather(shard, 'dp', axis=0, tiled=True)  154 us
    reduce_scatter x3, waiting for transfers between devices, over_dp(): return lax.psum_scatter(grad, 'dp', scatter_dimension=0, tiled=True)  132 us
    pallas_call x1, Pallas kernels, ffn(): pl.pallas_call(functools.partial(ffn_body, axis=axis, ft=ft, nt=nt), out_...  108 us
    unnamed x17, waiting for transfers between devices  71.6 us
    reduce_scatter x1, waiting for transfers between devices, local(): lax.psum_scatter(ffn_part, 'tensor', scatter_dimension=0, tiled=True)  56.5 us
    dot_general x7, matrix products, dot_f32(): lax.dot_general(left, right, (dims, ((), ())), preferred_element_type=jnp...  53.5 us
    all_gather x1, waiting for transfers between devices, local(): cot_rows = lax.all_gather(cotangent, 'tensor', axis=0, tiled=True)  44.6 us
    all_gather x1, waiting for transfers between devices, local(): joined = lax.all_gather(joined, 'dp', axis=0, tiled=True)  44.4 us
  transfers between devices with their start and end apart: 15, of which 14 were waited for; matrix products, arithmetic and copies ran while one was open for 12% of the time, Pallas kernels for 0%

profile of v2, /device:TPU:26, one launch (start us, length us, event | category | flops | bytes accessed | tf_op | source)
XLA Modules:
  0.0 973.4 jit_solution(10844496726370811688)
XLA Ops:
  9.1 30.6 %all-gather.10.cloned.1.call-done = bf16[2,192,1536]{2,1,0:T(8,128)(2,1)} async-done(((bf16[2,192,384]{2,1,0:T(8,128)(2,1)}), bf16[2,192,1536]{2,1,0:T(8,128)(2,1)}) %all-gather.10.cloned.1.call-update) | async-done | bytes 1179664 | tf_op jit(solution)/shard_map/all_gather | solution.py:371
  42.4 8.9 all-gather
  51.4 10.8 %all-gather.1 = bf16[4,1,384]{2,1,0:T(2,128)(2,1)S(1)} all-gather(bf16[1,1,384]{2,1,0:T(2,128)(2,1)S(1)} %reshape.237), channel_id=1, replica_groups=mesh['dp'=8,'tensor'=4] {'tensor'}, dimensions={0}, use_global_device_ids=true | all-gather | bytes 3840 | tf_op jit(solution)/shard_map/all_gather | solution.py:378
  64.3 44.4 %all-gather.12.cloned.1.call-done = bf16[1536,3584]{1,0:T(8,128)(2,1)} async-done(((bf16[192,3584]{1,0:T(8,128)(2,1)}), bf16[1536,3584]{1,0:T(8,128)(2,1)}) %all-gather.12.cloned.1.call-update) | async-done | bytes 11010064 | tf_op jit(solution)/shard_map/all_gather | solution.py:373
  108.7 4.6 fusion.17
  119.1 2.1 pad.10
  121.3 2.1 pad.11
  123.5 2.2 pad.12
  131.8 13.3 %all-gather.14.cloned.1.call-done = bf16[1024,512]{1,0:T(8,128)(2,1)} async-done(((bf16[256,512]{1,0:T(8,128)(2,1)}), bf16[1024,512]{1,0:T(8,128)(2,1)}) %all-gather.14.cloned.1.call-update) | async-done | bytes 1048592 | tf_op jit(solution)/shard_map/all_gather | solution.py:403
  145.1 2.1 constant_dynamic-slice_fusion.1
  149.0 2.4 fusion.9
  151.4 1.9 exponential_reduce_fusion
  155.0 2.4 convolution_convert_fusion.5
  157.5 4.2 multiply_reduce_fusion
  163.9 44.6 %all-gather.16.cloned.1.call-done.cot_ref = bf16[1024,1536]{1,0:T(8,128)(2,1)} async-done(((bf16[256,1536]{1,0:T(8,128)(2,1)}), bf16[1024,1536]{1,0:T(8,128)(2,1)}) %all-gather.16.cloned.1.call-update) | async-done | bytes 3145744 | tf_op jit(solution)/shard_map/all_gather | solution.py:388
  208.5 52.1 %all-gather.18.cloned.1.call-done.gate_ref = bf16[1536,2304]{1,0:T(8,128)(2,1)} async-done(((bf16[192,2304]{1,0:T(8,128)(2,1)}), bf16[1536,2304]{1,0:T(8,128)(2,1)}) %all-gather.18.cloned.1.call-update) | async-done | bytes 7077904 | tf_op jit(solution)/shard_map/all_gather | solution.py:385
  260.6 51.1 %all-gather.20.cloned.1.call-done.up_ref = bf16[1536,2304]{1,0:T(8,128)(2,1)} async-done(((bf16[192,2304]{1,0:T(8,128)(2,1)}), bf16[1536,2304]{1,0:T(8,128)(2,1)}) %all-gather.20.cloned.1.call-update) | async-done | bytes 7077904 | tf_op jit(solution)/shard_map/all_gather | solution.py:385
  311.6 50.6 %all-gather.22.cloned.1.call-done.down_ref = bf16[1536,2304]{1,0:T(8,128)(2,1)} async-done(((bf16[192,2304]{1,0:T(8,128)(2,1)}), bf16[1536,2304]{1,0:T(8,128)(2,1)}) %all-gather.22.cloned.1.call-update) | async-done | bytes 7077904 | tf_op jit(solution)/shard_map/all_gather | solution.py:385
  362.3 107.8 %ffn.1 = (bf16[1024,1536]{1,0:T(8,128)(2,1)}, bf16[1024,2304]{1,0:T(8,128)(2,1)}, bf16[1024,2304]{1,0:T(8,128)(2,1)}, bf16[1024,2304]{1,0:T(8,128)(2,1)}, bf16[1...) custom-call(bf16[256,1536]{1,0:T(8,128)(2,1)} %multiply_convert_fusion.two_ref, ...), custom_call_target="tpu_custom_call" | custom-call | flops 43486543872 | bytes 47185920 | tf_op jit(solution)/shard_map/ffn/pallas_call | solution.py:327
  473.4 56.5 %reduce-scatter.13.cloned.1.call-done = bf16[256,1536]{1,0:T(8,128)(2,1)} async-done(((bf16[1024,1536]{1,0:T(8,128)(2,1)}), bf16[256,1536]{1,0:T(8,128)(2,1)}) %reduce-scatter.13.cloned.1.call-update) | async-done | bytes 786448 | tf_op jit(solution)/shard_map/reduce_scatter | solution.py:432
  529.8 3.1 fusion.31
  532.9 4.7 fusion.20
  539.0 8.0 fusion.1
  547.1 7.0 fusion.43
  554.1 11.2 %fusion.3 = bf16[2,6,256,768]{2,3,1,0:T(8,128)(2,1)} fusion(f32[2,768,256,6]{2,1,3,0:T(8,128)} %get-tuple-element.139, f32[2,768,256,6]{2,1,3,0:T(8,128)} %copy-done.2, f32[2,6,256]{2,1,0:T(8,128)} %get-tuple-element.138, f32[2,6,256]{2,1,0:T(8,128)} %copy-done.22, pred[256,768]{0,1:T(8,128)(4,1)S(1)} %compare_and_fusion), kind=kLoop, calls=%fused_computation.9 | loop fusion | flops 14155776 | bytes 23814144 | tf_op jit(solution)/shard_map/convert_element_type | solution.py:447
  565.3 4.3 fusion.42
  570.6 9.1 dynamic_update_slice.3
  582.0 3.1 convolution_multiply_fusion
  586.3 3.6 convolution_convert_fusion.4
  589.9 17.0 %reduce-scatter.15.cloned.1.call-done = bf16[256,512]{0,1:T(8,128)(2,1)} async-done(((bf16[1024,512]{0,1:T(8,128)(2,1)}), bf16[256,512]{0,1:T(8,128)(2,1)}) %reduce-scatter.15.cloned.1.call-update) | async-done | bytes 262160 | tf_op jit(solution)/shard_map/reduce_scatter | solution.py:461
  614.0 2.0 convolution_convert_fusion.3
  616.2 5.0 pad_maximum_fusion
  621.4 12.8 %fusion = bf16[1536,2304]{0,1:T(8,128)(2,1)} fusion(bf16[1024,2304]{1,0:T(8,128)(2,1)} %get-tuple-element.25, bf16[1024,1536]{1,0:T(8,128)(2,1)} %all-gather.16.cloned.1.call-done.cot_ref), kind=kOutput, calls=%fused_computation.4 | convolution fusion | flops 7251296256 | bytes 14942208 | tf_op jit(solution)/shard_map/dot_general | solution.py:43
  634.2 10.9 %copy.161 = bf16[1536,2304]{1,0:T(8,128)(2,1)} copy(bf16[1536,2304]{0,1:T(8,128)(2,1)} %fusion) | data formatting | bytes 14155776
  645.3 12.4 %convolution_convert_fusion.1 = bf16[1536,2304]{1,0:T(8,128)(2,1)} fusion(bf16[1024,1536]{1,0:T(8,128)(2,1)} %get-tuple-element.22, bf16[1024,2304]{1,0:T(8,128)(2,1)} %get-tuple-element.24), kind=kOutput, calls=%fused_computation.1 | convolution fusion | flops 7251296256 | bytes 14942208 | tf_op jit(solution)/shard_map/dot_general | solution.py:43
  657.7 12.4 %convolution_convert_fusion.2 = bf16[1536,2304]{1,0:T(8,128)(2,1)} fusion(bf16[1024,1536]{1,0:T(8,128)(2,1)} %get-tuple-element.22, bf16[1024,2304]{1,0:T(8,128)(2,1)} %get-tuple-element.23), kind=kOutput, calls=%fused_computation.2 | convolution fusion | flops 7251296256 | bytes 14942208 | tf_op jit(solution)/shard_map/dot_general | solution.py:43
  670.6 6.1 fusion.39
  676.7 41.6 %psum.7 = f32[5120]{0:T(1024)S(1)} all-reduce(f32[5120]{0:T(1024)S(1)} %pad_maximum_fusion.13), channel_id=1, replica_groups=mesh['dp'=8,'tensor'=4] {'dp','tensor'}, use_global_device_ids=true, to_apply=%region_12.13 | all-reduce | flops 5120 | bytes 40960 | tf_op jit(solution)/shard_map/psum | solution.py:483
  722.5 2.9 copy.159
  725.4 4.5 reshape.246
  731.3 2.8 fusion.38
  734.0 42.0 %reduce-scatter.27.cloned.1.call-done = bf16[192,2304]{1,0:T(8,128)(2,1)} async-done(((bf16[1536,2304]{1,0:T(8,128)(2,1)}), bf16[192,2304]{1,0:T(8,128)(2,1)}) %reduce-scatter.27.cloned.1.call-update) | async-done | bytes 884752
  779.4 65.5 %reduce-scatter.23.cloned.1.call-done = bf16[192,2304]{1,0:T(8,128)(2,1)} async-done(((bf16[1536,2304]{1,0:T(8,128)(2,1)}), bf16[192,2304]{1,0:T(8,128)(2,1)}) %reduce-scatter.23.cloned.1.call-update) | async-done | bytes 884752 | tf_op jit(solution)/shard_map/reduce_scatter | solution.py:474
  845.0 2.5 slice_convert_fusion
  847.5 66.5 %reduce-scatter.21.cloned.1.call-done = bf16[192,2304]{1,0:T(8,128)(2,1)} async-done(((bf16[1536,2304]{1,0:T(8,128)(2,1)}), bf16[192,2304]{1,0:T(8,128)(2,1)}) %reduce-scatter.21.cloned.1.call-update) | async-done | bytes 884752 | tf_op jit(solution)/shard_map/reduce_scatter | solution.py:474
  914.0 2.5 slice_convert_fusion.1
  916.5 17.0 %reduce-scatter.19.cloned.1.call-done = bf16[48,512]{1,0:T(8,128)(2,1)} async-done(((bf16[192,512]{1,0:T(8,128)(2,1)}), bf16[48,512]{1,0:T(8,128)(2,1)}) %reduce-scatter.19.cloned.1.call-update) | async-done | bytes 49168 | tf_op jit(solution)/shard_map/reduce_scatter | solution.py:480
  934.9 28.9 %reduce-scatter.25.cloned.1.call-done = bf16[384,384]{1,0:T(8,128)(2,1)} async-done(((bf16[1536,384]{1,0:T(8,128)(2,1)}), bf16[384,384]{1,0:T(8,128)(2,1)}) %reduce-scatter.25.cloned.1.call-update) | async-done | bytes 294928
  (180 shorter events, 54.3 us)
Async XLA Ops:
  7.2 119.1 %copy-start = (s32[1,1024]{1,0:T(1,128)S(1)}, s32[1,1024]{1,0:T(1,128)}, u32[]{:S(2)}) copy-start(s32[1,1024]{1,0:T(1,128)} %param.16) | copy-start | bytes 12292
  7.2 33.9 %copy-start.25 = (bf16[192,256]{1,0:T(8,128)(2,1)S(1)}, bf16[192,256]{1,0:T(8,128)(2,1)}, u32[]{:S(2)}) copy-start(bf16[192,256]{1,0:T(8,128)(2,1)} %param.20) | copy-start | bytes 294916
  7.2 33.9 %copy-start.24 = (bf16[192,256]{1,0:T(8,128)(2,1)S(1)}, bf16[192,256]{1,0:T(8,128)(2,1)}, u32[]{:S(2)}) copy-start(bf16[192,256]{1,0:T(8,128)(2,1)} %param.22) | copy-start | bytes 294916
  7.2 32.5 %all-gather.10.cloned.1.call-start = ((), (), s32[]{:S(2)}) async-start(), calls=%async_computation.8 | async-start | bytes 1474560 | tf_op jit(solution)/shard_map/all_gather | solution.py:371
  9.1 33.3 %copy-start.34 = (bf16[192]{0:T(256)(128)(2,1)S(1)}, bf16[192]{0:T(256)(128)(2,1)}, u32[]{:S(2)}) copy-start(bf16[192]{0:T(256)(128)(2,1)} %param.17) | copy-start | bytes 1156
  9.1 33.3 %copy-start.35 = (bf16[192]{0:T(256)(128)(2,1)S(1)}, bf16[192]{0:T(256)(128)(2,1)}, u32[]{:S(2)}) copy-start(bf16[192]{0:T(256)(128)(2,1)} %param.25) | copy-start | bytes 1156
  9.1 42.4 %copy-start.31 = (bf16[384]{0:T(512)(128)(2,1)S(1)}, bf16[384]{0:T(512)(128)(2,1)}, u32[]{:S(2)}) copy-start(bf16[384]{0:T(512)(128)(2,1)} %param.19) | copy-start | bytes 2308
  9.1 99.7 %all-gather.12.cloned.1.call-start = ((), (), s32[]{:S(2)}) async-start(), calls=%async_computation.9 | async-start | bytes 12386304 | tf_op jit(solution)/shard_map/all_gather | solution.py:373
  41.1 22.9 %copy-start.32 = (bf16[256]{0:T(256)(128)(2,1)S(1)}, bf16[256]{0:T(256)(128)(2,1)}, u32[]{:S(2)}) copy-start(bf16[256]{0:T(256)(128)(2,1)} %param.23) | copy-start | bytes 1540
  41.1 22.9 %copy-start.33 = (bf16[256]{0:T(256)(128)(2,1)S(1)}, bf16[256]{0:T(256)(128)(2,1)}, u32[]{:S(2)}) copy-start(bf16[256]{0:T(256)(128)(2,1)} %param.21) | copy-start | bytes 1540
  41.1 23.0 %copy-start.5 = (bf16[256,1536]{1,0:T(8,128)(2,1)S(1)}, bf16[256,1536]{1,0:T(8,128)(2,1)}, u32[]{:S(2)}) copy-start(bf16[256,1536]{1,0:T(8,128)(2,1)} %param.15) | copy-start | bytes 2359300
  42.3 102.7 %all-gather.14.cloned.1.call-start = ((), (), s32[]{:S(2)}) async-start(), calls=%async_computation.10 | async-start | bytes 1310720 | tf_op jit(solution)/shard_map/all_gather | solution.py:403
  63.8 49.6 %copy-start.20 = (f32[256,64]{0,1:T(8,128)}, f32[256,64]{0,1:T(8,128)S(1)}, u32[]{:S(2)}) copy-start(f32[256,64]{0,1:T(8,128)S(1)} %get-tuple-element.132) | copy-start | bytes 196612
  64.1 49.3 %copy-start.26 = (f32[1536]{0:T(1024)}, f32[1536]{0:T(1024)S(1)}, u32[]{:S(2)}) copy-start(f32[1536]{0:T(1024)S(1)} %get-tuple-element.101) | copy-start | bytes 18436
  118.5 90.0 %all-gather.16.cloned.1.call-start = ((), (), s32[]{:S(2)}) async-start(), calls=%async_computation.11 | async-start | bytes 3932160 | tf_op jit(solution)/shard_map/all_gather | solution.py:388
  119.0 141.5 %all-gather.18.cloned.1.call-start = ((), (), s32[]{:S(2)}) async-start(), calls=%async_computation.12 | async-start | bytes 7962624 | tf_op jit(solution)/shard_map/all_gather | solution.py:385
  121.3 5.2 copy-start.30
  121.3 190.4 %all-gather.20.cloned.1.call-start = ((), (), s32[]{:S(2)}) async-start(), calls=%async_computation.13 | async-start | bytes 7962624 | tf_op jit(solution)/shard_map/all_gather | solution.py:385
  123.5 238.8 %all-gather.22.cloned.1.call-start = ((), (), s32[]{:S(2)}) async-start(), calls=%async_computation.14 | async-start | bytes 7962624 | tf_op jit(solution)/shard_map/all_gather | solution.py:385
  125.7 404.1 %reduce-scatter.13.cloned.1.call-start = ((), (), s32[]{:S(2)}) async-start(), calls=%async_computation.15 | async-start | bytes 3932160 | tf_op jit(solution)/shard_map/reduce_scatter | solution.py:432
  131.4 19.9 %copy-start.7 = (bf16[256,12,64]{2,0,1:T(8,128)(2,1)}, bf16[256,12,64]{2,0,1:T(8,128)(2,1)S(1)}, u32[]{:S(2)}) copy-start(bf16[256,12,64]{2,0,1:T(8,128)(2,1)S(1)} %copy.119) | copy-start | bytes 1179652
  131.8 19.6 %copy-start.9 = (bf16[256,12,64]{2,0,1:T(8,128)(2,1)}, bf16[256,12,64]{2,0,1:T(8,128)(2,1)S(1)}, u32[]{:S(2)}) copy-start(bf16[256,12,64]{2,0,1:T(8,128)(2,1)S(1)} %copy.120) | copy-start | bytes 1179652
  147.7 3.6 copy-start.12
  149.0 4.4 copy-start.15
  151.4 3.7 copy-start.2
  153.3 4.1 copy-start.22
  157.5 4.2 copy-start.17
  470.1 136.8 %reduce-scatter.15.cloned.1.call-start = ((), (), s32[]{:S(2)}) async-start(), calls=%async_computation.16 | async-start | bytes 1310720 | tf_op jit(solution)/shard_map/reduce_scatter | solution.py:461
  532.9 6.1 copy-start.16
  532.9 6.1 copy-start.23
  554.1 11.2 %copy-start.8 = (bf16[256,12,64]{2,0,1:T(8,128)(2,1)S(1)}, bf16[256,12,64]{2,0,1:T(8,128)(2,1)}, u32[]{:S(2)}) copy-start(bf16[256,12,64]{2,0,1:T(8,128)(2,1)} %copy-done.7) | copy-start | bytes 1179652
  554.1 11.2 %copy-start.10 = (bf16[256,12,64]{2,0,1:T(8,128)(2,1)S(1)}, bf16[256,12,64]{2,0,1:T(8,128)(2,1)}, u32[]{:S(2)}) copy-start(bf16[256,12,64]{2,0,1:T(8,128)(2,1)} %copy-done.9) | copy-start | bytes 1179652
  565.3 4.3 copy-start.21
  569.6 11.7 %copy-start.19 = (f32[256,64]{0,1:T(8,128)S(1)}, f32[256,64]{0,1:T(8,128)}, u32[]{:S(2)}) copy-start(f32[256,64]{0,1:T(8,128)} %get-tuple-element.131) | copy-start | bytes 196612
  569.6 12.4 %copy-start.13 = (bf16[768,2,128,1]{0,2,3,1:T(8,128)(2,1)S(1)}, bf16[768,2,128,1]{0,2,3,1:T(8,128)(2,1)}, u32[]{:S(2)}) copy-start(bf16[768,2,128,1]{0,2,3,1:T(8,128)(2,1)} %copy-done.12) | copy-start | bytes 1179652
  580.8 138.1 %reduce-scatter.17.cloned.1.call-start = ((), (), s32[]{:S(2)}) async-start(), calls=%async_computation.17 | async-start | bytes 12386304 | tf_op jit(solution)/shard_map/reduce_scatter | solution.py:474
  589.9 24.0 %copy-start.6 = (bf16[256,1536]{1,0:T(8,128)(2,1)S(1)}, bf16[256,1536]{1,0:T(8,128)(2,1)}, u32[]{:S(2)}) copy-start(bf16[256,1536]{1,0:T(8,128)(2,1)} %param.15) | copy-start | bytes 2359300
  589.9 24.0 %copy-start.27 = (f32[1536]{0:T(1024)S(1)}, f32[1536]{0:T(1024)}, u32[]{:S(2)}) copy-start(f32[1536]{0:T(1024)} %copy-done.26) | copy-start | bytes 18436
  613.9 2.2 slice-start
  614.0 2.3 slice-start.1
  621.3 154.7 %reduce-scatter.27.cloned.1.call-start = ((), (), s32[]{:S(2)}) async-start(), calls=%async_computation.22 | async-start | bytes 7962624
  645.1 199.9 %reduce-scatter.23.cloned.1.call-start = ((), (), s32[]{:S(2)}) async-start(), calls=%async_computation.20 | async-start | bytes 7962624 | tf_op jit(solution)/shard_map/reduce_scatter | solution.py:474
  657.7 256.3 %reduce-scatter.21.cloned.1.call-start = ((), (), s32[]{:S(2)}) async-start(), calls=%async_computation.19 | async-start | bytes 7962624 | tf_op jit(solution)/shard_map/reduce_scatter | solution.py:474
  670.2 263.3 %reduce-scatter.19.cloned.1.call-start = ((), (), s32[]{:S(2)}) async-start(), calls=%async_computation.18 | async-start | bytes 245760 | tf_op jit(solution)/shard_map/reduce_scatter | solution.py:480
  670.6 6.1 copy-start.28
  718.3 4.1 copy-start.29
  720.7 243.1 %reduce-scatter.25.cloned.1.call-start = ((), (), s32[]{:S(2)}) async-start(), calls=%async_computation.21 | async-start | bytes 1474560
  845.0 121.7 %copy-start.1 = (s32[1,1024]{1,0:T(1,128)S(1)}, s32[1,1024]{1,0:T(1,128)}, u32[]{:S(2)}) copy-start(s32[1,1024]{1,0:T(1,128)} %param.16) | copy-start | bytes 12292
  (5 other events, 6.3 us)
Sparse Core Ops, SparseCore 0:
  10.2 29.5 all-gather.9
  42.5 66.2 all-gather.11
  118.6 26.4 all-gather.13
  146.5 61.9 all-gather.15
  210.8 49.7 all-gather.17
  262.9 48.7 all-gather.19
  313.5 48.7 all-gather.21
  470.2 59.5 reduce-scatter.12
  580.9 25.9 reduce-scatter.14
  621.4 85.4 reduce-scatter.16
  710.4 65.5 reduce-scatter.26
  779.4 65.4 reduce-scatter.22
  848.5 65.4 reduce-scatter.20
  916.7 16.7 reduce-scatter.18
  935.6 28.0 reduce-scatter.24

commit v3 on v2

--- a/solution.py
+++ b/solution.py
@@ -67,7 +67,7 @@
 
 
 def ffn_body(
-    two_ref, cot_ref, gate_ref, up_ref, down_ref,
+    two_ref, cot_ref, weights_ref,
     rows_out, hid_out, dg_out, du_out, sum_out, dn_out,
     rows_v, cot_v, gate_v, up_v, down_v, hid_v, dg_v, du_v, part, land, below, above, res_v,
     tile_sem, load_sem, ag_send, ag_recv, rs_send, rs_recv, own_recv, out_sem,
@@ -76,7 +76,7 @@
     f32, bf16 = jnp.float32, jnp.bfloat16
     size = 4
     rows, width = two_ref.shape
-    units = gate_ref.shape[1]
+    units = weights_ref.shape[1] // 3
     n_f, n_n = units // ft, width // nt
     z = lax.axis_index(axis)
     has_low, has_high = z > 0, z < size - 1
@@ -100,8 +100,11 @@
     def tile_loads(f):
         cols = pl.ds(pl.multiple_of(f * ft, 128), ft)
         return [
-            pltpu.make_async_copy(src.at[:, cols], dst.at[:, cols], tile_sem.at[k, f])
-            for k, (src, dst) in enumerate(((gate_ref, gate_v), (up_ref, up_v), (down_ref, down_v)))
+            pltpu.make_async_copy(
+                weights_ref.at[:, pl.ds(pl.multiple_of(k * units + f * ft, 128), ft)],
+                dst.at[:, cols], tile_sem.at[k, f],
+            )
+            for k, dst in enumerate((gate_v, up_v, down_v))
         ]
 
     cot_load = pltpu.make_async_copy(cot_ref, cot_v, load_sem.at[1])
@@ -313,9 +316,9 @@
         copy.wait()
 
 
-def ffn(two, cot_rows, gate, up, down, axis="tensor", ft=768, nt=512, collective_id=1, limit=66_000_000):
+def ffn(two, cot_rows, weights, axis="tensor", ft=768, nt=512, collective_id=1, limit=66_000_000):
     rows, width = two.shape
-    units = gate.shape[1]
+    units = weights.shape[1] // 3
     size = 4
     length = rows * size
     n_f, n_n = units // ft, width // nt
@@ -330,7 +333,7 @@
             shape(length, width), shape(length, units), shape(length, units), shape(length, units),
             shape(length, width), shape(rows, width),
         ),
-        in_specs=[hbm] * 5,
+        in_specs=[hbm] * 3,
         out_specs=(hbm,) * 5 + (pl.BlockSpec(memory_space=pltpu.VMEM),),
         scratch_shapes=[
             vm((size, rows, width), bf16), vm((length, width), bf16),
@@ -350,7 +353,248 @@
             transcendentals=length * units,
         ),
         name="ffn",
-    )(two, cot_rows, gate, up, down)
+    )(two, cot_rows, weights)
+
+
+def square(d):
+    core, x, y = d % 2, (d // 2) % 2, d // 4
+    by_x, by_y = d + 2 - 4 * x, d + 4 - 8 * y
+    return by_x, by_y, d + 1 - 2 * core, by_x + 4 - 8 * y
+
+
+def front_body(
+    query_ref, out_ref, fixed_ref, ffn_ref, cot_ref,
+    att_all, ffn_all, cot_all, extra_out,
+    att_v, fill_sem, z_send, z_recv, cot_send, cot_recv, send, recv, keep_sem,
+    *, att_w, ffn_w, order, lead,
+):
+    d, z = lax.axis_index("dp"), lax.axis_index("tensor")
+    size = 4
+    by_x, by_y, mate, across = square(d)
+    rows = ffn_ref.shape[0]
+    half = rows // 2
+    part = query_ref.shape[1]
+    fixed = fixed_ref.shape[1]
+    chunk = cot_ref.shape[0]
+    tall = query_ref.shape[0]
+
+    barrier = pltpu.get_barrier_semaphore()
+    for peer in (by_x, by_y, mate):
+        pl.semaphore_signal(barrier, inc=1, device_id={"dp": peer}, device_id_type=MESH)
+    for hop in range(1, size):
+        pl.semaphore_signal(
+            barrier, inc=1, device_id={"tensor": (z + hop) % size}, device_id_type=MESH
+        )
+
+    def place(of, owner):
+        return pl.ds(pl.multiple_of(fixed + of * size * part + owner * part, 128), part)
+
+    fills = [pltpu.make_async_copy(fixed_ref, att_v.at[pl.ds(0, rows), pl.ds(0, fixed)], fill_sem.at[0])]
+    for of, ref in enumerate((query_ref, out_ref)):
+        fills.append(pltpu.make_async_copy(ref, att_v.at[:, place(of, z)], fill_sem.at[1 + of]))
+    at = pl.ds(pl.multiple_of(z * chunk, chunk), chunk)
+    fills.append(pltpu.make_async_copy(cot_ref, cot_all.at[at, :], fill_sem.at[3]))
+    for copy in fills:
+        copy.start()
+
+    pl.semaphore_wait(barrier, 3 + size - 1)
+
+    def z_copy(of, hop):
+        ref = (query_ref, out_ref)[of]
+        return pltpu.make_async_remote_copy(
+            src_ref=ref, dst_ref=att_v.at[:, place(of, z)], send_sem=z_send.at[of, hop - 1],
+            recv_sem=z_recv.at[of, hop - 1], device_id={"tensor": (z + hop) % size},
+            device_id_type=MESH,
+        )
+
+    def cot_copy(hop):
+        return pltpu.make_async_remote_copy(
+            src_ref=cot_ref, dst_ref=cot_all.at[at, :], send_sem=cot_send.at[hop - 1],
+            recv_sem=cot_recv.at[hop - 1], device_id={"tensor": (z + hop) % size},
+            device_id_type=MESH,
+        )
+
+    for of in range(2):
+        for hop in range(1, size):
+            z_copy(of, hop).start()
+    fills[0].wait()
+
+    def views(kind, p):
+        src, dst, wide = ((att_v, att_all, att_w), (ffn_ref, ffn_all, ffn_w))[kind]
+        return src, dst, pl.ds(pl.multiple_of(p * wide, 128), wide)
+
+    def slot(kind, p):
+        return p + kind * n_att
+
+    n_att = att_all.shape[1] // att_w
+
+    def block(dst, cols, owner, first=0, many=None):
+        many = rows if many is None else many
+        return dst.at[pl.ds(pl.multiple_of(owner * rows + first, 16), many), cols]
+
+    def remote(src, dst, way, at_slot, peer):
+        return pltpu.make_async_remote_copy(
+            src_ref=src, dst_ref=dst, send_sem=send.at[way, at_slot], recv_sem=recv.at[way, at_slot],
+            device_id={"dp": peer}, device_id_type=MESH,
+        )
+
+    def own(kind, p):
+        src, dst, cols = views(kind, p)
+        mine = src.at[pl.ds(0, rows), cols]
+        there = block(dst, cols, d)
+        s = slot(kind, p)
+        return [
+            remote(mine, there, 0, s, by_x), remote(mine, there, 1, s, by_y),
+            remote(mine, there, 2, s, mate),
+        ], pltpu.make_async_copy(mine, there, keep_sem.at[s])
+
+    def relays(kind, p, group):
+        _, dst, cols = views(kind, p)
+        s = slot(kind, p)
+        if group == 2:
+            whole = block(dst, cols, across)
+            return [remote(whole, whole, 7, s, mate)]
+        owner, peer = ((by_x, by_y), (by_y, by_x))[group]
+        piece, whole = block(dst, cols, owner, group * half, half), block(dst, cols, owner)
+        way = 3 + 2 * group
+        return [remote(piece, piece, way, s, peer), remote(whole, whole, way + 1, s, mate)]
+
+    def arrived(kind, p, way):
+        _, dst, cols = views(kind, p)
+        many = half if way in (3, 5) else rows
+        ref = block(dst, cols, d, 0, many)
+        pltpu.make_async_copy(ref, ref, recv.at[way, slot(kind, p)]).wait()
+
+    def begin(kind, p):
+        copies, keep = own(kind, p)
+        for copy in copies:
+            copy.start()
+        keep.start()
+
+    def pass_on(kind, p):
+        for group in range(2):
+            arrived(kind, p, group)
+            for copy in relays(kind, p, group):
+                copy.start()
+
+    def close(kind, p):
+        arrived(kind, p, 3)
+        arrived(kind, p, 5)
+        relays(kind, p, 2)[0].start()
+
+    def finish(kind, p):
+        for way in (2, 4, 6, 7):
+            arrived(kind, p, way)
+        copies, keep = own(kind, p)
+        for group in range(3):
+            copies = copies + relays(kind, p, group)
+        for copy in copies:
+            copy.wait_send()
+        keep.wait()
+
+    state = {"begun": 0, "query": False, "out": False}
+
+    def ready(kind, p):
+        if kind == 1 or (p + 1) * att_w <= fixed:
+            return
+        need = 1 if (p + 1) * att_w <= fixed + size * part else 2
+        for of in range(need):
+            if not state[("query", "out")[of]]:
+                state[("query", "out")[of]] = True
+                fills[1 + of].wait()
+                for hop in range(1, size):
+                    ref = att_v.at[:, place(of, z)]
+                    pltpu.make_async_copy(ref, ref, z_recv.at[of, hop - 1]).wait()
+                if of == 1:
+                    for hop in range(1, size):
+                        cot_copy(hop).start()
+
+    total = len(order)
+    for i in range(total + 1):
+        while state["begun"] < min(total, i + lead):
+            ready(*order[state["begun"]])
+            begin(*order[state["begun"]])
+            state["begun"] += 1
+        if i < total:
+            pass_on(*order[i])
+        if i > 0:
+            close(*order[i - 1])
+    for kind, p in order:
+        finish(kind, p)
+    keep = pltpu.make_async_copy(
+        att_v.at[pl.ds(rows, tall - rows), pl.ds(fixed, size * part)], extra_out, fill_sem.at[0]
+    )
+    keep.start()
+    for of in range(2):
+        for hop in range(1, size):
+            z_copy(of, hop).wait_send()
+    for hop in range(1, size):
+        pltpu.make_async_copy(cot_ref, cot_ref, cot_recv.at[hop - 1]).wait()
+        cot_copy(hop).wait_send()
+    fills[3].wait()
+    keep.wait()
+
+
+def front(query, out, fixed, ffn_w, cot, att_tile=512, ffn_tile=768, collective_id=2, limit=48_000_000):
+    tall, part = query.shape
+    rows, fixed_w = fixed.shape
+    size, ways = 4, 8
+    att_cols = fixed_w + 2 * size * part
+    n_att, n_ffn = att_cols // att_tile, ffn_w.shape[1] // ffn_tile
+    n_fixed = fixed_w // att_tile
+    third = n_ffn // 3
+    order = [(0, p) for p in range(n_fixed)] + [(1, p) for p in range(third)]
+    order += [(0, p) for p in range(n_fixed, n_att)] + [(1, p) for p in range(third, n_ffn)]
+    bf16 = jnp.bfloat16
+    hbm = pl.BlockSpec(memory_space=pl.ANY)
+    vmem = pl.BlockSpec(memory_space=pltpu.VMEM)
+    dma = pltpu.SemaphoreType.DMA
+    shape = lambda *s: jax.ShapeDtypeStruct(s, bf16)
+    slots = n_att + n_ffn
+    return pl.pallas_call(
+        functools.partial(front_body, att_w=att_tile, ffn_w=ffn_tile, order=tuple(order), lead=3),
+        out_shape=(
+            shape(8 * rows, att_cols), shape(8 * rows, ffn_w.shape[1]),
+            shape(size * cot.shape[0], cot.shape[1]), shape(tall - rows, size * part),
+        ),
+        in_specs=[vmem] * 5,
+        out_specs=(hbm,) * 4,
+        scratch_shapes=[
+            pltpu.VMEM((tall, att_cols), bf16), dma((4,)), dma((2, size - 1)), dma((2, size - 1)),
+            dma((size - 1,)), dma((size - 1,)), dma((ways, slots)), dma((ways, slots)), dma((slots,)),
+        ],
+        compiler_params=pltpu.CompilerParams(
+            collective_id=collective_id, has_side_effects=True, vmem_limit_bytes=limit
+        ),
+        cost_estimate=pl.CostEstimate(
+            flops=0, bytes_accessed=20 * rows * (att_cols + ffn_w.shape[1]), transcendentals=0
+        ),
+        name="front",
+    )(query, out, fixed, ffn_w, cot)
+
+
+def joined_units(gate_w, up_w, down_w, gain_one, gain_two, padded):
+    gap = padded - gate_w.shape[1]
+    wide = lambda w: jnp.pad(w, ((0, 0), (0, gap)))
+    tail = jnp.pad(jnp.stack([gain_one, gain_two], axis=1), ((0, 0), (0, gap - 2)))
+    return jnp.concatenate([wide(gate_w), wide(up_w), down_w, tail], axis=1)
+
+
+def gather_weights(query_w, query_b, out_w, kv_w, ffn_w, cotangent):
+    if lax.axis_size("dp") == 8 and lax.axis_size("tensor") == 4:
+        tail = jnp.pad(query_b[None, :], ((0, 15), (0, 0)))
+        tall_query = jnp.concatenate([query_w, tail], axis=0)
+        tall_out = jnp.pad(out_w, ((0, 16), (0, 0)))
+        att_all, ffn_all, cot_all, extra = front(tall_query, tall_out, kv_w, ffn_w, cotangent)
+        return att_all, ffn_all, cot_all, extra[0]
+    pair = lax.all_gather(jnp.stack([query_w, out_w]), "tensor", axis=2, tiled=True)
+    att = jnp.concatenate([kv_w, pair[0], pair[1]], axis=1)
+    return (
+        lax.all_gather(att, "dp", axis=0, tiled=True),
+        lax.all_gather(ffn_w, "dp", axis=0, tiled=True),
+        lax.all_gather(cotangent, "tensor", axis=0, tiled=True),
+        lax.all_gather(query_b, "tensor", axis=0, tiled=True),
+    )
 
 
 def local(
@@ -368,24 +612,18 @@
     heads = query_width // HEAD_DIM
     group = heads // KV_HEADS
     scale = HEAD_DIM ** (-0.5)
-    pair = lax.all_gather(jnp.stack([query_w, out_w]), "tensor", axis=2, tiled=True)
-    joined = jnp.concatenate([pair[0], key_w, value_w, pair[1]], axis=1)
-    joined = lax.all_gather(joined, "dp", axis=0, tiled=True)
-    qkv_width = query_width + 2 * kv_width
-    qkv_w = joined[:, :qkv_width]
-    out_full = joined[:, qkv_width:]
-    gains = lax.all_gather(jnp.stack([gain_one, gain_two]), "dp", axis=1, tiled=True).astype(f32)
-    full_query_b = lax.all_gather(query_b, "tensor", axis=0, tiled=True)
-    qkv_b = jnp.concatenate([full_query_b, key_b, value_b]).astype(f32)
     units = gate_w.shape[1]
     padded = -(-units // 768) * 768
-
-    def whole(shard):
-        shard = jnp.pad(shard, ((0, 0), (0, padded - units)))
-        return lax.all_gather(shard, "dp", axis=0, tiled=True)
-
-    full_gate, full_up, full_down = whole(gate_w), whole(up_w), whole(down_w)
-    cot_rows = lax.all_gather(cotangent, "tensor", axis=0, tiled=True)
+    fixed_width = 2 * kv_width
+    qkv_width = fixed_width + query_width
+    att_w, ffn_w, cot_rows, full_query_b = gather_weights(
+        query_w, query_b, out_w, jnp.concatenate([key_w, value_w], axis=1),
+        joined_units(gate_w, up_w, down_w, gain_one, gain_two, padded), cotangent,
+    )
+    gains = ffn_w[:, 2 * padded + units : 2 * padded + units + 2].T.astype(f32)
+    qkv_w = att_w[:, :qkv_width]
+    out_full = att_w[:, qkv_width:]
+    qkv_b = jnp.concatenate([key_b, value_b, full_query_b]).astype(f32)
 
     inputs = tokens.astype(f32)
     inverse_one = lax.rsqrt(jnp.mean(inputs * inputs, axis=-1, keepdims=True) + EPSILON)
@@ -394,21 +632,28 @@
     lin = jnp.dot(normed_one, qkv_w, preferred_element_type=f32) + qkv_b
     cosine, sine = angle_tables(rank * rows, rows, HEAD_DIM)
     cos_h, sin_h = cosine[:, None, :], sine[:, None, :]
-    query_rot = rotate(lin[:, :query_width].reshape(rows, heads, HEAD_DIM), cos_h, sin_h).astype(bf16)
+    query_rot = rotate(lin[:, fixed_width:].reshape(rows, heads, HEAD_DIM), cos_h, sin_h).astype(bf16)
     key_rot = rotate(
-        lin[:, query_width : query_width + kv_width].reshape(rows, KV_HEADS, HEAD_DIM), cos_h, sin_h
+        lin[:, :kv_width].reshape(rows, KV_HEADS, HEAD_DIM), cos_h, sin_h
     ).astype(bf16)
-    value_own = lin[:, query_width + kv_width :].astype(bf16)
+    value_own = lin[:, kv_width:fixed_width].astype(bf16)
     kv_own = jnp.concatenate([key_rot.reshape(rows, kv_width), value_own], axis=1)
-    kv_all = lax.all_gather(kv_own, "tensor", axis=0, tiled=True)
-    window = min(seq_length, rows + -(-DOC_MAX // rows) * rows)
-    first = jnp.maximum((rank + 1) * rows - window, 0)
-    kv_win = lax.dynamic_slice_in_dim(kv_all, first, window, 0)
+    back = min(tensor_size - 1, -(-DOC_MAX // rows))
+    window = (back + 1) * rows
+    first = (rank - back) * rows
+
+    def shift(value, hops):
+        pairs = [(i, i + hops) for i in range(tensor_size) if 0 <= i + hops < tensor_size]
+        return lax.ppermute(value, "tensor", pairs)
+
+    kv_win = jnp.concatenate([shift(kv_own, hops) for hops in range(back, 0, -1)] + [kv_own], axis=0)
     key_win = kv_win[:, :kv_width].reshape(window, KV_HEADS, HEAD_DIM)
     value_win = kv_win[:, kv_width:].reshape(window, KV_HEADS, HEAD_DIM)
     segment = segments[0]
     own_segment = lax.dynamic_slice_in_dim(segment, rank * rows, rows, 0)
-    win_segment = lax.dynamic_slice_in_dim(segment, first, window, 0)
+    win_segment = lax.dynamic_slice_in_dim(
+        jnp.concatenate([jnp.full((back * rows,), -1, segment.dtype), segment]), rank * rows, window, 0
+    )
     own_pos = rank * rows + jnp.arange(rows)
     win_pos = first + jnp.arange(window)
     allowed = (own_segment[:, None] == win_segment[None, :]) & (win_pos[None, :] <= own_pos[:, None])
@@ -427,7 +672,7 @@
     normed_two = (unit_two * gains[1]).astype(bf16)
 
     rows_two, hidden_low, d_gate, d_upper, ffn_part, d_normed_two = ffn(
-        normed_two, cot_rows, full_gate, full_up, full_down
+        normed_two, cot_rows, ffn_w
     )
     ffn_sum = lax.psum_scatter(ffn_part, "tensor", scatter_dimension=0, tiled=True).astype(f32)
     mixed = (middle + ffn_sum).astype(bf16)
@@ -455,13 +700,13 @@
     d_kv_win = jnp.concatenate(
         [d_key_win.reshape(window, kv_width), d_value_win.reshape(window, kv_width)], axis=1
     ).astype(bf16)
-    d_kv_all = lax.dynamic_update_slice(
-        jnp.zeros((seq_length, 2 * kv_width), bf16), d_kv_win, (first, 0)
-    )
-    d_kv = lax.psum_scatter(d_kv_all, "tensor", scatter_dimension=0, tiled=True).astype(f32)
+    d_kv = d_kv_win[back * rows :].astype(f32)
+    for hops in range(1, back + 1):
+        given = d_kv_win[(back - hops) * rows : (back - hops + 1) * rows]
+        d_kv = d_kv + shift(given, -hops).astype(f32)
     d_key_lin = rotate_back(d_kv[:, :kv_width].reshape(rows, KV_HEADS, HEAD_DIM), cos_h, sin_h)
     d_lin = jnp.concatenate(
-        [d_query_lin, d_key_lin.reshape(rows, kv_width).astype(bf16), d_kv[:, kv_width:].astype(bf16)],
+        [d_key_lin.reshape(rows, kv_width).astype(bf16), d_kv[:, kv_width:].astype(bf16), d_query_lin],
         axis=1,
     )
     d_normed_one = contract_cols(d_lin, qkv_w)
@@ -475,10 +720,10 @@
 
     sum_gate, sum_up, sum_down = (over_dp(g)[:, :units].astype(f32) for g in (grad_gate, grad_up, grad_down))
     part = over_dp(jnp.concatenate([grad_qkv, grad_out], axis=1))
-    pair = jnp.stack([part[:, :query_width], part[:, qkv_width:]])
+    pair = jnp.stack([part[:, fixed_width:qkv_width], part[:, qkv_width:]])
     pair = lax.psum_scatter(pair, "tensor", scatter_dimension=2, tiled=True).astype(f32)
     kv_part = lax.psum_scatter(
-        part[:, query_width:qkv_width], "tensor", scatter_dimension=0, tiled=True
+        part[:, :fixed_width], "tensor", scatter_dimension=0, tiled=True
     ).astype(f32)
     small = lax.psum(
         jnp.concatenate([bias_term, gain_one_term, gain_two_term]), ("dp", "tensor")
@@ -495,11 +740,11 @@
         input_grad,
         own(qkv_width, model_width),
         pair[0],
-        own(0, query_width),
+        own(fixed_width, query_width),
         kv_part[:, :kv_width],
-        small[query_width : query_width + kv_width],
+        small[:kv_width],
         kv_part[:, kv_width:],
-        small[query_width + kv_width : qkv_width],
+        small[kv_width:fixed_width],
         pair[1],
         own(qkv_width + model_width, model_width),
         sum_gate,

time: 983 us -> 821 us (0.84)
  waiting for transfers between devices: 581 us -> 310 us
  Pallas kernels: 108 us -> 246 us
  local copies, waits for them, and re-layouts: 72.7 us -> 44.7 us
  blocking collectives: 61.3 us -> 47.1 us
    all_gather x7 -> x0, waiting for transfers between devices: 287 us -> none  [the longest x3 154 us: whole(): return lax.all_gather(shard, 'dp', axis=0, tiled=True)]
    pallas_call x0 -> x1, Pallas kernels: none -> 137 us  [front(): pl.pallas_call(functools.partial(front_body, att_w=att_tile, ffn_w=ffn_ti...]
    reduce_scatter x3 -> x4, waiting for transfers between devices: 132 us -> 188 us  [over_dp(): return lax.psum_scatter(grad, 'dp', scatter_dimension=0, tiled=True)]
    unnamed x17 -> x8, waiting for transfers between devices: 71.6 us -> 29.1 us
    all_gather x2 -> x0, blocking collectives: 19.7 us -> none  [the longest x1 10.8 us: local(): full_query_b = lax.all_gather(query_b, 'tensor', axis=0, tiled=True)]
    reduce_scatter x2 -> x1, waiting for transfers between devices: 34 us -> 17 us  [local(): lax.psum_scatter(part[:, :fixed_width], 'tensor', scatter_dimension=0, ti...]
    ppermute x0 -> x4, waiting for transfers between devices: none -> 16.7 us  [shift(): return lax.ppermute(value, 'tensor', pairs)]
    unnamed x88 -> x109, local copies, waits for them, and re-layouts: 33.7 us -> 19.8 us
  transfers between devices with their start and end apart: 15 -> 11, of which waited for: 14 -> 9; matrix products, arithmetic and copies ran while one was open for 12% -> 9% of each run, Pallas kernels for 0% -> 0%
where the time goes in v3:
time: 821 us; the launch traced here: 810 us
  waiting for transfers between devices  310 us (38%)
  Pallas kernels  246 us (30%)
  matrix products  91.4 us (11%)
  blocking collectives  47.1 us (6%)
  other arithmetic  46.4 us (6%)
  local copies, waits for them, and re-layouts  44.7 us (5%)
  between operations  15.5 us (2%)
  starting transfers between devices  9.33 us (1%)
    reduce_scatter x4, waiting for transfers between devices, over_dp(): return lax.psum_scatter(grad, 'dp', scatter_dimension=0, tiled=True)  188 us
    pallas_call x1, Pallas kernels, front(): pl.pallas_call(functools.partial(front_body, att_w=att_tile, ffn_w=ffn_ti...  137 us
    pallas_call x1, Pallas kernels, ffn(): pl.pallas_call(functools.partial(ffn_body, axis=axis, ft=ft, nt=nt), out_...  109 us
    reduce_scatter x1, waiting for transfers between devices, local(): lax.psum_scatter(ffn_part, 'tensor', scatter_dimension=0, tiled=True)  58.6 us
    dot_general x7, matrix products, dot_f32(): lax.dot_general(left, right, (dims, ((), ())), preferred_element_type=jnp...  53.3 us
    psum x1, blocking collectives, local(): lax.psum(jnp.concatenate([bias_term, gain_one_term, gain_two_term]), ('dp...  47.1 us
    unnamed x8, waiting for transfers between devices  29.1 us
    unnamed x109, local copies, waits for them, and re-layouts  19.8 us
  transfers between devices with their start and end apart: 11, of which 9 were waited for; matrix products, arithmetic and copies ran while one was open for 9% of the time, Pallas kernels for 0%

profile of v3, /device:TPU:26, one launch (start us, length us, event | category | flops | bytes accessed | tf_op | source)
XLA Modules:
  0.0 810.5 jit_solution(3793477653758837767)
XLA Ops:
  7.3 2.2 pad.22
  12.9 3.7 concatenate.63.ffn_ref
  19.3 136.8 %front.1 = (bf16[1536,3584]{1,0:T(8,128)(2,1)}, bf16[1536,6912]{1,0:T(8,128)(2,1)}, bf16[1024,1536]{1,0:T(8,128)(2,1)S(1)}, bf16[16,1536]{1,0:T(8,128)(2,1)S(1)}) custom-call(bf16[208,384]{1,0:T(8,128)(2,1)S(1)} %copy-done.3, bf16[208,384]{1,0:T(8,128)(2,1)S(1)} %copy-done.2, bf16[192,512]{1,0:T(8,128)(2,1)S(1)} %copy-done.1, ...), custom_call_target="tpu_custom_call" | custom-call | bytes 40304640 | tf_op jit(solution)/shard_map/front/pallas_call | solution.py:554
  158.8 4.6 fusion.16
  169.6 1.8 collective-permute-start.1
  173.0 2.3 subtract_convert_fusion.1
  177.8 8.4 %collective-permute-done = bf16[256,512]{1,0:T(8,128)(2,1)} collective-permute-done((bf16[256,512]{1,0:T(8,128)(2,1)}, bf16[256,512]{1,0:T(8,128)(2,1)}, u32[]{:S(2)}, u32[]{:S(2)}) %collective-permute-start) | collective-permute-done | bytes 262176 | tf_op jit(solution)/shard_map/ppermute | solution.py:647
  188.3 1.8 reshape.221
  190.2 1.9 copy.102
  192.1 3.2 fusion.8
  195.3 3.5 copy-done.6
  198.9 1.9 exponential_reduce_fusion
  200.9 6.2 convolution_convert_fusion.5
  207.1 5.2 multiply_reduce_fusion
  212.4 2.5 multiply_convert_fusion.two_ref
  214.9 109.3 %ffn.1 = (bf16[1024,1536]{1,0:T(8,128)(2,1)}, bf16[1024,2304]{1,0:T(8,128)(2,1)}, bf16[1024,2304]{1,0:T(8,128)(2,1)}, bf16[1024,2304]{1,0:T(8,128)(2,1)}, bf16[1...) custom-call(bf16[256,1536]{1,0:T(8,128)(2,1)} %multiply_convert_fusion.two_ref, bf16[1024,1536]{1,0:T(8,128)(2,1)} %copy-done.4, ...), custom_call_target="tpu_custom_call" | custom-call | flops 43486543872 | bytes 47185920 | tf_op jit(solution)/shard_map/ffn/pallas_call | solution.py:330
  325.4 2.0 fusion.31
  327.4 58.6 %reduce-scatter.10.cloned.1.call-done = bf16[256,1536]{1,0:T(8,128)(2,1)} async-done(((bf16[1024,1536]{1,0:T(8,128)(2,1)}), bf16[256,1536]{1,0:T(8,128)(2,1)}) %reduce-scatter.10.cloned.1.call-update) | async-done | bytes 786448 | tf_op jit(solution)/shard_map/reduce_scatter | solution.py:677
  386.0 3.0 fusion.30
  389.0 4.3 fusion.19
  393.6 7.0 fusion.42
  400.6 7.7 fusion
  408.3 11.1 %fusion.2 = bf16[2,6,256,768]{2,3,1,0:T(8,128)(2,1)} fusion(f32[2,768,256,6]{2,1,3,0:T(8,128)} %get-tuple-element.75, f32[2,768,256,6]{2,1,3,0:T(8,128)} %copy-done.6, f32[2,6,256]{2,1,0:T(8,128)S(1)} %get-tuple-element.74, f32[2,6,256]{2,1,0:T(8,128)S(1)} %log_add_fusion, pred[256,768]{0,1:T(8,128)(4,1)S(1)} %copy-done.11), kind=kLoop, calls=%fused_computation.8 | loop fusion | flops 14155776 | bytes 23814144 | tf_op jit(solution)/shard_map/convert_element_type | solution.py:692
  419.5 4.3 fusion.41
  425.0 3.6 convolution_convert_fusion.4
  428.7 3.5 collective-permute-start.2
  432.2 2.5 collective-permute-start.3
  435.0 3.8 collective-permute-done.2
  438.8 4.5 collective-permute-done.3
  444.6 2.0 convolution_convert_fusion.3
  446.8 5.0 pad_maximum_fusion
  452.0 1.8 copy-done.48
  453.8 12.0 %convolution_convert_fusion.1 = bf16[1536,2304]{1,0:T(8,128)(2,1)} fusion(bf16[1024,1536]{1,0:T(8,128)(2,1)S(1)} %copy-done.48, bf16[1024,2304]{1,0:T(8,128)(2,1)} %get-tuple-element.32), kind=kOutput, calls=%fused_computation.1 | convolution fusion | flops 7251296256 | bytes 14942208 | tf_op jit(solution)/shard_map/dot_general | solution.py:43
  465.8 12.6 %convolution_convert_fusion.2 = bf16[1536,2304]{1,0:T(8,128)(2,1)} fusion(bf16[1024,1536]{1,0:T(8,128)(2,1)S(1)} %copy-done.48, bf16[1024,2304]{1,0:T(8,128)(2,1)} %get-tuple-element.31), kind=kOutput, calls=%fused_computation.2 | convolution fusion | flops 7251296256 | bytes 14942208 | tf_op jit(solution)/shard_map/dot_general | solution.py:43
  478.5 1.8 copy-done.5
  480.3 11.8 %convolution_convert_fusion = bf16[1536,2304]{1,0:T(8,128)(2,1)} fusion(bf16[1024,1536]{1,0:T(8,128)(2,1)S(1)} %copy-done.5, bf16[1024,2304]{1,0:T(8,128)(2,1)} %get-tuple-element.33), kind=kOutput, calls=%fused_computation | convolution fusion | flops 7251296256 | bytes 14942208 | tf_op jit(solution)/shard_map/dot_general | solution.py:43
  493.6 6.1 fusion.38
  499.7 47.1 %psum.7 = f32[5120]{0:T(1024)S(1)} all-reduce(f32[5120]{0:T(1024)S(1)} %pad_maximum_fusion.12), channel_id=1, replica_groups=mesh['dp'=8,'tensor'=4] {'dp','tensor'}, use_global_device_ids=true, to_apply=%region_11.12 | all-reduce | flops 5120 | bytes 40960 | tf_op jit(solution)/shard_map/psum | solution.py:728
  547.9 2.7 fusion.37
  555.2 1.7 reshape.234
  556.9 55.7 %reduce-scatter.18.cloned.1.call-done = bf16[192,2304]{1,0:T(8,128)(2,1)} async-done(((bf16[1536,2304]{1,0:T(8,128)(2,1)}), bf16[192,2304]{1,0:T(8,128)(2,1)}) %reduce-scatter.18.cloned.1.call-update) | async-done | bytes 884752 | tf_op jit(solution)/shard_map/reduce_scatter | solution.py:719
  612.6 2.5 slice_convert_fusion.1
  615.1 66.4 %reduce-scatter.16.cloned.1.call-done = bf16[192,2304]{1,0:T(8,128)(2,1)} async-done(((bf16[1536,2304]{1,0:T(8,128)(2,1)}), bf16[192,2304]{1,0:T(8,128)(2,1)}) %reduce-scatter.16.cloned.1.call-update) | async-done | bytes 884752 | tf_op jit(solution)/shard_map/reduce_scatter | solution.py:719
  681.5 2.5 slice_convert_fusion.2
  684.0 66.4 %reduce-scatter.20.cloned.1.call-done = bf16[192,2304]{1,0:T(8,128)(2,1)} async-done(((bf16[1536,2304]{1,0:T(8,128)(2,1)}), bf16[192,2304]{1,0:T(8,128)(2,1)}) %reduce-scatter.20.cloned.1.call-update) | async-done | bytes 884752 | tf_op jit(solution)/shard_map/reduce_scatter | solution.py:719
  750.4 2.5 slice_convert_fusion
  752.9 17.0 %reduce-scatter.14.cloned.1.call-done = bf16[48,512]{1,0:T(8,128)(2,1)} async-done(((bf16[192,512]{1,0:T(8,128)(2,1)}), bf16[48,512]{1,0:T(8,128)(2,1)}) %reduce-scatter.14.cloned.1.call-update) | async-done | bytes 49168 | tf_op jit(solution)/shard_map/reduce_scatter | solution.py:725
  771.3 29.0 %reduce-scatter.22.cloned.1.call-done = bf16[384,384]{1,0:T(8,128)(2,1)} async-done(((bf16[1536,384]{1,0:T(8,128)(2,1)}), bf16[384,384]{1,0:T(8,128)(2,1)}) %reduce-scatter.22.cloned.1.call-update) | async-done | bytes 294928
  (188 shorter events, 36.9 us)
Async XLA Ops:
  7.2 2.4 copy-start.32
  7.2 3.3 copy-start.46
  7.2 3.3 copy-start.47
  7.2 3.5 copy-start.43
  7.2 3.6 copy-start.38
  7.2 4.2 copy-start.41
  7.2 4.2 copy-start.40
  7.3 4.9 copy-start.39
  7.3 378.7 %reduce-scatter.10.cloned.1.call-start = ((), (), s32[]{:S(2)}) async-start(), calls=%async_computation.7 | async-start | bytes 3932160 | tf_op jit(solution)/shard_map/reduce_scatter | solution.py:677
  12.9 3.7 copy-start
  156.1 7.4 copy-start.4
  156.1 2.4 copy-start.12
  156.1 2.7 copy-start.44
  156.1 2.6 copy-start.45
  164.8 6.6 copy-start.28
  165.3 159.0 %copy-start.35 = (f32[256,64]{0,1:T(8,128)}, f32[256,64]{0,1:T(8,128)S(1)}, u32[]{:S(2)}) copy-start(f32[256,64]{0,1:T(8,128)S(1)} %get-tuple-element.67) | copy-start | bytes 196612
  166.5 4.8 slice-start.2
  168.3 17.9 %collective-permute-start = (bf16[256,512]{1,0:T(8,128)(2,1)}, bf16[256,512]{1,0:T(8,128)(2,1)}, u32[]{:S(2)}, u32[]{:S(2)}) collective-permute-start(bf16[256,512]{1,0:T(8,128)(2,1)} %pad_maximum_fusion.6), channel_id=1, source_target_pairs={{0,2},{1,3},{4,6},{5,7},{8,10},{9,11},{12,14},{13,15},{16,18},{17,... | collective-permute-start | bytes 786440 | tf_op jit(solution)/shard_map/ppermute | solution.py:647
  169.6 16.6 %collective-permute-start.1 = (bf16[256,512]{1,0:T(8,128)(2,1)}, bf16[256,512]{1,0:T(8,128)(2,1)}, u32[]{:S(2)}, u32[]{:S(2)}) collective-permute-start(bf16[256,512]{1,0:T(8,128)(2,1)} %pad_maximum_fusion.6), channel_id=1, source_target_pairs={{0,1},{1,2},{2,3},{4,5},{5,6},{6,7},{8,9},{9,10},{10,11},{12,13},{... | collective-permute-start | bytes 786440 | tf_op jit(solution)/shard_map/ppermute | solution.py:647
  171.4 4.0 copy-start.42
  175.8 16.3 %copy-start.15 = (bf16[256,12,64]{2,0,1:T(8,128)(2,1)}, bf16[256,12,64]{2,0,1:T(8,128)(2,1)S(1)}, u32[]{:S(2)}) copy-start(bf16[256,12,64]{2,0,1:T(8,128)(2,1)S(1)} %copy.74) | copy-start | bytes 1179652
  177.5 14.6 %copy-start.17 = (bf16[256,12,64]{2,0,1:T(8,128)(2,1)}, bf16[256,12,64]{2,0,1:T(8,128)(2,1)S(1)}, u32[]{:S(2)}) copy-start(bf16[256,12,64]{2,0,1:T(8,128)(2,1)S(1)} %copy.75) | copy-start | bytes 1179652
  177.8 23.2 %copy-start.10 = (pred[256,768]{0,1:T(8,128)(4,1)}, pred[256,768]{0,1:T(8,128)(4,1)S(1)}, u32[]{:S(2)}) copy-start(pred[256,768]{0,1:T(8,128)(4,1)S(1)} %compare_and_fusion) | copy-start | bytes 589828
  195.3 3.5 copy-start.6
  200.9 6.2 copy-start.26
  207.1 5.2 copy-start.33
  324.2 226.4 %reduce-scatter.12.cloned.1.call-start = ((), (), s32[]{:S(2)}) async-start(), calls=%async_computation.8 | async-start | bytes 12386304 | tf_op jit(solution)/shard_map/reduce_scatter | solution.py:719
  389.0 35.6 %copy-start.8 = (f32[256,1536]{1,0:T(8,128)}, f32[256,1536]{1,0:T(8,128)S(1)}, u32[]{:S(2)}) copy-start(f32[256,1536]{1,0:T(8,128)S(1)} %get-tuple-element.44) | copy-start | bytes 4718596
  389.0 4.6 copy-start.11
  393.6 7.0 copy-start.27
  408.3 11.1 %copy-start.16 = (bf16[256,12,64]{2,0,1:T(8,128)(2,1)S(1)}, bf16[256,12,64]{2,0,1:T(8,128)(2,1)}, u32[]{:S(2)}) copy-start(bf16[256,12,64]{2,0,1:T(8,128)(2,1)} %copy-done.15) | copy-start | bytes 1179652
  408.3 11.1 %copy-start.18 = (bf16[256,12,64]{2,0,1:T(8,128)(2,1)S(1)}, bf16[256,12,64]{2,0,1:T(8,128)(2,1)}, u32[]{:S(2)}) copy-start(bf16[256,12,64]{2,0,1:T(8,128)(2,1)} %copy-done.17) | copy-start | bytes 1179652
  419.4 4.4 copy-start.7
  419.4 4.4 copy-start.22
  425.0 3.7 copy-start.24
  425.0 9.7 %copy-start.36 = (f32[256,64]{0,1:T(8,128)S(1)}, f32[256,64]{0,1:T(8,128)}, u32[]{:S(2)}) copy-start(f32[256,64]{0,1:T(8,128)} %copy-done.35) | copy-start | bytes 196612
  428.7 10.2 %collective-permute-start.2 = (bf16[256,512]{0,1:T(8,128)(2,1)S(1)}, bf16[256,512]{0,1:T(8,128)(2,1)S(1)}, u32[]{:S(2)}, u32[]{:S(2)}) collective-permute-start(bf16[256,512]{0,1:T(8,128)(2,1)S(1)} %get-tuple-element.50), channel_id=1, source_target_pairs={{1,0},{2,1},{3,2},{5,4},{6,5},{7,6},{9,8},{10,9},{11,10},{13,12},{... | collective-permute-start | bytes 786440 | tf_op jit(solution)/shard_map/ppermute | solution.py:647
  432.2 11.1 %collective-permute-start.3 = (bf16[256,512]{0,1:T(8,128)(2,1)S(1)}, bf16[256,512]{0,1:T(8,128)(2,1)S(1)}, u32[]{:S(2)}, u32[]{:S(2)}) collective-permute-start(bf16[256,512]{0,1:T(8,128)(2,1)S(1)} %get-tuple-element.51), channel_id=1, source_target_pairs={{2,0},{3,1},{6,4},{7,5},{10,8},{11,9},{14,12},{15,13},{18,16},{19,... | collective-permute-start | bytes 786440 | tf_op jit(solution)/shard_map/ppermute | solution.py:647
  435.0 9.6 %copy-start.19 = (bf16[256,12,128]{0,2,1:T(8,128)(2,1)}, bf16[256,12,128]{0,2,1:T(8,128)(2,1)S(1)}, u32[]{:S(2)}) copy-start(bf16[256,12,128]{0,2,1:T(8,128)(2,1)S(1)} %pad_maximum_fusion.4) | copy-start | bytes 2359300
  435.0 8.8 %copy-start.31 = (f32[256,64]{1,0:T(8,128)S(1)}, f32[256,64]{1,0:T(8,128)}, u32[]{:S(2)}) copy-start(f32[256,64]{1,0:T(8,128)} %copy-done.30) | copy-start | bytes 196612
  435.0 8.8 %copy-start.37 = (f32[256,64]{1,0:T(8,128)S(1)}, f32[256,64]{1,0:T(8,128)}, u32[]{:S(2)}) copy-start(f32[256,64]{1,0:T(8,128)} %copy.87) | copy-start | bytes 196612
  444.6 2.2 slice-start.1
  451.9 160.7 %reduce-scatter.18.cloned.1.call-start = ((), (), s32[]{:S(2)}) async-start(), calls=%async_computation.11 | async-start | bytes 7962624 | tf_op jit(solution)/shard_map/reduce_scatter | solution.py:719
  465.7 215.8 %reduce-scatter.16.cloned.1.call-start = ((), (), s32[]{:S(2)}) async-start(), calls=%async_computation.10 | async-start | bytes 7962624 | tf_op jit(solution)/shard_map/reduce_scatter | solution.py:719
  478.5 271.9 %reduce-scatter.20.cloned.1.call-start = ((), (), s32[]{:S(2)}) async-start(), calls=%async_computation.12 | async-start | bytes 7962624 | tf_op jit(solution)/shard_map/reduce_scatter | solution.py:719
  492.1 277.8 %reduce-scatter.14.cloned.1.call-start = ((), (), s32[]{:S(2)}) async-start(), calls=%async_computation.9 | async-start | bytes 245760 | tf_op jit(solution)/shard_map/reduce_scatter | solution.py:725
  493.6 54.4 %copy-start.9 = (f32[256,1536]{1,0:T(8,128)S(1)}, f32[256,1536]{1,0:T(8,128)}, u32[]{:S(2)}) copy-start(f32[256,1536]{1,0:T(8,128)} %copy-done.8) | copy-start | bytes 4718596
  552.3 248.0 %reduce-scatter.22.cloned.1.call-start = ((), (), s32[]{:S(2)}) async-start(), calls=%async_computation.13 | async-start | bytes 1474560
  (15 other events, 19.3 us)
Sparse Core Ops, SparseCore 0:
  324.4 61.5 reduce-scatter.9
  452.0 91.4 reduce-scatter.11
  547.1 65.4 reduce-scatter.17
  616.0 65.4 reduce-scatter.15
  684.9 65.4 reduce-scatter.19
  753.1 16.7 reduce-scatter.13
  772.2 28.0 reduce-scatter.21

commit v4 on v2

--- a/solution.py
+++ b/solution.py
@@ -8,7 +8,6 @@
 from jax.sharding import PartitionSpec as P
 
 MESH = pl.DeviceIdType.MESH
-
 KV_HEADS = 2
 HEAD_DIM = 128
 DOC_MAX = 512
@@ -17,45 +16,221 @@
 NEGATIVE = -1e30
 
 
-def angle_tables(first, length, head_width):
-    position = (first + jnp.arange(length)).astype(jnp.float32)
-    exponent = jnp.arange(head_width // 2, dtype=jnp.float32) * (2.0 / head_width)
-    frequency = ROPE_BASE ** (-exponent)
-    angle = position[:, None] * frequency[None, :]
-    return (jnp.cos(angle), jnp.sin(angle))
-
-
-def rotate(values, cosine, sine):
-    half_width = values.shape[-1] // 2
-    first_half = values[..., :half_width]
-    second_half = values[..., half_width:]
-    return jnp.concatenate(
-        [first_half * cosine - second_half * sine, second_half * cosine + first_half * sine],
-        axis=-1,
+def square(d):
+    core, x, y = d % 2, (d // 2) % 2, d // 4
+    by_x, by_y = d + 2 - 4 * x, d + 4 - 8 * y
+    return by_x, by_y, d + 1 - 2 * core, by_x + 4 - 8 * y
+
+
+def front_body(
+    query_ref, out_ref, fixed_ref, ffn_ref, cot_ref,
+    att_all, ffn_all, cot_all, extra_out,
+    att_v, fill_sem, z_send, z_recv, cot_send, cot_recv, send, recv, keep_sem,
+    *, att_w, ffn_w, order, lead,
+):
+    d, z = lax.axis_index("dp"), lax.axis_index("tensor")
+    size = 4
+    by_x, by_y, mate, across = square(d)
+    rows = ffn_ref.shape[0]
+    half = rows // 2
+    part = query_ref.shape[1]
+    fixed = fixed_ref.shape[1]
+    chunk = cot_ref.shape[0]
+    tall = query_ref.shape[0]
+
+    barrier = pltpu.get_barrier_semaphore()
+    for peer in (by_x, by_y, mate):
+        pl.semaphore_signal(barrier, inc=1, device_id={"dp": peer}, device_id_type=MESH)
+    for hop in range(1, size):
+        pl.semaphore_signal(
+            barrier, inc=1, device_id={"tensor": (z + hop) % size}, device_id_type=MESH
+        )
+
+    def place(of, owner):
+        return pl.ds(pl.multiple_of(fixed + of * size * part + owner * part, 128), part)
+
+    fills = [pltpu.make_async_copy(fixed_ref, att_v.at[pl.ds(0, rows), pl.ds(0, fixed)], fill_sem.at[0])]
+    for of, ref in enumerate((query_ref, out_ref)):
+        fills.append(pltpu.make_async_copy(ref, att_v.at[:, place(of, z)], fill_sem.at[1 + of]))
+    at = pl.ds(pl.multiple_of(z * chunk, chunk), chunk)
+    fills.append(pltpu.make_async_copy(cot_ref, cot_all.at[at, :], fill_sem.at[3]))
+    for copy in fills:
+        copy.start()
+
+    pl.semaphore_wait(barrier, 3 + size - 1)
+
+    def z_copy(of, hop):
+        ref = (query_ref, out_ref)[of]
+        return pltpu.make_async_remote_copy(
+            src_ref=ref, dst_ref=att_v.at[:, place(of, z)], send_sem=z_send.at[of, hop - 1],
+            recv_sem=z_recv.at[of, hop - 1], device_id={"tensor": (z + hop) % size},
+            device_id_type=MESH,
+        )
+
+    def cot_copy(hop):
+        return pltpu.make_async_remote_copy(
+            src_ref=cot_ref, dst_ref=cot_all.at[at, :], send_sem=cot_send.at[hop - 1],
+            recv_sem=cot_recv.at[hop - 1], device_id={"tensor": (z + hop) % size},
+            device_id_type=MESH,
+        )
+
+    for of in range(2):
+        for hop in range(1, size):
+            z_copy(of, hop).start()
+    fills[0].wait()
+
+    def views(kind, p):
+        src, dst, wide = ((att_v, att_all, att_w), (ffn_ref, ffn_all, ffn_w))[kind]
+        return src, dst, pl.ds(pl.multiple_of(p * wide, 128), wide)
+
+    def slot(kind, p):
+        return p + kind * n_att
+
+    n_att = att_all.shape[1] // att_w
+
+    def block(dst, cols, owner, first=0, many=None):
+        many = rows if many is None else many
+        return dst.at[pl.ds(pl.multiple_of(owner * rows + first, 16), many), cols]
+
+    def remote(src, dst, way, at_slot, peer):
+        return pltpu.make_async_remote_copy(
+            src_ref=src, dst_ref=dst, send_sem=send.at[way, at_slot], recv_sem=recv.at[way, at_slot],
+            device_id={"dp": peer}, device_id_type=MESH,
+        )
+
+    def own(kind, p):
+        src, dst, cols = views(kind, p)
+        mine = src.at[pl.ds(0, rows), cols]
+        there = block(dst, cols, d)
+        s = slot(kind, p)
+        return [
+            remote(mine, there, 0, s, by_x), remote(mine, there, 1, s, by_y),
+            remote(mine, there, 2, s, mate),
+        ], pltpu.make_async_copy(mine, there, keep_sem.at[s])
+
+    def relays(kind, p, group):
+        _, dst, cols = views(kind, p)
+        s = slot(kind, p)
+        if group == 2:
+            whole = block(dst, cols, across)
+            return [remote(whole, whole, 7, s, mate)]
+        owner, peer = ((by_x, by_y), (by_y, by_x))[group]
+        piece, whole = block(dst, cols, owner, group * half, half), block(dst, cols, owner)
+        way = 3 + 2 * group
+        return [remote(piece, piece, way, s, peer), remote(whole, whole, way + 1, s, mate)]
+
+    def arrived(kind, p, way):
+        _, dst, cols = views(kind, p)
+        many = half if way in (3, 5) else rows
+        ref = block(dst, cols, d, 0, many)
+        pltpu.make_async_copy(ref, ref, recv.at[way, slot(kind, p)]).wait()
+
+    def begin(kind, p):
+        copies, keep = own(kind, p)
+        for copy in copies:
+            copy.start()
+        keep.start()
+
+    def pass_on(kind, p):
+        for group in range(2):
+            arrived(kind, p, group)
+            for copy in relays(kind, p, group):
+                copy.start()
+
+    def close(kind, p):
+        arrived(kind, p, 3)
+        arrived(kind, p, 5)
+        relays(kind, p, 2)[0].start()
+
+    def finish(kind, p):
+        for way in (2, 4, 6, 7):
+            arrived(kind, p, way)
+        copies, keep = own(kind, p)
+        for group in range(3):
+            copies = copies + relays(kind, p, group)
+        for copy in copies:
+            copy.wait_send()
+        keep.wait()
+
+    state = {"begun": 0, "query": False, "out": False}
+
+    def ready(kind, p):
+        if kind == 1 or (p + 1) * att_w <= fixed:
+            return
+        need = 1 if (p + 1) * att_w <= fixed + size * part else 2
+        for of in range(need):
+            if not state[("query", "out")[of]]:
+                state[("query", "out")[of]] = True
+                fills[1 + of].wait()
+                for hop in range(1, size):
+                    ref = att_v.at[:, place(of, z)]
+                    pltpu.make_async_copy(ref, ref, z_recv.at[of, hop - 1]).wait()
+                if of == 1:
+                    for hop in range(1, size):
+                        cot_copy(hop).start()
+
+    total = len(order)
+    for i in range(total + 1):
+        while state["begun"] < min(total, i + lead):
+            ready(*order[state["begun"]])
+            begin(*order[state["begun"]])
+            state["begun"] += 1
+        if i < total:
+            pass_on(*order[i])
+        if i > 0:
+            close(*order[i - 1])
+    for kind, p in order:
+        finish(kind, p)
+    keep = pltpu.make_async_copy(
+        att_v.at[pl.ds(rows, tall - rows), pl.ds(fixed, size * part)], extra_out, fill_sem.at[0]
     )
-
-
-def rotate_back(grads, cosine, sine):
-    return rotate(grads, cosine, -sine)
-
-
-def dot_f32(left, right, dims):
-    return lax.dot_general(left, right, (dims, ((), ())), preferred_element_type=jnp.float32)
-
-
-def contract_rows(left, right):
-    return dot_f32(left, right, ((0,), (0,)))
-
-
-def contract_cols(left, right):
-    return dot_f32(left, right, ((1,), (1,)))
-
-
-def norm_back(upstream, unit, inverse, gain):
-    scaled = upstream * gain
-    gain_term = jnp.sum(upstream * unit, axis=0)
-    input_term = inverse * (scaled - unit * jnp.mean(scaled * unit, axis=-1, keepdims=True))
-    return (gain_term, input_term)
+    keep.start()
+    for of in range(2):
+        for hop in range(1, size):
+            z_copy(of, hop).wait_send()
+    for hop in range(1, size):
+        pltpu.make_async_copy(cot_ref, cot_ref, cot_recv.at[hop - 1]).wait()
+        cot_copy(hop).wait_send()
+    fills[3].wait()
+    keep.wait()
+
+
+def front(query, out, fixed, ffn_w, cot, att_tile=512, ffn_tile=768, collective_id=2, limit=48_000_000):
+    tall, part = query.shape
+    rows, fixed_w = fixed.shape
+    size, ways = 4, 8
+    att_cols = fixed_w + 2 * size * part
+    n_att, n_ffn = att_cols // att_tile, ffn_w.shape[1] // ffn_tile
+    n_fixed = fixed_w // att_tile
+    third = n_ffn // 3
+    order = [(0, p) for p in range(n_fixed)] + [(1, p) for p in range(third)]
+    order += [(0, p) for p in range(n_fixed, n_att)] + [(1, p) for p in range(third, n_ffn)]
+    bf16 = jnp.bfloat16
+    hbm = pl.BlockSpec(memory_space=pl.ANY)
+    vmem = pl.BlockSpec(memory_space=pltpu.VMEM)
+    dma = pltpu.SemaphoreType.DMA
+    shape = lambda *s: jax.ShapeDtypeStruct(s, bf16)
+    slots = n_att + n_ffn
+    return pl.pallas_call(
+        functools.partial(front_body, att_w=att_tile, ffn_w=ffn_tile, order=tuple(order), lead=3),
+        out_shape=(
+            shape(8 * rows, att_cols), shape(8 * rows, ffn_w.shape[1]),
+            shape(size * cot.shape[0], cot.shape[1]), shape(tall - rows, size * part),
+        ),
+        in_specs=[vmem] * 5,
+        out_specs=(hbm,) * 4,
+        scratch_shapes=[
+            pltpu.VMEM((tall, att_cols), bf16), dma((4,)), dma((2, size - 1)), dma((2, size - 1)),
+            dma((size - 1,)), dma((size - 1,)), dma((ways, slots)), dma((ways, slots)), dma((slots,)),
+        ],
+        compiler_params=pltpu.CompilerParams(
+            collective_id=collective_id, has_side_effects=True, vmem_limit_bytes=limit
+        ),
+        cost_estimate=pl.CostEstimate(
+            flops=0, bytes_accessed=20 * rows * (att_cols + ffn_w.shape[1]), transcendentals=0
+        ),
+        name="front",
+    )(query, out, fixed, ffn_w, cot)
 
 
 def line_order(z, s):
@@ -67,7 +242,7 @@
 
 
 def ffn_body(
-    two_ref, cot_ref, gate_ref, up_ref, down_ref,
+    two_ref, cot_ref, weights_ref,
     rows_out, hid_out, dg_out, du_out, sum_out, dn_out,
     rows_v, cot_v, gate_v, up_v, down_v, hid_v, dg_v, du_v, part, land, below, above, res_v,
     tile_sem, load_sem, ag_send, ag_recv, rs_send, rs_recv, own_recv, out_sem,
@@ -76,7 +251,7 @@
     f32, bf16 = jnp.float32, jnp.bfloat16
     size = 4
     rows, width = two_ref.shape
-    units = gate_ref.shape[1]
+    units = weights_ref.shape[1] // 3
     n_f, n_n = units // ft, width // nt
     z = lax.axis_index(axis)
     has_low, has_high = z > 0, z < size - 1
@@ -100,8 +275,11 @@
     def tile_loads(f):
         cols = pl.ds(pl.multiple_of(f * ft, 128), ft)
         return [
-            pltpu.make_async_copy(src.at[:, cols], dst.at[:, cols], tile_sem.at[k, f])
-            for k, (src, dst) in enumerate(((gate_ref, gate_v), (up_ref, up_v), (down_ref, down_v)))
+            pltpu.make_async_copy(
+                weights_ref.at[:, pl.ds(pl.multiple_of(k * units + f * ft, 128), ft)],
+                dst.at[:, cols], tile_sem.at[k, f],
+            )
+            for k, dst in enumerate((gate_v, up_v, down_v))
         ]
 
     cot_load = pltpu.make_async_copy(cot_ref, cot_v, load_sem.at[1])
@@ -313,9 +491,9 @@
         copy.wait()
 
 
-def ffn(two, cot_rows, gate, up, down, axis="tensor", ft=768, nt=512, collective_id=1, limit=66_000_000):
+def ffn(two, cot_rows, weights, axis="tensor", ft=768, nt=512, collective_id=1, limit=66_000_000):
     rows, width = two.shape
-    units = gate.shape[1]
+    units = weights.shape[1] // 3
     size = 4
     length = rows * size
     n_f, n_n = units // ft, width // nt
@@ -330,7 +508,7 @@
             shape(length, width), shape(length, units), shape(length, units), shape(length, units),
             shape(length, width), shape(rows, width),
         ),
-        in_specs=[hbm] * 5,
+        in_specs=[hbm] * 3,
         out_specs=(hbm,) * 5 + (pl.BlockSpec(memory_space=pltpu.VMEM),),
         scratch_shapes=[
             vm((size, rows, width), bf16), vm((length, width), bf16),
@@ -350,7 +528,458 @@
             transcendentals=length * units,
         ),
         name="ffn",
-    )(two, cot_rows, gate, up, down)
+    )(two, cot_rows, weights)
+
+
+def back_body(
+    two_ref, cot_ref, hid_ref, dg_ref, du_ref, lhs_ref, rhs_ref, part_ref, small_ref,
+    ffn_out, query_out, out_out, kv_out, sum_out, small_out,
+    left_v, right_v, grad, mate_land, core_sum, x_land, y_land, second, x_last, y_last, stage, fin,
+    z_land, kv_land, sum_land, small_z, small_hop, small_next,
+    left_sem, right_sem, mate_send, mate_recv, one_send, one_recv, two_send, two_recv, stage_sem,
+    z_send, z_recv, kv_send, kv_recv, sum_send, sum_recv, own_sem, small_send, small_recv,
+    hop_send, hop_recv, *, n_f, wide, cols_out,
+):
+    f32, bf16 = jnp.float32, jnp.bfloat16
+    d, z = lax.axis_index("dp"), lax.axis_index("tensor")
+    size = 4
+    core, x, y = d % 2, (d // 2) % 2, d // 4
+    by_x, by_y, mate, _ = square(d)
+    here, at_x, at_y = 2 * y + x, 2 * y + 1 - x, 2 * (1 - y) + x
+    cross = 3 - here
+    block, half = core_sum.shape[2], core_sum.shape[2] // 2
+    n_ffn, n_att = 3 * n_f, rhs_ref.shape[1] // wide
+    total = n_ffn + n_att
+    chunk = sum_out.shape[0]
+    share = block // size
+    part_w = wide // 2
+
+    barrier = pltpu.get_barrier_semaphore()
+    for peer in (by_x, by_y, mate):
+        pl.semaphore_signal(barrier, inc=1, device_id={"dp": peer}, device_id_type=MESH)
+    for hop in range(1, size):
+        pl.semaphore_signal(
+            barrier, inc=1, device_id={"tensor": (z + hop) % size}, device_id_type=MESH
+        )
+
+    lefts = [
+        pltpu.make_async_copy(ref, left_v.at[k], left_sem.at[k])
+        for k, ref in enumerate((cot_ref, two_ref))
+    ]
+
+    def right_load(i, what):
+        cols = pl.ds(pl.multiple_of((i % n_f) * wide, 128), wide)
+        for m, ref in enumerate((hid_ref, dg_ref, du_ref)):
+            copy = pltpu.make_async_copy(ref.at[:, cols], right_v.at[i % 2], right_sem.at[i % 2])
+
+            @pl.when(i // n_f == m)
+            def _(copy=copy):
+                copy.start() if what == "start" else copy.wait()
+
+    lefts[0].start()
+    right_load(jnp.int32(0), "start")
+    lefts[1].start()
+
+    def chunk_rows(j):
+        return part_ref.at[pl.ds(pl.multiple_of(j * chunk, chunk), chunk), :]
+
+    own_part = pltpu.make_async_copy(chunk_rows(z), sum_land.at[size - 1], own_sem.at[0])
+    own_part.start()
+    pl.semaphore_wait(barrier, 3 + size - 1)
+
+    def dp_copy(src, dst, send_sem, recv_sem, peer):
+        return pltpu.make_async_remote_copy(
+            src_ref=src, dst_ref=dst, send_sem=send_sem, recv_sem=recv_sem,
+            device_id={"dp": peer}, device_id_type=MESH,
+        )
+
+    def z_copy(src, dst, send_sem, recv_sem, peer):
+        return pltpu.make_async_remote_copy(
+            src_ref=src, dst_ref=dst, send_sem=send_sem, recv_sem=recv_sem,
+            device_id={"tensor": peer}, device_id_type=MESH,
+        )
+
+    small_copies, sum_copies = [], []
+    for hop in range(1, size):
+        to, k = (z + hop) % size, hop - 1
+        small_copies.append(
+            z_copy(small_ref, small_z.at[k], small_send.at[k], small_recv.at[k], to)
+        )
+        sum_copies.append(
+            z_copy(chunk_rows(to), sum_land.at[k], sum_send.at[k], sum_recv.at[k], to)
+        )
+    for copy in small_copies + sum_copies:
+        copy.start()
+
+    hops = (mate, by_x, by_y)
+
+    def hop_copy(k):
+        return dp_copy(small_next.at[k], small_hop.at[k], hop_send.at[k], hop_recv.at[k], hops[k])
+
+    def mate_copy(i):
+        return dp_copy(
+            grad.at[i % 2, :, 1 - core], mate_land.at[i % 4], mate_send.at[i % 4],
+            mate_recv.at[i % 4], mate,
+        )
+
+    def one_copies(i):
+        s = core_sum.at[i % 4]
+        first, last = pl.ds(0, half), pl.ds(half, half)
+        plan = (
+            (s.at[at_x, first, :], x_land.at[i, 0], by_x), (s.at[cross, first, :], x_land.at[i, 1], by_x),
+            (s.at[at_y, last, :], y_land.at[i, 0], by_y), (s.at[cross, last, :], y_land.at[i, 1], by_y),
+        )
+        return [
+            dp_copy(src, dst, one_send.at[k, i], one_recv.at[k, i], peer)
+            for k, (src, dst, peer) in enumerate(plan)
+        ]
+
+    def two_copies(i):
+        return [
+            dp_copy(second.at[i % 4, 0], y_last.at[i], two_send.at[0, i], two_recv.at[0, i], by_y),
+            dp_copy(second.at[i % 4, 1], x_last.at[i], two_send.at[1, i], two_recv.at[1, i], by_x),
+        ]
+
+    def stage_copy(i):
+        cols = pl.ds(pl.multiple_of(i * wide, 128), wide)
+        return pltpu.make_async_copy(stage.at[i % 2], ffn_out.at[:, cols], stage_sem.at[i % 2])
+
+    def multiply(i):
+        @pl.when(jnp.logical_and(i >= 2, i < total))
+        def _():
+            mate_copy(i - 2).wait_send()
+
+        @pl.when(i + 1 < n_ffn)
+        def _():
+            right_load(i + 1, "start")
+
+        dims = (((0,), (0,)), ((), ()))
+
+        @pl.when(i < n_ffn)
+        def _():
+            @pl.when(i == 0)
+            def _():
+                lefts[0].wait()
+
+            @pl.when(i == n_f)
+            def _():
+                lefts[1].wait()
+
+            right_load(i, "wait")
+
+            def rows(k, carry):
+                at = pl.ds(pl.multiple_of(k * 2 * block, 128), 2 * block)
+                value = lax.dot_general(
+                    left_v[(i // n_f + 1) // 2, :, at], right_v[i % 2], dims, preferred_element_type=f32
+                )
+                grad[i % 2, k] = value.astype(bf16).reshape(2, block, wide)
+                return carry
+
+            lax.fori_loop(0, 4, rows, 0)
+
+        @pl.when(jnp.logical_and(i >= n_ffn, i < total))
+        def _():
+            a = i - n_ffn
+            cols = pl.ds(pl.multiple_of(a * wide, 128), wide)
+
+            def rows(k, carry):
+                at = pl.ds(pl.multiple_of(k * 2 * block, 128), 2 * block)
+                value = lax.dot_general(
+                    lhs_ref[(a // 2) % 2, :, at], rhs_ref[:, cols], dims, preferred_element_type=f32
+                )
+                grad[i % 2, k] = value.astype(bf16).reshape(2, block, wide)
+                return carry
+
+            lax.fori_loop(0, 4, rows, 0)
+
+        @pl.when(i < total)
+        def _():
+            mate_copy(i).start()
+
+    def sum_cores(i):
+        mate_copy(i).wait_recv()
+        for k in range(4):
+            core_sum[i % 4, k] = (
+                grad[i % 2, k, core].astype(f32) + mate_land[i % 4, k].astype(f32)
+            ).astype(bf16)
+        for copy in one_copies(i):
+            copy.start()
+
+    def sum_near(i):
+        for copy in one_copies(i):
+            copy.wait_recv()
+        s = core_sum.at[i % 4]
+        second[i % 4, 0] = (s[at_y, :half].astype(f32) + x_land[i, 1].astype(f32)).astype(bf16)
+        second[i % 4, 1] = (s[at_x, half:].astype(f32) + y_land[i, 1].astype(f32)).astype(bf16)
+        for copy in two_copies(i):
+            copy.start()
+
+    def z_sends(a, what):
+        for h in range(2):
+            owner = (a % 2) * 2 + h
+            hop = (owner - z + size) % size
+            src = fin.at[a, :, pl.ds(h * part_w, part_w)]
+
+            @pl.when(jnp.logical_and(a < 4, hop > 0))
+            def _(src=src, owner=owner, hop=hop, h=h):
+                copy = z_copy(
+                    src, z_land.at[a // 2, hop - 1], z_send.at[a, h], z_recv.at[a // 2, hop - 1], owner
+                )
+                copy.start() if what == "start" else copy.wait_send()
+
+        @pl.when(a == 4)
+        def _():
+            for hop in range(1, size):
+                to = (z + hop) % size
+                rows = pl.ds(pl.multiple_of(to * share, 16), share)
+                copy = z_copy(
+                    fin.at[4, rows, :], kv_land.at[hop - 1], kv_send.at[hop - 1], kv_recv.at[hop - 1], to
+                )
+                copy.start() if what == "start" else copy.wait_send()
+
+    def finish(i):
+        for copy in two_copies(i):
+            copy.wait_recv()
+        own = core_sum.at[i % 4, here]
+        top = own[:half].astype(f32) + x_land[i, 0].astype(f32) + y_last[i].astype(f32)
+        low = own[half:].astype(f32) + y_land[i, 0].astype(f32) + x_last[i].astype(f32)
+
+        @pl.when(i < n_ffn)
+        def _():
+            @pl.when(i >= 2)
+            def _():
+                stage_copy(i - 2).wait()
+
+            stage[i % 2, :half] = top
+            stage[i % 2, half:] = low
+            stage_copy(i).start()
+
+        @pl.when(i >= n_ffn)
+        def _():
+            a = i - n_ffn
+            fin[a, :half] = top.astype(bf16)
+            fin[a, half:] = low.astype(bf16)
+            z_sends(a, "start")
+
+        for copy in one_copies(i) + two_copies(i):
+            copy.wait_send()
+
+    def small_step(i):
+        @pl.when(i == 2)
+        def _():
+            for copy in small_copies:
+                copy.wait_recv()
+            small_next[0] = small_ref[...] + small_z[0] + small_z[1] + small_z[2]
+            hop_copy(0).start()
+
+        for k in range(2):
+
+            @pl.when(i == 3 + k)
+            def _(k=k):
+                hop_copy(k).wait_recv()
+                small_next[k + 1] = small_next[k] + small_hop[k]
+                hop_copy(k + 1).start()
+
+        @pl.when(i == 5)
+        def _():
+            hop_copy(2).wait_recv()
+            small_out[...] = small_next[2] + small_hop[2]
+
+    def turn(i, carry):
+        multiply(i)
+        for lag, work in ((1, sum_cores), (2, sum_near), (3, finish)):
+
+            @pl.when(jnp.logical_and(i >= lag, i - lag < total))
+            def _(lag=lag, work=work):
+                work(i - lag)
+
+        small_step(i)
+        return carry
+
+    lax.fori_loop(0, total + 3, turn, 0)
+    for i in (total - 2, total - 1):
+        mate_copy(i).wait_send()
+    for i in (n_ffn - 2, n_ffn - 1):
+        stage_copy(i).wait()
+    own_part.wait()
+    for copy in sum_copies:
+        copy.wait_recv()
+    acc = sum_land[size - 1].astype(f32)
+    for k in range(size - 1):
+        acc += sum_land[k].astype(f32)
+    sum_out[...] = acc.astype(bf16)
+    for of, dst in ((0, query_out), (1, out_out)):
+        for k in range(size - 1):
+            ref = z_land.at[of, k]
+            pltpu.make_async_copy(ref, ref, z_recv.at[of, k]).wait()
+        for h in range(4):
+
+            @pl.when(z == h)
+            def _(of=of, dst=dst, h=h):
+                acc = fin[2 * of + h // 2, :, (h % 2) * part_w : (h % 2 + 1) * part_w].astype(f32)
+                for k in range(size - 1):
+                    acc += z_land[of, k].astype(f32)
+                dst[...] = acc
+
+    for k in range(size - 1):
+        pltpu.make_async_copy(kv_land.at[k], kv_land.at[k], kv_recv.at[k]).wait()
+    rows = pl.ds(pl.multiple_of(z * share, 16), share)
+    acc = fin[4, rows, :].astype(f32)
+    for k in range(size - 1):
+        acc += kv_land[k].astype(f32)
+    kv_out[...] = acc
+    for a in range(n_att):
+        z_sends(a, "wait")
+    for copy in sum_copies + small_copies:
+        copy.wait_send()
+    for k in range(3):
+        hop_copy(k).wait_send()
+
+
+def back(two, cot_rows, hid, dg, du, lhs, rhs, ffn_part, small, wide=768, collective_id=3, limit=67_000_000):
+    length, width = two.shape
+    size, chunk, block = 4, lhs.shape[1], width // 8
+    units = hid.shape[1]
+    n_f, n_att = units // wide, rhs.shape[1] // wide
+    n_ffn = 3 * n_f
+    total = n_ffn + n_att
+    half, part_w, share = block // 2, wide // 2, block // size
+    bf16, f32 = jnp.bfloat16, jnp.float32
+    hbm = pl.BlockSpec(memory_space=pl.ANY)
+    vmem = pl.BlockSpec(memory_space=pltpu.VMEM)
+    vm = pltpu.VMEM
+    dma = pltpu.SemaphoreType.DMA
+    shape = jax.ShapeDtypeStruct
+    return pl.pallas_call(
+        functools.partial(back_body, n_f=n_f, wide=wide, cols_out=3 * units),
+        out_shape=(
+            shape((block, 3 * units), f32), shape((block, part_w), f32), shape((block, part_w), f32),
+            shape((share, wide), f32), shape((chunk, width), bf16), shape(small.shape, f32),
+        ),
+        in_specs=[hbm] * 5 + [vmem, vmem, hbm, vmem],
+        out_specs=(hbm,) + (vmem,) * 5,
+        scratch_shapes=[
+            vm((2, length, width), bf16), vm((2, length, wide), bf16), vm((2, 4, 2, block, wide), bf16),
+            vm((4, 4, block, wide), bf16), vm((4, 4, block, wide), bf16),
+            vm((total, 2, half, wide), bf16), vm((total, 2, half, wide), bf16),
+            vm((4, 2, half, wide), bf16), vm((total, half, wide), bf16), vm((total, half, wide), bf16),
+            vm((2, block, wide), f32), vm((n_att, block, wide), bf16),
+            vm((2, size - 1, block, part_w), bf16), vm((size - 1, share, wide), bf16),
+            vm((size, chunk, width), bf16), vm((3,) + small.shape, f32), vm((3,) + small.shape, f32),
+            vm((3,) + small.shape, f32),
+            dma((2,)), dma((2,)), dma((4,)), dma((4,)), dma((4, total)), dma((4, total)),
+            dma((2, total)), dma((2, total)), dma((2,)),
+            dma((4, 2)), dma((2, size - 1)), dma((size - 1,)), dma((size - 1,)), dma((size - 1,)),
+            dma((size - 1,)), dma((1,)), dma((size - 1,)), dma((size - 1,)), dma((3,)), dma((3,)),
+        ],
+        compiler_params=pltpu.CompilerParams(
+            collective_id=collective_id, has_side_effects=True, vmem_limit_bytes=limit
+        ),
+        cost_estimate=pl.CostEstimate(
+            flops=6 * length * width * units, bytes_accessed=8 * length * units, transcendentals=0
+        ),
+        name="back",
+    )(two, cot_rows, hid, dg, du, lhs, rhs, ffn_part, small)
+
+
+def angle_tables(first, length, head_width):
+    position = (first + jnp.arange(length)).astype(jnp.float32)
+    exponent = jnp.arange(head_width // 2, dtype=jnp.float32) * (2.0 / head_width)
+    frequency = ROPE_BASE ** (-exponent)
+    angle = position[:, None] * frequency[None, :]
+    return (jnp.cos(angle), jnp.sin(angle))
+
+
+def rotate(values, cosine, sine):
+    half_width = values.shape[-1] // 2
+    first_half = values[..., :half_width]
+    second_half = values[..., half_width:]
+    return jnp.concatenate(
+        [first_half * cosine - second_half * sine, second_half * cosine + first_half * sine],
+        axis=-1,
+    )
+
+
+def rotate_back(grads, cosine, sine):
+    return rotate(grads, cosine, -sine)
+
+
+def dot_f32(left, right, dims):
+    return lax.dot_general(left, right, (dims, ((), ())), preferred_element_type=jnp.float32)
+
+
+def contract_rows(left, right):
+    return dot_f32(left, right, ((0,), (0,)))
+
+
+def contract_cols(left, right):
+    return dot_f32(left, right, ((1,), (1,)))
+
+
+def norm_back(upstream, unit, inverse, gain):
+    scaled = upstream * gain
+    gain_term = jnp.sum(upstream * unit, axis=0)
+    input_term = inverse * (scaled - unit * jnp.mean(scaled * unit, axis=-1, keepdims=True))
+    return (gain_term, input_term)
+
+
+def joined_units(gate_w, up_w, down_w, gain_one, gain_two, padded):
+    gap = padded - gate_w.shape[1]
+    wide = lambda w: jnp.pad(w, ((0, 0), (0, gap)))
+    tail = jnp.pad(jnp.stack([gain_one, gain_two], axis=1), ((0, 0), (0, gap - 2)))
+    return jnp.concatenate([wide(gate_w), wide(up_w), down_w, tail], axis=1)
+
+
+def gather_weights(query_w, query_b, out_w, kv_w, ffn_w, cotangent):
+    if lax.axis_size("dp") == 8 and lax.axis_size("tensor") == 4:
+        tail = jnp.pad(query_b[None, :], ((0, 15), (0, 0)))
+        tall_query = jnp.concatenate([query_w, tail], axis=0)
+        tall_out = jnp.pad(out_w, ((0, 16), (0, 0)))
+        att_all, ffn_all, cot_all, extra = front(tall_query, tall_out, kv_w, ffn_w, cotangent)
+        return att_all, ffn_all, cot_all, extra[0]
+    pair = lax.all_gather(jnp.stack([query_w, out_w]), "tensor", axis=2, tiled=True)
+    att = jnp.concatenate([kv_w, pair[0], pair[1]], axis=1)
+    return (
+        lax.all_gather(att, "dp", axis=0, tiled=True),
+        lax.all_gather(ffn_w, "dp", axis=0, tiled=True),
+        lax.all_gather(cotangent, "tensor", axis=0, tiled=True),
+        lax.all_gather(query_b, "tensor", axis=0, tiled=True),
+    )
+
+
+def sum_grads(two, cot_rows, hid, dg, du, normed_one, d_attended, d_lin, context, ffn_part, small):
+    f32, bf16 = jnp.float32, jnp.bfloat16
+    padded = hid.shape[1]
+    fixed = d_lin.shape[1] - context.shape[1]
+    d_query = d_lin[:, fixed:]
+    if lax.axis_size("dp") == 8 and lax.axis_size("tensor") == 4:
+        gap = context.shape[1] // 2 - fixed
+        rhs = jnp.concatenate([d_query, context, jnp.pad(d_lin[:, :fixed], ((0, 0), (0, gap)))], axis=1)
+        lhs = jnp.stack([normed_one, d_attended])
+        flat, query, out, kv, ffn_sum, total = back(
+            two, cot_rows, hid, dg, du, lhs, rhs, ffn_part, small.reshape(-1, 128)
+        )
+        flat = [flat[:, k * padded : (k + 1) * padded] for k in range(3)]
+        return (*flat, query, out, kv, ffn_sum, total.reshape(-1))
+
+    def over_dp(left, right):
+        return lax.psum_scatter(
+            contract_rows(left, right).astype(bf16), "dp", scatter_dimension=0, tiled=True
+        )
+
+    def over_tensor(value, axis):
+        return lax.psum_scatter(value, "tensor", scatter_dimension=axis, tiled=True).astype(f32)
+
+    return (
+        over_dp(cot_rows, hid).astype(f32),
+        over_dp(two, dg).astype(f32),
+        over_dp(two, du).astype(f32),
+        over_tensor(over_dp(normed_one, d_query), 1),
+        over_tensor(over_dp(d_attended, context), 1),
+        over_tensor(over_dp(normed_one, d_lin[:, :fixed]), 0),
+        over_tensor(ffn_part, 0),
+        lax.psum(small, ("dp", "tensor")),
+    )
 
 
 def local(
@@ -368,24 +997,18 @@
     heads = query_width // HEAD_DIM
     group = heads // KV_HEADS
     scale = HEAD_DIM ** (-0.5)
-    pair = lax.all_gather(jnp.stack([query_w, out_w]), "tensor", axis=2, tiled=True)
-    joined = jnp.concatenate([pair[0], key_w, value_w, pair[1]], axis=1)
-    joined = lax.all_gather(joined, "dp", axis=0, tiled=True)
-    qkv_width = query_width + 2 * kv_width
-    qkv_w = joined[:, :qkv_width]
-    out_full = joined[:, qkv_width:]
-    gains = lax.all_gather(jnp.stack([gain_one, gain_two]), "dp", axis=1, tiled=True).astype(f32)
-    full_query_b = lax.all_gather(query_b, "tensor", axis=0, tiled=True)
-    qkv_b = jnp.concatenate([full_query_b, key_b, value_b]).astype(f32)
     units = gate_w.shape[1]
     padded = -(-units // 768) * 768
-
-    def whole(shard):
-        shard = jnp.pad(shard, ((0, 0), (0, padded - units)))
-        return lax.all_gather(shard, "dp", axis=0, tiled=True)
-
-    full_gate, full_up, full_down = whole(gate_w), whole(up_w), whole(down_w)
-    cot_rows = lax.all_gather(cotangent, "tensor", axis=0, tiled=True)
+    fixed_width = 2 * kv_width
+    qkv_width = fixed_width + query_width
+    att_w, ffn_w, cot_rows, full_query_b = gather_weights(
+        query_w, query_b, out_w, jnp.concatenate([key_w, value_w], axis=1),
+        joined_units(gate_w, up_w, down_w, gain_one, gain_two, padded), cotangent,
+    )
+    gains = ffn_w[:, 2 * padded + units : 2 * padded + units + 2].T.astype(f32)
+    qkv_w = att_w[:, :qkv_width]
+    out_full = att_w[:, qkv_width:]
+    qkv_b = jnp.concatenate([key_b, value_b, full_query_b]).astype(f32)
 
     inputs = tokens.astype(f32)
     inverse_one = lax.rsqrt(jnp.mean(inputs * inputs, axis=-1, keepdims=True) + EPSILON)
@@ -394,21 +1017,28 @@
     lin = jnp.dot(normed_one, qkv_w, preferred_element_type=f32) + qkv_b
     cosine, sine = angle_tables(rank * rows, rows, HEAD_DIM)
     cos_h, sin_h = cosine[:, None, :], sine[:, None, :]
-    query_rot = rotate(lin[:, :query_width].reshape(rows, heads, HEAD_DIM), cos_h, sin_h).astype(bf16)
+    query_rot = rotate(lin[:, fixed_width:].reshape(rows, heads, HEAD_DIM), cos_h, sin_h).astype(bf16)
     key_rot = rotate(
-        lin[:, query_width : query_width + kv_width].reshape(rows, KV_HEADS, HEAD_DIM), cos_h, sin_h
+        lin[:, :kv_width].reshape(rows, KV_HEADS, HEAD_DIM), cos_h, sin_h
     ).astype(bf16)
-    value_own = lin[:, query_width + kv_width :].astype(bf16)
+    value_own = lin[:, kv_width:fixed_width].astype(bf16)
     kv_own = jnp.concatenate([key_rot.reshape(rows, kv_width), value_own], axis=1)
-    kv_all = lax.all_gather(kv_own, "tensor", axis=0, tiled=True)
-    window = min(seq_length, rows + -(-DOC_MAX // rows) * rows)
-    first = jnp.maximum((rank + 1) * rows - window, 0)
-    kv_win = lax.dynamic_slice_in_dim(kv_all, first, window, 0)
+    back = min(tensor_size - 1, -(-DOC_MAX // rows))
+    window = (back + 1) * rows
+    first = (rank - back) * rows
+
+    def shift(value, hops):
+        pairs = [(i, i + hops) for i in range(tensor_size) if 0 <= i + hops < tensor_size]
+        return lax.ppermute(value, "tensor", pairs)
+
+    kv_win = jnp.concatenate([shift(kv_own, hops) for hops in range(back, 0, -1)] + [kv_own], axis=0)
     key_win = kv_win[:, :kv_width].reshape(window, KV_HEADS, HEAD_DIM)
     value_win = kv_win[:, kv_width:].reshape(window, KV_HEADS, HEAD_DIM)
     segment = segments[0]
     own_segment = lax.dynamic_slice_in_dim(segment, rank * rows, rows, 0)
-    win_segment = lax.dynamic_slice_in_dim(segment, first, window, 0)
+    win_segment = lax.dynamic_slice_in_dim(
+        jnp.concatenate([jnp.full((back * rows,), -1, segment.dtype), segment]), rank * rows, window, 0
+    )
     own_pos = rank * rows + jnp.arange(rows)
     win_pos = first + jnp.arange(window)
     allowed = (own_segment[:, None] == win_segment[None, :]) & (win_pos[None, :] <= own_pos[:, None])
@@ -427,20 +1057,13 @@
     normed_two = (unit_two * gains[1]).astype(bf16)
 
     rows_two, hidden_low, d_gate, d_upper, ffn_part, d_normed_two = ffn(
-        normed_two, cot_rows, full_gate, full_up, full_down
+        normed_two, cot_rows, ffn_w
     )
-    ffn_sum = lax.psum_scatter(ffn_part, "tensor", scatter_dimension=0, tiled=True).astype(f32)
-    mixed = (middle + ffn_sum).astype(bf16)
     d_normed_two = d_normed_two.astype(f32)
-    grad_down = contract_rows(cot_rows, hidden_low).astype(bf16)
-    grad_gate = contract_rows(rows_two, d_gate).astype(bf16)
-    grad_up = contract_rows(rows_two, d_upper).astype(bf16)
-
     gain_two_term, d_from_two = norm_back(d_normed_two, unit_two, inverse_two, gains[1])
     d_middle = cotangent.astype(f32) + d_from_two
     d_attended = d_middle.astype(bf16)
     d_context = jnp.dot(d_attended, out_full, preferred_element_type=f32).astype(bf16)
-    grad_out = contract_rows(d_attended, context).astype(bf16)
     d_context = d_context.reshape(rows, KV_HEADS, group, HEAD_DIM)
     d_probs = jnp.einsum("tagd,sad->agts", d_context, value_win, preferred_element_type=f32)
     row_delta = jnp.sum(probs * d_probs, axis=-1, keepdims=True)
@@ -455,34 +1078,26 @@
     d_kv_win = jnp.concatenate(
         [d_key_win.reshape(window, kv_width), d_value_win.reshape(window, kv_width)], axis=1
     ).astype(bf16)
-    d_kv_all = lax.dynamic_update_slice(
-        jnp.zeros((seq_length, 2 * kv_width), bf16), d_kv_win, (first, 0)
-    )
-    d_kv = lax.psum_scatter(d_kv_all, "tensor", scatter_dimension=0, tiled=True).astype(f32)
+    d_kv = d_kv_win[back * rows :].astype(f32)
+    for hops in range(1, back + 1):
+        given = d_kv_win[(back - hops) * rows : (back - hops + 1) * rows]
+        d_kv = d_kv + shift(given, -hops).astype(f32)
     d_key_lin = rotate_back(d_kv[:, :kv_width].reshape(rows, KV_HEADS, HEAD_DIM), cos_h, sin_h)
     d_lin = jnp.concatenate(
-        [d_query_lin, d_key_lin.reshape(rows, kv_width).astype(bf16), d_kv[:, kv_width:].astype(bf16)],
+        [d_key_lin.reshape(rows, kv_width).astype(bf16), d_kv[:, kv_width:].astype(bf16), d_query_lin],
         axis=1,
     )
     d_normed_one = contract_cols(d_lin, qkv_w)
-    grad_qkv = contract_rows(normed_one, d_lin).astype(bf16)
     bias_term = jnp.sum(d_lin.astype(f32), axis=0)
     gain_one_term, d_from_one = norm_back(d_normed_one, unit_one, inverse_one, gains[0])
     input_grad = (d_middle + d_from_one).astype(bf16)
 
-    def over_dp(grad):
-        return lax.psum_scatter(grad, "dp", scatter_dimension=0, tiled=True)
-
-    sum_gate, sum_up, sum_down = (over_dp(g)[:, :units].astype(f32) for g in (grad_gate, grad_up, grad_down))
-    part = over_dp(jnp.concatenate([grad_qkv, grad_out], axis=1))
-    pair = jnp.stack([part[:, :query_width], part[:, qkv_width:]])
-    pair = lax.psum_scatter(pair, "tensor", scatter_dimension=2, tiled=True).astype(f32)
-    kv_part = lax.psum_scatter(
-        part[:, query_width:qkv_width], "tensor", scatter_dimension=0, tiled=True
-    ).astype(f32)
-    small = lax.psum(
-        jnp.concatenate([bias_term, gain_one_term, gain_two_term]), ("dp", "tensor")
+    sums = sum_grads(
+        rows_two, cot_rows, hidden_low, d_gate, d_upper, normed_one, d_attended, d_lin, context,
+        ffn_part, jnp.concatenate([bias_term, gain_one_term, gain_two_term]),
     )
+    sum_down, sum_gate, sum_up, sum_query, sum_out, sum_kv, ffn_sum, small = sums
+    mixed = (middle + ffn_sum.astype(f32)).astype(bf16)
     place = lax.axis_index("dp") * tensor_size + rank
     devices = lax.axis_size("dp") * tensor_size
 
@@ -494,17 +1109,17 @@
         mixed,
         input_grad,
         own(qkv_width, model_width),
-        pair[0],
-        own(0, query_width),
-        kv_part[:, :kv_width],
-        small[query_width : query_width + kv_width],
-        kv_part[:, kv_width:],
-        small[query_width + kv_width : qkv_width],
-        pair[1],
+        sum_query,
+        own(fixed_width, query_width),
+        sum_kv[:, :kv_width],
+        small[:kv_width],
+        sum_kv[:, kv_width : 2 * kv_width],
+        small[kv_width:fixed_width],
+        sum_out,
         own(qkv_width + model_width, model_width),
-        sum_gate,
-        sum_up,
-        sum_down,
+        sum_gate[:, :units],
+        sum_up[:, :units],
+        sum_down[:, :units],
     )
 
 

time: 983 us -> 580 us (0.59)
  waiting for transfers between devices: 581 us -> 9.66 us
  Pallas kernels: 108 us -> 423 us
  blocking collectives: 61.3 us -> 0 us
  matrix products: 90 us -> 46.5 us
  local copies, waits for them, and re-layouts: 72.7 us -> 36 us
  between operations: 15 us -> 2.13 us
    pallas_call x0 -> x2, Pallas kernels: none -> 314 us  [the longest x1 178 us: back(): pl.pallas_call(functools.partial(back_body, n_f=n_f, wide=wide, cols_out=...]
    all_gather x7 -> x0, waiting for transfers between devices: 287 us -> none  [the longest x3 154 us: whole(): return lax.all_gather(shard, 'dp', axis=0, tiled=True)]
    reduce_scatter x6 -> x0, waiting for transfers between devices: 222 us -> none  [the longest x3 132 us: over_dp(): return lax.psum_scatter(grad, 'dp', scatter_dimension=0, tiled=True)]
    unnamed x17 -> x0, waiting for transfers between devices: 71.6 us -> none
    dot_general x7 -> x2, matrix products: 53.5 us -> 10.3 us  [dot_f32(): lax.dot_general(left, right, (dims, ((), ())), preferred_element_type=jnp...]
    psum x1 -> x0, blocking collectives: 41.6 us -> none  [local(): lax.psum(jnp.concatenate([bias_term, gain_one_term, gain_two_term]), ('dp...]
    unnamed x88 -> x114, local copies, waits for them, and re-layouts: 33.7 us -> 9.29 us
    all_gather x2 -> x0, blocking collectives: 19.7 us -> none  [the longest x1 10.8 us: local(): full_query_b = lax.all_gather(query_b, 'tensor', axis=0, tiled=True)]
  transfers between devices with their start and end apart: 15 -> 4, of which waited for: 14 -> 1; matrix products, arithmetic and copies ran while one was open for 12% -> 2% of each run, Pallas kernels for 0% -> 0%
where the time goes in v4:
time: 580 us; the launch traced here: 569 us
  Pallas kernels  423 us (73%)
  matrix products  46.5 us (8%)
  other arithmetic  41.4 us (7%)
  local copies, waits for them, and re-layouts  36 us (6%)
  starting transfers between devices  10.1 us (2%)
  waiting for transfers between devices  9.66 us (2%)
    pallas_call x1, Pallas kernels, back(): pl.pallas_call(functools.partial(back_body, n_f=n_f, wide=wide, cols_out=...  178 us
    pallas_call x1, Pallas kernels, front(): pl.pallas_call(functools.partial(front_body, att_w=att_tile, ffn_w=ffn_ti...  137 us
    pallas_call x1, Pallas kernels, ffn(): pl.pallas_call(functools.partial(ffn_body, axis=axis, ft=ft, nt=nt), out_...  109 us
  transfers between devices with their start and end apart: 4, of which 1 were waited for; matrix products, arithmetic and copies ran while one was open for 2% of the time, Pallas kernels for 0%

profile of v4, /device:TPU:26, one launch (start us, length us, event | category | flops | bytes accessed | tf_op | source)
XLA Modules:
  0.0 569.3 jit_solution(10448891020514933190)
XLA Ops:
  0.7 2.2 pad.26
  3.0 1.0 pad.27
  6.3 3.7 concatenate.66.ffn_ref
  10.0 0.9 copy-done.1
  10.9 0.9 copy-done.2
  11.8 0.9 copy-done.3
  12.7 136.8 %front.1 = (bf16[1536,3584]{1,0:T(8,128)(2,1)}, bf16[1536,6912]{1,0:T(8,128)(2,1)}, bf16[1024,1536]{1,0:T(8,128)(2,1)S(1)}, bf16[16,1536]{1,0:T(8,128)(2,1)S(1)}) custom-call(bf16[208,384]{1,0:T(8,128)(2,1)S(1)} %copy-done.3, bf16[208,384]{1,0:T(8,128)(2,1)S(1)} %copy-done.2, bf16[192,512]{1,0:T(8,128)(2,1)S(1)} %copy-done.1, ...), custom_call_target="tpu_custom_call" | custom-call | bytes 40304640 | tf_op jit(solution)/shard_map/front/pallas_call | solution.py:214
  149.6 1.6 convert_bitcast_fusion
  152.2 4.6 fusion.16
  156.9 1.3 copy-done.23
  160.6 1.3 collective-permute-start
  161.9 1.5 collective-permute-start.1
  163.5 1.6 copy.75
  165.1 1.6 subtract_convert_fusion.1
  168.8 9.7 %collective-permute-done = bf16[256,512]{1,0:T(8,128)(2,1)} collective-permute-done((bf16[256,512]{1,0:T(8,128)(2,1)}, bf16[256,512]{1,0:T(8,128)(2,1)}, u32[]{:S(2)}, u32[]{:S(2)}) %collective-permute-start) | collective-permute-done | bytes 262176 | tf_op jit(solution)/shard_map/ppermute | solution.py:1032
  178.5 1.2 maximum_maximum_fusion
  179.7 0.9 fusion.70
  180.6 1.1 reshape.229
  182.2 2.2 fusion.8
  184.5 3.6 copy-done.5
  188.0 1.9 exponential_reduce_fusion
  190.1 6.2 %convolution_convert_fusion = bf16[2,128,6,256]{3,1,2,0:T(8,128)(2,1)S(1)} fusion(bf16[768,2,128,1]{2,1,0,3:T(2,128)(2,1)S(1)} %bitcast.99, f32[2,768,256,6]{2,1,3,0:T(8,128)} %copy-done.5, f32[2,6,256]{2,1,0:T(8,128)S(1)} %log_add_fusion, pred[256,768]{0,1:T(8,128)(4,1)S(1)} %compare_and_fusion), kind=kOutput, calls=%fused_computation.50 | convolution fusion | flops 613810176 | bytes 10825728 | tf_op jit(solution)/shard_map/agts,sad->tagd/dot_general | solution.py:1052
  196.3 5.2 multiply_reduce_fusion
  201.5 2.5 multiply_convert_fusion.two_ref
  204.0 109.2 %ffn.1 = (bf16[1024,1536]{1,0:T(8,128)(2,1)}, bf16[1024,2304]{1,0:T(8,128)(2,1)}, bf16[1024,2304]{1,0:T(8,128)(2,1)}, bf16[1024,2304]{1,0:T(8,128)(2,1)}, bf16[1...) custom-call(bf16[256,1536]{1,0:T(8,128)(2,1)} %multiply_convert_fusion.two_ref, bf16[1024,1536]{1,0:T(8,128)(2,1)} %copy-done.4, ...), custom_call_target="tpu_custom_call" | custom-call | flops 43486543872 | bytes 47185920 | tf_op jit(solution)/shard_map/ffn/pallas_call | solution.py:505
  313.2 2.3 fusion.31
  315.6 2.8 convert_bitcast_fusion.1
  318.3 4.3 fusion.19
  322.9 6.2 %fusion.42 = bf16[2,128,768]{2,1,0:T(8,128)(2,1)S(1)} fusion(bf16[256,2,6,128]{0,3,2,1:T(8,128)(2,1)S(1)} %bitcast.95, f32[2,768,256,6]{2,1,3,0:T(8,128)} %copy-done.5, f32[2,6,256]{2,1,0:T(8,128)S(1)} %log_add_fusion, pred[256,768]{0,1:T(8,128)(4,1)S(1)} %copy-done.8), kind=kOutput, calls=%fused_computation.55 | convolution fusion | flops 613613568 | bytes 10825728 | tf_op jit(solution)/shard_map/agts,tagd->sad/dot_general | solution.py:1073
  329.2 7.5 %fusion = (f32[2,6,256]{2,1,0:T(8,128)S(1)}, f32[2,768,256,6]{2,1,3,0:T(8,128)}) fusion(f32[2,768,256,6]{2,1,3,0:T(8,128)} %copy-done.5, f32[2,6,256]{2,1,0:T(8,128)S(1)} %log_add_fusion, pred[256,768]{0,1:T(8,128)(4,1)S(1)} %copy-done.8, bf16[256,2,6,128]{0,3,2,1:T(8,128)(2,1)S(1)} %bitcast.96, bf16[768,2,128,1]{2,1,0,3:T(2,128)(2,1)S(1)} %bitcast.100), kind=kOutput, calls=%fused_computation.2 | convolution fusion | flops 615773184 | bytes 20275200 | tf_op jit(solution)/shard_map/tagd,sad->agts/dot_general | solution.py:1068
  336.7 11.1 %fusion.2 = bf16[2,6,256,768]{2,3,1,0:T(8,128)(2,1)} fusion(f32[2,768,256,6]{2,1,3,0:T(8,128)} %get-tuple-element.86, f32[2,768,256,6]{2,1,3,0:T(8,128)} %copy-done.5, f32[2,6,256]{2,1,0:T(8,128)S(1)} %get-tuple-element.85, f32[2,6,256]{2,1,0:T(8,128)S(1)} %log_add_fusion, pred[256,768]{0,1:T(8,128)(4,1)S(1)} %copy-done.8), kind=kLoop, calls=%fused_computation.4 | loop fusion | flops 14155776 | bytes 23814144 | tf_op jit(solution)/shard_map/convert_element_type | solution.py:1070
  347.8 4.4 fusion.41
  354.2 3.6 collective-permute-start.2
  357.8 3.7 collective-permute-start.3
  361.6 1.0 subtract_convert_fusion
  362.5 1.4 copy.93
  363.9 1.1 pad_maximum_fusion.4
  365.0 1.2 copy.92
  366.2 1.1 convert_add_fusion
  369.0 5.1 fusion.34
  374.2 1.4 fusion.38
  375.6 1.3 pad_maximum_fusion.1.lhs_ref
  377.5 1.4 pad_maximum_fusion.rhs_ref
  378.9 177.5 %back.1 = (f32[192,6912]{1,0:T(8,128)}, f32[192,384]{1,0:T(8,128)}, f32[192,384]{1,0:T(8,128)}, f32[48,768]{1,0:T(8,128)}, bf16[256,1536]{1,0:T(8,128)(2,1)}, /*index=5*/f32[40,128]{1,0:T(8,128)}) custom-call(bf16[1024,1536]{1,0:T(8,128)(2,1)} %get-tuple-element.34.two_ref, bf16[1024,1536]{1,0:T(8,128)(2,1)} %copy-done.4, ...), custom_call_target="tpu_custom_call" | custom-call | flops 21743271936 | bytes 18874368 | tf_op jit(solution)/shard_map/back/pallas_call | solution.py:853
  556.5 5.1 fusion.69
  561.6 2.6 add_convert_fusion
  564.8 1.3 slice_bitcast_fusion
  566.1 1.4 fusion.72
  (166 shorter events, 15.0 us)
Async XLA Ops:
  0.6 2.3 copy-start.34
  0.7 3.3 copy-start.53
  0.7 3.3 copy-start.54
  0.7 3.5 copy-start.50
  0.7 3.5 copy-start.42
  0.7 4.2 copy-start.45
  0.7 4.2 copy-start.44
  0.7 4.9 copy-start.43
  6.3 3.7 copy-start
  149.5 7.4 %copy-start.4 = (bf16[1024,1536]{1,0:T(8,128)(2,1)}, bf16[1024,1536]{1,0:T(8,128)(2,1)S(1)}, u32[]{:S(2)}) copy-start(bf16[1024,1536]{1,0:T(8,128)(2,1)S(1)} %get-tuple-element.33.cot_ref) | copy-start | bytes 9437188
  149.5 2.4 copy-start.17
  149.5 2.7 copy-start.51
  149.5 2.7 copy-start.52
  152.2 4.7 copy-start.48
  158.2 3.6 copy-start.28
  158.7 6.4 %copy-start.32 = (f32[256,64]{0,1:T(8,128)}, f32[256,64]{0,1:T(8,128)S(1)}, u32[]{:S(2)}) copy-start(f32[256,64]{0,1:T(8,128)S(1)} %get-tuple-element.80) | copy-start | bytes 196612
  158.7 8.9 %copy-start.37 = (f32[256,64]{0,1:T(8,128)}, f32[256,64]{0,1:T(8,128)S(1)}, u32[]{:S(2)}) copy-start(f32[256,64]{0,1:T(8,128)S(1)} %get-tuple-element.78) | copy-start | bytes 196612
  158.9 4.4 copy-start.24
  160.6 17.9 %collective-permute-start = (bf16[256,512]{1,0:T(8,128)(2,1)}, bf16[256,512]{1,0:T(8,128)(2,1)}, u32[]{:S(2)}, u32[]{:S(2)}) collective-permute-start(bf16[256,512]{1,0:T(8,128)(2,1)} %pad_maximum_fusion.7), channel_id=1, source_target_pairs={{0,2},{1,3},{4,6},{5,7},{8,10},{9,11},{12,14},{13,15},{16,18},{17,... | collective-permute-start | bytes 786440 | tf_op jit(solution)/shard_map/ppermute | solution.py:1032
  161.9 16.6 %collective-permute-start.1 = (bf16[256,512]{1,0:T(8,128)(2,1)}, bf16[256,512]{1,0:T(8,128)(2,1)}, u32[]{:S(2)}, u32[]{:S(2)}) collective-permute-start(bf16[256,512]{1,0:T(8,128)(2,1)} %pad_maximum_fusion.7), channel_id=1, source_target_pairs={{0,1},{1,2},{2,3},{4,5},{5,6},{6,7},{8,9},{9,10},{10,11},{12,13},{... | collective-permute-start | bytes 786440 | tf_op jit(solution)/shard_map/ppermute | solution.py:1032
  163.5 3.2 copy-start.47
  167.2 14.9 %copy-start.9 = (bf16[256,12,64]{2,0,1:T(8,128)(2,1)}, bf16[256,12,64]{2,0,1:T(8,128)(2,1)S(1)}, u32[]{:S(2)}) copy-start(bf16[256,12,64]{2,0,1:T(8,128)(2,1)S(1)} %copy.76) | copy-start | bytes 1179652
  167.6 14.6 %copy-start.11 = (bf16[256,12,64]{2,0,1:T(8,128)(2,1)}, bf16[256,12,64]{2,0,1:T(8,128)(2,1)S(1)}, u32[]{:S(2)}) copy-start(bf16[256,12,64]{2,0,1:T(8,128)(2,1)S(1)} %copy.77) | copy-start | bytes 1179652
  168.8 21.3 %copy-start.7 = (pred[256,768]{0,1:T(8,128)(4,1)}, pred[256,768]{0,1:T(8,128)(4,1)S(1)}, u32[]{:S(2)}) copy-start(pred[256,768]{0,1:T(8,128)(4,1)S(1)} %compare_and_fusion) | copy-start | bytes 589828
  182.2 2.3 copy-start.15
  184.4 3.6 copy-start.5
  190.1 6.2 %copy-start.26 = (bf16[768,2,128]{2,1,0:T(2,128)(2,1)}, bf16[768,2,128]{2,1,0:T(2,128)(2,1)S(1)}, u32[]{:S(2)}) copy-start(bf16[768,2,128]{2,1,0:T(2,128)(2,1)S(1)} %reshape.228) | copy-start | bytes 1179652
  190.1 6.2 %copy-start.18 = (bf16[256,1536]{1,0:T(8,128)(2,1)S(1)}, bf16[256,1536]{1,0:T(8,128)(2,1)}, u32[]{:S(2)}) copy-start(bf16[256,1536]{1,0:T(8,128)(2,1)} %param.15) | copy-start | bytes 2359300
  196.3 5.2 copy-start.35
  313.2 2.3 copy-start.21
  318.3 4.3 copy-start.13
  318.3 4.6 copy-start.8
  322.9 6.3 %copy-start.27 = (bf16[768,2,128]{2,1,0:T(2,128)(2,1)S(1)}, bf16[768,2,128]{2,1,0:T(2,128)(2,1)}, u32[]{:S(2)}) copy-start(bf16[768,2,128]{2,1,0:T(2,128)(2,1)} %copy-done.26) | copy-start | bytes 1179652
  336.7 11.1 %copy-start.10 = (bf16[256,12,64]{2,0,1:T(8,128)(2,1)S(1)}, bf16[256,12,64]{2,0,1:T(8,128)(2,1)}, u32[]{:S(2)}) copy-start(bf16[256,12,64]{2,0,1:T(8,128)(2,1)} %copy-done.9) | copy-start | bytes 1179652
  336.7 11.1 %copy-start.12 = (bf16[256,12,64]{2,0,1:T(8,128)(2,1)S(1)}, bf16[256,12,64]{2,0,1:T(8,128)(2,1)}, u32[]{:S(2)}) copy-start(bf16[256,12,64]{2,0,1:T(8,128)(2,1)} %copy-done.11) | copy-start | bytes 1179652
  347.8 4.4 copy-start.6
  347.8 4.4 copy-start.16
  353.0 8.6 %copy-start.33 = (f32[256,64]{0,1:T(8,128)S(1)}, f32[256,64]{0,1:T(8,128)}, u32[]{:S(2)}) copy-start(f32[256,64]{0,1:T(8,128)} %copy-done.32) | copy-start | bytes 196612
  353.0 8.5 %copy-start.38 = (f32[256,64]{0,1:T(8,128)S(1)}, f32[256,64]{0,1:T(8,128)}, u32[]{:S(2)}) copy-start(f32[256,64]{0,1:T(8,128)} %copy-done.37) | copy-start | bytes 196612
  354.2 12.0 %collective-permute-start.2 = (bf16[256,512]{1,0:T(8,128)(2,1)}, bf16[256,512]{1,0:T(8,128)(2,1)}, u32[]{:S(2)}, u32[]{:S(2)}) collective-permute-start(bf16[256,512]{1,0:T(8,128)(2,1)} %get-tuple-element.63), channel_id=1, source_target_pairs={{1,0},{2,1},{3,2},{5,4},{6,5},{7,6},{9,8},{10,9},{11,10},{13,12},{... | collective-permute-start | bytes 786440 | tf_op jit(solution)/shard_map/ppermute | solution.py:1032
  357.8 8.3 %collective-permute-start.3 = (bf16[256,512]{1,0:T(8,128)(2,1)}, bf16[256,512]{1,0:T(8,128)(2,1)}, u32[]{:S(2)}, u32[]{:S(2)}) collective-permute-start(bf16[256,512]{1,0:T(8,128)(2,1)} %get-tuple-element.64), channel_id=1, source_target_pairs={{2,0},{3,1},{6,4},{7,5},{10,8},{11,9},{14,12},{15,13},{18,16},{19,... | collective-permute-start | bytes 786440 | tf_op jit(solution)/shard_map/ppermute | solution.py:1032
  365.0 2.5 copy-start.31
  365.0 2.5 copy-start.39
  369.0 5.2 copy-start.14
  556.4 5.1 copy-start.36
  561.6 2.6 copy-start.46
  561.6 5.9 %copy-start.41 = (f32[192,384]{1,0:T(8,128)S(1)}, f32[192,384]{1,0:T(8,128)}, u32[]{:S(2)}) copy-start(f32[192,384]{1,0:T(8,128)} %get-tuple-element.109) | copy-start | bytes 884740
  561.6 6.6 %copy-start.40 = (f32[192,384]{1,0:T(8,128)S(1)}, f32[192,384]{1,0:T(8,128)}, u32[]{:S(2)}) copy-start(f32[192,384]{1,0:T(8,128)} %get-tuple-element.115) | copy-start | bytes 884740
  (11 other events, 15.7 us)

commit v5 on v4

--- a/solution.py
+++ b/solution.py
@@ -23,11 +23,13 @@
 
 
 def front_body(
-    query_ref, out_ref, fixed_ref, ffn_ref, cot_ref,
-    att_all, ffn_all, cot_all, extra_out,
-    att_v, fill_sem, z_send, z_recv, cot_send, cot_recv, send, recv, keep_sem,
-    *, att_w, ffn_w, order, lead,
+    x_ref, turn_ref, mask_ref, bias_ref, query_ref, out_ref, fixed_ref, ffn_ref, cot_ref,
+    att_all, ffn_all, cot_all, two_out, mid_out, one_out, query_rot, kv_win, lse_out, ctx_out, gain_out,
+    att_v, w_v, one_v, q_v, kv_v, ctx_v, mid_v, two_v,
+    fill_sem, z_send, z_recv, cot_send, cot_recv, send, recv, keep_sem, w_sem, kv_send, kv_recv, save_sem,
+    *, pieces, order, lead,
 ):
+    f32, bf16 = jnp.float32, jnp.bfloat16
     d, z = lax.axis_index("dp"), lax.axis_index("tensor")
     size = 4
     by_x, by_y, mate, across = square(d)
@@ -80,13 +82,11 @@
     fills[0].wait()
 
     def views(kind, p):
-        src, dst, wide = ((att_v, att_all, att_w), (ffn_ref, ffn_all, ffn_w))[kind]
-        return src, dst, pl.ds(pl.multiple_of(p * wide, 128), wide)
+        src, dst = ((att_v, att_all), (ffn_ref, ffn_all))[kind]
+        return src, dst, pl.ds(*pieces[kind][p])
 
     def slot(kind, p):
-        return p + kind * n_att
-
-    n_att = att_all.shape[1] // att_w
+        return p + kind * len(pieces[0])
 
     def block(dst, cols, owner, first=0, many=None):
         many = rows if many is None else many
@@ -142,22 +142,25 @@
         arrived(kind, p, 5)
         relays(kind, p, 2)[0].start()
 
-    def finish(kind, p):
+    def settle(kind, p):
         for way in (2, 4, 6, 7):
             arrived(kind, p, way)
-        copies, keep = own(kind, p)
+        own(kind, p)[1].wait()
+
+    def finish(kind, p):
+        copies = own(kind, p)[0]
         for group in range(3):
             copies = copies + relays(kind, p, group)
         for copy in copies:
             copy.wait_send()
-        keep.wait()
 
     state = {"begun": 0, "query": False, "out": False}
 
     def ready(kind, p):
-        if kind == 1 or (p + 1) * att_w <= fixed:
+        end = sum(pieces[kind][p])
+        if kind == 1 or end <= fixed:
             return
-        need = 1 if (p + 1) * att_w <= fixed + size * part else 2
+        need = 1 if end <= fixed + size * part else 2
         for of in range(need):
             if not state[("query", "out")[of]]:
                 state[("query", "out")[of]] = True
@@ -169,6 +172,160 @@
                     for hop in range(1, size):
                         cot_copy(hop).start()
 
+    def weight_load(p):
+        cols = pl.ds(*pieces[0][p])
+        return pltpu.make_async_copy(att_all.at[:, cols], w_v.at[:, cols], w_sem.at[p])
+
+    def take(first, last):
+        for p in range(first, last):
+            settle(0, p)
+            weight_load(p).start()
+
+    def held(first, last):
+        for p in range(first, last):
+            weight_load(p).wait()
+
+    saves = []
+
+    def save(src, dst):
+        copy = pltpu.make_async_copy(src, dst, save_sem.at[len(saves)])
+        copy.start()
+        saves.append(copy)
+
+    part_rows = max(16, chunk // 4)
+
+    def norm(value_of, row, dst):
+        gain = gain_out[row : row + 1, :]
+
+        def some(r, carry):
+            at_r = pl.ds(pl.multiple_of(r * part_rows, part_rows), part_rows)
+            value = value_of(at_r)
+            inverse = lax.rsqrt(jnp.mean(value * value, axis=-1, keepdims=True) + EPSILON)
+            dst[at_r, :] = (value * inverse * gain).astype(bf16)
+            return carry
+
+        lax.fori_loop(0, chunk // part_rows, some, 0)
+
+    def turned(value):
+        return value * turn_ref[0] + pltpu.roll(value, HEAD_DIM // 2, 1) * turn_ref[1]
+
+    lead_w = fixed - 2 * KV_HEADS * HEAD_DIM
+    kv_w = KV_HEADS * HEAD_DIM
+    heads = size * part // HEAD_DIM
+    scale = HEAD_DIM ** (-0.5)
+
+    def kv_copy(hop):
+        return pltpu.make_async_remote_copy(
+            src_ref=kv_v.at[2], dst_ref=kv_v.at[2 - hop], send_sem=kv_send.at[hop - 1],
+            recv_sem=kv_recv.at[hop - 1], device_id={"tensor": z + hop}, device_id_type=MESH,
+        )
+
+    def keys():
+        pick = (
+            lax.broadcasted_iota(jnp.int32, (8, lead_w), 0)
+            == lax.broadcasted_iota(jnp.int32, (8, lead_w), 1)
+        ).astype(bf16)
+        gain_out[...] = lax.dot_general(
+            pick, w_v[:, :lead_w], (((1,), (1,)), ((), ())), preferred_element_type=f32
+        )
+        norm(lambda at_r: x_ref[at_r, :].astype(f32), 0, one_v)
+        save(one_v, one_out)
+        lin = jnp.dot(one_v[...], w_v[:, lead_w:fixed], preferred_element_type=f32) + bias_ref[0:1, :]
+        for g in range(KV_HEADS):
+            cols = slice(g * HEAD_DIM, (g + 1) * HEAD_DIM)
+            kv_v[2, :, cols] = turned(lin[:, cols]).astype(bf16)
+        kv_v[2, :, kv_w:] = lin[:, kv_w:].astype(bf16)
+        for hop in (1, 2):
+
+            @pl.when(z + hop < size)
+            def _(hop=hop):
+                kv_copy(hop).start()
+
+            @pl.when(z < hop)
+            def _(hop=hop):
+                kv_v[2 - hop] = jnp.zeros(kv_v.shape[1:], bf16)
+
+    def queries():
+        def pair(h, carry):
+            cols = pl.ds(pl.multiple_of(h * 2 * HEAD_DIM, 128), 2 * HEAD_DIM)
+            from_w = pl.ds(pl.multiple_of(fixed + h * 2 * HEAD_DIM, 128), 2 * HEAD_DIM)
+            lin = jnp.dot(one_v[...], w_v[:, from_w], preferred_element_type=f32)
+            lin += att_v[pl.ds(rows, 16), from_w][0:1, :].astype(f32)
+            for k in range(2):
+                out_cols = pl.ds(pl.multiple_of(h * 2 * HEAD_DIM + k * HEAD_DIM, 128), HEAD_DIM)
+                q_v[:, out_cols] = turned(lin[:, k * HEAD_DIM : (k + 1) * HEAD_DIM]).astype(bf16)
+            return carry
+
+        lax.fori_loop(0, heads // 2, pair, 0)
+        save(q_v, query_rot)
+
+    def kv_wait():
+        for hop in (1, 2):
+
+            @pl.when(z >= hop)
+            def _(hop=hop):
+                pltpu.make_async_copy(kv_v.at[2 - hop], kv_v.at[2 - hop], kv_recv.at[hop - 1]).wait()
+
+        save(kv_v, kv_win)
+
+    def attend(first, last):
+        def head(h, carry):
+            cols = pl.ds(pl.multiple_of(h * HEAD_DIM, 128), HEAD_DIM)
+            group = h // (heads // KV_HEADS)
+            key_cols = pl.ds(pl.multiple_of(group * HEAD_DIM, 128), HEAD_DIM)
+            value_cols = pl.ds(pl.multiple_of(kv_w + group * HEAD_DIM, 128), HEAD_DIM)
+            key = kv_v[:, :, key_cols].reshape(3 * chunk, HEAD_DIM)
+            value = kv_v[:, :, value_cols].reshape(3 * chunk, HEAD_DIM)
+            scores = lax.dot_general(
+                q_v[:, cols], key, (((1,), (1,)), ((), ())), preferred_element_type=f32
+            )
+            scores = scores * scale + mask_ref[...]
+            largest = jnp.max(scores, axis=-1, keepdims=True)
+            powers = jnp.exp(scores - largest)
+            mass = jnp.sum(powers, axis=-1, keepdims=True)
+            lse_out[h] = largest + jnp.log(mass)
+            probs = (powers * (1.0 / mass)).astype(bf16)
+            ctx_v[:, cols] = jnp.dot(probs, value, preferred_element_type=f32).astype(bf16)
+            return carry
+
+        lax.fori_loop(first, last, head, 0)
+
+    def project():
+        save(ctx_v, ctx_out)
+        tile = min(512, w_v.shape[0])
+
+        def some(n, carry):
+            at_n = pl.ds(pl.multiple_of(n * tile, tile), tile)
+            added = lax.dot_general(
+                ctx_v[...], w_v[at_n, fixed + size * part :], (((1,), (1,)), ((), ())),
+                preferred_element_type=f32,
+            )
+            mid_v[:, at_n] = x_ref[:, at_n].astype(f32) + added
+            return carry
+
+        lax.fori_loop(0, w_v.shape[0] // tile, some, 0)
+        save(mid_v, mid_out)
+        norm(lambda at_r: mid_v[at_r, :], 1, two_v)
+        save(two_v, two_out)
+
+    n_att = len(pieces[0])
+    n_qkv = 1 + (n_att - 1) // 2
+    third = heads // 3 + (heads % 3 > 0)
+    last_q = order.index((0, n_qkv - 1))
+    last_out = order.index((0, n_att - 1))
+    work = [
+        (last_q + 1, lambda: take(0, n_qkv)),
+        (last_q + 2, lambda: held(0, n_qkv)),
+        (last_q + 2, keys),
+        (last_q + 3, queries),
+        (last_out + 1, lambda: take(n_qkv, n_att)),
+        (last_out + 1, kv_wait),
+        (last_out + 1, lambda: attend(0, third)),
+        (last_out + 2, lambda: attend(third, 2 * third)),
+        (last_out + 3, lambda: attend(2 * third, heads)),
+        (last_out + 4, lambda: held(n_qkv, n_att)),
+        (last_out + 4, project),
+    ]
     total = len(order)
     for i in range(total + 1):
         while state["begun"] < min(total, i + lead):
@@ -179,12 +336,21 @@
             pass_on(*order[i])
         if i > 0:
             close(*order[i - 1])
+        while work and (work[0][0] <= i or i == total):
+            work.pop(0)[1]()
+    for kind, p in order:
+        if kind == 1:
+            settle(kind, p)
     for kind, p in order:
         finish(kind, p)
-    keep = pltpu.make_async_copy(
-        att_v.at[pl.ds(rows, tall - rows), pl.ds(fixed, size * part)], extra_out, fill_sem.at[0]
-    )
-    keep.start()
+    for copy in saves:
+        copy.wait()
+    for hop in (1, 2):
+
+        @pl.when(z + hop < size)
+        def _(hop=hop):
+            kv_copy(hop).wait_send()
+
     for of in range(2):
         for hop in range(1, size):
             z_copy(of, hop).wait_send()
@@ -192,45 +358,63 @@
         pltpu.make_async_copy(cot_ref, cot_ref, cot_recv.at[hop - 1]).wait()
         cot_copy(hop).wait_send()
     fills[3].wait()
-    keep.wait()
-
-
-def front(query, out, fixed, ffn_w, cot, att_tile=512, ffn_tile=768, collective_id=2, limit=48_000_000):
+
+
+def front(
+    tokens, turn, mask, kv_bias, query, out, fixed, ffn_w, cot, att_tile=512, ffn_tile=768,
+    collective_id=2, limit=60_000_000,
+):
     tall, part = query.shape
     rows, fixed_w = fixed.shape
+    chunk, width = tokens.shape
     size, ways = 4, 8
-    att_cols = fixed_w + 2 * size * part
-    n_att, n_ffn = att_cols // att_tile, ffn_w.shape[1] // ffn_tile
-    n_fixed = fixed_w // att_tile
-    third = n_ffn // 3
-    order = [(0, p) for p in range(n_fixed)] + [(1, p) for p in range(third)]
-    order += [(0, p) for p in range(n_fixed, n_att)] + [(1, p) for p in range(third, n_ffn)]
-    bf16 = jnp.bfloat16
+    query_w = size * part
+    att_cols = fixed_w + 2 * query_w
+    pieces = (
+        [(0, fixed_w)] + [(fixed_w + p * att_tile, att_tile) for p in range(2 * query_w // att_tile)],
+        [(p * ffn_tile, ffn_tile) for p in range(ffn_w.shape[1] // ffn_tile)],
+    )
+    n_att, n_ffn = len(pieces[0]), len(pieces[1])
+    early = min(2, n_ffn)
+    order = [(0, 0)] + [(1, p) for p in range(early)] + [(0, p) for p in range(1, n_att)]
+    order += [(1, p) for p in range(early, n_ffn)]
+    bf16, f32 = jnp.bfloat16, jnp.float32
     hbm = pl.BlockSpec(memory_space=pl.ANY)
     vmem = pl.BlockSpec(memory_space=pltpu.VMEM)
+    vm = pltpu.VMEM
     dma = pltpu.SemaphoreType.DMA
     shape = lambda *s: jax.ShapeDtypeStruct(s, bf16)
+    wide = lambda *s: jax.ShapeDtypeStruct(s, f32)
     slots = n_att + n_ffn
+    kv_w = 2 * KV_HEADS * HEAD_DIM
+    heads = query_w // HEAD_DIM
     return pl.pallas_call(
-        functools.partial(front_body, att_w=att_tile, ffn_w=ffn_tile, order=tuple(order), lead=3),
+        functools.partial(front_body, pieces=pieces, order=order, lead=3),
         out_shape=(
             shape(8 * rows, att_cols), shape(8 * rows, ffn_w.shape[1]),
-            shape(size * cot.shape[0], cot.shape[1]), shape(tall - rows, size * part),
+            shape(size * cot.shape[0], cot.shape[1]),
+            shape(chunk, width), wide(chunk, width), shape(chunk, width), shape(chunk, query_w),
+            shape(3, chunk, kv_w), wide(heads, chunk, 1), shape(chunk, query_w), wide(8, width),
         ),
-        in_specs=[vmem] * 5,
-        out_specs=(hbm,) * 4,
+        in_specs=[vmem] * 9,
+        out_specs=(hbm,) * 8 + (vmem, hbm, vmem),
         scratch_shapes=[
-            pltpu.VMEM((tall, att_cols), bf16), dma((4,)), dma((2, size - 1)), dma((2, size - 1)),
+            vm((tall, att_cols), bf16), vm((8 * rows, att_cols), bf16), vm((chunk, width), bf16),
+            vm((chunk, query_w), bf16), vm((3, chunk, kv_w), bf16), vm((chunk, query_w), bf16),
+            vm((chunk, width), f32), vm((chunk, width), bf16),
+            dma((4,)), dma((2, size - 1)), dma((2, size - 1)),
             dma((size - 1,)), dma((size - 1,)), dma((ways, slots)), dma((ways, slots)), dma((slots,)),
+            dma((n_att,)), dma((2,)), dma((2,)), dma((6,)),
         ],
         compiler_params=pltpu.CompilerParams(
             collective_id=collective_id, has_side_effects=True, vmem_limit_bytes=limit
         ),
         cost_estimate=pl.CostEstimate(
-            flops=0, bytes_accessed=20 * rows * (att_cols + ffn_w.shape[1]), transcendentals=0
+            flops=2 * chunk * width * att_cols, bytes_accessed=20 * rows * (att_cols + ffn_w.shape[1]),
+            transcendentals=0,
         ),
         name="front",
-    )(query, out, fixed, ffn_w, cot)
+    )(tokens, turn, mask, kv_bias, query, out, fixed, ffn_w, cot)
 
 
 def line_order(z, s):
@@ -923,28 +1107,77 @@
     return (gain_term, input_term)
 
 
-def joined_units(gate_w, up_w, down_w, gain_one, gain_two, padded):
-    gap = padded - gate_w.shape[1]
+def joined_units(gate_w, up_w, down_w):
+    units = gate_w.shape[1]
+    gap = -(-units // 768) * 768 - units
     wide = lambda w: jnp.pad(w, ((0, 0), (0, gap)))
-    tail = jnp.pad(jnp.stack([gain_one, gain_two], axis=1), ((0, 0), (0, gap - 2)))
-    return jnp.concatenate([wide(gate_w), wide(up_w), down_w, tail], axis=1)
-
-
-def gather_weights(query_w, query_b, out_w, kv_w, ffn_w, cotangent):
-    if lax.axis_size("dp") == 8 and lax.axis_size("tensor") == 4:
-        tail = jnp.pad(query_b[None, :], ((0, 15), (0, 0)))
-        tall_query = jnp.concatenate([query_w, tail], axis=0)
+    return jnp.concatenate([wide(gate_w), wide(up_w), wide(down_w)], axis=1)
+
+
+def attention_branch(tokens, cosine, sine, mask, gains_w, query_w, query_b, kv_w, kv_b, out_w, ffn_w, cotangent):
+    f32, bf16 = jnp.float32, jnp.bfloat16
+    rows = tokens.shape[0]
+    size = lax.axis_size("tensor")
+    fixed_w = jnp.concatenate([gains_w, kv_w], axis=1)
+    if lax.axis_size("dp") == 8 and size == 4:
+        tall_query = jnp.concatenate([query_w, jnp.pad(query_b[None, :], ((0, 15), (0, 0)))], axis=0)
         tall_out = jnp.pad(out_w, ((0, 16), (0, 0)))
-        att_all, ffn_all, cot_all, extra = front(tall_query, tall_out, kv_w, ffn_w, cotangent)
-        return att_all, ffn_all, cot_all, extra[0]
+        turn = jnp.stack(
+            [jnp.concatenate([cosine, cosine], axis=1), jnp.concatenate([-sine, sine], axis=1)]
+        )
+        att_w, ffn_all, cot_rows, two, middle, one, query_rot, kv_win, lse, context, gains = front(
+            tokens, turn, mask, kv_b[None, :], tall_query, tall_out, fixed_w, ffn_w, cotangent
+        )
+        kv_win = kv_win.reshape(3 * rows, kv_w.shape[1])
+        return att_w, ffn_all, cot_rows, two, middle, one, query_rot, kv_win, lse, context, gains[:2]
     pair = lax.all_gather(jnp.stack([query_w, out_w]), "tensor", axis=2, tiled=True)
-    att = jnp.concatenate([kv_w, pair[0], pair[1]], axis=1)
-    return (
-        lax.all_gather(att, "dp", axis=0, tiled=True),
-        lax.all_gather(ffn_w, "dp", axis=0, tiled=True),
-        lax.all_gather(cotangent, "tensor", axis=0, tiled=True),
-        lax.all_gather(query_b, "tensor", axis=0, tiled=True),
+    att_w = jnp.concatenate([fixed_w, pair[0], pair[1]], axis=1)
+    att_w = lax.all_gather(att_w, "dp", axis=0, tiled=True)
+    ffn_all = lax.all_gather(ffn_w, "dp", axis=0, tiled=True)
+    cot_rows = lax.all_gather(cotangent, "tensor", axis=0, tiled=True)
+    full_query_b = lax.all_gather(query_b, "tensor", axis=0, tiled=True).astype(f32)
+    ahead = gains_w.shape[1]
+    kv_width = kv_w.shape[1] // 2
+    qkv_width = 2 * kv_width + full_query_b.shape[0]
+    heads = full_query_b.shape[0] // HEAD_DIM
+    gains = att_w[:, :2].T.astype(f32)
+    inputs = tokens.astype(f32)
+    inverse = lax.rsqrt(jnp.mean(inputs * inputs, axis=-1, keepdims=True) + EPSILON)
+    one = (inputs * inverse * gains[0]).astype(bf16)
+    lin = jnp.dot(one, att_w[:, ahead : ahead + qkv_width], preferred_element_type=f32)
+    lin = lin + jnp.concatenate([kv_b, full_query_b])
+    cos_h, sin_h = cosine[:, None, :], sine[:, None, :]
+    query_rot = rotate(lin[:, 2 * kv_width :].reshape(rows, heads, HEAD_DIM), cos_h, sin_h).astype(bf16)
+    key_rot = rotate(lin[:, :kv_width].reshape(rows, KV_HEADS, HEAD_DIM), cos_h, sin_h).astype(bf16)
+    kv_own = jnp.concatenate(
+        [key_rot.reshape(rows, kv_width), lin[:, kv_width : 2 * kv_width].astype(bf16)], axis=1
     )
+    back_chunks = mask.shape[1] // rows - 1
+    kv_win = jnp.concatenate(
+        [shift(kv_own, hops) for hops in range(back_chunks, 0, -1)] + [kv_own], axis=0
+    )
+    window = kv_win.shape[0]
+    key_win = kv_win[:, :kv_width].reshape(window, KV_HEADS, HEAD_DIM)
+    value_win = kv_win[:, kv_width:].reshape(window, KV_HEADS, HEAD_DIM)
+    grouped = query_rot.reshape(rows, KV_HEADS, heads // KV_HEADS, HEAD_DIM)
+    scores = jnp.einsum("tagd,sad->agts", grouped, key_win, preferred_element_type=f32)
+    scores = scores * HEAD_DIM ** (-0.5) + mask
+    largest = jnp.max(scores, axis=-1, keepdims=True)
+    lse = largest + jnp.log(jnp.sum(jnp.exp(scores - largest), axis=-1, keepdims=True))
+    probs = jnp.exp(scores - lse).astype(bf16)
+    context = jnp.einsum("agts,sad->tagd", probs, value_win, preferred_element_type=f32)
+    context = context.reshape(rows, heads * HEAD_DIM).astype(bf16)
+    middle = inputs + contract_cols(context, att_w[:, ahead + qkv_width :])
+    inverse = lax.rsqrt(jnp.mean(middle * middle, axis=-1, keepdims=True) + EPSILON)
+    two = (middle * inverse * gains[1]).astype(bf16)
+    query_rot = query_rot.reshape(rows, heads * HEAD_DIM)
+    return att_w, ffn_all, cot_rows, two, middle, one, query_rot, kv_win, lse, context, gains
+
+
+def shift(value, hops):
+    size = lax.axis_size("tensor")
+    pairs = [(i, i + hops) for i in range(size) if 0 <= i + hops < size]
+    return lax.ppermute(value, "tensor", pairs)
 
 
 def sum_grads(two, cot_rows, hid, dg, du, normed_one, d_attended, d_lin, context, ffn_part, small):
@@ -987,84 +1220,59 @@
     out_w, gain_two, gate_w, up_w, down_w, cotangent,
 ):
     bf16, f32 = jnp.bfloat16, jnp.float32
-    model_width = tokens.shape[1]
-    rows = tokens.shape[0]
+    rows, model_width = tokens.shape
     tensor_size = lax.axis_size("tensor")
     rank = lax.axis_index("tensor")
-    seq_length = rows * tensor_size
     kv_width = key_w.shape[1]
+    fixed_width = 2 * kv_width
     query_width = query_w.shape[1] * tensor_size
+    qkv_width = fixed_width + query_width
     heads = query_width // HEAD_DIM
     group = heads // KV_HEADS
     scale = HEAD_DIM ** (-0.5)
     units = gate_w.shape[1]
-    padded = -(-units // 768) * 768
-    fixed_width = 2 * kv_width
-    qkv_width = fixed_width + query_width
-    att_w, ffn_w, cot_rows, full_query_b = gather_weights(
-        query_w, query_b, out_w, jnp.concatenate([key_w, value_w], axis=1),
-        joined_units(gate_w, up_w, down_w, gain_one, gain_two, padded), cotangent,
-    )
-    gains = ffn_w[:, 2 * padded + units : 2 * padded + units + 2].T.astype(f32)
-    qkv_w = att_w[:, :qkv_width]
-    out_full = att_w[:, qkv_width:]
-    qkv_b = jnp.concatenate([key_b, value_b, full_query_b]).astype(f32)
-
-    inputs = tokens.astype(f32)
-    inverse_one = lax.rsqrt(jnp.mean(inputs * inputs, axis=-1, keepdims=True) + EPSILON)
-    unit_one = inputs * inverse_one
-    normed_one = (unit_one * gains[0]).astype(bf16)
-    lin = jnp.dot(normed_one, qkv_w, preferred_element_type=f32) + qkv_b
+    back_chunks = min(tensor_size - 1, -(-DOC_MAX // rows))
+    window = (back_chunks + 1) * rows
     cosine, sine = angle_tables(rank * rows, rows, HEAD_DIM)
     cos_h, sin_h = cosine[:, None, :], sine[:, None, :]
-    query_rot = rotate(lin[:, fixed_width:].reshape(rows, heads, HEAD_DIM), cos_h, sin_h).astype(bf16)
-    key_rot = rotate(
-        lin[:, :kv_width].reshape(rows, KV_HEADS, HEAD_DIM), cos_h, sin_h
-    ).astype(bf16)
-    value_own = lin[:, kv_width:fixed_width].astype(bf16)
-    kv_own = jnp.concatenate([key_rot.reshape(rows, kv_width), value_own], axis=1)
-    back = min(tensor_size - 1, -(-DOC_MAX // rows))
-    window = (back + 1) * rows
-    first = (rank - back) * rows
-
-    def shift(value, hops):
-        pairs = [(i, i + hops) for i in range(tensor_size) if 0 <= i + hops < tensor_size]
-        return lax.ppermute(value, "tensor", pairs)
-
-    kv_win = jnp.concatenate([shift(kv_own, hops) for hops in range(back, 0, -1)] + [kv_own], axis=0)
-    key_win = kv_win[:, :kv_width].reshape(window, KV_HEADS, HEAD_DIM)
-    value_win = kv_win[:, kv_width:].reshape(window, KV_HEADS, HEAD_DIM)
     segment = segments[0]
     own_segment = lax.dynamic_slice_in_dim(segment, rank * rows, rows, 0)
-    win_segment = lax.dynamic_slice_in_dim(
-        jnp.concatenate([jnp.full((back * rows,), -1, segment.dtype), segment]), rank * rows, window, 0
+    before = jnp.full((back_chunks * rows,), -1, segment.dtype)
+    win_segment = lax.dynamic_slice_in_dim(jnp.concatenate([before, segment]), rank * rows, window, 0)
+    own_pos = back_chunks * rows + jnp.arange(rows)
+    win_pos = jnp.arange(window)
+    allowed = (own_segment[:, None] == win_segment[None, :]) & (win_pos[None, :] <= own_pos[:, None])
+    mask = jnp.where(allowed, 0.0, NEGATIVE).astype(f32)
+    ahead = 128
+    gains_w = jnp.pad(jnp.stack([gain_one, gain_two], axis=1), ((0, 0), (0, ahead - 2)))
+    (
+        att_w, ffn_w, cot_rows, normed_two, middle, normed_one, query_rot, kv_win, lse, context, gains,
+    ) = attention_branch(
+        tokens, cosine, sine, mask, gains_w, query_w, query_b, jnp.concatenate([key_w, value_w], axis=1),
+        jnp.concatenate([key_b, value_b]).astype(f32), out_w, joined_units(gate_w, up_w, down_w), cotangent,
     )
-    own_pos = rank * rows + jnp.arange(rows)
-    win_pos = first + jnp.arange(window)
-    allowed = (own_segment[:, None] == win_segment[None, :]) & (win_pos[None, :] <= own_pos[:, None])
-    grouped = query_rot.reshape(rows, KV_HEADS, group, HEAD_DIM)
-    scores = jnp.einsum("tagd,sad->agts", grouped, key_win, preferred_element_type=f32) * scale
-    masked = jnp.where(allowed, scores, NEGATIVE)
-    largest = jnp.max(masked, axis=-1, keepdims=True)
-    log_total = largest + jnp.log(jnp.sum(jnp.exp(masked - largest), axis=-1, keepdims=True))
-    probs = jnp.exp(masked - log_total)
-    probs_low = probs.astype(bf16)
-    context = jnp.einsum("agts,sad->tagd", probs_low, value_win, preferred_element_type=f32)
-    context = context.reshape(rows, query_width).astype(bf16)
-    middle = inputs + contract_cols(context, out_full)
-    inverse_two = lax.rsqrt(jnp.mean(middle * middle, axis=-1, keepdims=True) + EPSILON)
-    unit_two = middle * inverse_two
-    normed_two = (unit_two * gains[1]).astype(bf16)
-
+    qkv_w = att_w[:, ahead : ahead + qkv_width]
+    out_full = att_w[:, ahead + qkv_width :]
     rows_two, hidden_low, d_gate, d_upper, ffn_part, d_normed_two = ffn(
         normed_two, cot_rows, ffn_w
     )
     d_normed_two = d_normed_two.astype(f32)
+    inputs = tokens.astype(f32)
+    inverse_one = lax.rsqrt(jnp.mean(inputs * inputs, axis=-1, keepdims=True) + EPSILON)
+    unit_one = inputs * inverse_one
+    inverse_two = lax.rsqrt(jnp.mean(middle * middle, axis=-1, keepdims=True) + EPSILON)
+    unit_two = middle * inverse_two
     gain_two_term, d_from_two = norm_back(d_normed_two, unit_two, inverse_two, gains[1])
     d_middle = cotangent.astype(f32) + d_from_two
     d_attended = d_middle.astype(bf16)
     d_context = jnp.dot(d_attended, out_full, preferred_element_type=f32).astype(bf16)
     d_context = d_context.reshape(rows, KV_HEADS, group, HEAD_DIM)
+    key_win = kv_win[:, :kv_width].reshape(window, KV_HEADS, HEAD_DIM)
+    value_win = kv_win[:, kv_width:].reshape(window, KV_HEADS, HEAD_DIM)
+    grouped = query_rot.reshape(rows, KV_HEADS, group, HEAD_DIM)
+    scores = jnp.einsum("tagd,sad->agts", grouped, key_win, preferred_element_type=f32) * scale + mask
+    probs = jnp.exp(scores - lse.reshape(KV_HEADS, group, rows, 1))
+    probs_low = probs.astype(bf16)
     d_probs = jnp.einsum("tagd,sad->agts", d_context, value_win, preferred_element_type=f32)
     row_delta = jnp.sum(probs * d_probs, axis=-1, keepdims=True)
     d_scores = (probs * (d_probs - row_delta)).astype(bf16)
@@ -1078,9 +1286,9 @@
     d_kv_win = jnp.concatenate(
         [d_key_win.reshape(window, kv_width), d_value_win.reshape(window, kv_width)], axis=1
     ).astype(bf16)
-    d_kv = d_kv_win[back * rows :].astype(f32)
-    for hops in range(1, back + 1):
-        given = d_kv_win[(back - hops) * rows : (back - hops + 1) * rows]
+    d_kv = d_kv_win[back_chunks * rows :].astype(f32)
+    for hops in range(1, back_chunks + 1):
+        given = d_kv_win[(back_chunks - hops) * rows : (back_chunks - hops + 1) * rows]
         d_kv = d_kv + shift(given, -hops).astype(f32)
     d_key_lin = rotate_back(d_kv[:, :kv_width].reshape(rows, KV_HEADS, HEAD_DIM), cos_h, sin_h)
     d_lin = jnp.concatenate(

time: 580 us -> 577 us (level); the launches traced: 569 us -> 574 us
  Pallas kernels: 423 us -> 468 us
  matrix products: 46.5 us -> 30.5 us
  waiting for transfers between devices: 9.66 us -> 0.01 us
    pallas_call x1, Pallas kernels: 137 us -> 180 us  [front(): pl.pallas_call(functools.partial(front_body, pieces=pieces, order=order,...]
    dot_general x2 -> x0, matrix products: 10.8 us -> none  [the longest x1 6.18 us: local(): jnp.einsum('agts,sad->tagd', probs_low, value_win, preferred_element_type...]
    ppermute x4 -> x2, waiting for transfers between devices: 9.66 us -> 0.01 us  [shift(): return lax.ppermute(value, 'tensor', pairs)]
  transfers between devices with their start and end apart: 4 -> 2, of which waited for: 1 -> 0; matrix products, arithmetic and copies ran while one was open for 2% -> 1% of each run, Pallas kernels for 0% -> 0%
where the time goes in v5:
time: 577 us; the launch traced here: 574 us
  Pallas kernels  468 us (81%)
  other arithmetic  36.8 us (6%)
  matrix products  30.5 us (5%)
  local copies, waits for them, and re-layouts  30.4 us (5%)
  starting transfers between devices  7.4 us (1%)
    pallas_call x1, Pallas kernels, front(): pl.pallas_call(functools.partial(front_body, pieces=pieces, order=order,...  180 us
    pallas_call x1, Pallas kernels, back(): pl.pallas_call(functools.partial(back_body, n_f=n_f, wide=wide, cols_out=...  179 us
    pallas_call x1, Pallas kernels, ffn(): pl.pallas_call(functools.partial(ffn_body, axis=axis, ft=ft, nt=nt), out_...  109 us
  transfers between devices with their start and end apart: 2, of which 0 were waited for; matrix products, arithmetic and copies ran while one was open for 1% of the time, Pallas kernels for 0%

profile of v5, /device:TPU:26, one launch (start us, length us, event | category | flops | bytes accessed | tf_op | source)
XLA Modules:
  0.0 574.4 jit_solution(190855623250597627)
XLA Ops:
  0.7 0.7 stack.30
  1.4 0.7 concatenate.59
  2.1 0.7 concatenate.60
  3.4 0.7 broadcast_in_dim.10
  4.3 0.7 constant_dynamic-slice_fusion
  5.0 0.8 pad_dynamic-slice_fusion
  6.8 0.7 fusion.57.query_ref
  7.5 0.7 pad.28.out_ref
  8.9 0.7 pad_maximum_fusion.6.turn_ref
  9.6 0.7 fusion.56.fixed_ref
  10.4 1.6 fusion.17.ffn_ref
  12.0 180.5 %front.1 = (bf16[1536,3712]{1,0:T(8,128)(2,1)}, bf16[1536,6912]{1,0:T(8,128)(2,1)}, bf16[1024,1536]{1,0:T(8,128)(2,1)}, bf16[256,1536]{1,0:T(8,128)(2,1)}, f32[2...) custom-call(bf16[256,1536]{1,0:T(8,128)(2,1)} %x_ref.1, ...), custom_call_target="tpu_custom_call" | custom-call | flops 2919235584 | bytes 40796160 | tf_op jit(solution)/shard_map/front/pallas_call | solution.py:391
  192.5 1.7 multiply_reduce_fusion
  194.8 0.9 slice_reduce_fusion
  195.8 108.9 %ffn.1 = (bf16[1024,1536]{1,0:T(8,128)(2,1)}, bf16[1024,2304]{1,0:T(8,128)(2,1)}, bf16[1024,2304]{1,0:T(8,128)(2,1)}, bf16[1024,2304]{1,0:T(8,128)(2,1)}, bf16[1...) custom-call(bf16[256,1536]{1,0:T(8,128)(2,1)} %get-tuple-element.38.two_ref, ...), custom_call_target="tpu_custom_call" | custom-call | flops 43486543872 | bytes 47185920 | tf_op jit(solution)/shard_map/ffn/pallas_call | solution.py:689
  304.7 2.2 fusion.29
  307.0 1.5 copy.65
  308.5 2.0 fusion.63
  310.5 1.9 copy.100
  312.5 1.9 copy.99
  314.4 2.7 convert_bitcast_fusion
  317.1 1.2 copy-done.2
  318.3 4.7 fusion.18
  323.0 1.4 copy.70
  324.4 1.4 fusion.66
  325.8 3.6 fusion.42
  329.5 1.2 copy.98
  330.7 7.5 %fusion = (f32[2,6,256]{2,1,0:T(8,128)S(1)}, f32[2,768,256,6]{2,1,3,0:T(8,128)}) fusion(f32[2,768,256,6]{2,1,3,0:T(8,128)} %copy-done, f32[2,6,256]{2,1,0:T(8,128)S(1)} %sub.31, f32[256,768]{0,1:T(8,128)S(1)} %copy.68, bf16[768,2,128,1]{0,2,3,1:T(8,128)(2,1)S(1)} %bitcast.104, bf16[256,2,6,128]{0,3,2,1:T(8,128)(2,1)S(1)} %bitcast.102), kind=kOutput, calls=%fused_computation.2 | convolution fusion | flops 615773184 | bytes 20865024 | tf_op jit(solution)/shard_map/tagd,sad->agts/dot_general | solution.py:1276
  338.2 11.1 %fusion.2 = bf16[2,6,256,768]{2,3,1,0:T(8,128)(2,1)} fusion(f32[2,768,256,6]{2,1,3,0:T(8,128)} %get-tuple-element.90, f32[2,768,256,6]{2,1,3,0:T(8,128)} %copy-done, f32[2,6,256]{2,1,0:T(8,128)S(1)} %get-tuple-element.89, f32[2,6,256]{2,1,0:T(8,128)S(1)} %sub.31, f32[256,768]{0,1:T(8,128)S(1)} %copy.68), kind=kLoop, calls=%fused_computation.4 | loop fusion | flops 14155776 | bytes 24403968 | tf_op jit(solution)/shard_map/convert_element_type | solution.py:1278
  349.2 4.0 fusion.41
  353.5 0.8 fusion.53
  354.3 4.8 collective-permute-start
  359.1 2.6 collective-permute-start.1
  361.7 0.8 fusion.36
  362.7 3.1 convolution_multiply_fusion
  366.7 1.2 copy.80
  367.9 2.4 pad_maximum_fusion.1.lhs_ref
  370.3 1.2 convert_add_fusion
  373.5 6.2 %fusion.31 = (f32[256]{0:T(256)S(1)}, f32[1536]{0:T(1024)S(1)}, f32[256,1536]{1,0:T(8,128)}) fusion(bf16[256,1536]{1,0:T(8,128)(2,1)S(1)} %copy-done.10, f32[1536]{0:T(1024)S(1)} %get-tuple-element.64, f32[256]{0:T(256)} %add_rsqrt_fusion, bf16[1536,3712]{1,0:T(8,128)(2,1)} %get-tuple-element.51, bf16[256,1536]{0,1:T(8,128)(2,1)S(1)} %bitcast.95, ...), kind=kOutput, calls=%fused_computation.41 | convolution fusion | flops 1616509184 | bytes 9713664 | tf_op jit(solution)/shard_map/dot_general | solution.py:1092
  380.3 1.4 pad_maximum_fusion.rhs_ref
  381.7 178.6 %back.1 = (f32[192,6912]{1,0:T(8,128)}, f32[192,384]{1,0:T(8,128)}, f32[192,384]{1,0:T(8,128)}, f32[48,768]{1,0:T(8,128)}, bf16[256,1536]{1,0:T(8,128)(2,1)}, /*index=5*/f32[40,128]{1,0:T(8,128)}) custom-call(bf16[1024,1536]{1,0:T(8,128)(2,1)} %get-tuple-element.41.two_ref, bf16[1024,1536]{1,0:T(8,128)(2,1)} %get-tuple-element.39.cot_ref, ...), custom_call_target="tpu_custom_call" | custom-call | flops 21743271936 | bytes 18874368 | tf_op jit(solution)/shard_map/back/pallas_call | solution.py:1037
  560.3 2.7 add_convert_fusion
  563.0 1.3 slice_bitcast_fusion
  565.0 5.2 fusion.62
  570.2 1.4 fusion.35
  571.6 1.4 fusion.65
  572.9 0.7 copy.106
  573.7 0.7 copy.107
  (109 shorter events, 7.7 us)
Async XLA Ops:
  0.6 6.2 %copy-start.30 = (bf16[192,384]{1,0:T(8,128)(2,1)S(1)}, bf16[192,384]{1,0:T(8,128)(2,1)}, u32[]{:S(2)}) copy-start(bf16[192,384]{1,0:T(8,128)(2,1)} %param.18) | copy-start | bytes 442372
  0.7 6.9 %copy-start.31 = (bf16[192,384]{1,0:T(8,128)(2,1)S(1)}, bf16[192,384]{1,0:T(8,128)(2,1)}, u32[]{:S(2)}) copy-start(bf16[192,384]{1,0:T(8,128)(2,1)} %param.24) | copy-start | bytes 442372
  5.7 3.9 copy-start.32
  5.7 3.9 copy-start.33
  5.9 4.4 copy-start.9
  6.0 4.4 copy-start.22
  6.2 4.1 copy-start.23
  6.2 4.1 copy-start.24
  8.8 3.2 copy-start.13
  8.8 3.2 copy-start.16
  192.5 1.9 copy-start.19
  307.0 7.4 %copy-start.1 = (f32[256,1536]{1,0:T(8,128)S(1)}, f32[256,1536]{1,0:T(8,128)}, u32[]{:S(2)}) copy-start(f32[256,1536]{1,0:T(8,128)} %get-tuple-element.37) | copy-start | bytes 4718596
  317.1 1.2 copy-start.2
  318.3 6.1 %copy-start.6 = (bf16[768,256]{0,1:T(8,128)(2,1)S(1)}, bf16[768,256]{0,1:T(8,128)(2,1)}, u32[]{:S(2)}) copy-start(bf16[768,256]{0,1:T(8,128)(2,1)} %copy.99) | copy-start | bytes 1179652
  325.8 3.7 copy-start
  325.8 4.9 copy-start.21
  330.7 22.8 %copy-start.4 = (bf16[768,256]{1,0:T(8,128)(2,1)}, bf16[768,256]{1,0:T(8,128)(2,1)S(1)}, u32[]{:S(2)}) copy-start(bf16[768,256]{1,0:T(8,128)(2,1)S(1)} %copy.98) | copy-start | bytes 1179652
  353.2 8.5 %copy-start.10 = (bf16[256,1536]{1,0:T(8,128)(2,1)S(1)}, bf16[256,1536]{1,0:T(8,128)(2,1)}, u32[]{:S(2)}) copy-start(bf16[256,1536]{1,0:T(8,128)(2,1)} %x_ref.1) | copy-start | bytes 2359300
  353.2 9.2 %copy-start.14 = (f32[256,64]{1,0:T(8,128)S(1)}, f32[256,64]{1,0:T(8,128)}, u32[]{:S(2)}) copy-start(f32[256,64]{1,0:T(8,128)} %copy-done.13) | copy-start | bytes 196612
  353.3 9.3 %copy-start.17 = (f32[256,64]{1,0:T(8,128)S(1)}, f32[256,64]{1,0:T(8,128)}, u32[]{:S(2)}) copy-start(f32[256,64]{1,0:T(8,128)} %copy-done.16) | copy-start | bytes 196612
  353.3 9.4 %copy-start.7 = (bf16[768,256]{0,1:T(8,128)(2,1)S(1)}, bf16[768,256]{0,1:T(8,128)(2,1)}, u32[]{:S(2)}) copy-start(bf16[768,256]{0,1:T(8,128)(2,1)} %copy.99) | copy-start | bytes 1179652
  354.3 16.0 %collective-permute-start = (bf16[256,512]{1,0:T(8,128)(2,1)}, bf16[256,512]{1,0:T(8,128)(2,1)}, u32[]{:S(2)}, u32[]{:S(2)}) collective-permute-start(bf16[256,512]{1,0:T(8,128)(2,1)} %get-tuple-element.73), channel_id=1, source_target_pairs={{1,0},{2,1},{3,2},{5,4},{6,5},{7,6},{9,8},{10,9},{11,10},{13,12},{... | collective-permute-start | bytes 786440 | tf_op jit(solution)/shard_map/ppermute | solution.py:1180
  359.1 11.2 %collective-permute-start.1 = (bf16[256,512]{1,0:T(8,128)(2,1)}, bf16[256,512]{1,0:T(8,128)(2,1)}, u32[]{:S(2)}, u32[]{:S(2)}) collective-permute-start(bf16[256,512]{1,0:T(8,128)(2,1)} %get-tuple-element.74), channel_id=1, source_target_pairs={{2,0},{3,1},{6,4},{7,5},{10,8},{11,9},{14,12},{15,13},{18,16},{19,... | collective-permute-start | bytes 786440 | tf_op jit(solution)/shard_map/ppermute | solution.py:1180
  362.7 3.2 copy-start.36
  366.6 1.2 copy-start.8
  366.7 3.6 copy-start.5
  370.3 1.4 copy-start.15
  370.3 1.4 copy-start.18
  372.7 0.7 copy-start.26
  372.8 0.7 copy-start.27
  373.5 6.8 %copy-start.12 = (bf16[256,1536]{1,0:T(8,128)(2,1)S(1)}, bf16[256,1536]{1,0:T(8,128)(2,1)}, u32[]{:S(2)}) copy-start(bf16[256,1536]{1,0:T(8,128)(2,1)} %copy.80) | copy-start | bytes 2359300
  373.5 6.8 %copy-start.25 = (bf16[256,1536]{1,0:T(8,128)(2,1)S(1)}, bf16[256,1536]{1,0:T(8,128)(2,1)}, u32[]{:S(2)}) copy-start(bf16[256,1536]{1,0:T(8,128)(2,1)} %get-tuple-element.52) | copy-start | bytes 2359300
  560.3 4.0 copy-start.34
  565.0 5.2 copy-start.3
  565.0 5.2 copy-start.11
  565.0 5.2 copy-start.20
  565.0 5.2 copy-start.35
  570.2 2.7 copy-start.29
  570.2 3.4 copy-start.28

commit v6 on v5

--- a/solution.py
+++ b/solution.py
@@ -69,12 +69,35 @@
             device_id_type=MESH,
         )
 
-    def cot_copy(hop):
+    has_low, has_high = z > 0, z < size - 1
+
+    def cot_copy(j, dz):
+        ref = cot_all.at[pl.ds(pl.multiple_of(j * chunk, chunk), chunk), :]
         return pltpu.make_async_remote_copy(
-            src_ref=cot_ref, dst_ref=cot_all.at[at, :], send_sem=cot_send.at[hop - 1],
-            recv_sem=cot_recv.at[hop - 1], device_id={"tensor": (z + hop) % size},
-            device_id_type=MESH,
-        )
+            src_ref=ref, dst_ref=ref, send_sem=cot_send.at[(dz + 1) // 2, j], recv_sem=cot_recv.at[j],
+            device_id={"tensor": z + dz}, device_id_type=MESH,
+        )
+
+    def cot_start():
+        fills[3].wait()
+        for dz, there in ((-1, has_low), (1, has_high)):
+
+            @pl.when(there)
+            def _(dz=dz):
+                cot_copy(z, dz).start()
+
+    def cot_step(hop):
+        for sign, onward in ((-1, has_high), (1, has_low)):
+            j = z + sign * hop
+            inside = (j >= 0) if sign == -1 else (j < size)
+
+            @pl.when(inside)
+            def _(j=j, sign=sign):
+                cot_copy(j, -sign).wait_recv()
+
+            @pl.when(jnp.logical_and(inside, onward))
+            def _(j=j, sign=sign):
+                cot_copy(j, -sign).start()
 
     for of in range(2):
         for hop in range(1, size):
@@ -169,8 +192,7 @@
                     ref = att_v.at[:, place(of, z)]
                     pltpu.make_async_copy(ref, ref, z_recv.at[of, hop - 1]).wait()
                 if of == 1:
-                    for hop in range(1, size):
-                        cot_copy(hop).start()
+                    cot_start()
 
     def weight_load(p):
         cols = pl.ds(*pieces[0][p])
@@ -314,6 +336,8 @@
     last_q = order.index((0, n_qkv - 1))
     last_out = order.index((0, n_att - 1))
     work = [
+        (last_q - 1, lambda: cot_step(1)),
+        (last_q + 1, lambda: cot_step(2)),
         (last_q + 1, lambda: take(0, n_qkv)),
         (last_q + 2, lambda: held(0, n_qkv)),
         (last_q + 2, keys),
@@ -325,6 +349,7 @@
         (last_out + 3, lambda: attend(2 * third, heads)),
         (last_out + 4, lambda: held(n_qkv, n_att)),
         (last_out + 4, project),
+        (last_out + 5, lambda: cot_step(3)),
     ]
     total = len(order)
     for i in range(total + 1):
@@ -354,10 +379,13 @@
     for of in range(2):
         for hop in range(1, size):
             z_copy(of, hop).wait_send()
-    for hop in range(1, size):
-        pltpu.make_async_copy(cot_ref, cot_ref, cot_recv.at[hop - 1]).wait()
-        cot_copy(hop).wait_send()
-    fills[3].wait()
+    for j in range(size):
+        for dz, there in ((-1, has_low), (1, has_high)):
+            came = jnp.logical_and((z <= j) if dz == -1 else (z >= j), there)
+
+            @pl.when(came)
+            def _(j=j, dz=dz):
+                cot_copy(j, dz).wait_send()
 
 
 def front(
@@ -403,7 +431,7 @@
             vm((chunk, query_w), bf16), vm((3, chunk, kv_w), bf16), vm((chunk, query_w), bf16),
             vm((chunk, width), f32), vm((chunk, width), bf16),
             dma((4,)), dma((2, size - 1)), dma((2, size - 1)),
-            dma((size - 1,)), dma((size - 1,)), dma((ways, slots)), dma((ways, slots)), dma((slots,)),
+            dma((2, size)), dma((size,)), dma((ways, slots)), dma((ways, slots)), dma((slots,)),
             dma((n_att,)), dma((2,)), dma((2,)), dma((6,)),
         ],
         compiler_params=pltpu.CompilerParams(
@@ -716,13 +744,16 @@
 
 
 def back_body(
-    two_ref, cot_ref, hid_ref, dg_ref, du_ref, lhs_ref, rhs_ref, part_ref, small_ref,
-    ffn_out, query_out, out_out, kv_out, sum_out, small_out,
+    two_ref, cot_ref, hid_ref, dg_ref, du_ref, part_ref, up_ref, x_ref, mid_ref, gain_ref, att_ref,
+    query_ref, win_ref, lse_ref, ctx_ref, one_ref, mask_ref, turn_ref,
+    ffn_out, query_out, out_out, kv_out, mixed_out, input_out, small_out,
+    up_v, own_v, x_v, mid_v, gain_v, w_v, query_v, win_v, lse_v, mask_v, turn_v, lhs_ref, rhs_ref,
+    d_mid, d_ctx, d_win, kv_give, kv_take, d_one, small_ref,
     left_v, right_v, grad, mate_land, core_sum, x_land, y_land, second, x_last, y_last, stage, fin,
-    z_land, kv_land, sum_land, small_z, small_hop, small_next,
+    z_land, kv_land, sum_land, small_z, small_hop, small_next, in_sem, give_send, give_recv,
     left_sem, right_sem, mate_send, mate_recv, one_send, one_recv, two_send, two_recv, stage_sem,
     z_send, z_recv, kv_send, kv_recv, sum_send, sum_recv, own_sem, small_send, small_recv,
-    hop_send, hop_recv, *, n_f, wide, cols_out,
+    hop_send, hop_recv, *, n_f, wide,
 ):
     f32, bf16 = jnp.float32, jnp.bfloat16
     d, z = lax.axis_index("dp"), lax.axis_index("tensor")
@@ -733,8 +764,9 @@
     cross = 3 - here
     block, half = core_sum.shape[2], core_sum.shape[2] // 2
     n_ffn, n_att = 3 * n_f, rhs_ref.shape[1] // wide
+    ring = x_land.shape[0]
     total = n_ffn + n_att
-    chunk = sum_out.shape[0]
+    chunk, width = mixed_out.shape
     share = block // size
     part_w = wide // 2
 
@@ -747,9 +779,23 @@
         )
 
     lefts = [
-        pltpu.make_async_copy(ref, left_v.at[k], left_sem.at[k])
-        for k, ref in enumerate((cot_ref, two_ref))
+        pltpu.make_async_copy(ref, left_v, left_sem.at[k]) for k, ref in enumerate((cot_ref, two_ref))
     ]
+    query_w = query_ref.shape[1]
+    kv_w = KV_HEADS * HEAD_DIM
+    heads = query_w // HEAD_DIM
+    scale = HEAD_DIM ** (-0.5)
+    ahead = att_ref.shape[1] - 2 * query_w - 2 * kv_w
+    own_rows = pl.ds(pl.multiple_of(z * chunk, chunk), chunk)
+    ctx_cols = pl.ds(query_w, query_w)
+    plan = (
+        (up_ref, up_v), (cot_ref.at[own_rows, :], own_v), (mid_ref, mid_v), (gain_ref, gain_v),
+        (att_ref.at[:, pl.ds(ahead + 2 * kv_w + query_w, query_w)], w_v.at[:, pl.ds(0, query_w)]),
+        (query_ref, query_v), (win_ref, win_v), (lse_ref, lse_v), (mask_ref, mask_v), (turn_ref, turn_v),
+        (ctx_ref, rhs_ref.at[:, ctx_cols]), (x_ref, x_v), (one_ref, lhs_ref.at[0]),
+        (att_ref.at[:, pl.ds(ahead, 2 * kv_w + query_w)], w_v),
+    )
+    loads = [pltpu.make_async_copy(src, dst, in_sem.at[k]) for k, (src, dst) in enumerate(plan)]
 
     def right_load(i, what):
         cols = pl.ds(pl.multiple_of((i % n_f) * wide, 128), wide)
@@ -762,7 +808,8 @@
 
     lefts[0].start()
     right_load(jnp.int32(0), "start")
-    lefts[1].start()
+    for copy in loads[:-1]:
+        copy.start()
 
     def chunk_rows(j):
         return part_ref.at[pl.ds(pl.multiple_of(j * chunk, chunk), chunk), :]
@@ -792,8 +839,9 @@
         sum_copies.append(
             z_copy(chunk_rows(to), sum_land.at[k], sum_send.at[k], sum_recv.at[k], to)
         )
-    for copy in small_copies + sum_copies:
+    for copy in sum_copies:
         copy.start()
+    rhs_ref[:, 2 * query_w + 2 * kv_w :] = jnp.zeros((chunk, rhs_ref.shape[1] - 2 * query_w - 2 * kv_w), bf16)
 
     hops = (mate, by_x, by_y)
 
@@ -810,18 +858,18 @@
         s = core_sum.at[i % 4]
         first, last = pl.ds(0, half), pl.ds(half, half)
         plan = (
-            (s.at[at_x, first, :], x_land.at[i, 0], by_x), (s.at[cross, first, :], x_land.at[i, 1], by_x),
-            (s.at[at_y, last, :], y_land.at[i, 0], by_y), (s.at[cross, last, :], y_land.at[i, 1], by_y),
+            (s.at[at_x, first, :], x_land.at[i % ring, 0], by_x), (s.at[cross, first, :], x_land.at[i % ring, 1], by_x),
+            (s.at[at_y, last, :], y_land.at[i % ring, 0], by_y), (s.at[cross, last, :], y_land.at[i % ring, 1], by_y),
         )
         return [
-            dp_copy(src, dst, one_send.at[k, i], one_recv.at[k, i], peer)
+            dp_copy(src, dst, one_send.at[k, i % ring], one_recv.at[k, i % ring], peer)
             for k, (src, dst, peer) in enumerate(plan)
         ]
 
     def two_copies(i):
         return [
-            dp_copy(second.at[i % 4, 0], y_last.at[i], two_send.at[0, i], two_recv.at[0, i], by_y),
-            dp_copy(second.at[i % 4, 1], x_last.at[i], two_send.at[1, i], two_recv.at[1, i], by_x),
+            dp_copy(second.at[i % 4, 0], y_last.at[i % ring], two_send.at[0, i % ring], two_recv.at[0, i % ring], by_y),
+            dp_copy(second.at[i % 4, 1], x_last.at[i % ring], two_send.at[1, i % ring], two_recv.at[1, i % ring], by_x),
         ]
 
     def stage_copy(i):
@@ -847,6 +895,7 @@
 
             @pl.when(i == n_f)
             def _():
+                lefts[1].start()
                 lefts[1].wait()
 
             right_load(i, "wait")
@@ -854,7 +903,7 @@
             def rows(k, carry):
                 at = pl.ds(pl.multiple_of(k * 2 * block, 128), 2 * block)
                 value = lax.dot_general(
-                    left_v[(i // n_f + 1) // 2, :, at], right_v[i % 2], dims, preferred_element_type=f32
+                    left_v[:, at], right_v[i % 2], dims, preferred_element_type=f32
                 )
                 grad[i % 2, k] = value.astype(bf16).reshape(2, block, wide)
                 return carry
@@ -893,8 +942,8 @@
         for copy in one_copies(i):
             copy.wait_recv()
         s = core_sum.at[i % 4]
-        second[i % 4, 0] = (s[at_y, :half].astype(f32) + x_land[i, 1].astype(f32)).astype(bf16)
-        second[i % 4, 1] = (s[at_x, half:].astype(f32) + y_land[i, 1].astype(f32)).astype(bf16)
+        second[i % 4, 0] = (s[at_y, :half].astype(f32) + x_land[i % ring, 1].astype(f32)).astype(bf16)
+        second[i % 4, 1] = (s[at_x, half:].astype(f32) + y_land[i % ring, 1].astype(f32)).astype(bf16)
         for copy in two_copies(i):
             copy.start()
 
@@ -925,8 +974,8 @@
         for copy in two_copies(i):
             copy.wait_recv()
         own = core_sum.at[i % 4, here]
-        top = own[:half].astype(f32) + x_land[i, 0].astype(f32) + y_last[i].astype(f32)
-        low = own[half:].astype(f32) + y_land[i, 0].astype(f32) + x_last[i].astype(f32)
+        top = own[:half].astype(f32) + x_land[i % ring, 0].astype(f32) + y_last[i % ring].astype(f32)
+        low = own[half:].astype(f32) + y_land[i % ring, 0].astype(f32) + x_last[i % ring].astype(f32)
 
         @pl.when(i < n_ffn)
         def _():
@@ -948,26 +997,183 @@
         for copy in one_copies(i) + two_copies(i):
             copy.wait_send()
 
+    def back_norm(upstream, value, gain, base, col):
+        inverse = lax.rsqrt(jnp.mean(value * value, axis=-1, keepdims=True) + EPSILON)
+        unit = value * inverse
+        scaled = upstream * gain
+        term = jnp.sum(upstream * unit, axis=0, keepdims=True)
+        small_ref[:, pl.ds(col, width)] += jnp.broadcast_to(term, (8, width))
+        return base + inverse * (scaled - unit * jnp.mean(scaled * unit, axis=-1, keepdims=True))
+
+    some_rows = max(16, chunk // 4)
+
+    def by_rows(work):
+        def some(r, carry):
+            work(pl.ds(pl.multiple_of(r * some_rows, some_rows), some_rows))
+            return carry
+
+        lax.fori_loop(0, chunk // some_rows, some, 0)
+
+    gain_one_at, gain_two_at = query_w + 2 * kv_w, query_w + 2 * kv_w + width
+
+    def open_branch():
+        for k in (0, 1, 2, 3):
+            loads[k].wait()
+        small_ref[...] = jnp.zeros_like(small_ref)
+
+        def work(at):
+            value = back_norm(
+                up_v[at, :].astype(f32), mid_v[at, :], gain_v[1:2, :], own_v[at, :].astype(f32), gain_two_at
+            )
+            d_mid[at, :] = value
+            lhs_ref[1, at, :] = value.astype(bf16)
+
+        by_rows(work)
+
+    def context_grads():
+        loads[4].wait()
+        tile = min(512, query_w)
+
+        def some(n, carry):
+            cols = pl.ds(pl.multiple_of(n * tile, tile), tile)
+            d_ctx[:, cols] = jnp.dot(lhs_ref[1], w_v[:, cols], preferred_element_type=f32).astype(bf16)
+            return carry
+
+        lax.fori_loop(0, query_w // tile, some, 0)
+        loads[-1].start()
+        for k in (5, 6, 7, 8, 9):
+            loads[k].wait()
+        d_win[...] = jnp.zeros_like(d_win)
+
+    def turned_back(value):
+        return value * turn_v[0] - pltpu.roll(value, HEAD_DIM // 2, 1) * turn_v[1]
+
+    def attend_back(first, last):
+        def head(h, carry):
+            cols = pl.ds(pl.multiple_of(h * HEAD_DIM, 128), HEAD_DIM)
+            group = h // (heads // KV_HEADS)
+            key_cols = pl.ds(pl.multiple_of(group * HEAD_DIM, 128), HEAD_DIM)
+            value_cols = pl.ds(pl.multiple_of(kv_w + group * HEAD_DIM, 128), HEAD_DIM)
+            key = win_v[:, :, key_cols].reshape(3 * chunk, HEAD_DIM)
+            value = win_v[:, :, value_cols].reshape(3 * chunk, HEAD_DIM)
+            query, given = query_v[:, cols], d_ctx[:, cols]
+            across, down = (((1,), (1,)), ((), ())), (((0,), (0,)), ((), ()))
+            scores = lax.dot_general(query, key, across, preferred_element_type=f32)
+            probs = jnp.exp(scores * scale + mask_v[...] - lse_v[h])
+            d_probs = lax.dot_general(given, value, across, preferred_element_type=f32)
+            delta = jnp.sum(probs * d_probs, axis=-1, keepdims=True)
+            d_scores = (probs * (d_probs - delta)).astype(bf16)
+            d_query = jnp.dot(d_scores, key, preferred_element_type=f32) * scale
+            rhs_ref[:, cols] = turned_back(d_query).astype(bf16)
+            d_key = lax.dot_general(d_scores, query, down, preferred_element_type=f32) * scale
+            d_value = lax.dot_general(probs.astype(bf16), given, down, preferred_element_type=f32)
+            d_win[:, :, key_cols] += d_key.reshape(3, chunk, HEAD_DIM)
+            d_win[:, :, value_cols] += d_value.reshape(3, chunk, HEAD_DIM)
+            return carry
+
+        lax.fori_loop(first, last, head, 0)
+
+    def give_copy(hop):
+        return z_copy(
+            kv_give.at[hop - 1], kv_take.at[hop - 1], give_send.at[hop - 1], give_recv.at[hop - 1], z - hop
+        )
+
+    def give():
+        for hop in (1, 2):
+
+            @pl.when(z >= hop)
+            def _(hop=hop):
+                kv_give[hop - 1] = d_win[2 - hop].astype(bf16)
+                give_copy(hop).start()
+
+    def take():
+        for hop in (1, 2):
+
+            @pl.when(z + hop < size)
+            def _(hop=hop):
+                pltpu.make_async_copy(kv_take.at[hop - 1], kv_take.at[hop - 1], give_recv.at[hop - 1]).wait()
+                d_win[2] += kv_take[hop - 1].astype(f32)
+
+        for g in range(KV_HEADS):
+            cols = slice(g * HEAD_DIM, (g + 1) * HEAD_DIM)
+            out_cols = slice(2 * query_w + g * HEAD_DIM, 2 * query_w + (g + 1) * HEAD_DIM)
+            rhs_ref[:, out_cols] = turned_back(d_win[2, :, cols]).astype(bf16)
+        rhs_ref[:, 2 * query_w + kv_w : 2 * query_w + 2 * kv_w] = d_win[2, :, kv_w:].astype(bf16)
+        ones = jnp.ones((8, chunk), bf16)
+        small_ref[:, :query_w] = jnp.dot(ones, rhs_ref[:, :query_w], preferred_element_type=f32)
+        small_ref[:, query_w : query_w + 2 * kv_w] = jnp.dot(
+            ones, rhs_ref[:, 2 * query_w : 2 * query_w + 2 * kv_w], preferred_element_type=f32
+        )
+
+    def one_grads():
+        loads[-1].wait()
+        tile = min(512, width)
+        across = (((1,), (1,)), ((), ()))
+
+        def some(n, carry):
+            at_n = pl.ds(pl.multiple_of(n * tile, tile), tile)
+            d_one[:, at_n] = lax.dot_general(
+                rhs_ref[:, :query_w], w_v[at_n, 2 * kv_w :], across, preferred_element_type=f32
+            ) + lax.dot_general(
+                rhs_ref[:, 2 * query_w : 2 * query_w + 2 * kv_w], w_v[at_n, : 2 * kv_w], across,
+                preferred_element_type=f32,
+            )
+            return carry
+
+        lax.fori_loop(0, width // tile, some, 0)
+
+    def close_branch():
+        loads[11].wait()
+
+        def work(at):
+            input_out[at, :] = back_norm(
+                d_one[at, :], x_v[at, :].astype(f32), gain_v[0:1, :], d_mid[at, :], gain_one_at
+            ).astype(bf16)
+
+        by_rows(work)
+        for copy in small_copies:
+            copy.start()
+
+    def small_first():
+        for copy in small_copies:
+            copy.wait_recv()
+        small_next[0] = small_ref[...] + small_z[0] + small_z[1] + small_z[2]
+        hop_copy(0).start()
+
+    def small_then(k):
+        hop_copy(k).wait_recv()
+        small_next[k + 1] = small_next[k] + small_hop[k]
+        hop_copy(k + 1).start()
+
+    def small_last():
+        hop_copy(2).wait_recv()
+        small_out[...] = small_next[2] + small_hop[2]
+
+    span = n_ffn - 1
+    quarter = heads // 4
+
+    def at_turn(k):
+        return min(k, span)
+
+    steps = [
+        (0, open_branch), (at_turn(1), context_grads),
+        (at_turn(2), lambda: attend_back(0, quarter)),
+        (at_turn(3), lambda: attend_back(quarter, 2 * quarter)),
+        (at_turn(4), lambda: attend_back(2 * quarter, 3 * quarter)),
+        (at_turn(5), lambda: attend_back(3 * quarter, heads)),
+        (at_turn(5), give),
+        (at_turn(7), take), (at_turn(7), lambda: [loads[k].wait() for k in (10, 12)]),
+        (n_ffn + 1, one_grads), (n_ffn + 2, close_branch),
+        (n_ffn + 4, small_first), (n_ffn + 5, lambda: small_then(0)), (n_ffn + 6, lambda: small_then(1)),
+        (n_ffn + 7, small_last),
+    ]
+
     def small_step(i):
-        @pl.when(i == 2)
-        def _():
-            for copy in small_copies:
-                copy.wait_recv()
-            small_next[0] = small_ref[...] + small_z[0] + small_z[1] + small_z[2]
-            hop_copy(0).start()
-
-        for k in range(2):
-
-            @pl.when(i == 3 + k)
-            def _(k=k):
-                hop_copy(k).wait_recv()
-                small_next[k + 1] = small_next[k] + small_hop[k]
-                hop_copy(k + 1).start()
-
-        @pl.when(i == 5)
-        def _():
-            hop_copy(2).wait_recv()
-            small_out[...] = small_next[2] + small_hop[2]
+        for when, step in steps:
+
+            @pl.when(i == when)
+            def _(step=step):
+                step()
 
     def turn(i, carry):
         multiply(i)
@@ -991,7 +1197,7 @@
     acc = sum_land[size - 1].astype(f32)
     for k in range(size - 1):
         acc += sum_land[k].astype(f32)
-    sum_out[...] = acc.astype(bf16)
+    mixed_out[...] = (mid_v[...] + acc).astype(bf16)
     for of, dst in ((0, query_out), (1, out_out)):
         for k in range(size - 1):
             ref = z_land.at[of, k]
@@ -1018,41 +1224,59 @@
         copy.wait_send()
     for k in range(3):
         hop_copy(k).wait_send()
-
-
-def back(two, cot_rows, hid, dg, du, lhs, rhs, ffn_part, small, wide=768, collective_id=3, limit=67_000_000):
+    for hop in (1, 2):
+
+        @pl.when(z >= hop)
+        def _(hop=hop):
+            give_copy(hop).wait_send()
+
+
+def back(
+    two, cot_rows, hid, dg, du, ffn_part, up, tokens, middle, gains, att_w, query_rot, kv_win, lse, context,
+    normed_one, mask, turn, wide=768, collective_id=3, limit=67_000_000,
+):
     length, width = two.shape
-    size, chunk, block = 4, lhs.shape[1], width // 8
-    units = hid.shape[1]
-    n_f, n_att = units // wide, rhs.shape[1] // wide
-    n_ffn = 3 * n_f
-    total = n_ffn + n_att
+    size, chunk, block = 4, tokens.shape[0], width // 8
+    units, query_w, kv_w = hid.shape[1], context.shape[1], kv_win.shape[2]
+    n_f, n_att = units // wide, (2 * query_w + wide) // wide
+    total = 3 * n_f + n_att
     half, part_w, share = block // 2, wide // 2, block // size
+    heads = lse.shape[0]
     bf16, f32 = jnp.bfloat16, jnp.float32
+    small = (8, query_w + kv_w + 2 * width)
+    ring = 5
     hbm = pl.BlockSpec(memory_space=pl.ANY)
     vmem = pl.BlockSpec(memory_space=pltpu.VMEM)
     vm = pltpu.VMEM
     dma = pltpu.SemaphoreType.DMA
     shape = jax.ShapeDtypeStruct
     return pl.pallas_call(
-        functools.partial(back_body, n_f=n_f, wide=wide, cols_out=3 * units),
+        functools.partial(back_body, n_f=n_f, wide=wide),
         out_shape=(
             shape((block, 3 * units), f32), shape((block, part_w), f32), shape((block, part_w), f32),
-            shape((share, wide), f32), shape((chunk, width), bf16), shape(small.shape, f32),
+            shape((share, wide), f32), shape((chunk, width), bf16), shape((chunk, width), bf16),
+            shape(small, f32),
         ),
-        in_specs=[hbm] * 5 + [vmem, vmem, hbm, vmem],
-        out_specs=(hbm,) + (vmem,) * 5,
+        in_specs=[hbm] * 18,
+        out_specs=(hbm,) + (vmem,) * 6,
         scratch_shapes=[
-            vm((2, length, width), bf16), vm((2, length, wide), bf16), vm((2, 4, 2, block, wide), bf16),
+            vm((chunk, width), bf16), vm((chunk, width), bf16), vm((chunk, width), bf16),
+            vm((chunk, width), f32), vm(gains.shape, f32), vm((width, kv_w + query_w), bf16),
+            vm((chunk, query_w), bf16), vm(kv_win.shape, bf16), vm((heads, chunk, 1), f32),
+            vm(mask.shape, f32), vm(turn.shape, f32), vm((2, chunk, width), bf16),
+            vm((chunk, 2 * query_w + wide), bf16), vm((chunk, width), f32), vm((chunk, query_w), bf16),
+            vm(kv_win.shape, f32), vm((2, chunk, kv_w), bf16), vm((2, chunk, kv_w), bf16),
+            vm((chunk, width), f32), vm(small, f32),
+            vm((length, width), bf16), vm((2, length, wide), bf16), vm((2, 4, 2, block, wide), bf16),
             vm((4, 4, block, wide), bf16), vm((4, 4, block, wide), bf16),
-            vm((total, 2, half, wide), bf16), vm((total, 2, half, wide), bf16),
-            vm((4, 2, half, wide), bf16), vm((total, half, wide), bf16), vm((total, half, wide), bf16),
+            vm((ring, 2, half, wide), bf16), vm((ring, 2, half, wide), bf16),
+            vm((4, 2, half, wide), bf16), vm((ring, half, wide), bf16), vm((ring, half, wide), bf16),
             vm((2, block, wide), f32), vm((n_att, block, wide), bf16),
             vm((2, size - 1, block, part_w), bf16), vm((size - 1, share, wide), bf16),
-            vm((size, chunk, width), bf16), vm((3,) + small.shape, f32), vm((3,) + small.shape, f32),
-            vm((3,) + small.shape, f32),
-            dma((2,)), dma((2,)), dma((4,)), dma((4,)), dma((4, total)), dma((4, total)),
-            dma((2, total)), dma((2, total)), dma((2,)),
+            vm((size, chunk, width), bf16), vm((3,) + small, f32), vm((3,) + small, f32),
+            vm((3,) + small, f32), dma((14,)), dma((2,)), dma((2,)),
+            dma((2,)), dma((2,)), dma((4,)), dma((4,)), dma((4, ring)), dma((4, ring)),
+            dma((2, ring)), dma((2, ring)), dma((2,)),
             dma((4, 2)), dma((2, size - 1)), dma((size - 1,)), dma((size - 1,)), dma((size - 1,)),
             dma((size - 1,)), dma((1,)), dma((size - 1,)), dma((size - 1,)), dma((3,)), dma((3,)),
         ],
@@ -1063,7 +1287,10 @@
             flops=6 * length * width * units, bytes_accessed=8 * length * units, transcendentals=0
         ),
         name="back",
-    )(two, cot_rows, hid, dg, du, lhs, rhs, ffn_part, small)
+    )(
+        two, cot_rows, hid, dg, du, ffn_part, up, tokens, middle, gains, att_w, query_rot, kv_win, lse, context,
+        normed_one, mask, turn,
+    )
 
 
 def angle_tables(first, length, head_width):
@@ -1129,7 +1356,7 @@
             tokens, turn, mask, kv_b[None, :], tall_query, tall_out, fixed_w, ffn_w, cotangent
         )
         kv_win = kv_win.reshape(3 * rows, kv_w.shape[1])
-        return att_w, ffn_all, cot_rows, two, middle, one, query_rot, kv_win, lse, context, gains[:2]
+        return att_w, ffn_all, cot_rows, two, middle, one, query_rot, kv_win, lse, context, gains
     pair = lax.all_gather(jnp.stack([query_w, out_w]), "tensor", axis=2, tiled=True)
     att_w = jnp.concatenate([fixed_w, pair[0], pair[1]], axis=1)
     att_w = lax.all_gather(att_w, "dp", axis=0, tiled=True)
@@ -1182,19 +1409,8 @@
 
 def sum_grads(two, cot_rows, hid, dg, du, normed_one, d_attended, d_lin, context, ffn_part, small):
     f32, bf16 = jnp.float32, jnp.bfloat16
-    padded = hid.shape[1]
     fixed = d_lin.shape[1] - context.shape[1]
     d_query = d_lin[:, fixed:]
-    if lax.axis_size("dp") == 8 and lax.axis_size("tensor") == 4:
-        gap = context.shape[1] // 2 - fixed
-        rhs = jnp.concatenate([d_query, context, jnp.pad(d_lin[:, :fixed], ((0, 0), (0, gap)))], axis=1)
-        lhs = jnp.stack([normed_one, d_attended])
-        flat, query, out, kv, ffn_sum, total = back(
-            two, cot_rows, hid, dg, du, lhs, rhs, ffn_part, small.reshape(-1, 128)
-        )
-        flat = [flat[:, k * padded : (k + 1) * padded] for k in range(3)]
-        return (*flat, query, out, kv, ffn_sum, total.reshape(-1))
-
     def over_dp(left, right):
         return lax.psum_scatter(
             contract_rows(left, right).astype(bf16), "dp", scatter_dimension=0, tiled=True
@@ -1215,48 +1431,34 @@
     )
 
 
-def local(
-    tokens, segments, gain_one, query_w, query_b, key_w, key_b, value_w, value_b,
-    out_w, gain_two, gate_w, up_w, down_w, cotangent,
+def branch_back(
+    tokens, cosine, sine, mask, att_w, cot_rows, rows_two, hidden_low, d_gate, d_upper, ffn_part,
+    d_normed_two, cotangent, middle, normed_one, query_rot, kv_win, lse, context, gains,
 ):
-    bf16, f32 = jnp.bfloat16, jnp.float32
-    rows, model_width = tokens.shape
-    tensor_size = lax.axis_size("tensor")
-    rank = lax.axis_index("tensor")
-    kv_width = key_w.shape[1]
-    fixed_width = 2 * kv_width
-    query_width = query_w.shape[1] * tensor_size
-    qkv_width = fixed_width + query_width
-    heads = query_width // HEAD_DIM
+    f32, bf16 = jnp.float32, jnp.bfloat16
+    rows = tokens.shape[0]
+    kv_width, query_width = kv_win.shape[1] // 2, query_rot.shape[1]
+    qkv_width = 2 * kv_width + query_width
+    ahead = att_w.shape[1] - qkv_width - query_width
+    heads, padded = query_width // HEAD_DIM, hidden_low.shape[1]
+    if lax.axis_size("dp") == 8 and lax.axis_size("tensor") == 4:
+        turn = jnp.stack(
+            [jnp.concatenate([cosine, cosine], axis=1), jnp.concatenate([-sine, sine], axis=1)]
+        )
+        flat, sum_query, sum_out, sum_kv, mixed, input_grad, small = back(
+            rows_two, cot_rows, hidden_low, d_gate, d_upper, ffn_part, d_normed_two, tokens, middle, gains,
+            att_w, query_rot, kv_win.reshape(-1, rows, 2 * kv_width), lse, context, normed_one, mask, turn,
+        )
+        flat = [flat[:, k * padded : (k + 1) * padded] for k in range(3)]
+        return mixed, input_grad, *flat, sum_query, sum_out, sum_kv, small[0]
     group = heads // KV_HEADS
+    window = kv_win.shape[0]
+    back_chunks = window // rows - 1
     scale = HEAD_DIM ** (-0.5)
-    units = gate_w.shape[1]
-    back_chunks = min(tensor_size - 1, -(-DOC_MAX // rows))
-    window = (back_chunks + 1) * rows
-    cosine, sine = angle_tables(rank * rows, rows, HEAD_DIM)
     cos_h, sin_h = cosine[:, None, :], sine[:, None, :]
-    segment = segments[0]
-    own_segment = lax.dynamic_slice_in_dim(segment, rank * rows, rows, 0)
-    before = jnp.full((back_chunks * rows,), -1, segment.dtype)
-    win_segment = lax.dynamic_slice_in_dim(jnp.concatenate([before, segment]), rank * rows, window, 0)
-    own_pos = back_chunks * rows + jnp.arange(rows)
-    win_pos = jnp.arange(window)
-    allowed = (own_segment[:, None] == win_segment[None, :]) & (win_pos[None, :] <= own_pos[:, None])
-    mask = jnp.where(allowed, 0.0, NEGATIVE).astype(f32)
-    ahead = 128
-    gains_w = jnp.pad(jnp.stack([gain_one, gain_two], axis=1), ((0, 0), (0, ahead - 2)))
-    (
-        att_w, ffn_w, cot_rows, normed_two, middle, normed_one, query_rot, kv_win, lse, context, gains,
-    ) = attention_branch(
-        tokens, cosine, sine, mask, gains_w, query_w, query_b, jnp.concatenate([key_w, value_w], axis=1),
-        jnp.concatenate([key_b, value_b]).astype(f32), out_w, joined_units(gate_w, up_w, down_w), cotangent,
-    )
+    d_normed_two = d_normed_two.astype(f32)
     qkv_w = att_w[:, ahead : ahead + qkv_width]
     out_full = att_w[:, ahead + qkv_width :]
-    rows_two, hidden_low, d_gate, d_upper, ffn_part, d_normed_two = ffn(
-        normed_two, cot_rows, ffn_w
-    )
-    d_normed_two = d_normed_two.astype(f32)
     inputs = tokens.astype(f32)
     inverse_one = lax.rsqrt(jnp.mean(inputs * inputs, axis=-1, keepdims=True) + EPSILON)
     unit_one = inputs * inverse_one
@@ -1302,10 +1504,52 @@
 
     sums = sum_grads(
         rows_two, cot_rows, hidden_low, d_gate, d_upper, normed_one, d_attended, d_lin, context,
-        ffn_part, jnp.concatenate([bias_term, gain_one_term, gain_two_term]),
+        ffn_part, jnp.concatenate([bias_term[2 * kv_width :], bias_term[: 2 * kv_width], gain_one_term, gain_two_term]),
     )
     sum_down, sum_gate, sum_up, sum_query, sum_out, sum_kv, ffn_sum, small = sums
     mixed = (middle + ffn_sum.astype(f32)).astype(bf16)
+    return mixed, input_grad, sum_down, sum_gate, sum_up, sum_query, sum_out, sum_kv, small
+
+
+def local(
+    tokens, segments, gain_one, query_w, query_b, key_w, key_b, value_w, value_b,
+    out_w, gain_two, gate_w, up_w, down_w, cotangent,
+):
+    bf16, f32 = jnp.bfloat16, jnp.float32
+    rows, model_width = tokens.shape
+    tensor_size = lax.axis_size("tensor")
+    rank = lax.axis_index("tensor")
+    kv_width = key_w.shape[1]
+    fixed_width = 2 * kv_width
+    query_width = query_w.shape[1] * tensor_size
+    qkv_width = fixed_width + query_width
+    units = gate_w.shape[1]
+    back_chunks = min(tensor_size - 1, -(-DOC_MAX // rows))
+    window = (back_chunks + 1) * rows
+    cosine, sine = angle_tables(rank * rows, rows, HEAD_DIM)
+    segment = segments[0]
+    own_segment = lax.dynamic_slice_in_dim(segment, rank * rows, rows, 0)
+    before = jnp.full((back_chunks * rows,), -1, segment.dtype)
+    win_segment = lax.dynamic_slice_in_dim(jnp.concatenate([before, segment]), rank * rows, window, 0)
+    own_pos = back_chunks * rows + jnp.arange(rows)
+    win_pos = jnp.arange(window)
+    allowed = (own_segment[:, None] == win_segment[None, :]) & (win_pos[None, :] <= own_pos[:, None])
+    mask = jnp.where(allowed, 0.0, NEGATIVE).astype(f32)
+    ahead = 128
+    gains_w = jnp.pad(jnp.stack([gain_one, gain_two], axis=1), ((0, 0), (0, ahead - 2)))
+    (
+        att_w, ffn_w, cot_rows, normed_two, middle, normed_one, query_rot, kv_win, lse, context, gains,
+    ) = attention_branch(
+        tokens, cosine, sine, mask, gains_w, query_w, query_b, jnp.concatenate([key_w, value_w], axis=1),
+        jnp.concatenate([key_b, value_b]).astype(f32), out_w, joined_units(gate_w, up_w, down_w), cotangent,
+    )
+    rows_two, hidden_low, d_gate, d_upper, ffn_part, d_normed_two = ffn(
+        normed_two, cot_rows, ffn_w
+    )
+    mixed, input_grad, sum_down, sum_gate, sum_up, sum_query, sum_out, sum_kv, small = branch_back(
+        tokens, cosine, sine, mask, att_w, cot_rows, rows_two, hidden_low, d_gate, d_upper, ffn_part,
+        d_normed_two, cotangent, middle, normed_one, query_rot, kv_win, lse, context, gains,
+    )
     place = lax.axis_index("dp") * tensor_size + rank
     devices = lax.axis_size("dp") * tensor_size
 
@@ -1318,11 +1562,11 @@
         input_grad,
         own(qkv_width, model_width),
         sum_query,
-        own(fixed_width, query_width),
+        own(0, query_width),
         sum_kv[:, :kv_width],
-        small[:kv_width],
+        small[query_width : query_width + kv_width],
         sum_kv[:, kv_width : 2 * kv_width],
-        small[kv_width:fixed_width],
+        small[query_width + kv_width : qkv_width],
         sum_out,
         own(qkv_width + model_width, model_width),
         sum_gate[:, :units],

time: 577 us -> 469 us (0.81)
  matrix products: 30.5 us -> 0 us
  other arithmetic: 36.8 us -> 7.25 us
  Pallas kernels: 468 us -> 444 us
  local copies, waits for them, and re-layouts: 30.4 us -> 14.2 us
  starting transfers between devices: 7.4 us -> 0 us
    dot_general x7 -> x0, matrix products: 30.5 us -> none  [the longest x1 7.49 us: local(): jnp.einsum('tagd,sad->agts', d_context, value_win, preferred_element_type...]
    pallas_call x1, Pallas kernels: 180 us -> 159 us  [front(): pl.pallas_call(functools.partial(front_body, pieces=pieces, order=order,...]
    convert_element_type x3 -> x0, other arithmetic: 15.1 us -> none  [the longest x1 11.1 us: local(): d_scores = (probs * (d_probs - row_delta)).astype(bf16)]
    ppermute x2 -> x0, starting transfers between devices: 7.4 us -> none  [shift(): return lax.ppermute(value, 'tensor', pairs)]
    another operation x4 -> x0, other arithmetic: 5.85 us -> none  [the longest x2 5.16 us: sum_grads(): lhs = jnp.stack([normed_one, d_attended])]
  transfers between devices with their start and end apart: 2 -> 0, of which waited for: 0 -> 0; matrix products, arithmetic and copies ran while one was open for 1% -> 0% of each run, Pallas kernels for 0% -> 0%
where the time goes in v6:
time: 469 us; the launch traced here: 467 us
  Pallas kernels  444 us (95%)
  local copies, waits for them, and re-layouts  14.2 us (3%)
  other arithmetic  7.25 us (2%)
    pallas_call x1, Pallas kernels, back(): pl.pallas_call(functools.partial(back_body, n_f=n_f, wide=wide), out_shap...  177 us
    pallas_call x1, Pallas kernels, front(): pl.pallas_call(functools.partial(front_body, pieces=pieces, order=order,...  159 us
    pallas_call x1, Pallas kernels, ffn(): pl.pallas_call(functools.partial(ffn_body, axis=axis, ft=ft, nt=nt), out_...  109 us

profile of v6, /device:TPU:26, one launch (start us, length us, event | category | flops | bytes accessed | tf_op | source)
XLA Modules:
  0.0 466.5 jit_solution(1070373495607334089)
XLA Ops:
  0.6 0.0 copy-start.1
  0.7 0.0 copy-start
  0.7 0.5 multiply_cosine_fusion
  1.2 0.1 maximum_bitcast_fusion
  1.4 0.7 pad_maximum_fusion.turn_ref
  2.1 0.8 pad_dynamic-slice_fusion
  2.9 0.7 constant_dynamic-slice_fusion.3
  3.5 1.1 fusion.7.mask_ref
  4.6 0.0 copy-done.1
  4.6 0.0 copy-done
  4.7 0.0 copy-start.8
  4.7 0.0 copy-start.9
  4.7 0.0 copy-start.11
  4.7 0.0 copy-start.6
  4.7 0.0 copy-start.7
  4.7 0.0 copy-start.14
  4.7 0.0 copy-start.15
  4.7 2.7 fusion.5.ffn_ref
  7.5 0.0 copy-done.12
  7.5 0.0 copy-done.13
  7.5 0.1 copy.31
  7.7 0.0 copy-done.8
  7.7 0.0 copy-done.9
  7.7 0.7 fusion.11.fixed_ref
  8.4 0.0 copy-done.11
  8.4 0.0 copy-done.6
  8.4 0.7 fusion.12.query_ref
  9.1 0.0 copy-done.7
  9.1 0.7 pad.24.out_ref
  9.8 0.0 copy-done.14
  9.8 0.0 copy-done.15
  9.8 0.6 maximum_convert_fusion.bias_ref
  10.4 158.6 %front.1 = (bf16[1536,3712]{1,0:T(8,128)(2,1)}, bf16[1536,6912]{1,0:T(8,128)(2,1)}, bf16[1024,1536]{1,0:T(8,128)(2,1)}, bf16[256,1536]{1,0:T(8,128)(2,1)}, f32[2...) custom-call(bf16[256,1536]{1,0:T(8,128)(2,1)} %x_ref.3, ...), custom_call_target="tpu_custom_call" | custom-call | flops 2919235584 | bytes 40796160 | tf_op jit(solution)/shard_map/front/pallas_call | solution.py:419
  169.1 109.0 %ffn.1 = (bf16[1024,1536]{1,0:T(8,128)(2,1)}, bf16[1024,2304]{1,0:T(8,128)(2,1)}, bf16[1024,2304]{1,0:T(8,128)(2,1)}, bf16[1024,2304]{1,0:T(8,128)(2,1)}, bf16[1...) custom-call(bf16[256,1536]{1,0:T(8,128)(2,1)} %get-tuple-element.38.two_ref, ...), custom_call_target="tpu_custom_call" | custom-call | flops 43486543872 | bytes 47185920 | tf_op jit(solution)/shard_map/ffn/pallas_call | solution.py:717
  278.0 176.6 %back.1 = (f32[192,6912]{1,0:T(8,128)}, f32[192,384]{1,0:T(8,128)}, f32[192,384]{1,0:T(8,128)}, f32[48,768]{1,0:T(8,128)}, bf16[256,1536]{1,0:T(8,128)(2,1)}, /*...) custom-call(bf16[1024,1536]{1,0:T(8,128)(2,1)} %get-tuple-element.41.two_ref, bf16[1024,1536]{1,0:T(8,128)(2,1)} %get-tuple-element.39.cot_ref, ...), custom_call_target="tpu_custom_call" | custom-call | flops 21743271936 | bytes 18874368 | tf_op jit(solution)/shard_map/back/pallas_call | solution.py:1253
  454.7 0.0 copy-start.10
  454.7 0.0 copy-start.3
  454.7 0.0 copy-start.2
  454.7 5.2 %fusion.17 = (f32[192,2240]{1,0:T(8,128)}, f32[192,2240]{1,0:T(8,128)}, f32[192,2240]{1,0:T(8,128)}) fusion(f32[192,6912]{1,0:T(8,128)} %get-tuple-element.61), kind=kLoop, calls=%fused_computation.39 | loop fusion | bytes 10321920 | tf_op jit(solution)/shard_map/slice | solution.py:1574
  459.8 0.6 fusion.19
  460.5 0.9 slice.38
  461.4 0.6 fusion.16
  462.0 1.3 fusion.18
  463.3 0.9 copy.36
  464.2 0.0 copy-done.2
  464.2 0.9 copy.37
  465.1 0.7 copy.38
  465.8 0.7 copy.39
  (17 shorter events, 0.1 us)
Async XLA Ops:
  0.6 4.0 copy-start.1
  0.7 4.0 copy-start
  4.6 2.8 copy-start.12
  4.6 2.8 copy-start.13
  4.7 3.0 copy-start.8
  4.7 3.0 copy-start.9
  4.7 3.7 copy-start.11
  4.7 3.7 copy-start.6
  4.7 4.4 copy-start.7
  4.7 5.1 %copy-start.14 = (bf16[256]{0:T(256)(128)(2,1)S(1)}, bf16[256]{0:T(256)(128)(2,1)}, u32[]{:S(2)}) copy-start(bf16[256]{0:T(256)(128)(2,1)} %param.21) | copy-start | bytes 1540
  4.7 5.1 %copy-start.15 = (bf16[256]{0:T(256)(128)(2,1)S(1)}, bf16[256]{0:T(256)(128)(2,1)}, u32[]{:S(2)}) copy-start(bf16[256]{0:T(256)(128)(2,1)} %param.23) | copy-start | bytes 1540
  454.7 5.2 %copy-start.10 = (f32[48,768]{1,0:T(8,128)S(1)}, f32[48,768]{1,0:T(8,128)}, u32[]{:S(2)}) copy-start(f32[48,768]{1,0:T(8,128)} %get-tuple-element.59) | copy-start | bytes 442372
  454.7 8.6 %copy-start.3 = (bf16[256,1536]{1,0:T(8,128)(2,1)S(1)}, bf16[256,1536]{1,0:T(8,128)(2,1)}, u32[]{:S(2)}) copy-start(bf16[256,1536]{1,0:T(8,128)(2,1)} %get-tuple-element.91) | copy-start | bytes 2359300
  454.7 9.5 %copy-start.2 = (bf16[256,1536]{1,0:T(8,128)(2,1)S(1)}, bf16[256,1536]{1,0:T(8,128)(2,1)}, u32[]{:S(2)}) copy-start(bf16[256,1536]{1,0:T(8,128)(2,1)} %get-tuple-element.92) | copy-start | bytes 2359300
  459.8 5.2 %copy-start.5 = (f32[192,384]{1,0:T(8,128)S(1)}, f32[192,384]{1,0:T(8,128)}, u32[]{:S(2)}) copy-start(f32[192,384]{1,0:T(8,128)} %get-tuple-element.94) | copy-start | bytes 884740
  459.8 6.0 %copy-start.4 = (f32[192,384]{1,0:T(8,128)S(1)}, f32[192,384]{1,0:T(8,128)}, u32[]{:S(2)}) copy-start(f32[192,384]{1,0:T(8,128)} %get-tuple-element.100) | copy-start | bytes 884740

commit v7 on v6

--- a/solution.py
+++ b/solution.py
@@ -24,9 +24,10 @@
 
 def front_body(
     x_ref, turn_ref, mask_ref, bias_ref, query_ref, out_ref, fixed_ref, ffn_ref, cot_ref,
-    att_all, ffn_all, cot_all, two_out, mid_out, one_out, query_rot, kv_win, lse_out, ctx_out, gain_out,
+    att_all, ffn_all, cot_all, two_all, mid_out, one_out, query_rot, kv_win, lse_out, ctx_out, gain_out,
     att_v, w_v, one_v, q_v, kv_v, ctx_v, mid_v, two_v,
     fill_sem, z_send, z_recv, cot_send, cot_recv, send, recv, keep_sem, w_sem, kv_send, kv_recv, save_sem,
+    two_send, two_recv,
     *, pieces, order, lead,
 ):
     f32, bf16 = jnp.float32, jnp.bfloat16
@@ -98,6 +99,35 @@
             @pl.when(jnp.logical_and(inside, onward))
             def _(j=j, sign=sign):
                 cot_copy(j, -sign).start()
+
+    def two_copy(j, dz, own):
+        ref = two_all.at[pl.ds(pl.multiple_of(j * chunk, chunk), chunk), :]
+        return pltpu.make_async_remote_copy(
+            src_ref=two_v if own else ref, dst_ref=ref, send_sem=two_send.at[(dz + 1) // 2, j],
+            recv_sem=two_recv.at[j], device_id={"tensor": z + dz}, device_id_type=MESH,
+        )
+
+    def two_start():
+        for dz, there in ((-1, has_low), (1, has_high)):
+
+            @pl.when(there)
+            def _(dz=dz):
+                two_copy(z, dz, True).start()
+
+    def two_step(hop):
+        for sign, onward in ((-1, has_high), (1, has_low)):
+            j = z + sign * hop
+            inside = (j >= 0) if sign == -1 else (j < size)
+
+            @pl.when(inside)
+            def _(j=j, sign=sign):
+                two_copy(j, -sign, False).wait_recv()
+
+            if hop == 1:
+
+                @pl.when(jnp.logical_and(inside, onward))
+                def _(j=j, sign=sign):
+                    two_copy(j, -sign, False).start()
 
     for of in range(2):
         for hop in range(1, size):
@@ -328,7 +358,8 @@
         lax.fori_loop(0, w_v.shape[0] // tile, some, 0)
         save(mid_v, mid_out)
         norm(lambda at_r: mid_v[at_r, :], 1, two_v)
-        save(two_v, two_out)
+        save(two_v, two_all.at[at, :])
+        two_start()
 
     n_att = len(pieces[0])
     n_qkv = 1 + (n_att - 1) // 2
@@ -341,19 +372,21 @@
         (last_q + 1, lambda: take(0, n_qkv)),
         (last_q + 2, lambda: held(0, n_qkv)),
         (last_q + 2, keys),
-        (last_q + 3, queries),
+        (last_q + 2, queries),
+        (last_q + 3, kv_wait),
+        (last_q + 3, lambda: attend(0, third)),
         (last_out + 1, lambda: take(n_qkv, n_att)),
-        (last_out + 1, kv_wait),
-        (last_out + 1, lambda: attend(0, third)),
-        (last_out + 2, lambda: attend(third, 2 * third)),
-        (last_out + 3, lambda: attend(2 * third, heads)),
-        (last_out + 4, lambda: held(n_qkv, n_att)),
-        (last_out + 4, project),
-        (last_out + 5, lambda: cot_step(3)),
+        (last_out + 1, lambda: attend(third, 2 * third)),
+        (last_out + 2, lambda: cot_step(3)),
+        (last_out + 2, lambda: attend(2 * third, heads)),
+        (last_out + 3, lambda: held(n_qkv, n_att)),
+        (last_out + 3, project),
+        (last_out + 5, lambda: two_step(1)),
+        (last_out + 20, lambda: two_step(2)),
     ]
     total = len(order)
     for i in range(total + 1):
-        while state["begun"] < min(total, i + lead):
+        while state["begun"] < min(total, i + (lead if i <= last_q else 2 * lead)):
             ready(*order[state["begun"]])
             begin(*order[state["begun"]])
             state["begun"] += 1
@@ -386,6 +419,12 @@
             @pl.when(came)
             def _(j=j, dz=dz):
                 cot_copy(j, dz).wait_send()
+
+            near = jnp.logical_and(came, (j - z <= 1) if dz == -1 else (z - j <= 1))
+
+            @pl.when(near)
+            def _(j=j, dz=dz):
+                two_copy(j, dz, False).wait_send()
 
 
 def front(
@@ -421,7 +460,7 @@
         out_shape=(
             shape(8 * rows, att_cols), shape(8 * rows, ffn_w.shape[1]),
             shape(size * cot.shape[0], cot.shape[1]),
-            shape(chunk, width), wide(chunk, width), shape(chunk, width), shape(chunk, query_w),
+            shape(size * chunk, width), wide(chunk, width), shape(chunk, width), shape(chunk, query_w),
             shape(3, chunk, kv_w), wide(heads, chunk, 1), shape(chunk, query_w), wide(8, width),
         ),
         in_specs=[vmem] * 9,
@@ -432,7 +471,7 @@
             vm((chunk, width), f32), vm((chunk, width), bf16),
             dma((4,)), dma((2, size - 1)), dma((2, size - 1)),
             dma((2, size)), dma((size,)), dma((ways, slots)), dma((ways, slots)), dma((slots,)),
-            dma((n_att,)), dma((2,)), dma((2,)), dma((6,)),
+            dma((n_att,)), dma((2,)), dma((2,)), dma((6,)), dma((2, size)), dma((size,)),
         ],
         compiler_params=pltpu.CompilerParams(
             collective_id=collective_id, has_side_effects=True, vmem_limit_bytes=limit
@@ -448,8 +487,8 @@
 def line_order(z, s):
     upper = z // 2
     near = z * (1 - upper) + (3 - z) * upper
-    inner = (1 - s // 3) * ((s + 1) % 3) + (s // 3) * 3
-    at = (1 - near) * s + near * inner
+    late = s // 2
+    at = (1 - late) * (2 + s) + late * ((3 - s) * (1 - near) + (s - 2) * near)
     return at * (1 - upper) + (3 - at) * upper
 
 
@@ -457,12 +496,12 @@
     two_ref, cot_ref, weights_ref,
     rows_out, hid_out, dg_out, du_out, sum_out, dn_out,
     rows_v, cot_v, gate_v, up_v, down_v, hid_v, dg_v, du_v, part, land, below, above, res_v,
-    tile_sem, load_sem, ag_send, ag_recv, rs_send, rs_recv, own_recv, out_sem,
+    tile_sem, load_sem, row_sem, ag_send, ag_recv, rs_send, rs_recv, own_recv, out_sem,
     *, axis, ft, nt,
 ):
     f32, bf16 = jnp.float32, jnp.bfloat16
     size = 4
-    rows, width = two_ref.shape
+    rows, width = two_ref.shape[0] // size, two_ref.shape[1]
     units = weights_ref.shape[1] // 3
     n_f, n_n = units // ft, width // nt
     z = lax.axis_index(axis)
@@ -481,8 +520,23 @@
     def _():
         pl.semaphore_signal(barrier, inc=1, device_id=to(1), device_id_type=MESH)
 
-    own_load = pltpu.make_async_copy(two_ref, rows_v.at[z], load_sem.at[0])
-    own_load.start()
+    def chunk_rows(j):
+        return two_ref.at[pl.ds(pl.multiple_of(j * rows, rows), rows), :]
+
+    def far(j):
+        return jnp.logical_or(j - z == 3, z - j == 3)
+
+    def row_load(j):
+        return pltpu.make_async_copy(chunk_rows(j), rows_v.at[j], row_sem.at[j])
+
+    def load_rows(s):
+        j = line_order(z, s)
+
+        @pl.when(jnp.logical_not(far(j)))
+        def _():
+            row_load(j).start()
+
+    load_rows(0)
 
     def tile_loads(f):
         cols = pl.ds(pl.multiple_of(f * ft, 128), ft)
@@ -500,25 +554,23 @@
             copy.start()
         if f == 0:
             cot_load.start()
+            for s in range(1, size):
+                load_rows(s)
 
     pl.semaphore_wait(barrier, (z + size - 1) // size + (2 * size - 2 - z) // size)
 
-    own_load.wait()
-
-    def ag_copy(j, dz):
-        way = (dz + 1) // 2
+    def far_copy():
+        j = 3 - 3 * (z // 2)
         return pltpu.make_async_remote_copy(
-            src_ref=rows_v.at[j], dst_ref=rows_v.at[j], send_sem=ag_send.at[way, j],
-            recv_sem=ag_recv.at[j], device_id=to(dz), device_id_type=MESH,
-        )
-
-    @pl.when(has_low)
+            src_ref=chunk_rows(j), dst_ref=rows_v.at[j], send_sem=ag_send.at[0], recv_sem=ag_recv.at[0],
+            device_id=to(2 * (z // 2) - 1), device_id_type=MESH,
+        )
+
+    middle = jnp.logical_and(has_low, has_high)
+
+    @pl.when(middle)
     def _():
-        ag_copy(z, -1).start()
-
-    @pl.when(has_high)
-    def _():
-        ag_copy(z, 1).start()
+        far_copy().start()
 
     def rs_copy(j, n, dz, own):
         way = (dz + 1) // 2
@@ -553,22 +605,29 @@
             )
         ]
 
+    def forward(j, n):
+        pltpu.make_async_copy(land.at[j, n], land.at[j, n], rs_recv.at[j, n]).wait()
+        part[j, n] = (part[j, n].astype(f32) + land[j, n].astype(f32)).astype(bf16)
+        pass_on(j, n, "start")
+
+    def forward_all(j):
+        def some(n, carry):
+            forward(j, n)
+            return carry
+
+        lax.fori_loop(0, n_n, some, 0)
+
     def step(s, carry):
-        for sign in (-1, 1):
-            j = z + sign * s
-            inside = jnp.logical_and(s > 0, (j >= 0) if sign == -1 else (j < size))
-
-            @pl.when(inside)
-            def _(j=j, sign=sign):
-                ag_copy(j, -sign).wait_recv()
-
-            onward = has_high if sign == -1 else has_low
-
-            @pl.when(jnp.logical_and(inside, onward))
-            def _(j=j, sign=sign):
-                ag_copy(j, -sign).start()
-
         j = line_order(z, s)
+
+        @pl.when(far(j))
+        def _():
+            pltpu.make_async_copy(rows_v.at[j], rows_v.at[j], ag_recv.at[0]).wait()
+
+        @pl.when(jnp.logical_not(far(j)))
+        def _():
+            row_load(j).wait()
+
         at = pl.ds(pl.multiple_of(j * rows, rows), rows)
 
         @pl.when(s == 0)
@@ -596,7 +655,13 @@
         lax.fori_loop(0, n_f, units_tile, 0)
         for copy in out_copies(j):
             copy.start()
-        ends = jnp.logical_and(s > 0, jnp.logical_not(jnp.logical_and(has_low, has_high)))
+        ends = jnp.logical_and(s < 3, jnp.logical_not(middle))
+
+        @pl.when(jnp.logical_and(middle, s == 3))
+        def _():
+            forward_all(3 - z)
+            forward_all(3 - 3 * (z // 2))
+
 
         def width_tile(n, carry):
             at_n = pl.ds(pl.multiple_of(n * nt, nt), nt)
@@ -625,33 +690,17 @@
         res_v[j, :, at_n] = total.astype(bf16)
         return carry
 
-    def forward(j, n):
-        pltpu.make_async_copy(land.at[j, n], land.at[j, n], rs_recv.at[j, n]).wait()
-        part[j, n] = (part[j, n].astype(f32) + land[j, n].astype(f32)).astype(bf16)
-        pass_on(j, n, "start")
-
-    middle = jnp.logical_and(has_low, has_high)
-
-    @pl.when(middle)
-    def _():
-        def first(n, carry):
-            forward(3 - z, n)
-            return carry
-
-        lax.fori_loop(0, n_n, first, 0)
-
-    lax.fori_loop(0, (size * n_n) // 2, down_tile, 0)
-
-    @pl.when(middle)
-    def _():
-        def second(n, carry):
-            forward(3 - 3 * (z // 2), n)
+    tiles = size * n_n
+    done = tiles // 3
+    lax.fori_loop(0, done, down_tile, 0)
+    for n in range(n_n):
+        until = tiles if n == n_n - 1 else done + (n + 1) * (tiles - done) // n_n
+
+        @pl.when(middle)
+        def _(n=n):
             forward(3 * (z // 2), n)
-            return carry
-
-        lax.fori_loop(0, n_n, second, 0)
-
-    lax.fori_loop((size * n_n) // 2, size * n_n, down_tile, 0)
+
+        lax.fori_loop(done + n * (tiles - done) // n_n, until, down_tile, 0)
     sum_copies = [
         pltpu.make_async_copy(
             res_v.at[j], sum_out.at[pl.ds(j * rows, rows), :], load_sem.at[2 + j]
@@ -680,14 +729,6 @@
     def drain(j, carry):
         for copy in out_copies(j):
             copy.wait()
-        for dz in (-1, 1):
-            came = jnp.logical_or(j == z, (j > z) if dz == -1 else (j < z))
-            there = has_low if dz == -1 else has_high
-
-            @pl.when(jnp.logical_and(came, there))
-            def _(dz=dz):
-                ag_copy(j, dz).wait_send()
-
         def sent(n, carry):
             @pl.when(j != z)
             def _():
@@ -699,15 +740,20 @@
         return carry
 
     lax.fori_loop(0, size, drain, 0)
+
+    @pl.when(middle)
+    def _():
+        far_copy().wait_send()
+
     for copy in sum_copies:
         copy.wait()
 
 
 def ffn(two, cot_rows, weights, axis="tensor", ft=768, nt=512, collective_id=1, limit=66_000_000):
-    rows, width = two.shape
+    size = 4
+    length, width = two.shape
+    rows = length // size
     units = weights.shape[1] // 3
-    size = 4
-    length = rows * size
     n_f, n_n = units // ft, width // nt
     bf16 = jnp.bfloat16
     hbm = pl.BlockSpec(memory_space=pl.ANY)
@@ -729,7 +775,7 @@
             vm((size, n_n, rows, nt), bf16), vm((size, n_n, rows, nt), bf16),
             vm((n_n, rows, nt), bf16), vm((n_n, rows, nt), bf16),
             vm((size, rows, width), bf16),
-            dma((3, n_f)), dma((2 + size,)), dma((2, size)), dma((size,)), dma((size, n_n)), dma((size, n_n)),
+            dma((3, n_f)), dma((2 + size,)), dma((size,)), dma((1,)), dma((1,)), dma((size, n_n)), dma((size, n_n)),
             dma((2, n_n)), dma((4, size)),
         ],
         compiler_params=pltpu.CompilerParams(
@@ -764,7 +810,7 @@
     cross = 3 - here
     block, half = core_sum.shape[2], core_sum.shape[2] // 2
     n_ffn, n_att = 3 * n_f, rhs_ref.shape[1] // wide
-    ring = x_land.shape[0]
+    ring, n_sum, n_last = x_land.shape[0], core_sum.shape[0], x_last.shape[0]
     total = n_ffn + n_att
     chunk, width = mixed_out.shape
     share = block // size
@@ -855,7 +901,7 @@
         )
 
     def one_copies(i):
-        s = core_sum.at[i % 4]
+        s = core_sum.at[i % n_sum]
         first, last = pl.ds(0, half), pl.ds(half, half)
         plan = (
             (s.at[at_x, first, :], x_land.at[i % ring, 0], by_x), (s.at[cross, first, :], x_land.at[i % ring, 1], by_x),
@@ -868,8 +914,8 @@
 
     def two_copies(i):
         return [
-            dp_copy(second.at[i % 4, 0], y_last.at[i % ring], two_send.at[0, i % ring], two_recv.at[0, i % ring], by_y),
-            dp_copy(second.at[i % 4, 1], x_last.at[i % ring], two_send.at[1, i % ring], two_recv.at[1, i % ring], by_x),
+            dp_copy(second.at[i % 4, 0], y_last.at[i % n_last], two_send.at[0, i % ring], two_recv.at[0, i % ring], by_y),
+            dp_copy(second.at[i % 4, 1], x_last.at[i % n_last], two_send.at[1, i % ring], two_recv.at[1, i % ring], by_x),
         ]
 
     def stage_copy(i):
@@ -932,7 +978,7 @@
     def sum_cores(i):
         mate_copy(i).wait_recv()
         for k in range(4):
-            core_sum[i % 4, k] = (
+            core_sum[i % n_sum, k] = (
                 grad[i % 2, k, core].astype(f32) + mate_land[i % 4, k].astype(f32)
             ).astype(bf16)
         for copy in one_copies(i):
@@ -941,7 +987,7 @@
     def sum_near(i):
         for copy in one_copies(i):
             copy.wait_recv()
-        s = core_sum.at[i % 4]
+        s = core_sum.at[i % n_sum]
         second[i % 4, 0] = (s[at_y, :half].astype(f32) + x_land[i % ring, 1].astype(f32)).astype(bf16)
         second[i % 4, 1] = (s[at_x, half:].astype(f32) + y_land[i % ring, 1].astype(f32)).astype(bf16)
         for copy in two_copies(i):
@@ -973,9 +1019,9 @@
     def finish(i):
         for copy in two_copies(i):
             copy.wait_recv()
-        own = core_sum.at[i % 4, here]
-        top = own[:half].astype(f32) + x_land[i % ring, 0].astype(f32) + y_last[i % ring].astype(f32)
-        low = own[half:].astype(f32) + y_land[i % ring, 0].astype(f32) + x_last[i % ring].astype(f32)
+        own = core_sum.at[i % n_sum, here]
+        top = own[:half].astype(f32) + x_land[i % ring, 0].astype(f32) + y_last[i % n_last].astype(f32)
+        low = own[half:].astype(f32) + y_land[i % ring, 0].astype(f32) + x_last[i % n_last].astype(f32)
 
         @pl.when(i < n_ffn)
         def _():
@@ -1177,7 +1223,7 @@
 
     def turn(i, carry):
         multiply(i)
-        for lag, work in ((1, sum_cores), (2, sum_near), (3, finish)):
+        for lag, work in ((1, sum_cores), (3, sum_near), (5, finish)):
 
             @pl.when(jnp.logical_and(i >= lag, i - lag < total))
             def _(lag=lag, work=work):
@@ -1186,7 +1232,7 @@
         small_step(i)
         return carry
 
-    lax.fori_loop(0, total + 3, turn, 0)
+    lax.fori_loop(0, total + 5, turn, 0)
     for i in (total - 2, total - 1):
         mate_copy(i).wait_send()
     for i in (n_ffn - 2, n_ffn - 1):
@@ -1244,7 +1290,7 @@
     heads = lse.shape[0]
     bf16, f32 = jnp.bfloat16, jnp.float32
     small = (8, query_w + kv_w + 2 * width)
-    ring = 5
+    ring = 8
     hbm = pl.BlockSpec(memory_space=pl.ANY)
     vmem = pl.BlockSpec(memory_space=pltpu.VMEM)
     vm = pltpu.VMEM
@@ -1268,9 +1314,9 @@
             vm(kv_win.shape, f32), vm((2, chunk, kv_w), bf16), vm((2, chunk, kv_w), bf16),
             vm((chunk, width), f32), vm(small, f32),
             vm((length, width), bf16), vm((2, length, wide), bf16), vm((2, 4, 2, block, wide), bf16),
-            vm((4, 4, block, wide), bf16), vm((4, 4, block, wide), bf16),
+            vm((4, 4, block, wide), bf16), vm((5, 4, block, wide), bf16),
             vm((ring, 2, half, wide), bf16), vm((ring, 2, half, wide), bf16),
-            vm((4, 2, half, wide), bf16), vm((ring, half, wide), bf16), vm((ring, half, wide), bf16),
+            vm((4, 2, half, wide), bf16), vm((6, half, wide), bf16), vm((6, half, wide), bf16),
             vm((2, block, wide), f32), vm((n_att, block, wide), bf16),
             vm((2, size - 1, block, part_w), bf16), vm((size - 1, share, wide), bf16),
             vm((size, chunk, width), bf16), vm((3,) + small, f32), vm((3,) + small, f32),
@@ -1397,6 +1443,7 @@
     middle = inputs + contract_cols(context, att_w[:, ahead + qkv_width :])
     inverse = lax.rsqrt(jnp.mean(middle * middle, axis=-1, keepdims=True) + EPSILON)
     two = (middle * inverse * gains[1]).astype(bf16)
+    two = lax.all_gather(two, "tensor", axis=0, tiled=True)
     query_rot = query_rot.reshape(rows, heads * HEAD_DIM)
     return att_w, ffn_all, cot_rows, two, middle, one, query_rot, kv_win, lse, context, gains
 

time: 469 us -> 467 us (level)
    pallas_call x1, Pallas kernels: 109 us -> 94 us  [ffn(): pl.pallas_call(functools.partial(ffn_body, axis=axis, ft=ft, nt=nt), out_...]
    pallas_call x1, Pallas kernels: 159 us -> 169 us  [front(): pl.pallas_call(functools.partial(front_body, pieces=pieces, order=order,...]
    pallas_call x1, Pallas kernels: 177 us -> 182 us  [back(): pl.pallas_call(functools.partial(back_body, n_f=n_f, wide=wide), out_shap...]
where the time goes in v7:
time: 467 us
  Pallas kernels  445 us (95%)
  local copies, waits for them, and re-layouts  14.2 us (3%)
  other arithmetic  7.38 us (2%)
    pallas_call x1, Pallas kernels, back(): pl.pallas_call(functools.partial(back_body, n_f=n_f, wide=wide), out_shap...  182 us
    pallas_call x1, Pallas kernels, front(): pl.pallas_call(functools.partial(front_body, pieces=pieces, order=order,...  169 us
    pallas_call x1, Pallas kernels, ffn(): pl.pallas_call(functools.partial(ffn_body, axis=axis, ft=ft, nt=nt), out_...  94 us

profile of v7, /device:TPU:26, one launch (start us, length us, event | category | flops | bytes accessed | tf_op | source)
XLA Modules:
  0.0 467.1 jit_solution(5345445950867869444)
XLA Ops:
  0.7 0.5 multiply_cosine_fusion
  1.2 0.1 maximum_bitcast_fusion
  1.4 0.7 pad_maximum_fusion.turn_ref
  2.1 0.0 copy-start.10
  2.1 0.0 copy-start.11
  2.1 0.0 copy-start.6
  2.1 0.0 copy-start.7
  2.1 0.8 pad_dynamic-slice_fusion
  2.9 0.7 constant_dynamic-slice_fusion.3
  3.6 0.0 copy-start.9
  3.6 0.0 copy-start.4
  3.6 1.1 fusion.7.mask_ref
  4.7 0.0 copy-start.5
  4.7 2.9 fusion.5.ffn_ref
  7.6 0.0 copy-done.10
  7.6 0.0 copy-done.11
  7.6 0.1 copy.31
  7.8 0.0 copy-done.6
  7.8 0.0 copy-done.7
  7.8 0.7 fusion.11.fixed_ref
  8.5 0.0 copy-done.9
  8.5 0.0 copy-done.4
  8.5 0.7 fusion.12.query_ref
  9.2 0.0 copy-done.5
  9.2 0.7 pad.24.out_ref
  9.9 0.0 copy-done.12
  9.9 0.0 copy-done.13
  9.9 0.6 maximum_convert_fusion.bias_ref
  10.5 168.7 %front.1 = (bf16[1536,3712]{1,0:T(8,128)(2,1)}, bf16[1536,6912]{1,0:T(8,128)(2,1)}, bf16[1024,1536]{1,0:T(8,128)(2,1)}, bf16[1024,1536]{1,0:T(8,128)(2,1)}, f32[...) custom-call(bf16[256,1536]{1,0:T(8,128)(2,1)} %x_ref.3, ...), custom_call_target="tpu_custom_call" | custom-call | flops 2919235584 | bytes 40796160 | tf_op jit(solution)/shard_map/front/pallas_call | solution.py:458
  179.2 94.0 %ffn.1 = (bf16[1024,1536]{1,0:T(8,128)(2,1)}, bf16[1024,2304]{1,0:T(8,128)(2,1)}, bf16[1024,2304]{1,0:T(8,128)(2,1)}, bf16[1024,2304]{1,0:T(8,128)(2,1)}, bf16[1...) custom-call(bf16[1024,1536]{1,0:T(8,128)(2,1)} %get-tuple-element.38.two_ref, ...), custom_call_target="tpu_custom_call" | custom-call | flops 43486543872 | bytes 47185920 | tf_op jit(solution)/shard_map/ffn/pallas_call | solution.py:763
  273.2 182.0 %back.1 = (f32[192,6912]{1,0:T(8,128)}, f32[192,384]{1,0:T(8,128)}, f32[192,384]{1,0:T(8,128)}, f32[48,768]{1,0:T(8,128)}, bf16[256,1536]{1,0:T(8,128)(2,1)}, /*...) custom-call(bf16[1024,1536]{1,0:T(8,128)(2,1)} %get-tuple-element.41.two_ref, bf16[1024,1536]{1,0:T(8,128)(2,1)} %get-tuple-element.39.cot_ref, ...), custom_call_target="tpu_custom_call" | custom-call | flops 21743271936 | bytes 18874368 | tf_op jit(solution)/shard_map/back/pallas_call | solution.py:1299
  455.2 0.0 copy-start.8
  455.3 0.0 copy-start.1
  455.3 0.0 copy-start
  455.3 5.2 %fusion.17 = (f32[192,2240]{1,0:T(8,128)}, f32[192,2240]{1,0:T(8,128)}, f32[192,2240]{1,0:T(8,128)}) fusion(f32[192,6912]{1,0:T(8,128)} %get-tuple-element.61), kind=kLoop, calls=%fused_computation.39 | loop fusion | bytes 10321920 | tf_op jit(solution)/shard_map/slice | solution.py:1621
  460.4 0.0 copy-done.8
  460.4 0.6 fusion.19
  461.1 0.9 slice.38
  462.0 0.6 fusion.16
  462.6 1.3 fusion.18
  463.9 0.0 copy-done.1
  463.9 0.9 copy.36
  464.8 0.0 copy-done
  464.8 0.9 copy.37
  465.7 0.0 copy-done.3
  465.7 0.7 copy.38
  466.4 0.0 copy-done.2
  466.4 0.7 copy.39
  (13 shorter events, 0.1 us)
Async XLA Ops:
  2.1 5.5 %copy-start.10 = (bf16[192]{0:T(256)(128)(2,1)S(1)}, bf16[192]{0:T(256)(128)(2,1)}, u32[]{:S(2)}) copy-start(bf16[192]{0:T(256)(128)(2,1)} %param.17) | copy-start | bytes 1156
  2.1 5.5 %copy-start.11 = (bf16[192]{0:T(256)(128)(2,1)S(1)}, bf16[192]{0:T(256)(128)(2,1)}, u32[]{:S(2)}) copy-start(bf16[192]{0:T(256)(128)(2,1)} %param.25) | copy-start | bytes 1156
  2.1 5.7 %copy-start.6 = (bf16[192,256]{1,0:T(8,128)(2,1)S(1)}, bf16[192,256]{1,0:T(8,128)(2,1)}, u32[]{:S(2)}) copy-start(bf16[192,256]{1,0:T(8,128)(2,1)} %param.22) | copy-start | bytes 294916
  2.1 5.7 %copy-start.7 = (bf16[192,256]{1,0:T(8,128)(2,1)S(1)}, bf16[192,256]{1,0:T(8,128)(2,1)}, u32[]{:S(2)}) copy-start(bf16[192,256]{1,0:T(8,128)(2,1)} %param.20) | copy-start | bytes 294916
  3.6 4.9 %copy-start.9 = (bf16[384]{0:T(512)(128)(2,1)S(1)}, bf16[384]{0:T(512)(128)(2,1)}, u32[]{:S(2)}) copy-start(bf16[384]{0:T(512)(128)(2,1)} %param.19) | copy-start | bytes 2308
  3.6 4.9 %copy-start.4 = (bf16[192,384]{1,0:T(8,128)(2,1)S(1)}, bf16[192,384]{1,0:T(8,128)(2,1)}, u32[]{:S(2)}) copy-start(bf16[192,384]{1,0:T(8,128)(2,1)} %param.18) | copy-start | bytes 442372
  4.7 4.5 copy-start.5
  4.7 5.2 %copy-start.12 = (bf16[256]{0:T(256)(128)(2,1)S(1)}, bf16[256]{0:T(256)(128)(2,1)}, u32[]{:S(2)}) copy-start(bf16[256]{0:T(256)(128)(2,1)} %param.21) | copy-start | bytes 1540
  4.7 5.2 %copy-start.13 = (bf16[256]{0:T(256)(128)(2,1)S(1)}, bf16[256]{0:T(256)(128)(2,1)}, u32[]{:S(2)}) copy-start(bf16[256]{0:T(256)(128)(2,1)} %param.23) | copy-start | bytes 1540
  455.2 5.2 %copy-start.8 = (f32[48,768]{1,0:T(8,128)S(1)}, f32[48,768]{1,0:T(8,128)}, u32[]{:S(2)}) copy-start(f32[48,768]{1,0:T(8,128)} %get-tuple-element.59) | copy-start | bytes 442372
  455.3 8.6 %copy-start.1 = (bf16[256,1536]{1,0:T(8,128)(2,1)S(1)}, bf16[256,1536]{1,0:T(8,128)(2,1)}, u32[]{:S(2)}) copy-start(bf16[256,1536]{1,0:T(8,128)(2,1)} %get-tuple-element.91) | copy-start | bytes 2359300
  455.3 9.5 %copy-start = (bf16[256,1536]{1,0:T(8,128)(2,1)S(1)}, bf16[256,1536]{1,0:T(8,128)(2,1)}, u32[]{:S(2)}) copy-start(bf16[256,1536]{1,0:T(8,128)(2,1)} %get-tuple-element.92) | copy-start | bytes 2359300
  460.4 5.2 %copy-start.3 = (f32[192,384]{1,0:T(8,128)S(1)}, f32[192,384]{1,0:T(8,128)}, u32[]{:S(2)}) copy-start(f32[192,384]{1,0:T(8,128)} %get-tuple-element.94) | copy-start | bytes 884740
  460.4 6.0 %copy-start.2 = (f32[192,384]{1,0:T(8,128)S(1)}, f32[192,384]{1,0:T(8,128)}, u32[]{:S(2)}) copy-start(f32[192,384]{1,0:T(8,128)} %get-tuple-element.100) | copy-start | bytes 884740

commit v8 on v7

--- a/solution.py
+++ b/solution.py
@@ -62,13 +62,33 @@
 
     pl.semaphore_wait(barrier, 3 + size - 1)
 
-    def z_copy(of, hop):
-        ref = (query_ref, out_ref)[of]
+    def z_copy(of, j, dz, own):
+        ref = att_v.at[:, place(of, j)]
         return pltpu.make_async_remote_copy(
-            src_ref=ref, dst_ref=att_v.at[:, place(of, z)], send_sem=z_send.at[of, hop - 1],
-            recv_sem=z_recv.at[of, hop - 1], device_id={"tensor": (z + hop) % size},
-            device_id_type=MESH,
-        )
+            src_ref=(query_ref, out_ref)[of] if own else ref, dst_ref=ref,
+            send_sem=z_send.at[of, (dz + 1) // 2, j], recv_sem=z_recv.at[of, j],
+            device_id={"tensor": z + dz}, device_id_type=MESH,
+        )
+
+    def z_start(of):
+        for dz, there in ((-1, has_low), (1, has_high)):
+
+            @pl.when(there)
+            def _(dz=dz):
+                z_copy(of, z, dz, True).start()
+
+    def z_step(of, hop):
+        for sign, onward in ((-1, has_high), (1, has_low)):
+            j = z + sign * hop
+            inside = (j >= 0) if sign == -1 else (j < size)
+
+            @pl.when(inside)
+            def _(j=j, sign=sign):
+                z_copy(of, j, -sign, False).wait_recv()
+
+            @pl.when(jnp.logical_and(inside, onward))
+            def _(j=j, sign=sign):
+                z_copy(of, j, -sign, False).start()
 
     has_low, has_high = z > 0, z < size - 1
 
@@ -130,8 +150,7 @@
                     two_copy(j, -sign, False).start()
 
     for of in range(2):
-        for hop in range(1, size):
-            z_copy(of, hop).start()
+        z_start(of)
     fills[0].wait()
 
     def views(kind, p):
@@ -218,9 +237,6 @@
             if not state[("query", "out")[of]]:
                 state[("query", "out")[of]] = True
                 fills[1 + of].wait()
-                for hop in range(1, size):
-                    ref = att_v.at[:, place(of, z)]
-                    pltpu.make_async_copy(ref, ref, z_recv.at[of, hop - 1]).wait()
                 if of == 1:
                     cot_start()
 
@@ -297,19 +313,21 @@
             def _(hop=hop):
                 kv_v[2 - hop] = jnp.zeros(kv_v.shape[1:], bf16)
 
-    def queries():
-        def pair(h, carry):
-            cols = pl.ds(pl.multiple_of(h * 2 * HEAD_DIM, 128), 2 * HEAD_DIM)
-            from_w = pl.ds(pl.multiple_of(fixed + h * 2 * HEAD_DIM, 128), 2 * HEAD_DIM)
+    per = pieces[0][1][1] // HEAD_DIM
+
+    def queries(first):
+        def pair(k, carry):
+            h = first + 2 * k
+            cols = pl.ds(pl.multiple_of(h * HEAD_DIM, 128), 2 * HEAD_DIM)
+            from_w = pl.ds(pl.multiple_of(fixed + h * HEAD_DIM, 128), 2 * HEAD_DIM)
             lin = jnp.dot(one_v[...], w_v[:, from_w], preferred_element_type=f32)
             lin += att_v[pl.ds(rows, 16), from_w][0:1, :].astype(f32)
-            for k in range(2):
-                out_cols = pl.ds(pl.multiple_of(h * 2 * HEAD_DIM + k * HEAD_DIM, 128), HEAD_DIM)
-                q_v[:, out_cols] = turned(lin[:, k * HEAD_DIM : (k + 1) * HEAD_DIM]).astype(bf16)
+            q_v[:, cols] = jnp.concatenate(
+                [turned(lin[:, :HEAD_DIM]), turned(lin[:, HEAD_DIM:])], axis=1
+            ).astype(bf16)
             return carry
 
-        lax.fori_loop(0, heads // 2, pair, 0)
-        save(q_v, query_rot)
+        lax.fori_loop(0, per // 2, pair, 0)
 
     def kv_wait():
         for hop in (1, 2):
@@ -342,55 +360,67 @@
 
         lax.fori_loop(first, last, head, 0)
 
-    def project():
-        save(ctx_v, ctx_out)
+    def project(k):
         tile = min(512, w_v.shape[0])
+        wide = per * HEAD_DIM
 
         def some(n, carry):
             at_n = pl.ds(pl.multiple_of(n * tile, tile), tile)
             added = lax.dot_general(
-                ctx_v[...], w_v[at_n, fixed + size * part :], (((1,), (1,)), ((), ())),
-                preferred_element_type=f32,
+                ctx_v[:, k * wide : (k + 1) * wide],
+                w_v[at_n, fixed + size * part + k * wide : fixed + size * part + (k + 1) * wide],
+                (((1,), (1,)), ((), ())), preferred_element_type=f32,
             )
-            mid_v[:, at_n] = x_ref[:, at_n].astype(f32) + added
+            so_far = mid_v[:, at_n] if k else x_ref[:, at_n].astype(f32)
+            mid_v[:, at_n] = so_far + added
             return carry
 
         lax.fori_loop(0, w_v.shape[0] // tile, some, 0)
-        save(mid_v, mid_out)
+
+    def second_norm():
         norm(lambda at_r: mid_v[at_r, :], 1, two_v)
         save(two_v, two_all.at[at, :])
         two_start()
+        save(mid_v, mid_out)
+        save(q_v, query_rot)
+        save(ctx_v, ctx_out)
 
     n_att = len(pieces[0])
-    n_qkv = 1 + (n_att - 1) // 2
-    third = heads // 3 + (heads % 3 > 0)
-    last_q = order.index((0, n_qkv - 1))
-    last_out = order.index((0, n_att - 1))
-    work = [
-        (last_q - 1, lambda: cot_step(1)),
-        (last_q + 1, lambda: cot_step(2)),
-        (last_q + 1, lambda: take(0, n_qkv)),
-        (last_q + 2, lambda: held(0, n_qkv)),
-        (last_q + 2, keys),
-        (last_q + 2, queries),
-        (last_q + 3, kv_wait),
-        (last_q + 3, lambda: attend(0, third)),
-        (last_out + 1, lambda: take(n_qkv, n_att)),
-        (last_out + 1, lambda: attend(third, 2 * third)),
-        (last_out + 2, lambda: cot_step(3)),
-        (last_out + 2, lambda: attend(2 * third, heads)),
-        (last_out + 3, lambda: held(n_qkv, n_att)),
-        (last_out + 3, project),
-        (last_out + 5, lambda: two_step(1)),
-        (last_out + 20, lambda: two_step(2)),
+    n_q = (n_att - 1) // 2
+    when_q, when_out = [[order.index((0, 1 + of * n_q + k)) for k in range(n_q)] for of in range(2)]
+    last_q, last_out = when_q[-1], when_out[-1]
+    work = [(2, lambda: take(0, 1)), (2, lambda: held(0, 1)), (2, keys)]
+    work += [(last_q + 1, lambda: cot_step(1)), (last_q + 4, lambda: cot_step(2)), (last_q + 6, lambda: cot_step(3))]
+    work += [(when_q[0] + 2, kv_wait)]
+    for k in range(n_q):
+        work += [
+            (when_q[k] + 2, lambda k=k: take(1 + k, 2 + k)), (when_q[k] + 3, lambda k=k: held(1 + k, 2 + k)),
+            (when_q[k] + 3, lambda k=k: queries(k * per)),
+            (when_q[k] + 3, lambda k=k: attend(k * per, (k + 1) * per)),
+        ]
+        late = 3 if k < n_q - 1 else 2
+        work += [
+            (when_out[k] + 2, lambda k=k: take(1 + n_q + k, 2 + n_q + k)),
+            (when_out[k] + late, lambda k=k: held(1 + n_q + k, 2 + n_q + k)),
+            (when_out[k] + late, lambda k=k: project(k)),
+        ]
+    work += [
+        (last_out + 2, second_norm), (last_out + 5, lambda: two_step(1)), (last_out + 20, lambda: two_step(2)),
     ]
+    work.sort(key=lambda step: step[0])
     total = len(order)
     for i in range(total + 1):
-        while state["begun"] < min(total, i + (lead if i <= last_q else 2 * lead)):
+        while state["begun"] < min(total, i + (lead if i <= last_out else 2 * lead)):
             ready(*order[state["begun"]])
             begin(*order[state["begun"]])
             state["begun"] += 1
-        if i < total:
+        if i == 0:
+            for hop in range(1, size):
+                for of in range(2):
+                    z_step(of, hop)
+                if hop < size - 1:
+                    pass_on(*order[hop - 1])
+        if size - 2 <= i < total:
             pass_on(*order[i])
         if i > 0:
             close(*order[i - 1])
@@ -409,9 +439,6 @@
         def _(hop=hop):
             kv_copy(hop).wait_send()
 
-    for of in range(2):
-        for hop in range(1, size):
-            z_copy(of, hop).wait_send()
     for j in range(size):
         for dz, there in ((-1, has_low), (1, has_high)):
             came = jnp.logical_and((z <= j) if dz == -1 else (z >= j), there)
@@ -419,6 +446,8 @@
             @pl.when(came)
             def _(j=j, dz=dz):
                 cot_copy(j, dz).wait_send()
+                for of in range(2):
+                    z_copy(of, j, dz, False).wait_send()
 
             near = jnp.logical_and(came, (j - z <= 1) if dz == -1 else (z - j <= 1))
 
@@ -469,7 +498,7 @@
             vm((tall, att_cols), bf16), vm((8 * rows, att_cols), bf16), vm((chunk, width), bf16),
             vm((chunk, query_w), bf16), vm((3, chunk, kv_w), bf16), vm((chunk, query_w), bf16),
             vm((chunk, width), f32), vm((chunk, width), bf16),
-            dma((4,)), dma((2, size - 1)), dma((2, size - 1)),
+            dma((4,)), dma((2, 2, size)), dma((2, size)),
             dma((2, size)), dma((size,)), dma((ways, slots)), dma((ways, slots)), dma((slots,)),
             dma((n_att,)), dma((2,)), dma((2,)), dma((6,)), dma((2, size)), dma((size,)),
         ],
@@ -793,12 +822,12 @@
     two_ref, cot_ref, hid_ref, dg_ref, du_ref, part_ref, up_ref, x_ref, mid_ref, gain_ref, att_ref,
     query_ref, win_ref, lse_ref, ctx_ref, one_ref, mask_ref, turn_ref,
     ffn_out, query_out, out_out, kv_out, mixed_out, input_out, small_out,
-    up_v, own_v, x_v, mid_v, gain_v, w_v, query_v, win_v, lse_v, mask_v, turn_v, lhs_ref, rhs_ref,
-    d_mid, d_ctx, d_win, kv_give, kv_take, d_one, small_ref,
+    up_v, own_v, mid_v, gain_v, w_v, query_v, win_v, lse_v, mask_v, turn_v, lhs_ref, rhs_ref,
+    d_mid, d_ctx, d_win, kv_give, kv_take, small_ref,
     left_v, right_v, grad, mate_land, core_sum, x_land, y_land, second, x_last, y_last, stage, fin,
-    z_land, kv_land, sum_land, small_z, small_hop, small_next, in_sem, give_send, give_recv,
+    z_land, kv_land, fold_land, fold_last, fold_own, small_z, small_hop, small_next, in_sem, give_send, give_recv,
     left_sem, right_sem, mate_send, mate_recv, one_send, one_recv, two_send, two_recv, stage_sem,
-    z_send, z_recv, kv_send, kv_recv, sum_send, sum_recv, own_sem, small_send, small_recv,
+    z_send, z_recv, kv_send, kv_recv, fold_send, fold_recv, last_recv, own_sem, small_send, small_recv,
     hop_send, hop_recv, *, n_f, wide,
 ):
     f32, bf16 = jnp.float32, jnp.bfloat16
@@ -811,6 +840,7 @@
     block, half = core_sum.shape[2], core_sum.shape[2] // 2
     n_ffn, n_att = 3 * n_f, rhs_ref.shape[1] // wide
     ring, n_sum, n_last = x_land.shape[0], core_sum.shape[0], x_last.shape[0]
+    n_grad, n_mate = grad.shape[0], mate_land.shape[0]
     total = n_ffn + n_att
     chunk, width = mixed_out.shape
     share = block // size
@@ -838,7 +868,7 @@
         (up_ref, up_v), (cot_ref.at[own_rows, :], own_v), (mid_ref, mid_v), (gain_ref, gain_v),
         (att_ref.at[:, pl.ds(ahead + 2 * kv_w + query_w, query_w)], w_v.at[:, pl.ds(0, query_w)]),
         (query_ref, query_v), (win_ref, win_v), (lse_ref, lse_v), (mask_ref, mask_v), (turn_ref, turn_v),
-        (ctx_ref, rhs_ref.at[:, ctx_cols]), (x_ref, x_v), (one_ref, lhs_ref.at[0]),
+        (ctx_ref, rhs_ref.at[:, ctx_cols]), (one_ref, lhs_ref.at[0]), (x_ref, up_v),
         (att_ref.at[:, pl.ds(ahead, 2 * kv_w + query_w)], w_v),
     )
     loads = [pltpu.make_async_copy(src, dst, in_sem.at[k]) for k, (src, dst) in enumerate(plan)]
@@ -854,14 +884,42 @@
 
     lefts[0].start()
     right_load(jnp.int32(0), "start")
-    for copy in loads[:-1]:
+    for copy in loads[:-2]:
         copy.start()
 
     def chunk_rows(j):
         return part_ref.at[pl.ds(pl.multiple_of(j * chunk, chunk), chunk), :]
 
-    own_part = pltpu.make_async_copy(chunk_rows(z), sum_land.at[size - 1], own_sem.at[0])
-    own_part.start()
+    upper = z // 2
+    inward = 1 - 2 * upper
+    middle = jnp.logical_and(z > 0, z < size - 1)
+
+    def fold_load(j):
+        return pltpu.make_async_copy(chunk_rows(j), fold_own, own_sem.at[0])
+
+    def fold_copy(k, first):
+        if first:
+            j = (3 - 3 * upper, 2 - upper, z + inward)[k]
+            src, to = chunk_rows(j), z + inward
+            dst = (fold_land.at[0], fold_land.at[1], fold_last.at[0])[k]
+            sem = (fold_recv.at[0], fold_recv.at[1], last_recv.at[0])[k]
+        else:
+            src, to = fold_land.at[k], z + (inward, inward, -inward)[k]
+            dst = (fold_land.at[2], fold_last.at[1], fold_last.at[1])[k]
+            sem = (fold_recv.at[2], last_recv.at[1], last_recv.at[1])[k]
+        return pltpu.make_async_remote_copy(
+            src_ref=src, dst_ref=dst, send_sem=fold_send.at[k], recv_sem=sem,
+            device_id={"tensor": to}, device_id_type=MESH,
+        )
+
+    def fold(k):
+        @pl.when(middle)
+        def _():
+            pltpu.make_async_copy(fold_land.at[k], fold_land.at[k], fold_recv.at[k]).wait()
+            fold_load(z).wait()
+            fold_land[k] = (fold_land[k].astype(f32) + fold_own[...].astype(f32)).astype(bf16)
+            fold_copy(k, False).start()
+            fold_load((2 - upper, 3 * upper, z)[k]).start()
     pl.semaphore_wait(barrier, 3 + size - 1)
 
     def dp_copy(src, dst, send_sem, recv_sem, peer):
@@ -876,17 +934,23 @@
             device_id={"tensor": peer}, device_id_type=MESH,
         )
 
-    small_copies, sum_copies = [], []
+    small_copies = []
     for hop in range(1, size):
         to, k = (z + hop) % size, hop - 1
         small_copies.append(
             z_copy(small_ref, small_z.at[k], small_send.at[k], small_recv.at[k], to)
         )
-        sum_copies.append(
-            z_copy(chunk_rows(to), sum_land.at[k], sum_send.at[k], sum_recv.at[k], to)
-        )
-    for copy in sum_copies:
-        copy.start()
+
+    @pl.when(jnp.logical_not(middle))
+    def _():
+        for k in range(3):
+            fold_copy(k, True).start()
+        fold_load(z).start()
+
+    @pl.when(middle)
+    def _():
+        fold_load(3 - 3 * upper).start()
+
     rhs_ref[:, 2 * query_w + 2 * kv_w :] = jnp.zeros((chunk, rhs_ref.shape[1] - 2 * query_w - 2 * kv_w), bf16)
 
     hops = (mate, by_x, by_y)
@@ -896,8 +960,8 @@
 
     def mate_copy(i):
         return dp_copy(
-            grad.at[i % 2, :, 1 - core], mate_land.at[i % 4], mate_send.at[i % 4],
-            mate_recv.at[i % 4], mate,
+            grad.at[i % n_grad, :, 1 - core], mate_land.at[i % n_mate], mate_send.at[i % n_mate],
+            mate_recv.at[i % n_mate], mate,
         )
 
     def one_copies(i):
@@ -914,8 +978,8 @@
 
     def two_copies(i):
         return [
-            dp_copy(second.at[i % 4, 0], y_last.at[i % n_last], two_send.at[0, i % ring], two_recv.at[0, i % ring], by_y),
-            dp_copy(second.at[i % 4, 1], x_last.at[i % n_last], two_send.at[1, i % ring], two_recv.at[1, i % ring], by_x),
+            dp_copy(second.at[i % 2, 0], y_last.at[i % n_last], two_send.at[0, i % ring], two_recv.at[0, i % ring], by_y),
+            dp_copy(second.at[i % 2, 1], x_last.at[i % n_last], two_send.at[1, i % ring], two_recv.at[1, i % ring], by_x),
         ]
 
     def stage_copy(i):
@@ -923,9 +987,9 @@
         return pltpu.make_async_copy(stage.at[i % 2], ffn_out.at[:, cols], stage_sem.at[i % 2])
 
     def multiply(i):
-        @pl.when(jnp.logical_and(i >= 2, i < total))
+        @pl.when(jnp.logical_and(i >= n_grad, i < total))
         def _():
-            mate_copy(i - 2).wait_send()
+            mate_copy(i - n_grad).wait_send()
 
         @pl.when(i + 1 < n_ffn)
         def _():
@@ -951,7 +1015,7 @@
                 value = lax.dot_general(
                     left_v[:, at], right_v[i % 2], dims, preferred_element_type=f32
                 )
-                grad[i % 2, k] = value.astype(bf16).reshape(2, block, wide)
+                grad[i % n_grad, k] = value.astype(bf16).reshape(2, block, wide)
                 return carry
 
             lax.fori_loop(0, 4, rows, 0)
@@ -966,7 +1030,7 @@
                 value = lax.dot_general(
                     lhs_ref[(a // 2) % 2, :, at], rhs_ref[:, cols], dims, preferred_element_type=f32
                 )
-                grad[i % 2, k] = value.astype(bf16).reshape(2, block, wide)
+                grad[i % n_grad, k] = value.astype(bf16).reshape(2, block, wide)
                 return carry
 
             lax.fori_loop(0, 4, rows, 0)
@@ -979,7 +1043,7 @@
         mate_copy(i).wait_recv()
         for k in range(4):
             core_sum[i % n_sum, k] = (
-                grad[i % 2, k, core].astype(f32) + mate_land[i % 4, k].astype(f32)
+                grad[i % n_grad, k, core].astype(f32) + mate_land[i % n_mate, k].astype(f32)
             ).astype(bf16)
         for copy in one_copies(i):
             copy.start()
@@ -988,8 +1052,8 @@
         for copy in one_copies(i):
             copy.wait_recv()
         s = core_sum.at[i % n_sum]
-        second[i % 4, 0] = (s[at_y, :half].astype(f32) + x_land[i % ring, 1].astype(f32)).astype(bf16)
-        second[i % 4, 1] = (s[at_x, half:].astype(f32) + y_land[i % ring, 1].astype(f32)).astype(bf16)
+        second[i % 2, 0] = (s[at_y, :half].astype(f32) + x_land[i % ring, 1].astype(f32)).astype(bf16)
+        second[i % 2, 1] = (s[at_x, half:].astype(f32) + y_land[i % ring, 1].astype(f32)).astype(bf16)
         for copy in two_copies(i):
             copy.start()
 
@@ -1086,7 +1150,8 @@
             return carry
 
         lax.fori_loop(0, query_w // tile, some, 0)
-        loads[-1].start()
+        for copy in loads[-2:]:
+            copy.start()
         for k in (5, 6, 7, 8, 9):
             loads[k].wait()
         d_win[...] = jnp.zeros_like(d_win)
@@ -1158,7 +1223,7 @@
 
         def some(n, carry):
             at_n = pl.ds(pl.multiple_of(n * tile, tile), tile)
-            d_one[:, at_n] = lax.dot_general(
+            d_win[n] = lax.dot_general(
                 rhs_ref[:, :query_w], w_v[at_n, 2 * kv_w :], across, preferred_element_type=f32
             ) + lax.dot_general(
                 rhs_ref[:, 2 * query_w : 2 * query_w + 2 * kv_w], w_v[at_n, : 2 * kv_w], across,
@@ -1169,11 +1234,11 @@
         lax.fori_loop(0, width // tile, some, 0)
 
     def close_branch():
-        loads[11].wait()
+        loads[-2].wait()
 
         def work(at):
             input_out[at, :] = back_norm(
-                d_one[at, :], x_v[at, :].astype(f32), gain_v[0:1, :], d_mid[at, :], gain_one_at
+                jnp.concatenate([d_win[n, at, :] for n in range(width // d_win.shape[2])], axis=1), up_v[at, :].astype(f32), gain_v[0:1, :], d_mid[at, :], gain_one_at
             ).astype(bf16)
 
         by_rows(work)
@@ -1208,7 +1273,8 @@
         (at_turn(4), lambda: attend_back(2 * quarter, 3 * quarter)),
         (at_turn(5), lambda: attend_back(3 * quarter, heads)),
         (at_turn(5), give),
-        (at_turn(7), take), (at_turn(7), lambda: [loads[k].wait() for k in (10, 12)]),
+        (at_turn(3), lambda: fold(0)), (at_turn(5), lambda: fold(1)), (at_turn(8), lambda: fold(2)),
+        (at_turn(7), take), (at_turn(7), lambda: [loads[k].wait() for k in (10, 11)]),
         (n_ffn + 1, one_grads), (n_ffn + 2, close_branch),
         (n_ffn + 4, small_first), (n_ffn + 5, lambda: small_then(0)), (n_ffn + 6, lambda: small_then(1)),
         (n_ffn + 7, small_last),
@@ -1223,7 +1289,7 @@
 
     def turn(i, carry):
         multiply(i)
-        for lag, work in ((1, sum_cores), (3, sum_near), (5, finish)):
+        for lag, work in ((1, sum_cores), (2, sum_near), (3, finish)):
 
             @pl.when(jnp.logical_and(i >= lag, i - lag < total))
             def _(lag=lag, work=work):
@@ -1232,18 +1298,23 @@
         small_step(i)
         return carry
 
-    lax.fori_loop(0, total + 5, turn, 0)
-    for i in (total - 2, total - 1):
+    lax.fori_loop(0, total + 3, turn, 0)
+    for i in range(total - n_grad, total):
         mate_copy(i).wait_send()
     for i in (n_ffn - 2, n_ffn - 1):
         stage_copy(i).wait()
-    own_part.wait()
-    for copy in sum_copies:
-        copy.wait_recv()
-    acc = sum_land[size - 1].astype(f32)
-    for k in range(size - 1):
-        acc += sum_land[k].astype(f32)
-    mixed_out[...] = (mid_v[...] + acc).astype(bf16)
+    fold_load(z).wait()
+    mid_v[...] += fold_own[...].astype(f32)
+
+    @pl.when(middle)
+    def _():
+        pltpu.make_async_copy(fold_last.at[0], fold_last.at[0], last_recv.at[0]).wait()
+        mid_v[...] += fold_last[0].astype(f32)
+
+    pltpu.make_async_copy(fold_last.at[1], fold_last.at[1], last_recv.at[1]).wait()
+    mixed_out[...] = (mid_v[...] + fold_last[1].astype(f32)).astype(bf16)
+    for k in range(3):
+        pltpu.make_async_copy(fold_land.at[k], fold_land.at[k], fold_send.at[k]).wait()
     for of, dst in ((0, query_out), (1, out_out)):
         for k in range(size - 1):
             ref = z_land.at[of, k]
@@ -1266,7 +1337,7 @@
     kv_out[...] = acc
     for a in range(n_att):
         z_sends(a, "wait")
-    for copy in sum_copies + small_copies:
+    for copy in small_copies:
         copy.wait_send()
     for k in range(3):
         hop_copy(k).wait_send()
@@ -1290,7 +1361,7 @@
     heads = lse.shape[0]
     bf16, f32 = jnp.bfloat16, jnp.float32
     small = (8, query_w + kv_w + 2 * width)
-    ring = 8
+    ring = 5
     hbm = pl.BlockSpec(memory_space=pl.ANY)
     vmem = pl.BlockSpec(memory_space=pltpu.VMEM)
     vm = pltpu.VMEM
@@ -1306,25 +1377,25 @@
         in_specs=[hbm] * 18,
         out_specs=(hbm,) + (vmem,) * 6,
         scratch_shapes=[
-            vm((chunk, width), bf16), vm((chunk, width), bf16), vm((chunk, width), bf16),
+            vm((chunk, width), bf16), vm((chunk, width), bf16),
             vm((chunk, width), f32), vm(gains.shape, f32), vm((width, kv_w + query_w), bf16),
             vm((chunk, query_w), bf16), vm(kv_win.shape, bf16), vm((heads, chunk, 1), f32),
             vm(mask.shape, f32), vm(turn.shape, f32), vm((2, chunk, width), bf16),
             vm((chunk, 2 * query_w + wide), bf16), vm((chunk, width), f32), vm((chunk, query_w), bf16),
             vm(kv_win.shape, f32), vm((2, chunk, kv_w), bf16), vm((2, chunk, kv_w), bf16),
-            vm((chunk, width), f32), vm(small, f32),
+            vm(small, f32),
             vm((length, width), bf16), vm((2, length, wide), bf16), vm((2, 4, 2, block, wide), bf16),
-            vm((4, 4, block, wide), bf16), vm((5, 4, block, wide), bf16),
+            vm((4, 4, block, wide), bf16), vm((4, 4, block, wide), bf16),
             vm((ring, 2, half, wide), bf16), vm((ring, 2, half, wide), bf16),
-            vm((4, 2, half, wide), bf16), vm((6, half, wide), bf16), vm((6, half, wide), bf16),
+            vm((2, 2, half, wide), bf16), vm((4, half, wide), bf16), vm((4, half, wide), bf16),
             vm((2, block, wide), f32), vm((n_att, block, wide), bf16),
             vm((2, size - 1, block, part_w), bf16), vm((size - 1, share, wide), bf16),
-            vm((size, chunk, width), bf16), vm((3,) + small, f32), vm((3,) + small, f32),
+            vm((3, chunk, width), bf16), vm((2, chunk, width), bf16), vm((chunk, width), bf16), vm((3,) + small, f32), vm((3,) + small, f32),
             vm((3,) + small, f32), dma((14,)), dma((2,)), dma((2,)),
-            dma((2,)), dma((2,)), dma((4,)), dma((4,)), dma((4, ring)), dma((4, ring)),
+            dma((2,)), dma((2,)), dma((6,)), dma((6,)), dma((4, ring)), dma((4, ring)),
             dma((2, ring)), dma((2, ring)), dma((2,)),
-            dma((4, 2)), dma((2, size - 1)), dma((size - 1,)), dma((size - 1,)), dma((size - 1,)),
-            dma((size - 1,)), dma((1,)), dma((size - 1,)), dma((size - 1,)), dma((3,)), dma((3,)),
+            dma((4, 2)), dma((2, size - 1)), dma((size - 1,)), dma((size - 1,)), dma((3,)),
+            dma((3,)), dma((2,)), dma((1,)), dma((size - 1,)), dma((size - 1,)), dma((3,)), dma((3,)),
         ],
         compiler_params=pltpu.CompilerParams(
             collective_id=collective_id, has_side_effects=True, vmem_limit_bytes=limit

time: 467 us -> 431 us (0.923)
  Pallas kernels: 445 us -> 409 us
    pallas_call x1, Pallas kernels: 182 us -> 163 us  [back(): pl.pallas_call(functools.partial(back_body, n_f=n_f, wide=wide), out_shap...]
    pallas_call x1, Pallas kernels: 169 us -> 159 us  [front(): pl.pallas_call(functools.partial(front_body, pieces=pieces, order=order,...]
    pallas_call x1, Pallas kernels: 94 us -> 87.1 us  [ffn(): pl.pallas_call(functools.partial(ffn_body, axis=axis, ft=ft, nt=nt), out_...]
where the time goes in v8:
time: 431 us
  Pallas kernels  409 us (95%)
  local copies, waits for them, and re-layouts  14.2 us (3%)
  other arithmetic  7.38 us (2%)
    pallas_call x1, Pallas kernels, back(): pl.pallas_call(functools.partial(back_body, n_f=n_f, wide=wide), out_shap...  163 us
    pallas_call x1, Pallas kernels, front(): pl.pallas_call(functools.partial(front_body, pieces=pieces, order=order,...  159 us
    pallas_call x1, Pallas kernels, ffn(): pl.pallas_call(functools.partial(ffn_body, axis=axis, ft=ft, nt=nt), out_...  87.1 us

profile of v8, /device:TPU:26, one launch (start us, length us, event | category | flops | bytes accessed | tf_op | source)
XLA Modules:
  0.0 431.1 jit_solution(2927733240991607553)
XLA Ops:
  0.7 0.5 multiply_cosine_fusion
  1.2 0.1 maximum_bitcast_fusion
  1.4 0.7 pad_maximum_fusion.turn_ref
  2.1 0.0 copy-start.10
  2.1 0.0 copy-start.11
  2.1 0.0 copy-start.6
  2.1 0.0 copy-start.7
  2.1 0.8 pad_dynamic-slice_fusion
  2.9 0.7 constant_dynamic-slice_fusion.3
  3.6 0.0 copy-start.9
  3.6 1.1 fusion.7.mask_ref
  4.7 0.0 copy-start.5
  4.7 0.0 copy-start.12
  4.7 2.9 fusion.5.ffn_ref
  7.6 0.0 copy-done.10
  7.6 0.0 copy-done.11
  7.6 0.1 copy.31
  7.8 0.0 copy-done.6
  7.8 0.0 copy-done.7
  7.8 0.7 fusion.11.fixed_ref
  8.5 0.0 copy-done.9
  8.5 0.0 copy-done.4
  8.5 0.7 fusion.12.query_ref
  9.2 0.0 copy-done.5
  9.2 0.7 pad.24.out_ref
  9.9 0.0 copy-done.12
  9.9 0.0 copy-done.13
  9.9 0.6 maximum_convert_fusion.bias_ref
  10.5 158.5 %front.1 = (bf16[1536,3712]{1,0:T(8,128)(2,1)}, bf16[1536,6912]{1,0:T(8,128)(2,1)}, bf16[1024,1536]{1,0:T(8,128)(2,1)}, bf16[1024,1536]{1,0:T(8,128)(2,1)}, f32[...) custom-call(bf16[256,1536]{1,0:T(8,128)(2,1)} %x_ref.3, ...), custom_call_target="tpu_custom_call" | custom-call | flops 2919235584 | bytes 40796160 | tf_op jit(solution)/shard_map/front/pallas_call | solution.py:487
  169.0 87.1 %ffn.1 = (bf16[1024,1536]{1,0:T(8,128)(2,1)}, bf16[1024,2304]{1,0:T(8,128)(2,1)}, bf16[1024,2304]{1,0:T(8,128)(2,1)}, bf16[1024,2304]{1,0:T(8,128)(2,1)}, bf16[1...) custom-call(bf16[1024,1536]{1,0:T(8,128)(2,1)} %get-tuple-element.38.two_ref, ...), custom_call_target="tpu_custom_call" | custom-call | flops 43486543872 | bytes 47185920 | tf_op jit(solution)/shard_map/ffn/pallas_call | solution.py:792
  256.1 163.1 %back.1 = (f32[192,6912]{1,0:T(8,128)}, f32[192,384]{1,0:T(8,128)}, f32[192,384]{1,0:T(8,128)}, f32[48,768]{1,0:T(8,128)}, bf16[256,1536]{1,0:T(8,128)(2,1)}, /*...) custom-call(bf16[1024,1536]{1,0:T(8,128)(2,1)} %get-tuple-element.41.two_ref, bf16[1024,1536]{1,0:T(8,128)(2,1)} %get-tuple-element.39.cot_ref, ...), custom_call_target="tpu_custom_call" | custom-call | flops 21743271936 | bytes 18874368 | tf_op jit(solution)/shard_map/back/pallas_call | solution.py:1370
  419.2 0.0 copy-start.8
  419.2 0.0 copy-start.1
  419.2 0.0 copy-start
  419.2 5.2 %fusion.17 = (f32[192,2240]{1,0:T(8,128)}, f32[192,2240]{1,0:T(8,128)}, f32[192,2240]{1,0:T(8,128)}) fusion(f32[192,6912]{1,0:T(8,128)} %get-tuple-element.61), kind=kLoop, calls=%fused_computation.39 | loop fusion | bytes 10321920 | tf_op jit(solution)/shard_map/slice | solution.py:1692
  424.4 0.0 copy-done.8
  424.4 0.6 fusion.19
  425.0 0.9 slice.38
  426.0 0.6 fusion.16
  426.6 1.3 fusion.18
  427.9 0.0 copy-done.1
  427.9 0.9 copy.36
  428.7 0.0 copy-done
  428.7 0.9 copy.37
  429.6 0.0 copy-done.3
  429.6 0.7 copy.38
  430.3 0.0 copy-done.2
  430.3 0.7 copy.39
  (13 shorter events, 0.1 us)
Async XLA Ops:
  2.1 5.5 %copy-start.10 = (bf16[192]{0:T(256)(128)(2,1)S(1)}, bf16[192]{0:T(256)(128)(2,1)}, u32[]{:S(2)}) copy-start(bf16[192]{0:T(256)(128)(2,1)} %param.17) | copy-start | bytes 1156
  2.1 5.5 %copy-start.11 = (bf16[192]{0:T(256)(128)(2,1)S(1)}, bf16[192]{0:T(256)(128)(2,1)}, u32[]{:S(2)}) copy-start(bf16[192]{0:T(256)(128)(2,1)} %param.25) | copy-start | bytes 1156
  2.1 5.7 %copy-start.6 = (bf16[192,256]{1,0:T(8,128)(2,1)S(1)}, bf16[192,256]{1,0:T(8,128)(2,1)}, u32[]{:S(2)}) copy-start(bf16[192,256]{1,0:T(8,128)(2,1)} %param.22) | copy-start | bytes 294916
  2.1 5.7 %copy-start.7 = (bf16[192,256]{1,0:T(8,128)(2,1)S(1)}, bf16[192,256]{1,0:T(8,128)(2,1)}, u32[]{:S(2)}) copy-start(bf16[192,256]{1,0:T(8,128)(2,1)} %param.20) | copy-start | bytes 294916
  3.6 4.9 %copy-start.9 = (bf16[384]{0:T(512)(128)(2,1)S(1)}, bf16[384]{0:T(512)(128)(2,1)}, u32[]{:S(2)}) copy-start(bf16[384]{0:T(512)(128)(2,1)} %param.19) | copy-start | bytes 2308
  3.6 4.9 %copy-start.4 = (bf16[192,384]{1,0:T(8,128)(2,1)S(1)}, bf16[192,384]{1,0:T(8,128)(2,1)}, u32[]{:S(2)}) copy-start(bf16[192,384]{1,0:T(8,128)(2,1)} %param.18) | copy-start | bytes 442372
  4.7 4.5 %copy-start.5 = (bf16[192,384]{1,0:T(8,128)(2,1)S(1)}, bf16[192,384]{1,0:T(8,128)(2,1)}, u32[]{:S(2)}) copy-start(bf16[192,384]{1,0:T(8,128)(2,1)} %param.24) | copy-start | bytes 442372
  4.7 5.2 %copy-start.12 = (bf16[256]{0:T(256)(128)(2,1)S(1)}, bf16[256]{0:T(256)(128)(2,1)}, u32[]{:S(2)}) copy-start(bf16[256]{0:T(256)(128)(2,1)} %param.21) | copy-start | bytes 1540
  4.7 5.2 %copy-start.13 = (bf16[256]{0:T(256)(128)(2,1)S(1)}, bf16[256]{0:T(256)(128)(2,1)}, u32[]{:S(2)}) copy-start(bf16[256]{0:T(256)(128)(2,1)} %param.23) | copy-start | bytes 1540
  419.2 5.2 %copy-start.8 = (f32[48,768]{1,0:T(8,128)S(1)}, f32[48,768]{1,0:T(8,128)}, u32[]{:S(2)}) copy-start(f32[48,768]{1,0:T(8,128)} %get-tuple-element.59) | copy-start | bytes 442372
  419.2 8.6 %copy-start.1 = (bf16[256,1536]{1,0:T(8,128)(2,1)S(1)}, bf16[256,1536]{1,0:T(8,128)(2,1)}, u32[]{:S(2)}) copy-start(bf16[256,1536]{1,0:T(8,128)(2,1)} %get-tuple-element.91) | copy-start | bytes 2359300
  419.2 9.5 %copy-start = (bf16[256,1536]{1,0:T(8,128)(2,1)S(1)}, bf16[256,1536]{1,0:T(8,128)(2,1)}, u32[]{:S(2)}) copy-start(bf16[256,1536]{1,0:T(8,128)(2,1)} %get-tuple-element.92) | copy-start | bytes 2359300
  424.4 5.2 %copy-start.3 = (f32[192,384]{1,0:T(8,128)S(1)}, f32[192,384]{1,0:T(8,128)}, u32[]{:S(2)}) copy-start(f32[192,384]{1,0:T(8,128)} %get-tuple-element.94) | copy-start | bytes 884740
  424.4 6.0 %copy-start.2 = (f32[192,384]{1,0:T(8,128)S(1)}, f32[192,384]{1,0:T(8,128)}, u32[]{:S(2)}) copy-start(f32[192,384]{1,0:T(8,128)} %get-tuple-element.100) | copy-start | bytes 884740

commit v9 on v8

--- a/solution.py
+++ b/solution.py
@@ -23,7 +23,7 @@
 
 
 def front_body(
-    x_ref, turn_ref, mask_ref, bias_ref, query_ref, out_ref, fixed_ref, ffn_ref, cot_ref,
+    x_ref, turn_ref, mask_ref, own_ref, ffn_ref, cot_ref,
     att_all, ffn_all, cot_all, two_all, mid_out, one_out, query_rot, kv_win, lse_out, ctx_out, gain_out,
     att_v, w_v, one_v, q_v, kv_v, ctx_v, mid_v, two_v,
     fill_sem, z_send, z_recv, cot_send, cot_recv, send, recv, keep_sem, w_sem, kv_send, kv_recv, save_sem,
@@ -36,10 +36,12 @@
     by_x, by_y, mate, across = square(d)
     rows = ffn_ref.shape[0]
     half = rows // 2
-    part = query_ref.shape[1]
-    fixed = fixed_ref.shape[1]
+    part = (att_v.shape[1] - own_ref.shape[1]) // (2 * size - 2)
+    fixed = own_ref.shape[1] - 2 * part
     chunk = cot_ref.shape[0]
-    tall = query_ref.shape[0]
+    tall = own_ref.shape[0]
+    query_ref, out_ref = own_ref.at[:, pl.ds(0, part)], own_ref.at[:, pl.ds(part, part)]
+    fixed_ref = own_ref.at[pl.ds(0, rows), pl.ds(2 * part, fixed)]
 
     barrier = pltpu.get_barrier_semaphore()
     for peer in (by_x, by_y, mate):
@@ -298,7 +300,8 @@
         )
         norm(lambda at_r: x_ref[at_r, :].astype(f32), 0, one_v)
         save(one_v, one_out)
-        lin = jnp.dot(one_v[...], w_v[:, lead_w:fixed], preferred_element_type=f32) + bias_ref[0:1, :]
+        lin = jnp.dot(one_v[...], w_v[:, lead_w:fixed], preferred_element_type=f32)
+        lin += own_ref[rows:, 2 * part + lead_w :][0:1, :].astype(f32)
         for g in range(KV_HEADS):
             cols = slice(g * HEAD_DIM, (g + 1) * HEAD_DIM)
             kv_v[2, :, cols] = turned(lin[:, cols]).astype(bf16)
@@ -410,7 +413,7 @@
     work.sort(key=lambda step: step[0])
     total = len(order)
     for i in range(total + 1):
-        while state["begun"] < min(total, i + (lead if i <= last_out else 2 * lead)):
+        while state["begun"] < min(total, i + lead):
             ready(*order[state["begun"]])
             begin(*order[state["begun"]])
             state["begun"] += 1
@@ -457,13 +460,12 @@
 
 
 def front(
-    tokens, turn, mask, kv_bias, query, out, fixed, ffn_w, cot, att_tile=512, ffn_tile=768,
+    tokens, turn, mask, own, ffn_w, cot, fixed_w, att_tile=512, ffn_tile=768,
     collective_id=2, limit=60_000_000,
 ):
-    tall, part = query.shape
-    rows, fixed_w = fixed.shape
+    tall, rows, size, ways = own.shape[0], ffn_w.shape[0], 4, 8
+    part = (own.shape[1] - fixed_w) // 2
     chunk, width = tokens.shape
-    size, ways = 4, 8
     query_w = size * part
     att_cols = fixed_w + 2 * query_w
     pieces = (
@@ -492,7 +494,7 @@
             shape(size * chunk, width), wide(chunk, width), shape(chunk, width), shape(chunk, query_w),
             shape(3, chunk, kv_w), wide(heads, chunk, 1), shape(chunk, query_w), wide(8, width),
         ),
-        in_specs=[vmem] * 9,
+        in_specs=[vmem] * 6,
         out_specs=(hbm,) * 8 + (vmem, hbm, vmem),
         scratch_shapes=[
             vm((tall, att_cols), bf16), vm((8 * rows, att_cols), bf16), vm((chunk, width), bf16),
@@ -510,7 +512,7 @@
             transcendentals=0,
         ),
         name="front",
-    )(tokens, turn, mask, kv_bias, query, out, fixed, ffn_w, cot)
+    )(tokens, turn, mask, own, ffn_w, cot)
 
 
 def line_order(z, s):
@@ -842,6 +844,7 @@
     ring, n_sum, n_last = x_land.shape[0], core_sum.shape[0], x_last.shape[0]
     n_grad, n_mate = grad.shape[0], mate_land.shape[0]
     total = n_ffn + n_att
+    cut = n_ffn - 1
     chunk, width = mixed_out.shape
     share = block // size
     part_w = wide // 2
@@ -873,6 +876,12 @@
     )
     loads = [pltpu.make_async_copy(src, dst, in_sem.at[k]) for k, (src, dst) in enumerate(plan)]
 
+    def is_ffn(i):
+        return jnp.logical_or(i < cut, i == total - 1)
+
+    def ffn_piece(i):
+        return i - (i // (total - 1)) * n_att
+
     def right_load(i, what):
         cols = pl.ds(pl.multiple_of((i % n_f) * wide, 128), wide)
         for m, ref in enumerate((hid_ref, dg_ref, du_ref)):
@@ -991,14 +1000,16 @@
         def _():
             mate_copy(i - n_grad).wait_send()
 
-        @pl.when(i + 1 < n_ffn)
+        @pl.when(is_ffn(i + 1))
         def _():
-            right_load(i + 1, "start")
+            right_load(ffn_piece(i + 1), "start")
 
         dims = (((0,), (0,)), ((), ()))
 
-        @pl.when(i < n_ffn)
+        @pl.when(is_ffn(i))
         def _():
+            f = ffn_piece(i)
+
             @pl.when(i == 0)
             def _():
                 lefts[0].wait()
@@ -1008,21 +1019,21 @@
                 lefts[1].start()
                 lefts[1].wait()
 
-            right_load(i, "wait")
+            right_load(f, "wait")
 
             def rows(k, carry):
                 at = pl.ds(pl.multiple_of(k * 2 * block, 128), 2 * block)
                 value = lax.dot_general(
-                    left_v[:, at], right_v[i % 2], dims, preferred_element_type=f32
+                    left_v[:, at], right_v[f % 2], dims, preferred_element_type=f32
                 )
                 grad[i % n_grad, k] = value.astype(bf16).reshape(2, block, wide)
                 return carry
 
             lax.fori_loop(0, 4, rows, 0)
 
-        @pl.when(jnp.logical_and(i >= n_ffn, i < total))
+        @pl.when(jnp.logical_and(i >= cut, i < total - 1))
         def _():
-            a = i - n_ffn
+            a = i - cut
             cols = pl.ds(pl.multiple_of(a * wide, 128), wide)
 
             def rows(k, carry):
@@ -1087,19 +1098,21 @@
         top = own[:half].astype(f32) + x_land[i % ring, 0].astype(f32) + y_last[i % n_last].astype(f32)
         low = own[half:].astype(f32) + y_land[i % ring, 0].astype(f32) + x_last[i % n_last].astype(f32)
 
-        @pl.when(i < n_ffn)
+        @pl.when(is_ffn(i))
         def _():
-            @pl.when(i >= 2)
+            f = ffn_piece(i)
+
+            @pl.when(f >= 2)
             def _():
-                stage_copy(i - 2).wait()
-
-            stage[i % 2, :half] = top
-            stage[i % 2, half:] = low
-            stage_copy(i).start()
-
-        @pl.when(i >= n_ffn)
+                stage_copy(f - 2).wait()
+
+            stage[f % 2, :half] = top
+            stage[f % 2, half:] = low
+            stage_copy(f).start()
+
+        @pl.when(jnp.logical_not(is_ffn(i)))
         def _():
-            a = i - n_ffn
+            a = i - cut
             fin[a, :half] = top.astype(bf16)
             fin[a, half:] = low.astype(bf16)
             z_sends(a, "start")
@@ -1260,7 +1273,7 @@
         hop_copy(2).wait_recv()
         small_out[...] = small_next[2] + small_hop[2]
 
-    span = n_ffn - 1
+    span = cut - 1
     quarter = heads // 4
 
     def at_turn(k):
@@ -1464,13 +1477,15 @@
     size = lax.axis_size("tensor")
     fixed_w = jnp.concatenate([gains_w, kv_w], axis=1)
     if lax.axis_size("dp") == 8 and size == 4:
-        tall_query = jnp.concatenate([query_w, jnp.pad(query_b[None, :], ((0, 15), (0, 0)))], axis=0)
-        tall_out = jnp.pad(out_w, ((0, 16), (0, 0)))
+        last = jnp.concatenate([query_b, jnp.zeros((query_b.shape[0] + gains_w.shape[1],), bf16), kv_b])
+        own = jnp.concatenate(
+            [jnp.concatenate([query_w, out_w, fixed_w], axis=1), jnp.pad(last[None, :], ((0, 15), (0, 0)))], axis=0
+        )
         turn = jnp.stack(
             [jnp.concatenate([cosine, cosine], axis=1), jnp.concatenate([-sine, sine], axis=1)]
         )
         att_w, ffn_all, cot_rows, two, middle, one, query_rot, kv_win, lse, context, gains = front(
-            tokens, turn, mask, kv_b[None, :], tall_query, tall_out, fixed_w, ffn_w, cotangent
+            tokens, turn, mask, own, ffn_w, cotangent, fixed_w.shape[1]
         )
         kv_win = kv_win.reshape(3 * rows, kv_w.shape[1])
         return att_w, ffn_all, cot_rows, two, middle, one, query_rot, kv_win, lse, context, gains
@@ -1489,7 +1504,7 @@
     inverse = lax.rsqrt(jnp.mean(inputs * inputs, axis=-1, keepdims=True) + EPSILON)
     one = (inputs * inverse * gains[0]).astype(bf16)
     lin = jnp.dot(one, att_w[:, ahead : ahead + qkv_width], preferred_element_type=f32)
-    lin = lin + jnp.concatenate([kv_b, full_query_b])
+    lin = lin + jnp.concatenate([kv_b.astype(f32), full_query_b])
     cos_h, sin_h = cosine[:, None, :], sine[:, None, :]
     query_rot = rotate(lin[:, 2 * kv_width :].reshape(rows, heads, HEAD_DIM), cos_h, sin_h).astype(bf16)
     key_rot = rotate(lin[:, :kv_width].reshape(rows, KV_HEADS, HEAD_DIM), cos_h, sin_h).astype(bf16)
@@ -1659,7 +1674,7 @@
         att_w, ffn_w, cot_rows, normed_two, middle, normed_one, query_rot, kv_win, lse, context, gains,
     ) = attention_branch(
         tokens, cosine, sine, mask, gains_w, query_w, query_b, jnp.concatenate([key_w, value_w], axis=1),
-        jnp.concatenate([key_b, value_b]).astype(f32), out_w, joined_units(gate_w, up_w, down_w), cotangent,
+        jnp.concatenate([key_b, value_b]), out_w, joined_units(gate_w, up_w, down_w), cotangent,
     )
     rows_two, hidden_low, d_gate, d_upper, ffn_part, d_normed_two = ffn(
         normed_two, cot_rows, ffn_w

time: 431 us -> 427 us (level)
  Pallas kernels: 409 us -> 402 us
    pallas_call x1, Pallas kernels: 159 us -> 147 us  [front(): pl.pallas_call(functools.partial(front_body, pieces=pieces, order=order,...]
where the time goes in v9:
time: 427 us; the launch traced here: 423 us
  Pallas kernels  402 us (94%)
  local copies, waits for them, and re-layouts  15.1 us (4%)
  other arithmetic  4.96 us (1%)
    pallas_call x1, Pallas kernels, back(): pl.pallas_call(functools.partial(back_body, n_f=n_f, wide=wide), out_shap...  166 us
    pallas_call x1, Pallas kernels, front(): pl.pallas_call(functools.partial(front_body, pieces=pieces, order=order,...  147 us
    pallas_call x1, Pallas kernels, ffn(): pl.pallas_call(functools.partial(ffn_body, axis=axis, ft=ft, nt=nt), out_...  88.7 us

profile of v9, /device:TPU:26, one launch (start us, length us, event | category | flops | bytes accessed | tf_op | source)
XLA Modules:
  0.0 423.4 jit_solution(2173286157651150774)
XLA Ops:
  0.6 0.0 copy-start.7
  0.7 0.0 copy-start.14
  0.7 0.0 copy-start.8
  0.7 0.0 copy-start.9
  0.7 0.0 copy-start.11
  0.7 0.0 copy-start.13
  0.7 0.0 copy-start.12
  0.7 0.0 copy-start.2
  0.7 0.0 copy-start.1
  0.7 0.0 copy-start
  0.8 0.5 multiply_cosine_fusion
  1.3 0.1 maximum_bitcast_fusion
  1.5 0.7 pad_maximum_fusion.turn_ref
  2.2 0.8 pad_dynamic-slice_fusion
  2.9 0.7 constant_dynamic-slice_fusion.3
  3.6 1.1 fusion.8.mask_ref
  4.7 0.9 constant_dynamic-update-slice_fusion.3
  5.7 0.0 copy-done.7
  5.7 0.0 copy-done.14
  5.7 0.7 stack.25
  6.4 0.1 copy.31
  6.6 0.0 copy-done.8
  6.6 0.0 copy-done.9
  6.6 0.0 copy-done.11
  6.7 0.0 copy-done.13
  6.7 0.0 copy-done.12
  6.7 0.9 fusion.9.own_ref
  7.6 0.0 copy-done.2
  7.6 0.0 copy-done.1
  7.6 0.0 copy-done
  7.6 1.6 fusion.5.ffn_ref
  9.2 147.3 %front.1 = (bf16[1536,3712]{1,0:T(8,128)(2,1)}, bf16[1536,6912]{1,0:T(8,128)(2,1)}, bf16[1024,1536]{1,0:T(8,128)(2,1)}, bf16[1024,1536]{1,0:T(8,128)(2,1)}, f32[...) custom-call(bf16[256,1536]{1,0:T(8,128)(2,1)} %x_ref.3, ...), custom_call_target="tpu_custom_call" | custom-call | flops 2919235584 | bytes 40796160 | tf_op jit(solution)/shard_map/front/pallas_call | solution.py:489
  156.5 88.7 %ffn.1 = (bf16[1024,1536]{1,0:T(8,128)(2,1)}, bf16[1024,2304]{1,0:T(8,128)(2,1)}, bf16[1024,2304]{1,0:T(8,128)(2,1)}, bf16[1024,2304]{1,0:T(8,128)(2,1)}, bf16[1...) custom-call(bf16[1024,1536]{1,0:T(8,128)(2,1)} %get-tuple-element.38.two_ref, ...), custom_call_target="tpu_custom_call" | custom-call | flops 43486543872 | bytes 47185920 | tf_op jit(solution)/shard_map/ffn/pallas_call | solution.py:794
  245.2 166.4 %back.1 = (f32[192,6912]{1,0:T(8,128)}, f32[192,384]{1,0:T(8,128)}, f32[192,384]{1,0:T(8,128)}, f32[48,768]{1,0:T(8,128)}, bf16[256,1536]{1,0:T(8,128)(2,1)}, /*...) custom-call(bf16[1024,1536]{1,0:T(8,128)(2,1)} %get-tuple-element.41.two_ref, bf16[1024,1536]{1,0:T(8,128)(2,1)} %get-tuple-element.39.cot_ref, ...), custom_call_target="tpu_custom_call" | custom-call | flops 21743271936 | bytes 18874368 | tf_op jit(solution)/shard_map/back/pallas_call | solution.py:1383
  411.6 0.0 copy-start.10
  411.6 0.0 copy-start.4
  411.6 0.0 copy-start.3
  411.6 5.2 %fusion.14 = (f32[192,2240]{1,0:T(8,128)}, f32[192,2240]{1,0:T(8,128)}, f32[192,2240]{1,0:T(8,128)}) fusion(f32[192,6912]{1,0:T(8,128)} %get-tuple-element.61), kind=kLoop, calls=%fused_computation.40 | loop fusion | bytes 10321920 | tf_op jit(solution)/shard_map/slice | solution.py:1707
  416.8 0.0 copy-done.10
  416.8 0.6 fusion.16
  417.4 0.9 slice.38
  418.3 0.6 fusion.13
  418.9 1.3 fusion.15
  420.2 0.0 copy-done.4
  420.2 0.9 copy.40
  421.1 0.9 copy.41
  422.0 0.7 copy.42
  422.7 0.7 copy.43
  (17 shorter events, 0.1 us)
Async XLA Ops:
  0.6 5.0 %copy-start.7 = (bf16[192,384]{1,0:T(8,128)(2,1)S(1)}, bf16[192,384]{1,0:T(8,128)(2,1)}, u32[]{:S(2)}) copy-start(bf16[192,384]{1,0:T(8,128)(2,1)} %param.24) | copy-start | bytes 442372
  0.7 5.0 %copy-start.14 = (bf16[192]{0:T(256)(128)(2,1)S(1)}, bf16[192]{0:T(256)(128)(2,1)}, u32[]{:S(2)}) copy-start(bf16[192]{0:T(256)(128)(2,1)} %param.17) | copy-start | bytes 1156
  0.7 5.9 %copy-start.8 = (bf16[192,256]{1,0:T(8,128)(2,1)S(1)}, bf16[192,256]{1,0:T(8,128)(2,1)}, u32[]{:S(2)}) copy-start(bf16[192,256]{1,0:T(8,128)(2,1)} %param.20) | copy-start | bytes 294916
  0.7 5.9 %copy-start.9 = (bf16[192,256]{1,0:T(8,128)(2,1)S(1)}, bf16[192,256]{1,0:T(8,128)(2,1)}, u32[]{:S(2)}) copy-start(bf16[192,256]{1,0:T(8,128)(2,1)} %param.22) | copy-start | bytes 294916
  0.7 6.0 %copy-start.11 = (bf16[384]{0:T(512)(128)(2,1)S(1)}, bf16[384]{0:T(512)(128)(2,1)}, u32[]{:S(2)}) copy-start(bf16[384]{0:T(512)(128)(2,1)} %param.19) | copy-start | bytes 2308
  0.7 6.0 %copy-start.13 = (bf16[256]{0:T(256)(128)(2,1)S(1)}, bf16[256]{0:T(256)(128)(2,1)}, u32[]{:S(2)}) copy-start(bf16[256]{0:T(256)(128)(2,1)} %param.21) | copy-start | bytes 1540
  0.7 6.0 %copy-start.12 = (bf16[256]{0:T(256)(128)(2,1)S(1)}, bf16[256]{0:T(256)(128)(2,1)}, u32[]{:S(2)}) copy-start(bf16[256]{0:T(256)(128)(2,1)} %param.23) | copy-start | bytes 1540
  0.7 6.9 %copy-start.2 = (bf16[192,2240]{1,0:T(8,128)(2,1)S(1)}, bf16[192,2240]{1,0:T(8,128)(2,1)}, u32[]{:S(2)}) copy-start(bf16[192,2240]{1,0:T(8,128)(2,1)} %param.26) | copy-start | bytes 2580484
  0.7 6.8 %copy-start.1 = (bf16[192,2240]{1,0:T(8,128)(2,1)S(1)}, bf16[192,2240]{1,0:T(8,128)(2,1)}, u32[]{:S(2)}) copy-start(bf16[192,2240]{1,0:T(8,128)(2,1)} %param.27) | copy-start | bytes 2580484
  0.7 6.8 %copy-start = (bf16[192,2240]{1,0:T(8,128)(2,1)S(1)}, bf16[192,2240]{1,0:T(8,128)(2,1)}, u32[]{:S(2)}) copy-start(bf16[192,2240]{1,0:T(8,128)(2,1)} %param.28) | copy-start | bytes 2580484
  411.6 5.2 %copy-start.10 = (f32[48,768]{1,0:T(8,128)S(1)}, f32[48,768]{1,0:T(8,128)}, u32[]{:S(2)}) copy-start(f32[48,768]{1,0:T(8,128)} %get-tuple-element.59) | copy-start | bytes 442372
  411.6 8.6 %copy-start.4 = (bf16[256,1536]{1,0:T(8,128)(2,1)S(1)}, bf16[256,1536]{1,0:T(8,128)(2,1)}, u32[]{:S(2)}) copy-start(bf16[256,1536]{1,0:T(8,128)(2,1)} %get-tuple-element.91) | copy-start | bytes 2359300
  411.6 9.5 %copy-start.3 = (bf16[256,1536]{1,0:T(8,128)(2,1)S(1)}, bf16[256,1536]{1,0:T(8,128)(2,1)}, u32[]{:S(2)}) copy-start(bf16[256,1536]{1,0:T(8,128)(2,1)} %get-tuple-element.92) | copy-start | bytes 2359300
  416.8 5.2 %copy-start.6 = (f32[192,384]{1,0:T(8,128)S(1)}, f32[192,384]{1,0:T(8,128)}, u32[]{:S(2)}) copy-start(f32[192,384]{1,0:T(8,128)} %get-tuple-element.94) | copy-start | bytes 884740
  416.8 6.0 %copy-start.5 = (f32[192,384]{1,0:T(8,128)S(1)}, f32[192,384]{1,0:T(8,128)}, u32[]{:S(2)}) copy-start(f32[192,384]{1,0:T(8,128)} %get-tuple-element.100) | copy-start | bytes 884740
